TPU v7x, 8 devices: a whole 2x2x1 slice. The times are simulated.
8 devices in a mesh: dp: 1 (over z), ing: 2 (over y), grp: 4 (over x, core).
Axes of the slice: x: 2, y: 2, z: 1, core: 2. Of those that a mesh axis runs over, the one named last changes fastest.
Arguments:
- x_tokens: bfloat16 [4096, 1536], P(('dp', 'grp', 'ing'))
- expert_ids: int32 [4096, 6], P(('dp', 'grp', 'ing'))
- gate_vals: float32 [4096, 6], P(('dp', 'grp', 'ing'))
- y_grad: bfloat16 [4096, 1536], P(('dp', 'grp', 'ing'))
- w_gate: bfloat16 [64, 1536, 512], P(('grp', 'ing'))
- w_up: bfloat16 [64, 1536, 512], P(('grp', 'ing'))
- w_down: bfloat16 [64, 512, 1536], P(('grp', 'ing'))
Outputs:
- output 1: bfloat16 [4096, 1536], P(('dp', 'grp', 'ing'))
- output 2: bfloat16 [4096, 1536], P(('dp', 'grp', 'ing'))
- output 3: float32 [64, 1536, 512], P(('dp', 'grp', 'ing'))
- output 4: float32 [64, 1536, 512], P(('dp', 'grp', 'ing'))
- output 5: float32 [64, 512, 1536], P(('dp', 'grp', 'ing'))
All inputs are finite; a program needn't handle non-finite values.
Results may differ from a plain program's by a relative error of at most 0.00959982.
Values are sent between devices in bfloat16 or wider.
A program may use at most 1 GiB of HBM per device.

v0:
```python
import functools

import jax
import jax.numpy as jnp
from jax import lax
from jax.experimental import pallas as pl
from jax.experimental.pallas import tpu as pltpu
from jax.sharding import PartitionSpec as P


BF = jnp.bfloat16
F32 = jnp.float32
PAIR = 2

KERNEL_ORDER = (('f', 2), ('f', 0), ('b', 2), ('f', 1), ('b', 1), ('b', 0), ('f', 3), ('b', 3))


def dot(a, b):
    return lax.dot_general(a, b, (((1,), (0,)), ((), ())), preferred_element_type=F32)


def dot_bt(a, b):
    return lax.dot_general(a, b, (((1,), (1,)), ((), ())), preferred_element_type=F32)


def dot_at(a, b):
    return lax.dot_general(a, b, (((0,), (0,)), ((), ())), preferred_element_type=F32)


def pick_rows(tok_col, rows_ref):
    tokens = rows_ref.shape[0]
    lanes = lax.broadcasted_iota(jnp.int32, (tok_col.shape[0], tokens), 1)
    one_hot = jnp.where(tok_col == lanes, 1.0, 0.0).astype(BF)
    return dot(one_hot, rows_ref[...])


def store_by_expert(dst_ref, rows, cap):
    for e in range(dst_ref.shape[0]):
        dst_ref[e] = jnp.concatenate([r[e * cap:(e + 1) * cap] for r in rows], axis=0).astype(BF)


def keep_rows(dst_ref, rows, e, cap, pad):
    zeros = jnp.zeros((pad - cap, rows.shape[1]), F32)
    for s in range(PAIR):
        padded = jnp.concatenate([rows[s * cap:(s + 1) * cap], zeros], axis=0).astype(BF)
        dst_ref[s, pl.ds(pl.multiple_of(e * pad, pad), pad), :] = padded


def fwd_kernel(cap, pad, xa_ref, xb_ref, tok_ref, q_ref, g_ref, w1_ref, w3_ref, w2_ref, xg_ref, a_ref, u_ref, v_ref, p0_ref, p1_ref, xg_scr, o_scr):
    e = pl.program_id(0)

    @pl.when(e == 0)
    def _():
        store_by_expert(xg_scr, [pick_rows(tok_ref[s], r) for s, r in enumerate((xa_ref, xb_ref))], cap)

    xg = xg_scr[e]
    xg_ref[0] = xg
    h1 = dot(xg, w1_ref[0])
    h3 = dot(xg, w3_ref[0])
    sig = jax.nn.sigmoid(h1)
    silu = h1 * sig
    act = (silu * h3).astype(BF)
    a_ref[0] = act
    u_ref[0] = h3 * (sig * (1.0 + h1 * (1.0 - sig)))
    v_ref[0] = silu
    keep_rows(o_scr, dot(act, w2_ref[0]), e, cap, pad)

    @pl.when(e == pl.num_programs(0) - 1)
    def _():
        for s, p_ref in enumerate((p0_ref, p1_ref)):
            slots = lax.broadcasted_iota(jnp.int32, (p_ref.shape[0], q_ref.shape[2]), 0)
            hit = q_ref[s] == slots
            rest = g_ref[s]
            total = None
            for _ in range(3):
                part = rest.astype(BF)
                term = dot(jnp.where(hit, part.astype(F32), 0.0).astype(BF), o_scr[s])
                total = term if total is None else total + term
                rest = rest - part.astype(F32)
            p_ref[...] = total


def bwd_kernel(cap, pad, dya_ref, dyb_ref, tok_ref, gcol_ref, q_ref, w1_ref, w3_ref, w2_ref, u_ref, v_ref, d_ref, dh1_ref, dh3_ref, p0_ref, p1_ref, d_scr, r_scr):
    e = pl.program_id(0)

    @pl.when(e == 0)
    def _():
        store_by_expert(d_scr, [gcol_ref[s] * pick_rows(tok_ref[s], r) for s, r in enumerate((dya_ref, dyb_ref))], cap)

    d = d_scr[e]
    d_ref[0] = d
    da = dot_bt(d, w2_ref[0])
    dh1 = (da * u_ref[0]).astype(BF)
    dh3 = (da * v_ref[0]).astype(BF)
    dh1_ref[0] = dh1
    dh3_ref[0] = dh3
    keep_rows(r_scr, dot_bt(dh1, w1_ref[0]) + dot_bt(dh3, w3_ref[0]), e, cap, pad)

    @pl.when(e == pl.num_programs(0) - 1)
    def _():
        for s, p_ref in enumerate((p0_ref, p1_ref)):
            slots = lax.broadcasted_iota(jnp.int32, (p_ref.shape[0], q_ref.shape[2]), 0)
            p_ref[...] = dot(jnp.where(q_ref[s] == slots, 1.0, 0.0).astype(BF), r_scr[s])


def whole(shape):
    return pl.BlockSpec(shape, lambda e: (0,) * len(shape))


def per_expert(shape):
    return pl.BlockSpec((1,) + shape[1:], lambda e: (e,) + (0,) * (len(shape) - 1))


def of_pair(pair, shape):
    return pl.BlockSpec((PAIR,) + shape[1:], lambda e: (pair,) + (0,) * (len(shape) - 1))


def params():
    return pltpu.CompilerParams(dimension_semantics=("arbitrary",), vmem_limit_bytes=60 * 1024 * 1024)


def forward_pair(pair, xa, xb, tok_col, q_row, g_row, w1, w3, w2, cap, pad, grp_cap):
    experts, hidden, ff = w1.shape
    rows = PAIR * cap
    outs = [((experts, rows, hidden), BF), ((experts, rows, ff), BF), ((experts, rows, ff), F32), ((experts, rows, ff), F32), ((grp_cap, hidden), F32), ((grp_cap, hidden), F32)]
    return pl.pallas_call(
        functools.partial(fwd_kernel, cap, pad),
        grid=(experts,),
        in_specs=[whole(xa.shape), whole(xb.shape), of_pair(pair, tok_col.shape), of_pair(pair, q_row.shape), of_pair(pair, g_row.shape), per_expert(w1.shape), per_expert(w3.shape), per_expert(w2.shape)],
        out_specs=[per_expert(s) if len(s) == 3 else whole(s) for s, _ in outs],
        out_shape=[jax.ShapeDtypeStruct(s, t) for s, t in outs],
        scratch_shapes=[pltpu.VMEM((experts, rows, hidden), BF), pltpu.VMEM((PAIR, experts * pad, hidden), BF)],
        compiler_params=params(),
        cost_estimate=pl.CostEstimate(flops=14 * 10**9, bytes_accessed=50 * 10**6, transcendentals=0),
        name="fwd_pair",
    )(xa, xb, tok_col, q_row, g_row, w1, w3, w2)


def backward_pair(pair, dya, dyb, tok_col, g_col, q_row, w1, w3, w2, u, v, cap, pad, grp_cap):
    experts, hidden, ff = w1.shape
    rows = PAIR * cap
    outs = [((experts, rows, hidden), BF), ((experts, rows, ff), BF), ((experts, rows, ff), BF), ((grp_cap, hidden), F32), ((grp_cap, hidden), F32)]
    return pl.pallas_call(
        functools.partial(bwd_kernel, cap, pad),
        grid=(experts,),
        in_specs=[whole(dya.shape), whole(dyb.shape), of_pair(pair, tok_col.shape), of_pair(pair, g_col.shape), of_pair(pair, q_row.shape), per_expert(w1.shape), per_expert(w3.shape), per_expert(w2.shape), per_expert(u.shape), per_expert(v.shape)],
        out_specs=[per_expert(s) if len(s) == 3 else whole(s) for s, _ in outs],
        out_shape=[jax.ShapeDtypeStruct(s, t) for s, t in outs],
        scratch_shapes=[pltpu.VMEM((experts, rows, hidden), BF), pltpu.VMEM((PAIR, experts * pad, hidden), BF)],
        compiler_params=params(),
        cost_estimate=pl.CostEstimate(flops=14 * 10**9, bytes_accessed=50 * 10**6, transcendentals=0),
        name="bwd_pair",
    )(dya, dyb, tok_col, g_col, q_row, w1, w3, w2, u, v)


def dw_kernel(chunks, *refs):
    ins, (g1_ref, g3_ref, g2_ref) = refs[:5 * chunks], refs[5 * chunks:]

    def joined(k):
        return jnp.concatenate([ins[k * chunks + c][0] for c in range(chunks)], axis=0)

    x, a, d, dh1, dh3 = (joined(k) for k in range(5))
    g1_ref[0] = dot_at(x, dh1)
    g3_ref[0] = dot_at(x, dh3)
    g2_ref[0] = dot_at(a, d)


def weight_grads(xs, acts, ds, dh1s, dh3s):
    chunks = len(xs)
    experts, _, hidden = xs[0].shape
    ff = acts[0].shape[2]
    args = [*xs, *acts, *ds, *dh1s, *dh3s]
    outs = [(experts, hidden, ff), (experts, hidden, ff), (experts, ff, hidden)]
    return pl.pallas_call(
        functools.partial(dw_kernel, chunks),
        grid=(experts,),
        in_specs=[per_expert(a.shape) for a in args],
        out_specs=[per_expert(s) for s in outs],
        out_shape=[jax.ShapeDtypeStruct(s, F32) for s in outs],
        compiler_params=params(),
        cost_estimate=pl.CostEstimate(flops=25 * 10**9, bytes_accessed=120 * 10**6, transcendentals=0),
        name="weight_grads",
    )(*args)


def final_kernel(groups, *refs):
    q_ref, out_ref = refs[groups], refs[groups + 1]
    total = None
    for h in range(groups):
        lanes = lax.broadcasted_iota(jnp.int32, (out_ref.shape[0], refs[h].shape[0]), 1)
        one_hot = jnp.where(q_ref[:, h:h + 1] == lanes, 1.0, 0.0).astype(BF)
        term = dot(one_hot, refs[h][...])
        total = term if total is None else total + term
    out_ref[...] = total.astype(BF)


def collect(parts, q_cols):
    groups = len(parts)
    tokens = q_cols.shape[0]
    hidden = parts[0].shape[1]
    block = tokens // 4
    return pl.pallas_call(
        functools.partial(final_kernel, groups),
        grid=(4,),
        in_specs=[whole(p.shape) for p in parts] + [pl.BlockSpec((block, groups), lambda e: (e, 0))],
        out_specs=pl.BlockSpec((block, hidden), lambda e: (e, 0)),
        out_shape=jax.ShapeDtypeStruct((tokens, hidden), BF),
        compiler_params=params(),
        cost_estimate=pl.CostEstimate(flops=2 * 10**9, bytes_accessed=5 * 10**6, transcendentals=0),
        name="collect",
    )(*parts, q_cols)


def after(earlier, value):
    return lax.optimization_barrier((earlier, value))[1]


def slot_tables(ids, gates, first_exp, experts, group, per_group, cap):
    sources, _, tokens = ids.shape
    eq = ids[:, None] == (first_exp + jnp.arange(experts))[None, :, None, None]
    hit = jnp.any(eq, axis=2)
    gate = jnp.sum(jnp.where(eq, gates[:, None], 0.0), axis=2)
    member = jnp.any(ids // per_group == group, axis=1, keepdims=True)
    pos = count_earlier(jnp.concatenate([hit, member], axis=1).reshape(sources * (experts + 1), tokens))
    pos = pos.reshape(sources, experts + 1, tokens)
    exp_pos, grp_pos = pos[:, :experts], pos[:, experts:]
    taken = hit[:, :, None, :] & (exp_pos[:, :, None, :] == jnp.arange(cap, dtype=F32)[None, None, :, None])
    numbers = jnp.arange(1, tokens + 1, dtype=F32)[None, None, None, :]
    tok = jnp.sum(jnp.where(taken, numbers, 0.0), axis=3) - 1.0
    place = jnp.sum(jnp.where(taken, grp_pos[:, :, None, :] + 1.0, 0.0), axis=3) - 1.0
    weight = jnp.sum(jnp.where(taken, gate[:, :, None, :], 0.0), axis=3)
    return tok, place, weight


def count_earlier(marks):
    tokens = marks.shape[1]
    earlier = (jnp.arange(tokens)[:, None] < jnp.arange(tokens)[None, :]).astype(BF)
    return jnp.dot(marks.astype(BF), earlier, preferred_element_type=F32)


def solution(mesh):
    groups = mesh.shape['grp']
    inner = mesh.shape['ing']
    devices = groups * inner
    tok_spec = P(('dp', 'grp', 'ing'), None)
    weight_spec = P(('grp', 'ing'), None, None)
    grad_spec = P(('dp', 'grp', 'ing'), None, None)

    def hop_y(a):
        return lax.ppermute(a, 'ing', [(0, 1), (1, 0)])

    def hop_g(a, bits):
        return lax.ppermute(a, 'grp', [(g, g ^ bits) for g in range(groups)])

    def device_fn(x_loc, ids_loc, gates_loc, dy_loc, w1, w3, w2):
        tokens, _ = x_loc.shape
        top_k = ids_loc.shape[1]
        experts = w1.shape[0]
        num_exp = experts * devices
        grp_cap = tokens * 2 // groups
        cap = 3 * tokens * top_k // (2 * num_exp)
        pad = -(-cap // 16) * 16
        grp, ing = lax.axis_index('grp'), lax.axis_index('ing')

        per_group = experts * inner
        packed = jnp.concatenate([ids_loc.T.astype(F32), gates_loc.T], axis=0)
        routing = lax.all_gather(packed, ('grp', 'ing'))
        order = [((grp ^ (2 * dx + dc)) * inner + (ing ^ dy)) for dx, dy in ((0, 1), (1, 1), (0, 0), (1, 0)) for dc in (0, 1)]

        x_loc, dy_loc, routing = lax.optimization_barrier((x_loc, dy_loc, routing))
        x_far = hop_y(x_loc)
        x_near_c = hop_g(x_loc, 1)
        x_near_x = hop_g(x_loc, 2)
        dy_far = hop_y(dy_loc)
        dy_near_c = hop_g(dy_loc, 1)
        x_far_c, x_far_x = hop_g(x_far, 1), hop_g(x_far, 2)
        x_near_xc, x_far_xc = hop_g(x_near_x, 1), hop_g(x_far_x, 1)
        dy_far_c, dy_far_x = hop_g(dy_far, 1), hop_g(dy_far, 2)
        dy_far_xc = hop_g(dy_far_x, 1)
        dy_near_x = hop_g(after(x_far_x, dy_loc), 2)
        dy_near_xc = hop_g(dy_near_x, 1)
        x_pairs = [(x_far, x_far_c), (x_far_x, x_far_xc), (x_loc, x_near_c), (x_near_x, x_near_xc)]
        dy_pairs = [(dy_far, dy_far_c), (dy_far_x, dy_far_xc), (dy_loc, dy_near_c), (dy_near_x, dy_near_xc)]

        routing = jnp.take(routing, jnp.stack(order), axis=0)
        ids_rel, gates_rel = routing[:, :top_k].astype(jnp.int32), routing[:, top_k:]
        tok_rel, place_rel, weight_rel = slot_tables(ids_rel, gates_rel, (grp * inner + ing) * experts, experts, grp, per_group, cap)
        own_groups = ids_loc.T[None] // per_group == (grp ^ jnp.arange(groups))[:, None, None]
        own_member = jnp.any(own_groups, axis=1)
        q_cols = jnp.where(own_member, count_earlier(own_member), -1.0).astype(jnp.int32).T
        slots = experts * cap
        tok_cols = tok_rel.astype(jnp.int32).reshape(devices, slots, 1)
        g_cols = weight_rel.reshape(devices, slots, 1)
        spare = ((0, 0), (0, 0), (0, pad - cap))
        q_rows = jnp.pad(place_rel, spare, constant_values=-1.0).astype(jnp.int32).reshape(devices, 1, experts * pad)
        g_rows = jnp.pad(weight_rel, spare).reshape(devices, 1, experts * pad)

        fwd, bwd = [None] * 4, [None] * 4
        last = None
        for step, c in KERNEL_ORDER:
            rows = x_pairs[c] if step == 'f' else dy_pairs[c]
            places = q_rows if last is None else after(last, q_rows)
            if step == 'f':
                fwd[c] = forward_pair(c, *rows, tok_cols, places, g_rows, w1, w3, w2, cap, pad, grp_cap)
                last = fwd[c][4]
            else:
                bwd[c] = backward_pair(c, *rows, tok_cols, g_cols, places, w1, w3, w2, fwd[c][2], fwd[c][3], cap, pad, grp_cap)
                last = bwd[c][3]

        grads = weight_grads([f[0] for f in fwd], [f[1] for f in fwd], [b[0] for b in bwd], [b[1] for b in bwd], [b[2] for b in bwd])

        def combine(results):
            sums = []
            for far, near in ((0, 2), (1, 3)):
                for s in (0, 1):
                    sums.append((results[near][s] + hop_y(results[far][s])).astype(BF))
            return [sums[0]] + [hop_g(sums[k], k) for k in (1, 2, 3)]

        y_out = collect(combine([f[4:6] for f in fwd]), q_cols)
        dx_out = collect(combine([b[3:5] for b in bwd]), q_cols)
        return y_out, dx_out, grads[0], grads[1], grads[2]

    return jax.shard_map(device_fn, mesh=mesh, in_specs=(tok_spec, tok_spec, tok_spec, tok_spec, weight_spec, weight_spec, weight_spec), out_specs=(tok_spec, tok_spec, grad_spec, grad_spec, grad_spec), check_vma=False)
```

profile of v0, /device:TPU:0, one launch (start us, length us, event | category | flops | bytes accessed | tf_op | source)
XLA Modules:
  0.0 498.7 jit_solution(17045598767136620831)
XLA Ops:
  0.6 0.7 bitcast_convert_fusion
  1.4 0.7 maximum_bitcast_fusion
  2.1 14.4 %all-gather.1 = f32[8,12,512]{2,1,0:T(8,128)S(1)} all-gather(f32[1,12,512]{2,1,0:T(8,128)S(1)} %maximum_bitcast_fusion), channel_id=2, replica_groups=mesh['dp'=1,'ing'=2,'grp'=4] {'grp','ing'}, dimensions={0}, use_global_device_ids=true | all-gather | bytes 221184 | tf_op jit(solution)/shard_map/all_gather | solution.py:267
  17.0 1.5 collective-permute-start.1
  19.1 0.7 add_select_fusion.1
  20.0 0.6 gather_fusion
  21.6 7.4 %select_reduce_fusion = (f32[8,8,72]{2,1,0:T(8,128)S(1)}, f32[8,8,72]{2,1,0:T(8,128)S(1)}, f32[8,8,72]{2,1,0:T(8,128)S(1)}) fusion(f32[8,8,512]{2,1,0:T(8,128)S(1)} %fusion.6, f32[8,8,512]{2,1,0:T(8,128)S(1)} %slice.19, pred[8,8,512]{2,1,0:T(8,128)(4,1)S(1)} %compare_reduce_fusion, f32[8,512]{1,0:T(8,128)S(1)} %bitcast.48, f32[512]{0:T(512)S(1)} %iota_add_fusion), kind=kLoop, calls=%fused_computation.1 | loop fusion | flops 18860544 | bytes 368640 | tf_op jit(solution)/shard_map/reduce_sum | solution.py:231
  29.1 25.5 %collective-permute-done.1.xa_ref = bf16[512,1536]{1,0:T(8,128)(2,1)} collective-permute-done((bf16[512,1536]{1,0:T(8,128)(2,1)}, bf16[512,1536]{1,0:T(8,128)(2,1)}, u32[]{:S(2)}, u32[]{:S(2)}) %collective-permute-start.1) | collective-permute-done | bytes 1572896 | tf_op jit(solution)/shard_map/ppermute | solution.py:250
  54.6 1.5 collective-permute-start.12
  56.3 0.7 reshape.434.q_ref
  57.0 2.1 reshape.450.gcol_ref
  59.2 0.7 reshape.435.g_ref
  59.9 2.1 convert_element_type.70.tok_ref
  61.9 1.0 fusion.1.refs_4_
  63.5 22.1 %collective-permute-done.8.dya_ref = bf16[512,1536]{1,0:T(8,128)(2,1)S(1)} collective-permute-done((bf16[512,1536]{1,0:T(8,128)(2,1)}, bf16[512,1536]{1,0:T(8,128)(2,1)S(1)}, u32[]{:S(2)}, u32[]{:S(2)}) %collective-permute-start.8) | collective-permute-done | bytes 1572896 | tf_op jit(solution)/shard_map/ppermute | solution.py:250
  86.1 27.2 %fwd_pair.4 = (bf16[8,144,1536]{2,1,0:T(8,128)(2,1)}, bf16[8,144,512]{2,1,0:T(8,128)(2,1)}, f32[8,144,512]{2,1,0:T(8,128)}, f32[8,144,512]{2,1,0:T(8,128)}, f32[256,1536]{1,0:T(8,128)}, /*index=5*/f32[256,1536]{1,0:T(8,128)}) custom-call(bf16[512,1536]{1,0:T(8,128)(2,1)} %xa_ref, bf16[512,1536]{1,0:T(8,128)(2,1)} %collective-permute-done.xb_ref, ...), custom_call_target="tpu_custom_call" | custom-call | flops 14000000000 | bytes 50000000 | tf_op jit(solution)/shard_map/fwd_pair/pallas_call | solution.py:126
  113.9 27.8 %fwd_pair.5 = (bf16[8,144,1536]{2,1,0:T(8,128)(2,1)}, bf16[8,144,512]{2,1,0:T(8,128)(2,1)}, f32[8,144,512]{2,1,0:T(8,128)}, f32[8,144,512]{2,1,0:T(8,128)}, f32[256,1536]{1,0:T(8,128)}, /*index=5*/f32[256,1536]{1,0:T(8,128)}) custom-call(bf16[512,1536]{1,0:T(8,128)(2,1)} %collective-permute-done.1.xa_ref, bf16[512,1536]{1,0:T(8,128)(2,1)} %collective-permute-done.2.xb_ref, ...), custom_call_target="tpu_custom_call" | custom-call | flops 14000000000 | bytes 50000000 | tf_op jit(solution)/shard_map/fwd_pair/pallas_call | solution.py:126
  141.7 1.5 collective-permute-start.3
  143.4 27.6 %bwd_pair.4 = (bf16[8,144,1536]{2,1,0:T(8,128)(2,1)}, bf16[8,144,512]{2,1,0:T(8,128)(2,1)}, bf16[8,144,512]{2,1,0:T(8,128)(2,1)}, f32[256,1536]{1,0:T(8,128)}, f32[256,1536]{1,0:T(8,128)}) custom-call(bf16[512,1536]{1,0:T(8,128)(2,1)} %dya_ref, bf16[512,1536]{1,0:T(8,128)(2,1)} %collective-permute-done.14.dyb_ref, ...), custom_call_target="tpu_custom_call" | custom-call | flops 14000000000 | bytes 50000000 | tf_op jit(solution)/shard_map/bwd_pair/pallas_call | solution.py:143
  171.6 27.4 %fwd_pair.6 = (bf16[8,144,1536]{2,1,0:T(8,128)(2,1)}, bf16[8,144,512]{2,1,0:T(8,128)(2,1)}, f32[8,144,512]{2,1,0:T(8,128)}, f32[8,144,512]{2,1,0:T(8,128)}, f32[256,1536]{1,0:T(8,128)}, /*index=5*/f32[256,1536]{1,0:T(8,128)}) custom-call(bf16[512,1536]{1,0:T(8,128)(2,1)} %collective-permute-done.12.xa_ref, bf16[512,1536]{1,0:T(8,128)(2,1)} %collective-permute-done.13.xb_ref, ...), custom_call_target="tpu_custom_call" | custom-call | flops 14000000000 | bytes 50000000 | tf_op jit(solution)/shard_map/fwd_pair/pallas_call | solution.py:126
  199.0 1.5 collective-permute-start.4
  200.5 27.2 %bwd_pair.5 = (bf16[8,144,1536]{2,1,0:T(8,128)(2,1)}, bf16[8,144,512]{2,1,0:T(8,128)(2,1)}, bf16[8,144,512]{2,1,0:T(8,128)(2,1)}, f32[256,1536]{1,0:T(8,128)}, f32[256,1536]{1,0:T(8,128)}) custom-call(bf16[512,1536]{1,0:T(8,128)(2,1)} %copy-done.11, bf16[512,1536]{1,0:T(8,128)(2,1)} %collective-permute-done.11.dyb_ref, ...), custom_call_target="tpu_custom_call" | custom-call | flops 14000000000 | bytes 50000000 | tf_op jit(solution)/shard_map/bwd_pair/pallas_call | solution.py:143
  228.3 27.3 %bwd_pair.6 = (bf16[8,144,1536]{2,1,0:T(8,128)(2,1)}, bf16[8,144,512]{2,1,0:T(8,128)(2,1)}, bf16[8,144,512]{2,1,0:T(8,128)(2,1)}, f32[256,1536]{1,0:T(8,128)}, f32[256,1536]{1,0:T(8,128)}) custom-call(bf16[512,1536]{1,0:T(8,128)(2,1)} %copy-done.9, bf16[512,1536]{1,0:T(8,128)(2,1)} %collective-permute-done.9.dyb_ref, ...), custom_call_target="tpu_custom_call" | custom-call | flops 14000000000 | bytes 50000000 | tf_op jit(solution)/shard_map/bwd_pair/pallas_call | solution.py:143
  255.6 1.1 copy-done.8
  256.7 1.5 collective-permute-start.19
  258.2 1.6 add_convert_fusion.6
  260.4 27.5 %fwd_pair.7 = (bf16[8,144,1536]{2,1,0:T(8,128)(2,1)}, bf16[8,144,512]{2,1,0:T(8,128)(2,1)}, f32[8,144,512]{2,1,0:T(8,128)}, f32[8,144,512]{2,1,0:T(8,128)}, f32[256,1536]{1,0:T(8,128)}, /*index=5*/f32[256,1536]{1,0:T(8,128)}) custom-call(bf16[512,1536]{1,0:T(8,128)(2,1)} %collective-permute-done.6.xa_ref, bf16[512,1536]{1,0:T(8,128)(2,1)} %collective-permute-done.7.xb_ref, ...), custom_call_target="tpu_custom_call" | custom-call | flops 14000000000 | bytes 50000000 | tf_op jit(solution)/shard_map/fwd_pair/pallas_call | solution.py:126
  288.4 2.5 add_convert_fusion.7.refs_0_
  290.9 1.5 collective-permute-start.20
  292.4 27.4 %bwd_pair.7 = (bf16[8,144,1536]{2,1,0:T(8,128)(2,1)}, bf16[8,144,512]{2,1,0:T(8,128)(2,1)}, bf16[8,144,512]{2,1,0:T(8,128)(2,1)}, f32[256,1536]{1,0:T(8,128)}, f32[256,1536]{1,0:T(8,128)}) custom-call(bf16[512,1536]{1,0:T(8,128)(2,1)} %collective-permute-done.22.dya_ref, bf16[512,1536]{1,0:T(8,128)(2,1)} %collective-permute-done.23.dyb_ref, ...), custom_call_target="tpu_custom_call" | custom-call | flops 14000000000 | bytes 50000000 | tf_op jit(solution)/shard_map/bwd_pair/pallas_call | solution.py:143
  319.8 17.9 %collective-permute-done.15 = f32[256,1536]{1,0:T(8,128)} collective-permute-done((f32[256,1536]{1,0:T(8,128)}, f32[256,1536]{1,0:T(8,128)}, u32[]{:S(2)}, u32[]{:S(2)}) %collective-permute-start.15) | collective-permute-done | bytes 1572896 | tf_op jit(solution)/shard_map/ppermute | solution.py:250
  337.7 1.5 collective-permute-start.26
  339.2 2.5 add_convert_fusion.5
  341.7 29.7 %collective-permute-done.20 = f32[256,1536]{1,0:T(8,128)} collective-permute-done((f32[256,1536]{1,0:T(8,128)}, f32[256,1536]{1,0:T(8,128)}, u32[]{:S(2)}, u32[]{:S(2)}) %collective-permute-start.20) | collective-permute-done | bytes 1572896 | tf_op jit(solution)/shard_map/ppermute | solution.py:250
  371.4 1.5 collective-permute-start.17
  372.9 1.7 add_convert_fusion.2
  374.8 2.6 add_convert_fusion.1
  377.4 27.6 %collective-permute-done.26 = f32[256,1536]{1,0:T(8,128)S(1)} collective-permute-done((f32[256,1536]{1,0:T(8,128)}, f32[256,1536]{1,0:T(8,128)S(1)}, u32[]{:S(2)}, u32[]{:S(2)}) %collective-permute-start.26) | collective-permute-done | bytes 1572896 | tf_op jit(solution)/shard_map/ppermute | solution.py:250
  405.0 1.5 collective-permute-start.25
  406.5 1.1 add_convert_fusion
  407.6 30.1 %collective-permute-done.17 = f32[256,1536]{1,0:T(8,128)S(1)} collective-permute-done((f32[256,1536]{1,0:T(8,128)S(1)}, f32[256,1536]{1,0:T(8,128)S(1)}, u32[]{:S(2)}, u32[]{:S(2)}) %collective-permute-start.17) | collective-permute-done | bytes 1572896 | tf_op jit(solution)/shard_map/ppermute | solution.py:250
  437.8 1.1 add_convert_fusion.4
  438.9 1.6 collective-permute-start.18
  440.5 1.5 collective-permute-start.16
  442.0 44.1 %weight_grads.1 = (f32[8,1536,512]{2,1,0:T(8,128)}, f32[8,1536,512]{2,1,0:T(8,128)}, f32[8,512,1536]{2,1,0:T(8,128)}) custom-call(bf16[8,144,1536]{2,1,0:T(8,128)(2,1)} %get-tuple-element.98.refs_0_, bf16[8,144,1536]{2,1,0:T(8,128)(2,1)} %get-tuple-element.99.refs_1_, bf16[8,144,1536]{2,1,0:T(8,128)(2,1)} %get-tuple-element.100.refs_2_, ...), custom_call_target="tpu_custom_call" | custom-call | flops 24999999488 | bytes 120000000 | tf_op jit(solution)/shard_map/weight_grads/pallas_call | solution.py:174
  486.1 1.1 add_convert_fusion.3.refs_0_
  487.2 5.5 %collect.3 = bf16[512,1536]{1,0:T(8,128)(2,1)} custom-call(bf16[256,1536]{1,0:T(8,128)(2,1)} %add_convert_fusion.3.refs_0_, bf16[256,1536]{1,0:T(8,128)(2,1)} %copy-done.12, bf16[256,1536]{1,0:T(8,128)(2,1)} %collective-permute-done.25.refs_2_, bf16[256,1536]{1,0:T(8,128)(2,1)} %collective-permute-done.27.refs_3_, s32[512,4]{1,0:T(8,128)} %fusion.1.refs_4_), custom_call_target="tpu_custom_call" | custom-call | flops 2000000000 | bytes 5000000 | tf_op jit(solution)/shard_map/collect/pallas_call | solution.py:202
  492.7 5.5 %collect.2 = bf16[512,1536]{1,0:T(8,128)(2,1)} custom-call(bf16[256,1536]{1,0:T(8,128)(2,1)} %add_convert_fusion.7.refs_0_, bf16[256,1536]{1,0:T(8,128)(2,1)} %collective-permute-done.5.refs_1_, bf16[256,1536]{1,0:T(8,128)(2,1)} %collective-permute-done.16.refs_2_, bf16[256,1536]{1,0:T(8,128)(2,1)} %collective-permute-done.18.refs_3_, s32[512,4]{1,0:T(8,128)} %fusion.1.refs_4_), custom_call_target="tpu_custom_call" | custom-call | flops 2000000000 | bytes 5000000 | tf_op jit(solution)/shard_map/collect/pallas_call | solution.py:202
  (88 shorter events, 6.8 us)
Async XLA Ops:
  16.5 96.9 %collective-permute-start.6 = (bf16[512,1536]{1,0:T(8,128)(2,1)}, bf16[512,1536]{1,0:T(8,128)(2,1)}, u32[]{:S(2)}, u32[]{:S(2)}) collective-permute-start(bf16[512,1536]{1,0:T(8,128)(2,1)} %xa_ref), channel_id=1, source_target_pairs={{0,2},{1,3},{2,0},{3,1},{4,6},{5,7},{6,4},{7,5}} | collective-permute-start | bytes 4718600 | tf_op jit(solution)/shard_map/ppermute | solution.py:253
  17.0 37.6 %collective-permute-start.1 = (bf16[512,1536]{1,0:T(8,128)(2,1)}, bf16[512,1536]{1,0:T(8,128)(2,1)}, u32[]{:S(2)}, u32[]{:S(2)}) collective-permute-start(bf16[512,1536]{1,0:T(8,128)(2,1)} %xa_ref), channel_id=1, source_target_pairs={{0,4},{4,0},{1,5},{5,1},{2,6},{6,2},{3,7},{7,3}} | collective-permute-start | bytes 4718600 | tf_op jit(solution)/shard_map/ppermute | solution.py:250
  18.5 44.4 %collective-permute-start = (bf16[512,1536]{1,0:T(8,128)(2,1)}, bf16[512,1536]{1,0:T(8,128)(2,1)}, u32[]{:S(2)}, u32[]{:S(2)}) collective-permute-start(bf16[512,1536]{1,0:T(8,128)(2,1)} %xa_ref), channel_id=1, source_target_pairs={{0,1},{1,0},{2,3},{3,2},{4,5},{5,4},{6,7},{7,6}} | collective-permute-start | bytes 4718600 | tf_op jit(solution)/shard_map/ppermute | solution.py:253
  18.5 67.1 %collective-permute-start.8 = (bf16[512,1536]{1,0:T(8,128)(2,1)}, bf16[512,1536]{1,0:T(8,128)(2,1)S(1)}, u32[]{:S(2)}, u32[]{:S(2)}) collective-permute-start(bf16[512,1536]{1,0:T(8,128)(2,1)} %dya_ref), channel_id=1, source_target_pairs={{0,4},{4,0},{1,5},{5,1},{2,6},{6,2},{3,7},{7,3}} | collective-permute-start | bytes 4718600 | tf_op jit(solution)/shard_map/ppermute | solution.py:250
  54.6 58.8 %collective-permute-start.12 = (bf16[512,1536]{1,0:T(8,128)(2,1)}, bf16[512,1536]{1,0:T(8,128)(2,1)}, u32[]{:S(2)}, u32[]{:S(2)}) collective-permute-start(bf16[512,1536]{1,0:T(8,128)(2,1)} %collective-permute-done.1.xa_ref), channel_id=1, source_target_pairs={{0,2},{1,3},{2,0},{3,1},{4,6},{5,7},{6,4},{7,5}} | collective-permute-start | bytes 4718600 | tf_op jit(solution)/shard_map/ppermute | solution.py:253
  56.1 57.8 %collective-permute-start.2 = (bf16[512,1536]{1,0:T(8,128)(2,1)}, bf16[512,1536]{1,0:T(8,128)(2,1)}, u32[]{:S(2)}, u32[]{:S(2)}) collective-permute-start(bf16[512,1536]{1,0:T(8,128)(2,1)} %collective-permute-done.1.xa_ref), channel_id=1, source_target_pairs={{0,1},{1,0},{2,3},{3,2},{4,5},{5,4},{6,7},{7,6}} | collective-permute-start | bytes 4718600 | tf_op jit(solution)/shard_map/ppermute | solution.py:253
  63.0 78.8 %collective-permute-start.14 = (bf16[512,1536]{1,0:T(8,128)(2,1)}, bf16[512,1536]{1,0:T(8,128)(2,1)}, u32[]{:S(2)}, u32[]{:S(2)}) collective-permute-start(bf16[512,1536]{1,0:T(8,128)(2,1)} %dya_ref), channel_id=1, source_target_pairs={{0,1},{1,0},{2,3},{3,2},{4,5},{5,4},{6,7},{7,6}} | collective-permute-start | bytes 4718600 | tf_op jit(solution)/shard_map/ppermute | solution.py:253
  85.6 27.7 %copy-start.9 = (bf16[512,1536]{1,0:T(8,128)(2,1)}, bf16[512,1536]{1,0:T(8,128)(2,1)S(1)}, u32[]{:S(2)}) copy-start(bf16[512,1536]{1,0:T(8,128)(2,1)S(1)} %collective-permute-done.8.dya_ref) | copy-start | bytes 4718596
  85.6 57.6 %collective-permute-start.10 = (bf16[512,1536]{1,0:T(8,128)(2,1)S(1)}, bf16[512,1536]{1,0:T(8,128)(2,1)S(1)}, u32[]{:S(2)}, u32[]{:S(2)}) collective-permute-start(bf16[512,1536]{1,0:T(8,128)(2,1)S(1)} %collective-permute-done.8.dya_ref), channel_id=1, source_target_pairs={{0,2},{1,3},{2,0},{3,1},{4,6},{5,7},{6,4},{7,5}} | collective-permute-start | bytes 4718600 | tf_op jit(solution)/shard_map/ppermute | solution.py:253
  113.3 114.4 %collective-permute-start.9 = (bf16[512,1536]{1,0:T(8,128)(2,1)S(1)}, bf16[512,1536]{1,0:T(8,128)(2,1)}, u32[]{:S(2)}, u32[]{:S(2)}) collective-permute-start(bf16[512,1536]{1,0:T(8,128)(2,1)S(1)} %collective-permute-done.8.dya_ref), channel_id=1, source_target_pairs={{0,1},{1,0},{2,3},{3,2},{4,5},{5,4},{6,7},{7,6}} | collective-permute-start | bytes 4718600 | tf_op jit(solution)/shard_map/ppermute | solution.py:253
  113.4 146.4 %collective-permute-start.7 = (bf16[512,1536]{1,0:T(8,128)(2,1)}, bf16[512,1536]{1,0:T(8,128)(2,1)}, u32[]{:S(2)}, u32[]{:S(2)}) collective-permute-start(bf16[512,1536]{1,0:T(8,128)(2,1)} %collective-permute-done.6.xa_ref), channel_id=1, source_target_pairs={{0,1},{1,0},{2,3},{3,2},{4,5},{5,4},{6,7},{7,6}} | collective-permute-start | bytes 4718600 | tf_op jit(solution)/shard_map/ppermute | solution.py:253
  113.9 57.2 %collective-permute-start.13 = (bf16[512,1536]{1,0:T(8,128)(2,1)}, bf16[512,1536]{1,0:T(8,128)(2,1)}, u32[]{:S(2)}, u32[]{:S(2)}) collective-permute-start(bf16[512,1536]{1,0:T(8,128)(2,1)} %collective-permute-done.12.xa_ref), channel_id=1, source_target_pairs={{0,1},{1,0},{2,3},{3,2},{4,5},{5,4},{6,7},{7,6}} | collective-permute-start | bytes 4718600 | tf_op jit(solution)/shard_map/ppermute | solution.py:253
  141.7 146.1 %collective-permute-start.3 = (f32[256,1536]{1,0:T(8,128)}, f32[256,1536]{1,0:T(8,128)}, u32[]{:S(2)}, u32[]{:S(2)}) collective-permute-start(f32[256,1536]{1,0:T(8,128)} %get-tuple-element.67), channel_id=1, source_target_pairs={{0,4},{4,0},{1,5},{5,1},{2,6},{6,2},{3,7},{7,3}} | collective-permute-start | bytes 4718600 | tf_op jit(solution)/shard_map/ppermute | solution.py:250
  143.2 27.8 %copy-start.11 = (bf16[512,1536]{1,0:T(8,128)(2,1)}, bf16[512,1536]{1,0:T(8,128)(2,1)S(1)}, u32[]{:S(2)}) copy-start(bf16[512,1536]{1,0:T(8,128)(2,1)S(1)} %collective-permute-done.10.dya_ref) | copy-start | bytes 4718596
  143.2 55.7 %collective-permute-start.11 = (bf16[512,1536]{1,0:T(8,128)(2,1)S(1)}, bf16[512,1536]{1,0:T(8,128)(2,1)}, u32[]{:S(2)}, u32[]{:S(2)}) collective-permute-start(bf16[512,1536]{1,0:T(8,128)(2,1)S(1)} %collective-permute-done.10.dya_ref), channel_id=1, source_target_pairs={{0,1},{1,0},{2,3},{3,2},{4,5},{5,4},{6,7},{7,6}} | collective-permute-start | bytes 4718600 | tf_op jit(solution)/shard_map/ppermute | solution.py:253
  171.1 89.3 %collective-permute-start.22 = (bf16[512,1536]{1,0:T(8,128)(2,1)}, bf16[512,1536]{1,0:T(8,128)(2,1)}, u32[]{:S(2)}, u32[]{:S(2)}) collective-permute-start(bf16[512,1536]{1,0:T(8,128)(2,1)} %dya_ref), channel_id=1, source_target_pairs={{0,2},{1,3},{2,0},{3,1},{4,6},{5,7},{6,4},{7,5}} | collective-permute-start | bytes 4718600 | tf_op jit(solution)/shard_map/ppermute | solution.py:253
  199.0 56.6 %collective-permute-start.4 = (f32[256,1536]{1,0:T(8,128)}, f32[256,1536]{1,0:T(8,128)S(1)}, u32[]{:S(2)}, u32[]{:S(2)}) collective-permute-start(f32[256,1536]{1,0:T(8,128)} %get-tuple-element.69), channel_id=1, source_target_pairs={{0,4},{4,0},{1,5},{5,1},{2,6},{6,2},{3,7},{7,3}} | collective-permute-start | bytes 4718600 | tf_op jit(solution)/shard_map/ppermute | solution.py:250
  227.7 146.9 %collective-permute-start.24 = (f32[256,1536]{1,0:T(8,128)}, f32[256,1536]{1,0:T(8,128)}, u32[]{:S(2)}, u32[]{:S(2)}) collective-permute-start(f32[256,1536]{1,0:T(8,128)} %get-tuple-element.80), channel_id=1, source_target_pairs={{0,4},{4,0},{1,5},{5,1},{2,6},{6,2},{3,7},{7,3}} | collective-permute-start | bytes 4718600 | tf_op jit(solution)/shard_map/ppermute | solution.py:250
  228.3 29.9 %copy-start.3 = (f32[256,1536]{1,0:T(8,128)S(1)}, f32[256,1536]{1,0:T(8,128)}, u32[]{:S(2)}) copy-start(f32[256,1536]{1,0:T(8,128)} %get-tuple-element.68) | copy-start | bytes 4718596
  255.6 1.1 copy-start.8
  256.7 182.2 %collective-permute-start.19 = (f32[256,1536]{1,0:T(8,128)}, f32[256,1536]{1,0:T(8,128)S(1)}, u32[]{:S(2)}, u32[]{:S(2)}) collective-permute-start(f32[256,1536]{1,0:T(8,128)} %get-tuple-element.84), channel_id=1, source_target_pairs={{0,4},{4,0},{1,5},{5,1},{2,6},{6,2},{3,7},{7,3}} | collective-permute-start | bytes 4718600 | tf_op jit(solution)/shard_map/ppermute | solution.py:250
  259.8 28.6 %copy-start.1 = (f32[256,1536]{1,0:T(8,128)S(1)}, f32[256,1536]{1,0:T(8,128)}, u32[]{:S(2)}) copy-start(f32[256,1536]{1,0:T(8,128)} %get-tuple-element.65) | copy-start | bytes 4718596
  259.8 77.9 %collective-permute-start.15 = (f32[256,1536]{1,0:T(8,128)}, f32[256,1536]{1,0:T(8,128)}, u32[]{:S(2)}, u32[]{:S(2)}) collective-permute-start(f32[256,1536]{1,0:T(8,128)} %get-tuple-element.76), channel_id=1, source_target_pairs={{0,4},{4,0},{1,5},{5,1},{2,6},{6,2},{3,7},{7,3}} | collective-permute-start | bytes 4718600 | tf_op jit(solution)/shard_map/ppermute | solution.py:250
  260.4 30.5 %collective-permute-start.23 = (bf16[512,1536]{1,0:T(8,128)(2,1)}, bf16[512,1536]{1,0:T(8,128)(2,1)}, u32[]{:S(2)}, u32[]{:S(2)}) collective-permute-start(bf16[512,1536]{1,0:T(8,128)(2,1)} %collective-permute-done.22.dya_ref), channel_id=1, source_target_pairs={{0,1},{1,0},{2,3},{3,2},{4,5},{5,4},{6,7},{7,6}} | collective-permute-start | bytes 4718600 | tf_op jit(solution)/shard_map/ppermute | solution.py:253
  287.9 204.8 %collective-permute-start.5 = (bf16[256,1536]{1,0:T(8,128)(2,1)S(1)}, bf16[256,1536]{1,0:T(8,128)(2,1)}, u32[]{:S(2)}, u32[]{:S(2)}) collective-permute-start(bf16[256,1536]{1,0:T(8,128)(2,1)S(1)} %add_convert_fusion.6), channel_id=1, source_target_pairs={{0,1},{1,0},{2,3},{3,2},{4,5},{5,4},{6,7},{7,6}} | collective-permute-start | bytes 2359304 | tf_op jit(solution)/shard_map/ppermute | solution.py:253
  290.9 80.5 %collective-permute-start.20 = (f32[256,1536]{1,0:T(8,128)}, f32[256,1536]{1,0:T(8,128)}, u32[]{:S(2)}, u32[]{:S(2)}) collective-permute-start(f32[256,1536]{1,0:T(8,128)} %get-tuple-element.90), channel_id=1, source_target_pairs={{0,4},{4,0},{1,5},{5,1},{2,6},{6,2},{3,7},{7,3}} | collective-permute-start | bytes 4718600 | tf_op jit(solution)/shard_map/ppermute | solution.py:250
  292.4 46.8 %copy-start.6 = (f32[256,1536]{1,0:T(8,128)S(1)}, f32[256,1536]{1,0:T(8,128)}, u32[]{:S(2)}) copy-start(f32[256,1536]{1,0:T(8,128)} %get-tuple-element.86) | copy-start | bytes 4718596
  337.7 33.7 %copy-start.10 = (f32[256,1536]{1,0:T(8,128)S(1)}, f32[256,1536]{1,0:T(8,128)}, u32[]{:S(2)}) copy-start(f32[256,1536]{1,0:T(8,128)} %get-tuple-element.88) | copy-start | bytes 4718596
  337.7 35.2 %copy-start.2 = (f32[256,1536]{1,0:T(8,128)S(1)}, f32[256,1536]{1,0:T(8,128)}, u32[]{:S(2)}) copy-start(f32[256,1536]{1,0:T(8,128)} %get-tuple-element.89) | copy-start | bytes 4718596
  337.7 67.3 %collective-permute-start.26 = (f32[256,1536]{1,0:T(8,128)}, f32[256,1536]{1,0:T(8,128)S(1)}, u32[]{:S(2)}, u32[]{:S(2)}) collective-permute-start(f32[256,1536]{1,0:T(8,128)} %get-tuple-element.97), channel_id=1, source_target_pairs={{0,4},{4,0},{1,5},{5,1},{2,6},{6,2},{3,7},{7,3}} | collective-permute-start | bytes 4718600 | tf_op jit(solution)/shard_map/ppermute | solution.py:250
  371.4 66.3 %collective-permute-start.17 = (f32[256,1536]{1,0:T(8,128)S(1)}, f32[256,1536]{1,0:T(8,128)S(1)}, u32[]{:S(2)}, u32[]{:S(2)}) collective-permute-start(f32[256,1536]{1,0:T(8,128)S(1)} %copy-done.10), channel_id=1, source_target_pairs={{0,4},{4,0},{1,5},{5,1},{2,6},{6,2},{3,7},{7,3}} | collective-permute-start | bytes 4718600 | tf_op jit(solution)/shard_map/ppermute | solution.py:250
  372.9 1.9 copy-start.7
  374.7 65.9 %collective-permute-start.21 = (bf16[256,1536]{1,0:T(8,128)(2,1)S(1)}, bf16[256,1536]{1,0:T(8,128)(2,1)S(1)}, u32[]{:S(2)}, u32[]{:S(2)}) collective-permute-start(bf16[256,1536]{1,0:T(8,128)(2,1)S(1)} %add_convert_fusion.2), channel_id=1, source_target_pairs={{0,1},{1,0},{2,3},{3,2},{4,5},{5,4},{6,7},{7,6}} | collective-permute-start | bytes 2359304 | tf_op jit(solution)/shard_map/ppermute | solution.py:253
  374.8 31.7 %copy-start.5 = (f32[256,1536]{1,0:T(8,128)S(1)}, f32[256,1536]{1,0:T(8,128)}, u32[]{:S(2)}) copy-start(f32[256,1536]{1,0:T(8,128)} %get-tuple-element.96) | copy-start | bytes 4718596
  405.0 82.2 %collective-permute-start.25 = (bf16[256,1536]{1,0:T(8,128)(2,1)}, bf16[256,1536]{1,0:T(8,128)(2,1)}, u32[]{:S(2)}, u32[]{:S(2)}) collective-permute-start(bf16[256,1536]{1,0:T(8,128)(2,1)} %add_convert_fusion.1), channel_id=1, source_target_pairs={{0,2},{1,3},{2,0},{3,1},{4,6},{5,7},{6,4},{7,5}} | collective-permute-start | bytes 2359304 | tf_op jit(solution)/shard_map/ppermute | solution.py:253
  406.5 31.3 %copy-start.4 = (f32[256,1536]{1,0:T(8,128)S(1)}, f32[256,1536]{1,0:T(8,128)}, u32[]{:S(2)}) copy-start(f32[256,1536]{1,0:T(8,128)} %get-tuple-element.87) | copy-start | bytes 4718596
  437.7 49.5 %collective-permute-start.27 = (bf16[256,1536]{1,0:T(8,128)(2,1)}, bf16[256,1536]{1,0:T(8,128)(2,1)}, u32[]{:S(2)}, u32[]{:S(2)}) collective-permute-start(bf16[256,1536]{1,0:T(8,128)(2,1)} %add_convert_fusion), channel_id=1, source_target_pairs={{0,3},{1,2},{2,1},{3,0},{4,7},{5,6},{6,5},{7,4}} | collective-permute-start | bytes 2359304 | tf_op jit(solution)/shard_map/ppermute | solution.py:253
  438.9 53.8 %collective-permute-start.18 = (bf16[256,1536]{1,0:T(8,128)(2,1)}, bf16[256,1536]{1,0:T(8,128)(2,1)}, u32[]{:S(2)}, u32[]{:S(2)}) collective-permute-start(bf16[256,1536]{1,0:T(8,128)(2,1)} %add_convert_fusion.4), channel_id=1, source_target_pairs={{0,3},{1,2},{2,1},{3,0},{4,7},{5,6},{6,5},{7,4}} | collective-permute-start | bytes 2359304 | tf_op jit(solution)/shard_map/ppermute | solution.py:253
  440.5 1.5 copy-start.12
  440.5 52.2 %collective-permute-start.16 = (bf16[256,1536]{1,0:T(8,128)(2,1)}, bf16[256,1536]{1,0:T(8,128)(2,1)}, u32[]{:S(2)}, u32[]{:S(2)}) collective-permute-start(bf16[256,1536]{1,0:T(8,128)(2,1)} %add_convert_fusion.5), channel_id=1, source_target_pairs={{0,2},{1,3},{2,0},{3,1},{4,6},{5,7},{6,4},{7,5}} | collective-permute-start | bytes 2359304 | tf_op jit(solution)/shard_map/ppermute | solution.py:253
  442.0 44.1 %copy-start = (f32[256,1536]{1,0:T(8,128)S(1)}, f32[256,1536]{1,0:T(8,128)}, u32[]{:S(2)}) copy-start(f32[256,1536]{1,0:T(8,128)} %get-tuple-element.74) | copy-start | bytes 4718596
where the time goes:
time: 507 us; the launch traced here: 499 us
  Pallas kernels  274 us (54%)
  waiting for transfers between devices  153 us (30%)
  other arithmetic  24.5 us (5%)
  starting transfers between devices  21.8 us (4%)
  blocking collectives  14.4 us (3%)
  local copies, waits for them, and re-layouts  7.88 us (2%)
    ppermute x10, waiting for transfers between devices, hop_y(): return lax.ppermute(a, 'ing', [(0, 1), (1, 0)])  153 us
    pallas_call x4, Pallas kernels, forward_pair(): pl.pallas_call(functools.partial(fwd_kernel, cap, pad), grid=(experts,),...  110 us
    pallas_call x4, Pallas kernels, backward_pair(): pl.pallas_call(functools.partial(bwd_kernel, cap, pad), grid=(experts,),...  110 us
    pallas_call x1, Pallas kernels, weight_grads(): pl.pallas_call(functools.partial(dw_kernel, chunks), grid=(experts,), in_...  44.1 us
    all_gather x1, blocking collectives, device_fn(): routing = lax.all_gather(packed, ('grp', 'ing'))  14.4 us
    convert_element_type x8, other arithmetic, combine(): sums.append((results[near][s] + hop_y(results[far][s])).astype(BF))  14.2 us
    ppermute x10, starting transfers between devices, hop_y(): return lax.ppermute(a, 'ing', [(0, 1), (1, 0)])  12.1 us
    pallas_call x2, Pallas kernels, collect(): pl.pallas_call(functools.partial(final_kernel, groups), grid=(4,), in_spe...  11.1 us
  transfers between devices with their start and end apart: 28, of which 6 were waited for; matrix products, arithmetic and copies ran while one was open for 6% of the time, Pallas kernels for 54%

commit v1 on v0

--- a/solution.py
+++ b/solution.py
@@ -263,16 +263,17 @@
         grp, ing = lax.axis_index('grp'), lax.axis_index('ing')
 
         per_group = experts * inner
-        packed = jnp.concatenate([ids_loc.T.astype(F32), gates_loc.T], axis=0)
-        routing = lax.all_gather(packed, ('grp', 'ing'))
-        order = [((grp ^ (2 * dx + dc)) * inner + (ing ^ dy)) for dx, dy in ((0, 1), (1, 1), (0, 0), (1, 0)) for dc in (0, 1)]
-
-        x_loc, dy_loc, routing = lax.optimization_barrier((x_loc, dy_loc, routing))
+        own = jnp.concatenate([ids_loc.T.astype(F32), gates_loc.T], axis=0)[None]
+        pair = jnp.concatenate([own, hop_y(own)], axis=0)
+        pair_c = hop_g(pair, 1)
+        quad_x = hop_g(jnp.concatenate([pair, pair_c], axis=0), 2)
+        routing = jnp.stack([pair[1], pair_c[1], quad_x[1], quad_x[3], pair[0], pair_c[0], quad_x[0], quad_x[2]])
+
         x_far = hop_y(x_loc)
-        x_near_c = hop_g(x_loc, 1)
-        x_near_x = hop_g(x_loc, 2)
         dy_far = hop_y(dy_loc)
-        dy_near_c = hop_g(dy_loc, 1)
+        x_near_c = hop_g(after(pair_c, x_loc), 1)
+        x_near_x = hop_g(after(quad_x, x_loc), 2)
+        dy_near_c = hop_g(after(x_near_c, dy_loc), 1)
         x_far_c, x_far_x = hop_g(x_far, 1), hop_g(x_far, 2)
         x_near_xc, x_far_xc = hop_g(x_near_x, 1), hop_g(x_far_x, 1)
         dy_far_c, dy_far_x = hop_g(dy_far, 1), hop_g(dy_far, 2)
@@ -282,7 +283,6 @@
         x_pairs = [(x_far, x_far_c), (x_far_x, x_far_xc), (x_loc, x_near_c), (x_near_x, x_near_xc)]
         dy_pairs = [(dy_far, dy_far_c), (dy_far_x, dy_far_xc), (dy_loc, dy_near_c), (dy_near_x, dy_near_xc)]
 
-        routing = jnp.take(routing, jnp.stack(order), axis=0)
         ids_rel, gates_rel = routing[:, :top_k].astype(jnp.int32), routing[:, top_k:]
         tok_rel, place_rel, weight_rel = slot_tables(ids_rel, gates_rel, (grp * inner + ing) * experts, experts, grp, per_group, cap)
         own_groups = ids_loc.T[None] // per_group == (grp ^ jnp.arange(groups))[:, None, None]

time: 507 us -> 498 us (0.982)
  blocking collectives: 14.4 us -> 0 us
    all_gather x1 -> x0, blocking collectives: 14.4 us -> none  [device_fn(): routing = lax.all_gather(packed, ('grp', 'ing'))]
    ppermute x18 -> x20, waiting for transfers between devices: 0.05 us -> 5.34 us  [hop_g(): return lax.ppermute(a, 'grp', [(g, g ^ bits) for g in range(groups)])]
    ppermute x10 -> x11, waiting for transfers between devices: 153 us -> 149 us  [hop_y(): return lax.ppermute(a, 'ing', [(0, 1), (1, 0)])]
    ppermute x10 -> x11, starting transfers between devices: 12.1 us -> 14 us  [hop_y(): return lax.ppermute(a, 'ing', [(0, 1), (1, 0)])]
    ppermute x18 -> x20, starting transfers between devices: 9.68 us -> 11.4 us  [hop_g(): return lax.ppermute(a, 'grp', [(g, g ^ bits) for g in range(groups)])]
  transfers between devices with their start and end apart: 28 -> 31, of which waited for: 6 -> 8; matrix products, arithmetic and copies ran while one was open for 6% -> 6% of each run, Pallas kernels for 54% -> 55%
where the time goes in v1:
time: 498 us; the launch traced here: 489 us
  Pallas kernels  274 us (55%)
  waiting for transfers between devices  154 us (31%)
  starting transfers between devices  25.4 us (5%)
  other arithmetic  24.4 us (5%)
  local copies, waits for them, and re-layouts  8.17 us (2%)
    ppermute x11, waiting for transfers between devices, hop_y(): return lax.ppermute(a, 'ing', [(0, 1), (1, 0)])  149 us
    pallas_call x4, Pallas kernels, forward_pair(): pl.pallas_call(functools.partial(fwd_kernel, cap, pad), grid=(experts,),...  110 us
    pallas_call x4, Pallas kernels, backward_pair(): pl.pallas_call(functools.partial(bwd_kernel, cap, pad), grid=(experts,),...  109 us
    pallas_call x1, Pallas kernels, weight_grads(): pl.pallas_call(functools.partial(dw_kernel, chunks), grid=(experts,), in_...  44.1 us
    convert_element_type x8, other arithmetic, combine(): sums.append((results[near][s] + hop_y(results[far][s])).astype(BF))  14.2 us
    ppermute x11, starting transfers between devices, hop_y(): return lax.ppermute(a, 'ing', [(0, 1), (1, 0)])  14 us
    ppermute x20, starting transfers between devices, hop_g(): return lax.ppermute(a, 'grp', [(g, g ^ bits) for g in range(groups)])  11.4 us
    pallas_call x2, Pallas kernels, collect(): pl.pallas_call(functools.partial(final_kernel, groups), grid=(4,), in_spe...  11.1 us
  transfers between devices with their start and end apart: 31, of which 8 were waited for; matrix products, arithmetic and copies ran while one was open for 6% of the time, Pallas kernels for 55%

profile of v1, /device:TPU:0, one launch (start us, length us, event | category | flops | bytes accessed | tf_op | source)
XLA Modules:
  0.0 489.2 jit_solution(17721922107793569020)
XLA Ops:
  2.1 3.4 collective-permute-start
  5.5 2.0 collective-permute-start.11
  8.5 1.0 fusion.1.refs_4_
  9.6 1.2 collective-permute-done.1
  10.9 1.5 collective-permute-start.3
  12.4 4.1 collective-permute-done.3
  17.2 1.5 collective-permute-start.9
  18.9 7.4 %select_reduce_fusion = (f32[8,8,72]{2,1,0:T(8,128)S(1)}, f32[8,8,72]{2,1,0:T(8,128)S(1)}, f32[8,8,72]{2,1,0:T(8,128)S(1)}) fusion(f32[8,8,512]{2,1,0:T(8,128)S(1)} %fusion.6, f32[8,8,512]{2,1,0:T(8,128)S(1)} %slice.47, pred[8,8,512]{2,1,0:T(8,128)(4,1)S(1)} %compare_reduce_fusion, f32[8,512]{1,0:T(8,128)S(1)} %bitcast.32, f32[512]{0:T(512)S(1)} %iota_add_fusion), kind=kLoop, calls=%fused_computation | loop fusion | flops 18860544 | bytes 368640 | tf_op jit(solution)/shard_map/reduce_sum | solution.py:231
  26.3 16.7 %collective-permute-done.4.xa_ref = bf16[512,1536]{1,0:T(8,128)(2,1)} collective-permute-done((bf16[512,1536]{1,0:T(8,128)(2,1)}, bf16[512,1536]{1,0:T(8,128)(2,1)}, u32[]{:S(2)}, u32[]{:S(2)}) %collective-permute-start.4) | collective-permute-done | bytes 1572896 | tf_op jit(solution)/shard_map/ppermute | solution.py:250
  43.0 1.5 collective-permute-start.15
  45.2 2.2 reshape.89.gcol_ref
  48.1 2.1 convert_element_type.70.tok_ref
  50.2 25.0 %collective-permute-done.11.dya_ref = bf16[512,1536]{1,0:T(8,128)(2,1)S(1)} collective-permute-done((bf16[512,1536]{1,0:T(8,128)(2,1)}, bf16[512,1536]{1,0:T(8,128)(2,1)S(1)}, u32[]{:S(2)}, u32[]{:S(2)}) %collective-permute-start.11) | collective-permute-done | bytes 1572896 | tf_op jit(solution)/shard_map/ppermute | solution.py:250
  75.2 1.5 collective-permute-start.13
  76.8 27.2 %fwd_pair.4 = (bf16[8,144,1536]{2,1,0:T(8,128)(2,1)}, bf16[8,144,512]{2,1,0:T(8,128)(2,1)}, f32[8,144,512]{2,1,0:T(8,128)}, f32[8,144,512]{2,1,0:T(8,128)}, f32[256,1536]{1,0:T(8,128)}, /*index=5*/f32[256,1536]{1,0:T(8,128)}) custom-call(bf16[512,1536]{1,0:T(8,128)(2,1)} %xa_ref.1, bf16[512,1536]{1,0:T(8,128)(2,1)} %collective-permute-done.2.xb_ref, ...), custom_call_target="tpu_custom_call" | custom-call | flops 14000000000 | bytes 50000000 | tf_op jit(solution)/shard_map/fwd_pair/pallas_call | solution.py:126
  105.0 27.8 %fwd_pair.5 = (bf16[8,144,1536]{2,1,0:T(8,128)(2,1)}, bf16[8,144,512]{2,1,0:T(8,128)(2,1)}, f32[8,144,512]{2,1,0:T(8,128)}, f32[8,144,512]{2,1,0:T(8,128)}, f32[256,1536]{1,0:T(8,128)}, /*index=5*/f32[256,1536]{1,0:T(8,128)}) custom-call(bf16[512,1536]{1,0:T(8,128)(2,1)} %collective-permute-done.4.xa_ref, bf16[512,1536]{1,0:T(8,128)(2,1)} %collective-permute-done.5.xb_ref, ...), custom_call_target="tpu_custom_call" | custom-call | flops 14000000000 | bytes 50000000 | tf_op jit(solution)/shard_map/fwd_pair/pallas_call | solution.py:126
  132.8 0.8 collective-permute-start.6
  133.7 27.2 %bwd_pair.4 = (bf16[8,144,1536]{2,1,0:T(8,128)(2,1)}, bf16[8,144,512]{2,1,0:T(8,128)(2,1)}, bf16[8,144,512]{2,1,0:T(8,128)(2,1)}, f32[256,1536]{1,0:T(8,128)}, f32[256,1536]{1,0:T(8,128)}) custom-call(bf16[512,1536]{1,0:T(8,128)(2,1)} %dya_ref.1, bf16[512,1536]{1,0:T(8,128)(2,1)} %collective-permute-done.17.dyb_ref, ...), custom_call_target="tpu_custom_call" | custom-call | flops 14000000000 | bytes 50000000 | tf_op jit(solution)/shard_map/bwd_pair/pallas_call | solution.py:143
  162.1 27.4 %fwd_pair.6 = (bf16[8,144,1536]{2,1,0:T(8,128)(2,1)}, bf16[8,144,512]{2,1,0:T(8,128)(2,1)}, f32[8,144,512]{2,1,0:T(8,128)}, f32[8,144,512]{2,1,0:T(8,128)}, f32[256,1536]{1,0:T(8,128)}, /*index=5*/f32[256,1536]{1,0:T(8,128)}) custom-call(bf16[512,1536]{1,0:T(8,128)(2,1)} %collective-permute-done.15.xa_ref, bf16[512,1536]{1,0:T(8,128)(2,1)} %copy-done.13, ...), custom_call_target="tpu_custom_call" | custom-call | flops 14000000000 | bytes 50000000 | tf_op jit(solution)/shard_map/fwd_pair/pallas_call | solution.py:126
  189.5 1.2 collective-permute-start.7
  190.7 27.3 %bwd_pair.5 = (bf16[8,144,1536]{2,1,0:T(8,128)(2,1)}, bf16[8,144,512]{2,1,0:T(8,128)(2,1)}, bf16[8,144,512]{2,1,0:T(8,128)(2,1)}, f32[256,1536]{1,0:T(8,128)}, f32[256,1536]{1,0:T(8,128)}) custom-call(bf16[512,1536]{1,0:T(8,128)(2,1)} %collective-permute-done.13.dya_ref, bf16[512,1536]{1,0:T(8,128)(2,1)} %collective-permute-done.14.dyb_ref, ...), custom_call_target="tpu_custom_call" | custom-call | flops 14000000000 | bytes 50000000 | tf_op jit(solution)/shard_map/bwd_pair/pallas_call | solution.py:143
  218.1 0.8 collective-permute-start.27
  218.9 27.3 %bwd_pair.6 = (bf16[8,144,1536]{2,1,0:T(8,128)(2,1)}, bf16[8,144,512]{2,1,0:T(8,128)(2,1)}, bf16[8,144,512]{2,1,0:T(8,128)(2,1)}, f32[256,1536]{1,0:T(8,128)}, f32[256,1536]{1,0:T(8,128)}) custom-call(bf16[512,1536]{1,0:T(8,128)(2,1)} %copy-done.11, bf16[512,1536]{1,0:T(8,128)(2,1)} %collective-permute-done.12.dyb_ref, ...), custom_call_target="tpu_custom_call" | custom-call | flops 14000000000 | bytes 50000000 | tf_op jit(solution)/shard_map/bwd_pair/pallas_call | solution.py:143
  246.2 1.1 copy-done.8
  247.3 1.2 collective-permute-start.22
  248.5 1.6 add_convert_fusion.6
  250.2 0.8 collective-permute-start.18
  251.0 27.4 %fwd_pair.7 = (bf16[8,144,1536]{2,1,0:T(8,128)(2,1)}, bf16[8,144,512]{2,1,0:T(8,128)(2,1)}, f32[8,144,512]{2,1,0:T(8,128)}, f32[8,144,512]{2,1,0:T(8,128)}, f32[256,1536]{1,0:T(8,128)}, /*index=5*/f32[256,1536]{1,0:T(8,128)}) custom-call(bf16[512,1536]{1,0:T(8,128)(2,1)} %collective-permute-done.9.xa_ref, bf16[512,1536]{1,0:T(8,128)(2,1)} %collective-permute-done.10.xb_ref, ...), custom_call_target="tpu_custom_call" | custom-call | flops 14000000000 | bytes 50000000 | tf_op jit(solution)/shard_map/fwd_pair/pallas_call | solution.py:126
  278.9 2.5 add_convert_fusion.7.refs_0_
  281.4 1.2 collective-permute-start.23
  282.6 27.4 %bwd_pair.7 = (bf16[8,144,1536]{2,1,0:T(8,128)(2,1)}, bf16[8,144,512]{2,1,0:T(8,128)(2,1)}, bf16[8,144,512]{2,1,0:T(8,128)(2,1)}, f32[256,1536]{1,0:T(8,128)}, f32[256,1536]{1,0:T(8,128)}) custom-call(bf16[512,1536]{1,0:T(8,128)(2,1)} %collective-permute-done.25.dya_ref, bf16[512,1536]{1,0:T(8,128)(2,1)} %collective-permute-done.26.dyb_ref, ...), custom_call_target="tpu_custom_call" | custom-call | flops 14000000000 | bytes 50000000 | tf_op jit(solution)/shard_map/bwd_pair/pallas_call | solution.py:143
  310.0 18.2 %collective-permute-done.18 = f32[256,1536]{1,0:T(8,128)} collective-permute-done((f32[256,1536]{1,0:T(8,128)}, f32[256,1536]{1,0:T(8,128)}, u32[]{:S(2)}, u32[]{:S(2)}) %collective-permute-start.18) | collective-permute-done | bytes 1572896 | tf_op jit(solution)/shard_map/ppermute | solution.py:250
  328.2 1.2 collective-permute-start.29
  329.4 2.5 add_convert_fusion.5
  331.9 30.0 %collective-permute-done.23 = f32[256,1536]{1,0:T(8,128)} collective-permute-done((f32[256,1536]{1,0:T(8,128)}, f32[256,1536]{1,0:T(8,128)}, u32[]{:S(2)}, u32[]{:S(2)}) %collective-permute-start.23) | collective-permute-done | bytes 1572896 | tf_op jit(solution)/shard_map/ppermute | solution.py:250
  361.9 1.2 collective-permute-start.20
  363.1 1.7 add_convert_fusion.2
  365.0 2.6 add_convert_fusion.1
  367.7 27.9 %collective-permute-done.29 = f32[256,1536]{1,0:T(8,128)S(1)} collective-permute-done((f32[256,1536]{1,0:T(8,128)}, f32[256,1536]{1,0:T(8,128)S(1)}, u32[]{:S(2)}, u32[]{:S(2)}) %collective-permute-start.29) | collective-permute-done | bytes 1572896 | tf_op jit(solution)/shard_map/ppermute | solution.py:250
  395.5 0.9 collective-permute-start.28
  396.4 1.1 add_convert_fusion
  397.5 31.3 %collective-permute-done.20 = f32[256,1536]{1,0:T(8,128)S(1)} collective-permute-done((f32[256,1536]{1,0:T(8,128)S(1)}, f32[256,1536]{1,0:T(8,128)S(1)}, u32[]{:S(2)}, u32[]{:S(2)}) %collective-permute-start.20) | collective-permute-done | bytes 1572896 | tf_op jit(solution)/shard_map/ppermute | solution.py:250
  428.8 1.1 add_convert_fusion.4
  429.9 1.7 collective-permute-start.21
  432.5 44.1 %weight_grads.1 = (f32[8,1536,512]{2,1,0:T(8,128)}, f32[8,1536,512]{2,1,0:T(8,128)}, f32[8,512,1536]{2,1,0:T(8,128)}) custom-call(bf16[8,144,1536]{2,1,0:T(8,128)(2,1)} %get-tuple-element.98.refs_0_, bf16[8,144,1536]{2,1,0:T(8,128)(2,1)} %get-tuple-element.99.refs_1_, bf16[8,144,1536]{2,1,0:T(8,128)(2,1)} %get-tuple-element.100.refs_2_, ...), custom_call_target="tpu_custom_call" | custom-call | flops 24999999488 | bytes 120000000 | tf_op jit(solution)/shard_map/weight_grads/pallas_call | solution.py:174
  476.6 1.1 add_convert_fusion.3.refs_0_
  477.7 5.5 %collect.3 = bf16[512,1536]{1,0:T(8,128)(2,1)} custom-call(bf16[256,1536]{1,0:T(8,128)(2,1)} %add_convert_fusion.3.refs_0_, bf16[256,1536]{1,0:T(8,128)(2,1)} %copy-done.14, bf16[256,1536]{1,0:T(8,128)(2,1)} %collective-permute-done.28.refs_2_, bf16[256,1536]{1,0:T(8,128)(2,1)} %collective-permute-done.30.refs_3_, s32[512,4]{1,0:T(8,128)} %fusion.1.refs_4_), custom_call_target="tpu_custom_call" | custom-call | flops 2000000000 | bytes 5000000 | tf_op jit(solution)/shard_map/collect/pallas_call | solution.py:202
  483.2 5.5 %collect.2 = bf16[512,1536]{1,0:T(8,128)(2,1)} custom-call(bf16[256,1536]{1,0:T(8,128)(2,1)} %add_convert_fusion.7.refs_0_, bf16[256,1536]{1,0:T(8,128)(2,1)} %collective-permute-done.8.refs_1_, bf16[256,1536]{1,0:T(8,128)(2,1)} %collective-permute-done.19.refs_2_, bf16[256,1536]{1,0:T(8,128)(2,1)} %collective-permute-done.21.refs_3_, s32[512,4]{1,0:T(8,128)} %fusion.1.refs_4_), custom_call_target="tpu_custom_call" | custom-call | flops 2000000000 | bytes 5000000 | tf_op jit(solution)/shard_map/collect/pallas_call | solution.py:202
  (100 shorter events, 8.7 us)
Async XLA Ops:
  0.6 15.9 %copy-start.9 = (f32[512,6]{0,1:T(8,128)S(1)}, f32[512,6]{0,1:T(8,128)}, u32[]{:S(2)}) copy-start(f32[512,6]{0,1:T(8,128)} %param.9) | copy-start | bytes 36868
  2.1 7.5 %collective-permute-start = (f32[1,12,512]{2,1,0:T(8,128)S(1)}, f32[1,12,512]{2,1,0:T(8,128)S(1)}, u32[]{:S(2)}, u32[]{:S(2)}) collective-permute-start(f32[1,12,512]{2,1,0:T(8,128)S(1)} %maximum_bitcast_fusion), channel_id=1, source_target_pairs={{0,4},{4,0},{1,5},{5,1},{2,6},{6,2},{3,7},{7,3}} | collective-permute-start | bytes 73736 | tf_op jit(solution)/shard_map/ppermute | solution.py:250
  5.5 37.6 %collective-permute-start.4 = (bf16[512,1536]{1,0:T(8,128)(2,1)}, bf16[512,1536]{1,0:T(8,128)(2,1)}, u32[]{:S(2)}, u32[]{:S(2)}) collective-permute-start(bf16[512,1536]{1,0:T(8,128)(2,1)} %xa_ref.1), channel_id=1, source_target_pairs={{0,4},{4,0},{1,5},{5,1},{2,6},{6,2},{3,7},{7,3}} | collective-permute-start | bytes 4718600 | tf_op jit(solution)/shard_map/ppermute | solution.py:250
  5.5 69.7 %collective-permute-start.11 = (bf16[512,1536]{1,0:T(8,128)(2,1)}, bf16[512,1536]{1,0:T(8,128)(2,1)S(1)}, u32[]{:S(2)}, u32[]{:S(2)}) collective-permute-start(bf16[512,1536]{1,0:T(8,128)(2,1)} %dya_ref.1), channel_id=1, source_target_pairs={{0,4},{4,0},{1,5},{5,1},{2,6},{6,2},{3,7},{7,3}} | collective-permute-start | bytes 4718600 | tf_op jit(solution)/shard_map/ppermute | solution.py:250
  8.5 8.7 %copy-start.10 = (bf16[512,1536]{1,0:T(8,128)(2,1)S(1)}, bf16[512,1536]{1,0:T(8,128)(2,1)}, u32[]{:S(2)}) copy-start(bf16[512,1536]{1,0:T(8,128)(2,1)} %xa_ref.1) | copy-start | bytes 4718596
  9.6 1.3 collective-permute-start.1
  10.9 5.6 %collective-permute-start.3 = (f32[4,12,512]{2,1,0:T(8,128)S(1)}, f32[4,12,512]{2,1,0:T(8,128)S(1)}, u32[]{:S(2)}, u32[]{:S(2)}) collective-permute-start(f32[4,12,512]{2,1,0:T(8,128)S(1)} %pad_maximum_fusion), channel_id=1, source_target_pairs={{0,2},{1,3},{2,0},{3,1},{4,6},{5,7},{6,4},{7,5}} | collective-permute-start | bytes 294920 | tf_op jit(solution)/shard_map/ppermute | solution.py:253
  12.4 64.4 %collective-permute-start.2 = (bf16[512,1536]{1,0:T(8,128)(2,1)}, bf16[512,1536]{1,0:T(8,128)(2,1)}, u32[]{:S(2)}, u32[]{:S(2)}) collective-permute-start(bf16[512,1536]{1,0:T(8,128)(2,1)} %xa_ref.1), channel_id=1, source_target_pairs={{0,1},{1,0},{2,3},{3,2},{4,5},{5,4},{6,7},{7,6}} | collective-permute-start | bytes 4718600 | tf_op jit(solution)/shard_map/ppermute | solution.py:253
  17.2 86.7 %collective-permute-start.9 = (bf16[512,1536]{1,0:T(8,128)(2,1)S(1)}, bf16[512,1536]{1,0:T(8,128)(2,1)}, u32[]{:S(2)}, u32[]{:S(2)}) collective-permute-start(bf16[512,1536]{1,0:T(8,128)(2,1)S(1)} %copy-done.10), channel_id=1, source_target_pairs={{0,2},{1,3},{2,0},{3,1},{4,6},{5,7},{6,4},{7,5}} | collective-permute-start | bytes 4718600 | tf_op jit(solution)/shard_map/ppermute | solution.py:253
  43.0 61.5 %collective-permute-start.15 = (bf16[512,1536]{1,0:T(8,128)(2,1)}, bf16[512,1536]{1,0:T(8,128)(2,1)}, u32[]{:S(2)}, u32[]{:S(2)}) collective-permute-start(bf16[512,1536]{1,0:T(8,128)(2,1)} %collective-permute-done.4.xa_ref), channel_id=1, source_target_pairs={{0,2},{1,3},{2,0},{3,1},{4,6},{5,7},{6,4},{7,5}} | collective-permute-start | bytes 4718600 | tf_op jit(solution)/shard_map/ppermute | solution.py:253
  44.5 60.0 %collective-permute-start.5 = (bf16[512,1536]{1,0:T(8,128)(2,1)}, bf16[512,1536]{1,0:T(8,128)(2,1)}, u32[]{:S(2)}, u32[]{:S(2)}) collective-permute-start(bf16[512,1536]{1,0:T(8,128)(2,1)} %collective-permute-done.4.xa_ref), channel_id=1, source_target_pairs={{0,1},{1,0},{2,3},{3,2},{4,5},{5,4},{6,7},{7,6}} | collective-permute-start | bytes 4718600 | tf_op jit(solution)/shard_map/ppermute | solution.py:253
  75.2 28.7 %copy-start.11 = (bf16[512,1536]{1,0:T(8,128)(2,1)}, bf16[512,1536]{1,0:T(8,128)(2,1)S(1)}, u32[]{:S(2)}) copy-start(bf16[512,1536]{1,0:T(8,128)(2,1)S(1)} %collective-permute-done.11.dya_ref) | copy-start | bytes 4718596
  75.2 57.6 %collective-permute-start.13 = (bf16[512,1536]{1,0:T(8,128)(2,1)S(1)}, bf16[512,1536]{1,0:T(8,128)(2,1)}, u32[]{:S(2)}, u32[]{:S(2)}) collective-permute-start(bf16[512,1536]{1,0:T(8,128)(2,1)S(1)} %collective-permute-done.11.dya_ref), channel_id=1, source_target_pairs={{0,2},{1,3},{2,0},{3,1},{4,6},{5,7},{6,4},{7,5}} | collective-permute-start | bytes 4718600 | tf_op jit(solution)/shard_map/ppermute | solution.py:253
  76.8 56.9 %collective-permute-start.17 = (bf16[512,1536]{1,0:T(8,128)(2,1)}, bf16[512,1536]{1,0:T(8,128)(2,1)}, u32[]{:S(2)}, u32[]{:S(2)}) collective-permute-start(bf16[512,1536]{1,0:T(8,128)(2,1)} %dya_ref.1), channel_id=1, source_target_pairs={{0,1},{1,0},{2,3},{3,2},{4,5},{5,4},{6,7},{7,6}} | collective-permute-start | bytes 4718600 | tf_op jit(solution)/shard_map/ppermute | solution.py:253
  104.0 114.1 %collective-permute-start.12 = (bf16[512,1536]{1,0:T(8,128)(2,1)S(1)}, bf16[512,1536]{1,0:T(8,128)(2,1)}, u32[]{:S(2)}, u32[]{:S(2)}) collective-permute-start(bf16[512,1536]{1,0:T(8,128)(2,1)S(1)} %collective-permute-done.11.dya_ref), channel_id=1, source_target_pairs={{0,1},{1,0},{2,3},{3,2},{4,5},{5,4},{6,7},{7,6}} | collective-permute-start | bytes 4718600 | tf_op jit(solution)/shard_map/ppermute | solution.py:253
  104.5 145.7 %collective-permute-start.10 = (bf16[512,1536]{1,0:T(8,128)(2,1)}, bf16[512,1536]{1,0:T(8,128)(2,1)}, u32[]{:S(2)}, u32[]{:S(2)}) collective-permute-start(bf16[512,1536]{1,0:T(8,128)(2,1)} %collective-permute-done.9.xa_ref), channel_id=1, source_target_pairs={{0,1},{1,0},{2,3},{3,2},{4,5},{5,4},{6,7},{7,6}} | collective-permute-start | bytes 4718600 | tf_op jit(solution)/shard_map/ppermute | solution.py:253
  104.5 56.4 %collective-permute-start.16 = (bf16[512,1536]{1,0:T(8,128)(2,1)}, bf16[512,1536]{1,0:T(8,128)(2,1)S(1)}, u32[]{:S(2)}, u32[]{:S(2)}) collective-permute-start(bf16[512,1536]{1,0:T(8,128)(2,1)} %collective-permute-done.15.xa_ref), channel_id=1, source_target_pairs={{0,1},{1,0},{2,3},{3,2},{4,5},{5,4},{6,7},{7,6}} | collective-permute-start | bytes 4718600 | tf_op jit(solution)/shard_map/ppermute | solution.py:253
  132.8 145.5 %collective-permute-start.6 = (f32[256,1536]{1,0:T(8,128)}, f32[256,1536]{1,0:T(8,128)}, u32[]{:S(2)}, u32[]{:S(2)}) collective-permute-start(f32[256,1536]{1,0:T(8,128)} %get-tuple-element.66), channel_id=1, source_target_pairs={{0,4},{4,0},{1,5},{5,1},{2,6},{6,2},{3,7},{7,3}} | collective-permute-start | bytes 4718600 | tf_op jit(solution)/shard_map/ppermute | solution.py:250
  133.7 55.8 %collective-permute-start.14 = (bf16[512,1536]{1,0:T(8,128)(2,1)}, bf16[512,1536]{1,0:T(8,128)(2,1)}, u32[]{:S(2)}, u32[]{:S(2)}) collective-permute-start(bf16[512,1536]{1,0:T(8,128)(2,1)} %collective-permute-done.13.dya_ref), channel_id=1, source_target_pairs={{0,1},{1,0},{2,3},{3,2},{4,5},{5,4},{6,7},{7,6}} | collective-permute-start | bytes 4718600 | tf_op jit(solution)/shard_map/ppermute | solution.py:253
  160.9 1.2 copy-start.13
  161.0 90.0 %collective-permute-start.25 = (bf16[512,1536]{1,0:T(8,128)(2,1)}, bf16[512,1536]{1,0:T(8,128)(2,1)}, u32[]{:S(2)}, u32[]{:S(2)}) collective-permute-start(bf16[512,1536]{1,0:T(8,128)(2,1)} %dya_ref.1), channel_id=1, source_target_pairs={{0,2},{1,3},{2,0},{3,1},{4,6},{5,7},{6,4},{7,5}} | collective-permute-start | bytes 4718600 | tf_op jit(solution)/shard_map/ppermute | solution.py:253
  189.5 56.7 %collective-permute-start.7 = (f32[256,1536]{1,0:T(8,128)}, f32[256,1536]{1,0:T(8,128)S(1)}, u32[]{:S(2)}, u32[]{:S(2)}) collective-permute-start(f32[256,1536]{1,0:T(8,128)} %get-tuple-element.68), channel_id=1, source_target_pairs={{0,4},{4,0},{1,5},{5,1},{2,6},{6,2},{3,7},{7,3}} | collective-permute-start | bytes 4718600 | tf_op jit(solution)/shard_map/ppermute | solution.py:250
  218.1 146.8 %collective-permute-start.27 = (f32[256,1536]{1,0:T(8,128)}, f32[256,1536]{1,0:T(8,128)}, u32[]{:S(2)}, u32[]{:S(2)}) collective-permute-start(f32[256,1536]{1,0:T(8,128)} %get-tuple-element.80), channel_id=1, source_target_pairs={{0,4},{4,0},{1,5},{5,1},{2,6},{6,2},{3,7},{7,3}} | collective-permute-start | bytes 4718600 | tf_op jit(solution)/shard_map/ppermute | solution.py:250
  218.9 29.7 %copy-start.3 = (f32[256,1536]{1,0:T(8,128)S(1)}, f32[256,1536]{1,0:T(8,128)}, u32[]{:S(2)}) copy-start(f32[256,1536]{1,0:T(8,128)} %get-tuple-element.67) | copy-start | bytes 4718596
  246.2 1.1 copy-start.8
  247.3 182.5 %collective-permute-start.22 = (f32[256,1536]{1,0:T(8,128)}, f32[256,1536]{1,0:T(8,128)S(1)}, u32[]{:S(2)}, u32[]{:S(2)}) collective-permute-start(f32[256,1536]{1,0:T(8,128)} %get-tuple-element.84), channel_id=1, source_target_pairs={{0,4},{4,0},{1,5},{5,1},{2,6},{6,2},{3,7},{7,3}} | collective-permute-start | bytes 4718600 | tf_op jit(solution)/shard_map/ppermute | solution.py:250
  250.1 28.8 %copy-start.1 = (f32[256,1536]{1,0:T(8,128)S(1)}, f32[256,1536]{1,0:T(8,128)}, u32[]{:S(2)}) copy-start(f32[256,1536]{1,0:T(8,128)} %get-tuple-element.64) | copy-start | bytes 4718596
  250.2 78.0 %collective-permute-start.18 = (f32[256,1536]{1,0:T(8,128)}, f32[256,1536]{1,0:T(8,128)}, u32[]{:S(2)}, u32[]{:S(2)}) collective-permute-start(f32[256,1536]{1,0:T(8,128)} %get-tuple-element.76), channel_id=1, source_target_pairs={{0,4},{4,0},{1,5},{5,1},{2,6},{6,2},{3,7},{7,3}} | collective-permute-start | bytes 4718600 | tf_op jit(solution)/shard_map/ppermute | solution.py:250
  251.0 30.4 %collective-permute-start.26 = (bf16[512,1536]{1,0:T(8,128)(2,1)}, bf16[512,1536]{1,0:T(8,128)(2,1)}, u32[]{:S(2)}, u32[]{:S(2)}) collective-permute-start(bf16[512,1536]{1,0:T(8,128)(2,1)} %collective-permute-done.25.dya_ref), channel_id=1, source_target_pairs={{0,1},{1,0},{2,3},{3,2},{4,5},{5,4},{6,7},{7,6}} | collective-permute-start | bytes 4718600 | tf_op jit(solution)/shard_map/ppermute | solution.py:253
  278.4 204.8 %collective-permute-start.8 = (bf16[256,1536]{1,0:T(8,128)(2,1)S(1)}, bf16[256,1536]{1,0:T(8,128)(2,1)}, u32[]{:S(2)}, u32[]{:S(2)}) collective-permute-start(bf16[256,1536]{1,0:T(8,128)(2,1)S(1)} %add_convert_fusion.6), channel_id=1, source_target_pairs={{0,1},{1,0},{2,3},{3,2},{4,5},{5,4},{6,7},{7,6}} | collective-permute-start | bytes 2359304 | tf_op jit(solution)/shard_map/ppermute | solution.py:253
  281.4 80.5 %collective-permute-start.23 = (f32[256,1536]{1,0:T(8,128)}, f32[256,1536]{1,0:T(8,128)}, u32[]{:S(2)}, u32[]{:S(2)}) collective-permute-start(f32[256,1536]{1,0:T(8,128)} %get-tuple-element.90), channel_id=1, source_target_pairs={{0,4},{4,0},{1,5},{5,1},{2,6},{6,2},{3,7},{7,3}} | collective-permute-start | bytes 4718600 | tf_op jit(solution)/shard_map/ppermute | solution.py:250
  282.6 46.8 %copy-start.6 = (f32[256,1536]{1,0:T(8,128)S(1)}, f32[256,1536]{1,0:T(8,128)}, u32[]{:S(2)}) copy-start(f32[256,1536]{1,0:T(8,128)} %get-tuple-element.86) | copy-start | bytes 4718596
  328.2 33.7 %copy-start.12 = (f32[256,1536]{1,0:T(8,128)S(1)}, f32[256,1536]{1,0:T(8,128)}, u32[]{:S(2)}) copy-start(f32[256,1536]{1,0:T(8,128)} %get-tuple-element.88) | copy-start | bytes 4718596
  328.2 34.9 %copy-start.2 = (f32[256,1536]{1,0:T(8,128)S(1)}, f32[256,1536]{1,0:T(8,128)}, u32[]{:S(2)}) copy-start(f32[256,1536]{1,0:T(8,128)} %get-tuple-element.89) | copy-start | bytes 4718596
  328.2 67.3 %collective-permute-start.29 = (f32[256,1536]{1,0:T(8,128)}, f32[256,1536]{1,0:T(8,128)S(1)}, u32[]{:S(2)}, u32[]{:S(2)}) collective-permute-start(f32[256,1536]{1,0:T(8,128)} %get-tuple-element.97), channel_id=1, source_target_pairs={{0,4},{4,0},{1,5},{5,1},{2,6},{6,2},{3,7},{7,3}} | collective-permute-start | bytes 4718600 | tf_op jit(solution)/shard_map/ppermute | solution.py:250
  361.9 66.9 %collective-permute-start.20 = (f32[256,1536]{1,0:T(8,128)S(1)}, f32[256,1536]{1,0:T(8,128)S(1)}, u32[]{:S(2)}, u32[]{:S(2)}) collective-permute-start(f32[256,1536]{1,0:T(8,128)S(1)} %copy-done.12), channel_id=1, source_target_pairs={{0,4},{4,0},{1,5},{5,1},{2,6},{6,2},{3,7},{7,3}} | collective-permute-start | bytes 4718600 | tf_op jit(solution)/shard_map/ppermute | solution.py:250
  363.1 1.9 copy-start.7
  364.9 66.7 %collective-permute-start.24 = (bf16[256,1536]{1,0:T(8,128)(2,1)S(1)}, bf16[256,1536]{1,0:T(8,128)(2,1)S(1)}, u32[]{:S(2)}, u32[]{:S(2)}) collective-permute-start(bf16[256,1536]{1,0:T(8,128)(2,1)S(1)} %add_convert_fusion.2), channel_id=1, source_target_pairs={{0,1},{1,0},{2,3},{3,2},{4,5},{5,4},{6,7},{7,6}} | collective-permute-start | bytes 2359304 | tf_op jit(solution)/shard_map/ppermute | solution.py:253
  365.0 31.4 %copy-start.5 = (f32[256,1536]{1,0:T(8,128)S(1)}, f32[256,1536]{1,0:T(8,128)}, u32[]{:S(2)}) copy-start(f32[256,1536]{1,0:T(8,128)} %get-tuple-element.96) | copy-start | bytes 4718596
  395.5 82.1 %collective-permute-start.28 = (bf16[256,1536]{1,0:T(8,128)(2,1)}, bf16[256,1536]{1,0:T(8,128)(2,1)}, u32[]{:S(2)}, u32[]{:S(2)}) collective-permute-start(bf16[256,1536]{1,0:T(8,128)(2,1)} %add_convert_fusion.1), channel_id=1, source_target_pairs={{0,2},{1,3},{2,0},{3,1},{4,6},{5,7},{6,4},{7,5}} | collective-permute-start | bytes 2359304 | tf_op jit(solution)/shard_map/ppermute | solution.py:253
  396.4 32.4 %copy-start.4 = (f32[256,1536]{1,0:T(8,128)S(1)}, f32[256,1536]{1,0:T(8,128)}, u32[]{:S(2)}) copy-start(f32[256,1536]{1,0:T(8,128)} %get-tuple-element.87) | copy-start | bytes 4718596
  428.8 48.9 %collective-permute-start.30 = (bf16[256,1536]{1,0:T(8,128)(2,1)}, bf16[256,1536]{1,0:T(8,128)(2,1)}, u32[]{:S(2)}, u32[]{:S(2)}) collective-permute-start(bf16[256,1536]{1,0:T(8,128)(2,1)} %add_convert_fusion), channel_id=1, source_target_pairs={{0,3},{1,2},{2,1},{3,0},{4,7},{5,6},{6,5},{7,4}} | collective-permute-start | bytes 2359304 | tf_op jit(solution)/shard_map/ppermute | solution.py:253
  429.9 53.3 %collective-permute-start.21 = (bf16[256,1536]{1,0:T(8,128)(2,1)}, bf16[256,1536]{1,0:T(8,128)(2,1)}, u32[]{:S(2)}, u32[]{:S(2)}) collective-permute-start(bf16[256,1536]{1,0:T(8,128)(2,1)} %add_convert_fusion.4), channel_id=1, source_target_pairs={{0,3},{1,2},{2,1},{3,0},{4,7},{5,6},{6,5},{7,4}} | collective-permute-start | bytes 2359304 | tf_op jit(solution)/shard_map/ppermute | solution.py:253
  431.6 0.9 copy-start.14
  431.6 51.6 %collective-permute-start.19 = (bf16[256,1536]{1,0:T(8,128)(2,1)}, bf16[256,1536]{1,0:T(8,128)(2,1)}, u32[]{:S(2)}, u32[]{:S(2)}) collective-permute-start(bf16[256,1536]{1,0:T(8,128)(2,1)} %add_convert_fusion.5), channel_id=1, source_target_pairs={{0,2},{1,3},{2,0},{3,1},{4,6},{5,7},{6,4},{7,5}} | collective-permute-start | bytes 2359304 | tf_op jit(solution)/shard_map/ppermute | solution.py:253
  432.5 44.1 %copy-start = (f32[256,1536]{1,0:T(8,128)S(1)}, f32[256,1536]{1,0:T(8,128)}, u32[]{:S(2)}) copy-start(f32[256,1536]{1,0:T(8,128)} %get-tuple-element.74) | copy-start | bytes 4718596

commit v2 on v1

--- a/solution.py
+++ b/solution.py
@@ -12,7 +12,7 @@
 F32 = jnp.float32
 PAIR = 2
 
-KERNEL_ORDER = (('f', 2), ('f', 0), ('b', 2), ('f', 1), ('b', 1), ('b', 0), ('f', 3), ('b', 3))
+KERNEL_ORDER = (('f', 0), ('n', 2), ('f', 1), ('b', 0), ('b', 1), ('n', 3))
 
 
 def dot(a, b):
@@ -46,38 +46,54 @@
         dst_ref[s, pl.ds(pl.multiple_of(e * pad, pad), pad), :] = padded
 
 
-def fwd_kernel(cap, pad, xa_ref, xb_ref, tok_ref, q_ref, g_ref, w1_ref, w3_ref, w2_ref, xg_ref, a_ref, u_ref, v_ref, p0_ref, p1_ref, xg_scr, o_scr):
-    e = pl.program_id(0)
-
-    @pl.when(e == 0)
-    def _():
-        store_by_expert(xg_scr, [pick_rows(tok_ref[s], r) for s, r in enumerate((xa_ref, xb_ref))], cap)
-
-    xg = xg_scr[e]
-    xg_ref[0] = xg
+def spread_rows(dst_ref, tok_ref, row_refs, cap, gcol_ref=None):
+    picked = [pick_rows(tok_ref[s], r) for s, r in enumerate(row_refs)]
+    if gcol_ref is not None:
+        picked = [gcol_ref[s] * p for s, p in enumerate(picked)]
+    store_by_expert(dst_ref, picked, cap)
+
+
+def forward_expert(xg, w1_ref, w3_ref):
     h1 = dot(xg, w1_ref[0])
     h3 = dot(xg, w3_ref[0])
     sig = jax.nn.sigmoid(h1)
     silu = h1 * sig
     act = (silu * h3).astype(BF)
+    return act, h3 * (sig * (1.0 + h1 * (1.0 - sig))), silu
+
+
+def group_sums(p_refs, q_ref, rows_scr, g_ref=None):
+    for s, p_ref in enumerate(p_refs):
+        slots = lax.broadcasted_iota(jnp.int32, (p_ref.shape[0], q_ref.shape[2]), 0)
+        hit = q_ref[s] == slots
+        if g_ref is None:
+            p_ref[...] = dot(jnp.where(hit, 1.0, 0.0).astype(BF), rows_scr[s])
+            continue
+        rest = g_ref[s]
+        total = None
+        for _ in range(3):
+            part = rest.astype(BF)
+            term = dot(jnp.where(hit, part.astype(F32), 0.0).astype(BF), rows_scr[s])
+            total = term if total is None else total + term
+            rest = rest - part.astype(F32)
+        p_ref[...] = total
+
+
+def fwd_kernel(cap, pad, xa_ref, xb_ref, tok_ref, q_ref, g_ref, w1_ref, w3_ref, w2_ref, xg_ref, a_ref, u_ref, v_ref, p0_ref, p1_ref, xg_scr, o_scr):
+    e = pl.program_id(0)
+
+    @pl.when(e == 0)
+    def _():
+        spread_rows(xg_scr, tok_ref, (xa_ref, xb_ref), cap)
+
+    xg_ref[0] = xg_scr[e]
+    act, u_ref[0], v_ref[0] = forward_expert(xg_scr[e], w1_ref, w3_ref)
     a_ref[0] = act
-    u_ref[0] = h3 * (sig * (1.0 + h1 * (1.0 - sig)))
-    v_ref[0] = silu
     keep_rows(o_scr, dot(act, w2_ref[0]), e, cap, pad)
 
     @pl.when(e == pl.num_programs(0) - 1)
     def _():
-        for s, p_ref in enumerate((p0_ref, p1_ref)):
-            slots = lax.broadcasted_iota(jnp.int32, (p_ref.shape[0], q_ref.shape[2]), 0)
-            hit = q_ref[s] == slots
-            rest = g_ref[s]
-            total = None
-            for _ in range(3):
-                part = rest.astype(BF)
-                term = dot(jnp.where(hit, part.astype(F32), 0.0).astype(BF), o_scr[s])
-                total = term if total is None else total + term
-                rest = rest - part.astype(F32)
-            p_ref[...] = total
+        group_sums((p0_ref, p1_ref), q_ref, o_scr, g_ref)
 
 
 def bwd_kernel(cap, pad, dya_ref, dyb_ref, tok_ref, gcol_ref, q_ref, w1_ref, w3_ref, w2_ref, u_ref, v_ref, d_ref, dh1_ref, dh3_ref, p0_ref, p1_ref, d_scr, r_scr):
@@ -85,11 +101,10 @@
 
     @pl.when(e == 0)
     def _():
-        store_by_expert(d_scr, [gcol_ref[s] * pick_rows(tok_ref[s], r) for s, r in enumerate((dya_ref, dyb_ref))], cap)
-
-    d = d_scr[e]
-    d_ref[0] = d
-    da = dot_bt(d, w2_ref[0])
+        spread_rows(d_scr, tok_ref, (dya_ref, dyb_ref), cap, gcol_ref)
+
+    d_ref[0] = d_scr[e]
+    da = dot_bt(d_scr[e], w2_ref[0])
     dh1 = (da * u_ref[0]).astype(BF)
     dh3 = (da * v_ref[0]).astype(BF)
     dh1_ref[0] = dh1
@@ -98,9 +113,33 @@
 
     @pl.when(e == pl.num_programs(0) - 1)
     def _():
-        for s, p_ref in enumerate((p0_ref, p1_ref)):
-            slots = lax.broadcasted_iota(jnp.int32, (p_ref.shape[0], q_ref.shape[2]), 0)
-            p_ref[...] = dot(jnp.where(q_ref[s] == slots, 1.0, 0.0).astype(BF), r_scr[s])
+        group_sums((p0_ref, p1_ref), q_ref, r_scr)
+
+
+def near_kernel(cap, pad, xa_ref, xb_ref, dya_ref, dyb_ref, tok_ref, gcol_ref, q_ref, g_ref, w1_ref, w3_ref, w2_ref, xg_ref, a_ref, d_ref, dh1_ref, dh3_ref, y0_ref, y1_ref, z0_ref, z1_ref, xg_scr, d_scr, o_scr, r_scr):
+    e = pl.program_id(0)
+
+    @pl.when(e == 0)
+    def _():
+        spread_rows(xg_scr, tok_ref, (xa_ref, xb_ref), cap)
+        spread_rows(d_scr, tok_ref, (dya_ref, dyb_ref), cap, gcol_ref)
+
+    xg_ref[0] = xg_scr[e]
+    d_ref[0] = d_scr[e]
+    act, u, v = forward_expert(xg_scr[e], w1_ref, w3_ref)
+    a_ref[0] = act
+    keep_rows(o_scr, dot(act, w2_ref[0]), e, cap, pad)
+    da = dot_bt(d_scr[e], w2_ref[0])
+    dh1 = (da * u).astype(BF)
+    dh3 = (da * v).astype(BF)
+    dh1_ref[0] = dh1
+    dh3_ref[0] = dh3
+    keep_rows(r_scr, dot_bt(dh1, w1_ref[0]) + dot_bt(dh3, w3_ref[0]), e, cap, pad)
+
+    @pl.when(e == pl.num_programs(0) - 1)
+    def _():
+        group_sums((y0_ref, y1_ref), q_ref, o_scr, g_ref)
+        group_sums((z0_ref, z1_ref), q_ref, r_scr)
 
 
 def whole(shape):
@@ -109,6 +148,10 @@
 
 def per_expert(shape):
     return pl.BlockSpec((1,) + shape[1:], lambda e: (e,) + (0,) * (len(shape) - 1))
+
+
+def once(shape):
+    return pl.BlockSpec(shape, lambda e: (0,) * len(shape), pipeline_mode=pl.Buffered(1))
 
 
 def of_pair(pair, shape):
@@ -151,6 +194,25 @@
         cost_estimate=pl.CostEstimate(flops=14 * 10**9, bytes_accessed=50 * 10**6, transcendentals=0),
         name="bwd_pair",
     )(dya, dyb, tok_col, g_col, q_row, w1, w3, w2, u, v)
+
+
+def near_pair(pair, xa, xb, dya, dyb, tok_col, g_col, q_row, g_row, w1, w3, w2, cap, pad, grp_cap):
+    experts, hidden, ff = w1.shape
+    rows = PAIR * cap
+    wide, narrow, part = ((experts, rows, hidden), BF), ((experts, rows, ff), BF), ((grp_cap, hidden), F32)
+    outs = [wide, narrow, wide, narrow, narrow, part, part, part, part]
+    tables = [tok_col, g_col, q_row, g_row]
+    return pl.pallas_call(
+        functools.partial(near_kernel, cap, pad),
+        grid=(experts,),
+        in_specs=[once(xa.shape)] * 4 + [of_pair(pair, t.shape) for t in tables] + [per_expert(w1.shape), per_expert(w3.shape), per_expert(w2.shape)],
+        out_specs=[per_expert(s) if len(s) == 3 else whole(s) for s, _ in outs],
+        out_shape=[jax.ShapeDtypeStruct(s, t) for s, t in outs],
+        scratch_shapes=[pltpu.VMEM((experts, rows, hidden), BF)] * 2 + [pltpu.VMEM((PAIR, experts * pad, hidden), BF)] * 2,
+        compiler_params=params(),
+        cost_estimate=pl.CostEstimate(flops=28 * 10**9, bytes_accessed=70 * 10**6, transcendentals=0),
+        name="near_pair",
+    )(xa, xb, dya, dyb, *tables, w1, w3, w2)
 
 
 def dw_kernel(chunks, *refs):
@@ -295,19 +357,22 @@
         q_rows = jnp.pad(place_rel, spare, constant_values=-1.0).astype(jnp.int32).reshape(devices, 1, experts * pad)
         g_rows = jnp.pad(weight_rel, spare).reshape(devices, 1, experts * pad)
 
-        fwd, bwd = [None] * 4, [None] * 4
+        xs, acts, ds, dh1s, dh3s, y_sums, dx_sums = ([None] * 4 for _ in range(7))
+        saved = {}
         last = None
         for step, c in KERNEL_ORDER:
-            rows = x_pairs[c] if step == 'f' else dy_pairs[c]
             places = q_rows if last is None else after(last, q_rows)
-            if step == 'f':
-                fwd[c] = forward_pair(c, *rows, tok_cols, places, g_rows, w1, w3, w2, cap, pad, grp_cap)
-                last = fwd[c][4]
+            if step == 'n':
+                xs[c], acts[c], ds[c], dh1s[c], dh3s[c], *sums = near_pair(c, *x_pairs[c], *dy_pairs[c], tok_cols, g_cols, places, g_rows, w1, w3, w2, cap, pad, grp_cap)
+                y_sums[c], dx_sums[c] = sums[:PAIR], sums[PAIR:]
+            elif step == 'f':
+                xs[c], acts[c], *saved[c], y0, y1 = forward_pair(c, *x_pairs[c], tok_cols, places, g_rows, w1, w3, w2, cap, pad, grp_cap)
+                y_sums[c] = (y0, y1)
             else:
-                bwd[c] = backward_pair(c, *rows, tok_cols, g_cols, places, w1, w3, w2, fwd[c][2], fwd[c][3], cap, pad, grp_cap)
-                last = bwd[c][3]
-
-        grads = weight_grads([f[0] for f in fwd], [f[1] for f in fwd], [b[0] for b in bwd], [b[1] for b in bwd], [b[2] for b in bwd])
+                ds[c], dh1s[c], dh3s[c], *dx_sums[c] = backward_pair(c, *dy_pairs[c], tok_cols, g_cols, places, w1, w3, w2, *saved[c], cap, pad, grp_cap)
+            last = (y_sums if step == 'f' else dx_sums)[c][0]
+
+        grads = weight_grads(xs, acts, ds, dh1s, dh3s)
 
         def combine(results):
             sums = []
@@ -316,8 +381,8 @@
                     sums.append((results[near][s] + hop_y(results[far][s])).astype(BF))
             return [sums[0]] + [hop_g(sums[k], k) for k in (1, 2, 3)]
 
-        y_out = collect(combine([f[4:6] for f in fwd]), q_cols)
-        dx_out = collect(combine([b[3:5] for b in bwd]), q_cols)
+        y_out = collect(combine(y_sums), q_cols)
+        dx_out = collect(combine(dx_sums), q_cols)
         return y_out, dx_out, grads[0], grads[1], grads[2]
 
     return jax.shard_map(device_fn, mesh=mesh, in_specs=(tok_spec, tok_spec, tok_spec, tok_spec, weight_spec, weight_spec, weight_spec), out_specs=(tok_spec, tok_spec, grad_spec, grad_spec, grad_spec), check_vma=False)

time: 498 us -> 519 us (1.042)
  waiting for transfers between devices: 154 us -> 208 us
  Pallas kernels: 274 us -> 241 us
    pallas_call x0 -> x2, Pallas kernels: none -> 77.7 us  [near_pair(): pl.pallas_call(functools.partial(near_kernel, cap, pad), grid=(experts,),...]
    pallas_call x4 -> x2, Pallas kernels: 110 us -> 54.4 us  [forward_pair(): pl.pallas_call(functools.partial(fwd_kernel, cap, pad), grid=(experts,),...]
    pallas_call x4 -> x2, Pallas kernels: 109 us -> 54.5 us  [backward_pair(): pl.pallas_call(functools.partial(bwd_kernel, cap, pad), grid=(experts,),...]
    ppermute x11, waiting for transfers between devices: 149 us -> 190 us  [hop_y(): return lax.ppermute(a, 'ing', [(0, 1), (1, 0)])]
    ppermute x20, waiting for transfers between devices: 5.34 us -> 18.4 us  [hop_g(): return lax.ppermute(a, 'grp', [(g, g ^ bits) for g in range(groups)])]
  transfers between devices with their start and end apart: 31 -> 31, of which waited for: 8 -> 8; matrix products, arithmetic and copies ran while one was open for 6% -> 6% of each run, Pallas kernels for 55% -> 46%
where the time goes in v2:
time: 519 us; the launch traced here: 510 us
  Pallas kernels  241 us (46%)
  waiting for transfers between devices  208 us (40%)
  other arithmetic  26.2 us (5%)
  starting transfers between devices  24.1 us (5%)
  local copies, waits for them, and re-layouts  7.37 us (1%)
    ppermute x11, waiting for transfers between devices, hop_y(): return lax.ppermute(a, 'ing', [(0, 1), (1, 0)])  190 us
    pallas_call x2, Pallas kernels, near_pair(): pl.pallas_call(functools.partial(near_kernel, cap, pad), grid=(experts,),...  77.7 us
    pallas_call x2, Pallas kernels, backward_pair(): pl.pallas_call(functools.partial(bwd_kernel, cap, pad), grid=(experts,),...  54.5 us
    pallas_call x2, Pallas kernels, forward_pair(): pl.pallas_call(functools.partial(fwd_kernel, cap, pad), grid=(experts,),...  54.4 us
    pallas_call x1, Pallas kernels, weight_grads(): pl.pallas_call(functools.partial(dw_kernel, chunks), grid=(experts,), in_...  43.8 us
    ppermute x20, waiting for transfers between devices, hop_g(): return lax.ppermute(a, 'grp', [(g, g ^ bits) for g in range(groups)])  18.4 us
    convert_element_type x8, other arithmetic, combine(): sums.append((results[near][s] + hop_y(results[far][s])).astype(BF))  15.9 us
    ppermute x11, starting transfers between devices, hop_y(): return lax.ppermute(a, 'ing', [(0, 1), (1, 0)])  13.1 us
  transfers between devices with their start and end apart: 31, of which 8 were waited for; matrix products, arithmetic and copies ran while one was open for 6% of the time, Pallas kernels for 46%

profile of v2, /device:TPU:0, one launch (start us, length us, event | category | flops | bytes accessed | tf_op | source)
XLA Modules:
  0.0 510.1 jit_solution(5392972927821677848)
XLA Ops:
  2.1 3.4 collective-permute-start
  5.5 2.0 collective-permute-start.15
  8.5 1.0 fusion.1.refs_4_
  9.6 1.2 collective-permute-done.1
  10.9 1.5 collective-permute-start.4
  12.4 4.1 collective-permute-done.4
  17.2 1.5 collective-permute-start.10
  18.7 24.3 %collective-permute-done.5.xa_ref = bf16[512,1536]{1,0:T(8,128)(2,1)S(1)} collective-permute-done((bf16[512,1536]{1,0:T(8,128)(2,1)}, bf16[512,1536]{1,0:T(8,128)(2,1)S(1)}, u32[]{:S(2)}, u32[]{:S(2)}) %collective-permute-start.5) | collective-permute-done | bytes 1572896 | tf_op jit(solution)/shard_map/ppermute | solution.py:312
  43.1 7.4 %select_reduce_fusion = (f32[8,8,72]{2,1,0:T(8,128)S(1)}, f32[8,8,72]{2,1,0:T(8,128)S(1)}, f32[8,8,72]{2,1,0:T(8,128)S(1)}) fusion(f32[8,512]{1,0:T(8,128)S(1)} %bitcast.32, f32[8,8,512]{2,1,0:T(8,128)S(1)} %slice.47, pred[8,8,512]{2,1,0:T(8,128)(4,1)S(1)} %compare_reduce_fusion, f32[8,8,512]{2,1,0:T(8,128)S(1)} %fusion.6, f32[512]{0:T(512)S(1)} %iota_add_fusion), kind=kLoop, calls=%fused_computation | loop fusion | flops 18860544 | bytes 368640 | tf_op jit(solution)/shard_map/reduce_sum | solution.py:292
  50.6 1.5 collective-permute-start.12
  52.1 1.1 copy-done.11
  54.2 2.1 reshape.89.gcol_ref
  57.0 2.1 convert_element_type.70.tok_ref
  59.1 16.3 %collective-permute-done.15.dya_ref = bf16[512,1536]{1,0:T(8,128)(2,1)} collective-permute-done((bf16[512,1536]{1,0:T(8,128)(2,1)}, bf16[512,1536]{1,0:T(8,128)(2,1)}, u32[]{:S(2)}, u32[]{:S(2)}) %collective-permute-start.15) | collective-permute-done | bytes 1572896 | tf_op jit(solution)/shard_map/ppermute | solution.py:312
  75.3 1.5 collective-permute-start.16
  77.1 27.1 %fwd_pair.2 = (bf16[8,144,1536]{2,1,0:T(8,128)(2,1)}, bf16[8,144,512]{2,1,0:T(8,128)(2,1)}, f32[8,144,512]{2,1,0:T(8,128)}, f32[8,144,512]{2,1,0:T(8,128)}, f32[256,1536]{1,0:T(8,128)}, /*index=5*/f32[256,1536]{1,0:T(8,128)}) custom-call(bf16[512,1536]{1,0:T(8,128)(2,1)} %copy-done.10, bf16[512,1536]{1,0:T(8,128)(2,1)} %collective-permute-done.6.xb_ref, ...), custom_call_target="tpu_custom_call" | custom-call | flops 14000000000 | bytes 50000000 | tf_op jit(solution)/shard_map/fwd_pair/pallas_call | solution.py:169
  104.3 0.8 collective-permute-start.7
  105.1 39.0 %near_pair.2 = (bf16[8,144,1536]{2,1,0:T(8,128)(2,1)}, bf16[8,144,512]{2,1,0:T(8,128)(2,1)}, bf16[8,144,1536]{2,1,0:T(8,128)(2,1)}, bf16[8,144,512]{2,1,0:T(8,12...) custom-call(bf16[512,1536]{1,0:T(8,128)(2,1)} %xa_ref.1, ...), custom_call_target="tpu_custom_call" | custom-call | flops 28000000000 | bytes 70000000 | tf_op jit(solution)/shard_map/near_pair/pallas_call | solution.py:205
  144.8 27.3 %fwd_pair.3 = (bf16[8,144,1536]{2,1,0:T(8,128)(2,1)}, bf16[8,144,512]{2,1,0:T(8,128)(2,1)}, f32[8,144,512]{2,1,0:T(8,128)}, f32[8,144,512]{2,1,0:T(8,128)}, f32[256,1536]{1,0:T(8,128)}, /*index=5*/f32[256,1536]{1,0:T(8,128)}) custom-call(bf16[512,1536]{1,0:T(8,128)(2,1)} %collective-permute-done.12.xa_ref, bf16[512,1536]{1,0:T(8,128)(2,1)} %collective-permute-done.19.xb_ref, ...), custom_call_target="tpu_custom_call" | custom-call | flops 14000000000 | bytes 50000000 | tf_op jit(solution)/shard_map/fwd_pair/pallas_call | solution.py:169
  172.1 1.3 collective-permute-start.8
  173.4 27.2 %bwd_pair.2 = (bf16[8,144,1536]{2,1,0:T(8,128)(2,1)}, bf16[8,144,512]{2,1,0:T(8,128)(2,1)}, bf16[8,144,512]{2,1,0:T(8,128)(2,1)}, f32[256,1536]{1,0:T(8,128)}, f32[256,1536]{1,0:T(8,128)}) custom-call(bf16[512,1536]{1,0:T(8,128)(2,1)} %collective-permute-done.15.dya_ref, bf16[512,1536]{1,0:T(8,128)(2,1)} %collective-permute-done.18.dyb_ref, ...), custom_call_target="tpu_custom_call" | custom-call | flops 14000000000 | bytes 50000000 | tf_op jit(solution)/shard_map/bwd_pair/pallas_call | solution.py:186
  200.7 27.3 %bwd_pair.3 = (bf16[8,144,1536]{2,1,0:T(8,128)(2,1)}, bf16[8,144,512]{2,1,0:T(8,128)(2,1)}, bf16[8,144,512]{2,1,0:T(8,128)(2,1)}, f32[256,1536]{1,0:T(8,128)}, f32[256,1536]{1,0:T(8,128)}) custom-call(bf16[512,1536]{1,0:T(8,128)(2,1)} %collective-permute-done.16.dya_ref, bf16[512,1536]{1,0:T(8,128)(2,1)} %collective-permute-done.17.dyb_ref, ...), custom_call_target="tpu_custom_call" | custom-call | flops 14000000000 | bytes 50000000 | tf_op jit(solution)/shard_map/bwd_pair/pallas_call | solution.py:186
  228.0 0.8 collective-permute-start.27
  228.8 1.2 collective-permute-start.24
  230.0 3.1 add_convert_fusion.6
  233.1 0.8 collective-permute-start.29
  233.9 1.1 add_convert_fusion.7.refs_0_
  235.0 1.2 collective-permute-start.25
  236.3 0.8 collective-permute-start.22
  237.0 38.7 %near_pair.3 = (bf16[8,144,1536]{2,1,0:T(8,128)(2,1)}, bf16[8,144,512]{2,1,0:T(8,128)(2,1)}, bf16[8,144,1536]{2,1,0:T(8,128)(2,1)}, bf16[8,144,512]{2,1,0:T(8,12...) custom-call(bf16[512,1536]{1,0:T(8,128)(2,1)} %collective-permute-do, ...), custom_call_target="tpu_custom_call" | custom-call | flops 28000000000 | bytes 70000000 | tf_op jit(solution)/shard_map/near_pair/pallas_call | solution.py:205
  275.8 90.9 %collective-permute-done.25 = f32[256,1536]{1,0:T(8,128)} collective-permute-done((f32[256,1536]{1,0:T(8,128)}, f32[256,1536]{1,0:T(8,128)}, u32[]{:S(2)}, u32[]{:S(2)}) %collective-permute-start.25) | collective-permute-done | bytes 1572896 | tf_op jit(solution)/shard_map/ppermute | solution.py:312
  366.7 0.8 collective-permute-start.20
  367.5 1.7 add_convert_fusion.2
  369.6 2.7 add_convert_fusion
  372.3 28.1 %collective-permute-done.22 = f32[256,1536]{1,0:T(8,128)} collective-permute-done((f32[256,1536]{1,0:T(8,128)}, f32[256,1536]{1,0:T(8,128)}, u32[]{:S(2)}, u32[]{:S(2)}) %collective-permute-start.22) | collective-permute-done | bytes 1572896 | tf_op jit(solution)/shard_map/ppermute | solution.py:312
  400.4 2.7 add_convert_fusion.4
  403.1 30.5 %collective-permute-done.20 = f32[256,1536]{1,0:T(8,128)S(1)} collective-permute-done((f32[256,1536]{1,0:T(8,128)}, f32[256,1536]{1,0:T(8,128)S(1)}, u32[]{:S(2)}, u32[]{:S(2)}) %collective-permute-start.20) | collective-permute-done | bytes 1572896 | tf_op jit(solution)/shard_map/ppermute | solution.py:312
  433.5 0.8 collective-permute-start.23
  434.3 1.1 add_convert_fusion.5
  435.4 0.8 collective-permute-start.21
  436.1 2.5 add_convert_fusion.1
  438.6 1.3 collective-permute-start.28
  439.9 0.8 collective-permute-start.30
  440.7 43.8 %weight_grads.1 = (f32[8,1536,512]{2,1,0:T(8,128)}, f32[8,1536,512]{2,1,0:T(8,128)}, f32[8,512,1536]{2,1,0:T(8,128)}) custom-call(bf16[8,144,1536]{2,1,0:T(8,128)(2,1)} %get-tuple-element.86.refs_0_, bf16[8,144,1536]{2,1,0:T(8,128)(2,1)} %get-tuple-element.87.refs_1_, bf16[8,144,1536]{2,1,0:T(8,128)(2,1)} %get-tuple-element.88.refs_2_, ...), custom_call_target="tpu_custom_call" | custom-call | flops 24999999488 | bytes 120000000 | tf_op jit(solution)/shard_map/weight_grads/pallas_call | solution.py:236
  484.5 1.1 add_convert_fusion.3.refs_0_
  485.6 5.5 %collect.2 = bf16[512,1536]{1,0:T(8,128)(2,1)} custom-call(bf16[256,1536]{1,0:T(8,128)(2,1)} %add_convert_fusion.7.refs_0_, bf16[256,1536]{1,0:T(8,128)(2,1)} %copy-done.13, bf16[256,1536]{1,0:T(8,128)(2,1)} %collective-permute-done.21.refs_2_, bf16[256,1536]{1,0:T(8,128)(2,1)} %collective-permute-done.23.refs_3_, s32[512,4]{1,0:T(8,128)} %fusion.1.refs_4_), custom_call_target="tpu_custom_call" | custom-call | flops 2000000000 | bytes 5000000 | tf_op jit(solution)/shard_map/collect/pallas_call | solution.py:264
  491.1 13.0 %collective-permute-done.30.refs_3_ = bf16[256,1536]{1,0:T(8,128)(2,1)} collective-permute-done((bf16[256,1536]{1,0:T(8,128)(2,1)}, bf16[256,1536]{1,0:T(8,128)(2,1)}, u32[]{:S(2)}, u32[]{:S(2)}) %collective-permute-start.30) | collective-permute-done | bytes 786464 | tf_op jit(solution)/shard_map/ppermute | solution.py:315
  504.2 5.5 %collect.3 = bf16[512,1536]{1,0:T(8,128)(2,1)} custom-call(bf16[256,1536]{1,0:T(8,128)(2,1)} %add_convert_fusion.3.refs_0_, bf16[256,1536]{1,0:T(8,128)(2,1)} %collective-permute-done.26.refs_1_, bf16[256,1536]{1,0:T(8,128)(2,1)} %collective-permute-done.28.refs_2_, bf16[256,1536]{1,0:T(8,128)(2,1)} %collective-permute-done.30.refs_3_, s32[512,4]{1,0:T(8,128)} %fusion.1.refs_4_), custom_call_target="tpu_custom_call" | custom-call | flops 2000000000 | bytes 5000000 | tf_op jit(solution)/shard_map/collect/pallas_call | solution.py:264
  (96 shorter events, 6.5 us)
Async XLA Ops:
  0.6 15.8 %copy-start.8 = (f32[512,6]{0,1:T(8,128)S(1)}, f32[512,6]{0,1:T(8,128)}, u32[]{:S(2)}) copy-start(f32[512,6]{0,1:T(8,128)} %param.9) | copy-start | bytes 36868
  2.1 7.5 %collective-permute-start = (f32[1,12,512]{2,1,0:T(8,128)S(1)}, f32[1,12,512]{2,1,0:T(8,128)S(1)}, u32[]{:S(2)}, u32[]{:S(2)}) collective-permute-start(f32[1,12,512]{2,1,0:T(8,128)S(1)} %maximum_bitcast_fusion), channel_id=1, source_target_pairs={{0,4},{4,0},{1,5},{5,1},{2,6},{6,2},{3,7},{7,3}} | collective-permute-start | bytes 73736 | tf_op jit(solution)/shard_map/ppermute | solution.py:312
  5.5 37.5 %collective-permute-start.5 = (bf16[512,1536]{1,0:T(8,128)(2,1)}, bf16[512,1536]{1,0:T(8,128)(2,1)S(1)}, u32[]{:S(2)}, u32[]{:S(2)}) collective-permute-start(bf16[512,1536]{1,0:T(8,128)(2,1)} %xa_ref.1), channel_id=1, source_target_pairs={{0,4},{4,0},{1,5},{5,1},{2,6},{6,2},{3,7},{7,3}} | collective-permute-start | bytes 4718600 | tf_op jit(solution)/shard_map/ppermute | solution.py:312
  5.5 69.8 %collective-permute-start.15 = (bf16[512,1536]{1,0:T(8,128)(2,1)}, bf16[512,1536]{1,0:T(8,128)(2,1)}, u32[]{:S(2)}, u32[]{:S(2)}) collective-permute-start(bf16[512,1536]{1,0:T(8,128)(2,1)} %dya_ref.1), channel_id=1, source_target_pairs={{0,4},{4,0},{1,5},{5,1},{2,6},{6,2},{3,7},{7,3}} | collective-permute-start | bytes 4718600 | tf_op jit(solution)/shard_map/ppermute | solution.py:312
  8.5 8.6 %copy-start.9 = (bf16[512,1536]{1,0:T(8,128)(2,1)S(1)}, bf16[512,1536]{1,0:T(8,128)(2,1)}, u32[]{:S(2)}) copy-start(bf16[512,1536]{1,0:T(8,128)(2,1)} %xa_ref.1) | copy-start | bytes 4718596
  9.6 1.3 collective-permute-start.1
  10.9 5.6 %collective-permute-start.4 = (f32[4,12,512]{2,1,0:T(8,128)S(1)}, f32[4,12,512]{2,1,0:T(8,128)S(1)}, u32[]{:S(2)}, u32[]{:S(2)}) collective-permute-start(f32[4,12,512]{2,1,0:T(8,128)S(1)} %pad_maximum_fusion), channel_id=1, source_target_pairs={{0,2},{1,3},{2,0},{3,1},{4,6},{5,7},{6,4},{7,5}} | collective-permute-start | bytes 294920 | tf_op jit(solution)/shard_map/ppermute | solution.py:315
  12.4 39.7 %collective-permute-start.2 = (bf16[512,1536]{1,0:T(8,128)(2,1)}, bf16[512,1536]{1,0:T(8,128)(2,1)S(1)}, u32[]{:S(2)}, u32[]{:S(2)}) collective-permute-start(bf16[512,1536]{1,0:T(8,128)(2,1)} %xa_ref.1), channel_id=1, source_target_pairs={{0,1},{1,0},{2,3},{3,2},{4,5},{5,4},{6,7},{7,6}} | collective-permute-start | bytes 4718600 | tf_op jit(solution)/shard_map/ppermute | solution.py:315
  17.2 58.2 %collective-permute-start.10 = (bf16[512,1536]{1,0:T(8,128)(2,1)S(1)}, bf16[512,1536]{1,0:T(8,128)(2,1)}, u32[]{:S(2)}, u32[]{:S(2)}) collective-permute-start(bf16[512,1536]{1,0:T(8,128)(2,1)S(1)} %copy-done.9), channel_id=1, source_target_pairs={{0,2},{1,3},{2,0},{3,1},{4,6},{5,7},{6,4},{7,5}} | collective-permute-start | bytes 4718600 | tf_op jit(solution)/shard_map/ppermute | solution.py:315
  42.9 13.3 %copy-start.10 = (bf16[512,1536]{1,0:T(8,128)(2,1)}, bf16[512,1536]{1,0:T(8,128)(2,1)S(1)}, u32[]{:S(2)}) copy-start(bf16[512,1536]{1,0:T(8,128)(2,1)S(1)} %collective-permute-done.5.xa_ref) | copy-start | bytes 4718596
  42.9 33.9 %collective-permute-start.6 = (bf16[512,1536]{1,0:T(8,128)(2,1)S(1)}, bf16[512,1536]{1,0:T(8,128)(2,1)}, u32[]{:S(2)}, u32[]{:S(2)}) collective-permute-start(bf16[512,1536]{1,0:T(8,128)(2,1)S(1)} %collective-permute-done.5.xa_ref), channel_id=1, source_target_pairs={{0,1},{1,0},{2,3},{3,2},{4,5},{5,4},{6,7},{7,6}} | collective-permute-start | bytes 4718600 | tf_op jit(solution)/shard_map/ppermute | solution.py:315
  50.6 53.7 %collective-permute-start.12 = (bf16[512,1536]{1,0:T(8,128)(2,1)S(1)}, bf16[512,1536]{1,0:T(8,128)(2,1)}, u32[]{:S(2)}, u32[]{:S(2)}) collective-permute-start(bf16[512,1536]{1,0:T(8,128)(2,1)S(1)} %collective-permute-done.5.xa_ref), channel_id=1, source_target_pairs={{0,2},{1,3},{2,0},{3,1},{4,6},{5,7},{6,4},{7,5}} | collective-permute-start | bytes 4718600 | tf_op jit(solution)/shard_map/ppermute | solution.py:315
  52.1 1.1 copy-start.11
  53.2 51.9 %collective-permute-start.3 = (bf16[512,1536]{1,0:T(8,128)(2,1)}, bf16[512,1536]{1,0:T(8,128)(2,1)}, u32[]{:S(2)}, u32[]{:S(2)}) collective-permute-start(bf16[512,1536]{1,0:T(8,128)(2,1)} %dya_ref.1), channel_id=1, source_target_pairs={{0,1},{1,0},{2,3},{3,2},{4,5},{5,4},{6,7},{7,6}} | collective-permute-start | bytes 4718600 | tf_op jit(solution)/shard_map/ppermute | solution.py:315
  75.3 96.8 %collective-permute-start.18 = (bf16[512,1536]{1,0:T(8,128)(2,1)}, bf16[512,1536]{1,0:T(8,128)(2,1)}, u32[]{:S(2)}, u32[]{:S(2)}) collective-permute-start(bf16[512,1536]{1,0:T(8,128)(2,1)} %collective-permute-done.15.dya_ref), channel_id=1, source_target_pairs={{0,1},{1,0},{2,3},{3,2},{4,5},{5,4},{6,7},{7,6}} | collective-permute-start | bytes 4718600 | tf_op jit(solution)/shard_map/ppermute | solution.py:315
  75.3 68.8 %collective-permute-start.16 = (bf16[512,1536]{1,0:T(8,128)(2,1)}, bf16[512,1536]{1,0:T(8,128)(2,1)}, u32[]{:S(2)}, u32[]{:S(2)}) collective-permute-start(bf16[512,1536]{1,0:T(8,128)(2,1)} %collective-permute-done.15.dya_ref), channel_id=1, source_target_pairs={{0,2},{1,3},{2,0},{3,1},{4,6},{5,7},{6,4},{7,5}} | collective-permute-start | bytes 4718600 | tf_op jit(solution)/shard_map/ppermute | solution.py:315
  76.9 158.1 %collective-permute-start.11 = (bf16[512,1536]{1,0:T(8,128)(2,1)}, bf16[512,1536]{1,0:T(8,128)(2,1)}, u32[]{:S(2)}, u32[]{:S(2)}) collective-permute-start(bf16[512,1536]{1,0:T(8,128)(2,1)} %collective-permute-done.10.xa_ref), channel_id=1, source_target_pairs={{0,1},{1,0},{2,3},{3,2},{4,5},{5,4},{6,7},{7,6}} | collective-permute-start | bytes 4718600 | tf_op jit(solution)/shard_map/ppermute | solution.py:315
  104.3 128.8 %collective-permute-start.7 = (f32[256,1536]{1,0:T(8,128)}, f32[256,1536]{1,0:T(8,128)S(1)}, u32[]{:S(2)}, u32[]{:S(2)}) collective-permute-start(f32[256,1536]{1,0:T(8,128)} %get-tuple-element.59), channel_id=1, source_target_pairs={{0,4},{4,0},{1,5},{5,1},{2,6},{6,2},{3,7},{7,3}} | collective-permute-start | bytes 4718600 | tf_op jit(solution)/shard_map/ppermute | solution.py:312
  105.1 39.5 %collective-permute-start.19 = (bf16[512,1536]{1,0:T(8,128)(2,1)}, bf16[512,1536]{1,0:T(8,128)(2,1)}, u32[]{:S(2)}, u32[]{:S(2)}) collective-permute-start(bf16[512,1536]{1,0:T(8,128)(2,1)} %collective-permute-done.12.xa_ref), channel_id=1, source_target_pairs={{0,1},{1,0},{2,3},{3,2},{4,5},{5,4},{6,7},{7,6}} | collective-permute-start | bytes 4718600 | tf_op jit(solution)/shard_map/ppermute | solution.py:315
  144.1 28.0 %copy-start.12 = (f32[256,1536]{1,0:T(8,128)S(1)}, f32[256,1536]{1,0:T(8,128)}, u32[]{:S(2)}) copy-start(f32[256,1536]{1,0:T(8,128)} %get-tuple-element.63) | copy-start | bytes 4718596
  144.1 56.5 %collective-permute-start.13 = (bf16[512,1536]{1,0:T(8,128)(2,1)}, bf16[512,1536]{1,0:T(8,128)(2,1)}, u32[]{:S(2)}, u32[]{:S(2)}) collective-permute-start(bf16[512,1536]{1,0:T(8,128)(2,1)} %dya_ref.1), channel_id=1, source_target_pairs={{0,2},{1,3},{2,0},{3,1},{4,6},{5,7},{6,4},{7,5}} | collective-permute-start | bytes 4718600 | tf_op jit(solution)/shard_map/ppermute | solution.py:315
  144.6 56.1 %collective-permute-start.17 = (bf16[512,1536]{1,0:T(8,128)(2,1)}, bf16[512,1536]{1,0:T(8,128)(2,1)}, u32[]{:S(2)}, u32[]{:S(2)}) collective-permute-start(bf16[512,1536]{1,0:T(8,128)(2,1)} %collective-permute-done.16.dya_ref), channel_id=1, source_target_pairs={{0,1},{1,0},{2,3},{3,2},{4,5},{5,4},{6,7},{7,6}} | collective-permute-start | bytes 4718600 | tf_op jit(solution)/shard_map/ppermute | solution.py:315
  172.1 56.6 %collective-permute-start.8 = (f32[256,1536]{1,0:T(8,128)S(1)}, f32[256,1536]{1,0:T(8,128)}, u32[]{:S(2)}, u32[]{:S(2)}) collective-permute-start(f32[256,1536]{1,0:T(8,128)S(1)} %copy-done.12), channel_id=1, source_target_pairs={{0,4},{4,0},{1,5},{5,1},{2,6},{6,2},{3,7},{7,3}} | collective-permute-start | bytes 4718600 | tf_op jit(solution)/shard_map/ppermute | solution.py:312
  200.7 35.6 %collective-permute-start.14 = (bf16[512,1536]{1,0:T(8,128)(2,1)}, bf16[512,1536]{1,0:T(8,128)(2,1)}, u32[]{:S(2)}, u32[]{:S(2)}) collective-permute-start(bf16[512,1536]{1,0:T(8,128)(2,1)} %collective-permute-done.13.dya_ref), channel_id=1, source_target_pairs={{0,1},{1,0},{2,3},{3,2},{4,5},{5,4},{6,7},{7,6}} | collective-permute-start | bytes 4718600 | tf_op jit(solution)/shard_map/ppermute | solution.py:315
  228.0 207.4 %collective-permute-start.27 = (f32[256,1536]{1,0:T(8,128)}, f32[256,1536]{1,0:T(8,128)}, u32[]{:S(2)}, u32[]{:S(2)}) collective-permute-start(f32[256,1536]{1,0:T(8,128)} %get-tuple-element.76), channel_id=1, source_target_pairs={{0,4},{4,0},{1,5},{5,1},{2,6},{6,2},{3,7},{7,3}} | collective-permute-start | bytes 4718600 | tf_op jit(solution)/shard_map/ppermute | solution.py:312
  228.8 211.1 %collective-permute-start.24 = (f32[256,1536]{1,0:T(8,128)}, f32[256,1536]{1,0:T(8,128)S(1)}, u32[]{:S(2)}, u32[]{:S(2)}) collective-permute-start(f32[256,1536]{1,0:T(8,128)} %get-tuple-element.72), channel_id=1, source_target_pairs={{0,4},{4,0},{1,5},{5,1},{2,6},{6,2},{3,7},{7,3}} | collective-permute-start | bytes 4718600 | tf_op jit(solution)/shard_map/ppermute | solution.py:312
  230.0 3.9 copy-start.2
  233.1 136.1 %collective-permute-start.29 = (f32[256,1536]{1,0:T(8,128)}, f32[256,1536]{1,0:T(8,128)}, u32[]{:S(2)}, u32[]{:S(2)}) collective-permute-start(f32[256,1536]{1,0:T(8,128)} %get-tuple-element.85), channel_id=1, source_target_pairs={{0,4},{4,0},{1,5},{5,1},{2,6},{6,2},{3,7},{7,3}} | collective-permute-start | bytes 4718600 | tf_op jit(solution)/shard_map/ppermute | solution.py:312
  235.0 131.7 %collective-permute-start.25 = (f32[256,1536]{1,0:T(8,128)}, f32[256,1536]{1,0:T(8,128)}, u32[]{:S(2)}, u32[]{:S(2)}) collective-permute-start(f32[256,1536]{1,0:T(8,128)} %get-tuple-element.82), channel_id=1, source_target_pairs={{0,4},{4,0},{1,5},{5,1},{2,6},{6,2},{3,7},{7,3}} | collective-permute-start | bytes 4718600 | tf_op jit(solution)/shard_map/ppermute | solution.py:312
  236.3 131.2 %copy-start.1 = (f32[256,1536]{1,0:T(8,128)S(1)}, f32[256,1536]{1,0:T(8,128)}, u32[]{:S(2)}) copy-start(f32[256,1536]{1,0:T(8,128)} %get-tuple-element.81) | copy-start | bytes 4718596
  236.3 164.1 %collective-permute-start.22 = (f32[256,1536]{1,0:T(8,128)}, f32[256,1536]{1,0:T(8,128)}, u32[]{:S(2)}, u32[]{:S(2)}) collective-permute-start(f32[256,1536]{1,0:T(8,128)} %get-tuple-element.80), channel_id=1, source_target_pairs={{0,4},{4,0},{1,5},{5,1},{2,6},{6,2},{3,7},{7,3}} | collective-permute-start | bytes 4718600 | tf_op jit(solution)/shard_map/ppermute | solution.py:312
  366.7 66.8 %collective-permute-start.20 = (f32[256,1536]{1,0:T(8,128)}, f32[256,1536]{1,0:T(8,128)S(1)}, u32[]{:S(2)}, u32[]{:S(2)}) collective-permute-start(f32[256,1536]{1,0:T(8,128)} %get-tuple-element.68), channel_id=1, source_target_pairs={{0,4},{4,0},{1,5},{5,1},{2,6},{6,2},{3,7},{7,3}} | collective-permute-start | bytes 4718600 | tf_op jit(solution)/shard_map/ppermute | solution.py:312
  367.5 1.8 copy-start.7
  367.5 2.1 copy-start.6
  369.2 69.4 %collective-permute-start.9 = (bf16[256,1536]{1,0:T(8,128)(2,1)S(1)}, bf16[256,1536]{1,0:T(8,128)(2,1)S(1)}, u32[]{:S(2)}, u32[]{:S(2)}) collective-permute-start(bf16[256,1536]{1,0:T(8,128)(2,1)S(1)} %copy-done.7), channel_id=1, source_target_pairs={{0,1},{1,0},{2,3},{3,2},{4,5},{5,4},{6,7},{7,6}} | collective-permute-start | bytes 2359304 | tf_op jit(solution)/shard_map/ppermute | solution.py:315
  369.6 30.8 %copy-start.5 = (f32[256,1536]{1,0:T(8,128)S(1)}, f32[256,1536]{1,0:T(8,128)}, u32[]{:S(2)}) copy-start(f32[256,1536]{1,0:T(8,128)} %get-tuple-element.79) | copy-start | bytes 4718596
  400.4 90.7 %collective-permute-start.26 = (bf16[256,1536]{1,0:T(8,128)(2,1)S(1)}, bf16[256,1536]{1,0:T(8,128)(2,1)}, u32[]{:S(2)}, u32[]{:S(2)}) collective-permute-start(bf16[256,1536]{1,0:T(8,128)(2,1)S(1)} %add_convert_fusion.2), channel_id=1, source_target_pairs={{0,1},{1,0},{2,3},{3,2},{4,5},{5,4},{6,7},{7,6}} | collective-permute-start | bytes 2359304 | tf_op jit(solution)/shard_map/ppermute | solution.py:315
  400.4 33.9 %copy-start.4 = (f32[256,1536]{1,0:T(8,128)S(1)}, f32[256,1536]{1,0:T(8,128)}, u32[]{:S(2)}) copy-start(f32[256,1536]{1,0:T(8,128)} %get-tuple-element.78) | copy-start | bytes 4718596
  433.5 52.1 %collective-permute-start.23 = (bf16[256,1536]{1,0:T(8,128)(2,1)}, bf16[256,1536]{1,0:T(8,128)(2,1)}, u32[]{:S(2)}, u32[]{:S(2)}) collective-permute-start(bf16[256,1536]{1,0:T(8,128)(2,1)} %add_convert_fusion.4), channel_id=1, source_target_pairs={{0,3},{1,2},{2,1},{3,0},{4,7},{5,6},{6,5},{7,4}} | collective-permute-start | bytes 2359304 | tf_op jit(solution)/shard_map/ppermute | solution.py:315
  434.3 1.8 copy-start.3
  435.4 50.3 %collective-permute-start.21 = (bf16[256,1536]{1,0:T(8,128)(2,1)}, bf16[256,1536]{1,0:T(8,128)(2,1)}, u32[]{:S(2)}, u32[]{:S(2)}) collective-permute-start(bf16[256,1536]{1,0:T(8,128)(2,1)} %add_convert_fusion.5), channel_id=1, source_target_pairs={{0,2},{1,3},{2,0},{3,1},{4,6},{5,7},{6,4},{7,5}} | collective-permute-start | bytes 2359304 | tf_op jit(solution)/shard_map/ppermute | solution.py:315
  438.6 2.1 copy-start.13
  438.6 52.5 %collective-permute-start.28 = (bf16[256,1536]{1,0:T(8,128)(2,1)}, bf16[256,1536]{1,0:T(8,128)(2,1)}, u32[]{:S(2)}, u32[]{:S(2)}) collective-permute-start(bf16[256,1536]{1,0:T(8,128)(2,1)} %add_convert_fusion.1), channel_id=1, source_target_pairs={{0,2},{1,3},{2,0},{3,1},{4,6},{5,7},{6,4},{7,5}} | collective-permute-start | bytes 2359304 | tf_op jit(solution)/shard_map/ppermute | solution.py:315
  439.9 64.3 %collective-permute-start.30 = (bf16[256,1536]{1,0:T(8,128)(2,1)}, bf16[256,1536]{1,0:T(8,128)(2,1)}, u32[]{:S(2)}, u32[]{:S(2)}) collective-permute-start(bf16[256,1536]{1,0:T(8,128)(2,1)} %add_convert_fusion), channel_id=1, source_target_pairs={{0,3},{1,2},{2,1},{3,0},{4,7},{5,6},{6,5},{7,4}} | collective-permute-start | bytes 2359304 | tf_op jit(solution)/shard_map/ppermute | solution.py:315
  440.7 43.8 %copy-start = (f32[256,1536]{1,0:T(8,128)S(1)}, f32[256,1536]{1,0:T(8,128)}, u32[]{:S(2)}) copy-start(f32[256,1536]{1,0:T(8,128)} %get-tuple-element.66) | copy-start | bytes 4718596

commit v3 on v2

--- a/solution.py
+++ b/solution.py
@@ -10,6 +10,8 @@
 
 BF = jnp.bfloat16
 F32 = jnp.float32
+ALONE = 1024.0
+SENT_SHARE = 7, 8
 PAIR = 2
 
 KERNEL_ORDER = (('f', 0), ('n', 2), ('f', 1), ('b', 0), ('b', 1), ('n', 3))
@@ -62,21 +64,22 @@
     return act, h3 * (sig * (1.0 + h1 * (1.0 - sig))), silu
 
 
+def weighted_rows(hit, weight, rows):
+    if weight is None:
+        return dot(jnp.where(hit, 1.0, 0.0).astype(BF), rows)
+    rest, total = weight, None
+    for _ in range(3):
+        part = rest.astype(BF)
+        term = dot(jnp.where(hit, part.astype(F32), 0.0).astype(BF), rows)
+        total = term if total is None else total + term
+        rest = rest - part.astype(F32)
+    return total
+
+
 def group_sums(p_refs, q_ref, rows_scr, g_ref=None):
     for s, p_ref in enumerate(p_refs):
         slots = lax.broadcasted_iota(jnp.int32, (p_ref.shape[0], q_ref.shape[2]), 0)
-        hit = q_ref[s] == slots
-        if g_ref is None:
-            p_ref[...] = dot(jnp.where(hit, 1.0, 0.0).astype(BF), rows_scr[s])
-            continue
-        rest = g_ref[s]
-        total = None
-        for _ in range(3):
-            part = rest.astype(BF)
-            term = dot(jnp.where(hit, part.astype(F32), 0.0).astype(BF), rows_scr[s])
-            total = term if total is None else total + term
-            rest = rest - part.astype(F32)
-        p_ref[...] = total
+        p_ref[...] = weighted_rows(q_ref[s] == slots, None if g_ref is None else g_ref[s], rows_scr[s])
 
 
 def fwd_kernel(cap, pad, xa_ref, xb_ref, tok_ref, q_ref, g_ref, w1_ref, w3_ref, w2_ref, xg_ref, a_ref, u_ref, v_ref, p0_ref, p1_ref, xg_scr, o_scr):
@@ -114,6 +117,66 @@
     @pl.when(e == pl.num_programs(0) - 1)
     def _():
         group_sums((p0_ref, p1_ref), q_ref, r_scr)
+
+
+def unit_rows(u_refs, unit_ref, rows_scr, weight_ref=None):
+    for s, u_ref in enumerate(u_refs):
+        units = lax.broadcasted_iota(jnp.int32, (u_ref.shape[0], unit_ref.shape[2]), 0)
+        u_ref[...] = weighted_rows(unit_ref[s] == units, None if weight_ref is None else weight_ref[s], rows_scr[s]).astype(BF)
+
+
+def far_fwd_kernel(cap, pad, xa_ref, xb_ref, tok_ref, q_ref, g_ref, unit_ref, form_ref, over_ref, w1_ref, w3_ref, w2_ref, xg_ref, a_ref, u_ref, v_ref, p0_ref, p1_ref, r0_ref, r1_ref, xg_scr, o_scr):
+    e = pl.program_id(0)
+
+    @pl.when(e == 0)
+    def _():
+        spread_rows(xg_scr, tok_ref, (xa_ref, xb_ref), cap)
+
+    xg_ref[0] = xg_scr[e]
+    act, u_ref[0], v_ref[0] = forward_expert(xg_scr[e], w1_ref, w3_ref)
+    a_ref[0] = act
+    keep_rows(o_scr, dot(act, w2_ref[0]), e, cap, pad)
+    done = e == pl.num_programs(0) - 1
+
+    @pl.when(done & (over_ref[0] == 0))
+    def _():
+        unit_rows((r0_ref, r1_ref), unit_ref, o_scr, form_ref)
+
+    @pl.when(done & (over_ref[0] != 0))
+    def _():
+        group_sums((p0_ref, p1_ref), q_ref, o_scr, g_ref)
+
+
+def far_bwd_kernel(cap, pad, dya_ref, dyb_ref, tok_ref, gcol_ref, q_ref, unit_ref, over_ref, w1_ref, w3_ref, w2_ref, u_ref, v_ref, d_ref, dh1_ref, dh3_ref, p0_ref, p1_ref, r0_ref, r1_ref, d_scr, r_scr):
+    e = pl.program_id(0)
+
+    @pl.when(e == 0)
+    def _():
+        spread_rows(d_scr, tok_ref, (dya_ref, dyb_ref), cap, gcol_ref)
+
+    d_ref[0] = d_scr[e]
+    da = dot_bt(d_scr[e], w2_ref[0])
+    dh1 = (da * u_ref[0]).astype(BF)
+    dh3 = (da * v_ref[0]).astype(BF)
+    dh1_ref[0] = dh1
+    dh3_ref[0] = dh3
+    keep_rows(r_scr, dot_bt(dh1, w1_ref[0]) + dot_bt(dh3, w3_ref[0]), e, cap, pad)
+    done = e == pl.num_programs(0) - 1
+
+    @pl.when(done & (over_ref[0] == 0))
+    def _():
+        unit_rows((r0_ref, r1_ref), unit_ref, r_scr)
+
+    @pl.when(done & (over_ref[0] != 0))
+    def _():
+        group_sums((p0_ref, p1_ref), q_ref, r_scr)
+
+
+def merge_kernel(weighted, n0_ref, n1_ref, r0_ref, r1_ref, place_ref, weight_ref, p0_ref, p1_ref):
+    for s, (n_ref, r_ref, p_ref) in enumerate(((n0_ref, r0_ref, p0_ref), (n1_ref, r1_ref, p1_ref))):
+        places = lax.broadcasted_iota(jnp.int32, (n_ref.shape[0], r_ref.shape[0]), 0)
+        total = weighted_rows(place_ref[s] == places, weight_ref[s] if weighted else None, r_ref[...])
+        p_ref[...] = (n_ref[...] + total).astype(BF)
 
 
 def near_kernel(cap, pad, xa_ref, xb_ref, dya_ref, dyb_ref, tok_ref, gcol_ref, q_ref, g_ref, w1_ref, w3_ref, w2_ref, xg_ref, a_ref, d_ref, dh1_ref, dh3_ref, y0_ref, y1_ref, z0_ref, z1_ref, xg_scr, d_scr, o_scr, r_scr):
@@ -194,6 +257,64 @@
         cost_estimate=pl.CostEstimate(flops=14 * 10**9, bytes_accessed=50 * 10**6, transcendentals=0),
         name="bwd_pair",
     )(dya, dyb, tok_col, g_col, q_row, w1, w3, w2, u, v)
+
+
+def flag():
+    return pl.BlockSpec(memory_space=pltpu.SMEM)
+
+
+def far_forward_pair(pair, xa, xb, tok_col, q_row, g_row, unit_row, form_row, over, w1, w3, w2, cap, pad, grp_cap, units):
+    experts, hidden, ff = w1.shape
+    rows = PAIR * cap
+    part, sent = ((grp_cap, hidden), F32), ((units, hidden), BF)
+    outs = [((experts, rows, hidden), BF), ((experts, rows, ff), BF), ((experts, rows, ff), F32), ((experts, rows, ff), F32), part, part, sent, sent]
+    tables = [tok_col, q_row, g_row, unit_row, form_row]
+    return pl.pallas_call(
+        functools.partial(far_fwd_kernel, cap, pad),
+        grid=(experts,),
+        in_specs=[whole(xa.shape), whole(xb.shape)] + [of_pair(pair, t.shape) for t in tables] + [flag(), per_expert(w1.shape), per_expert(w3.shape), per_expert(w2.shape)],
+        out_specs=[per_expert(s) if len(s) == 3 else whole(s) for s, _ in outs],
+        out_shape=[jax.ShapeDtypeStruct(s, t) for s, t in outs],
+        scratch_shapes=[pltpu.VMEM((experts, rows, hidden), BF), pltpu.VMEM((PAIR, experts * pad, hidden), BF)],
+        compiler_params=params(),
+        cost_estimate=pl.CostEstimate(flops=14 * 10**9, bytes_accessed=50 * 10**6, transcendentals=0),
+        name="far_fwd_pair",
+    )(xa, xb, *tables, over, w1, w3, w2)
+
+
+def far_backward_pair(pair, dya, dyb, tok_col, g_col, q_row, unit_row, over, w1, w3, w2, u, v, cap, pad, grp_cap, units):
+    experts, hidden, ff = w1.shape
+    rows = PAIR * cap
+    part, sent = ((grp_cap, hidden), F32), ((units, hidden), BF)
+    outs = [((experts, rows, hidden), BF), ((experts, rows, ff), BF), ((experts, rows, ff), BF), part, part, sent, sent]
+    tables = [tok_col, g_col, q_row, unit_row]
+    return pl.pallas_call(
+        functools.partial(far_bwd_kernel, cap, pad),
+        grid=(experts,),
+        in_specs=[whole(dya.shape), whole(dyb.shape)] + [of_pair(pair, t.shape) for t in tables] + [flag(), per_expert(w1.shape), per_expert(w3.shape), per_expert(w2.shape), per_expert(u.shape), per_expert(v.shape)],
+        out_specs=[per_expert(s) if len(s) == 3 else whole(s) for s, _ in outs],
+        out_shape=[jax.ShapeDtypeStruct(s, t) for s, t in outs],
+        scratch_shapes=[pltpu.VMEM((experts, rows, hidden), BF), pltpu.VMEM((PAIR, experts * pad, hidden), BF)],
+        compiler_params=params(),
+        cost_estimate=pl.CostEstimate(flops=14 * 10**9, bytes_accessed=50 * 10**6, transcendentals=0),
+        name="far_bwd_pair",
+    )(dya, dyb, *tables, over, w1, w3, w2, u, v)
+
+
+def merge_pair(pair, near, sent, place, weight, weighted):
+    grp_cap, hidden = near[0].shape
+    units = sent[0].shape[0]
+    block = hidden // 3
+    return pl.pallas_call(
+        functools.partial(merge_kernel, weighted),
+        grid=(3,),
+        in_specs=[pl.BlockSpec((grp_cap, block), lambda n: (0, n))] * 2 + [pl.BlockSpec((units, block), lambda n: (0, n))] * 2 + [of_pair(pair, place.shape), of_pair(pair, weight.shape)],
+        out_specs=[pl.BlockSpec((grp_cap, block), lambda n: (0, n))] * 2,
+        out_shape=[jax.ShapeDtypeStruct((grp_cap, hidden), BF)] * 2,
+        compiler_params=params(),
+        cost_estimate=pl.CostEstimate(flops=2 * 10**9, bytes_accessed=8 * 10**6, transcendentals=0),
+        name="merge_pair",
+    )(*near, *sent, place, weight)
 
 
 def near_pair(pair, xa, xb, dya, dyb, tok_col, g_col, q_row, g_row, w1, w3, w2, cap, pad, grp_cap):
@@ -291,7 +412,26 @@
     tok = jnp.sum(jnp.where(taken, numbers, 0.0), axis=3) - 1.0
     place = jnp.sum(jnp.where(taken, grp_pos[:, :, None, :] + 1.0, 0.0), axis=3) - 1.0
     weight = jnp.sum(jnp.where(taken, gate[:, :, None, :], 0.0), axis=3)
-    return tok, place, weight
+    here = jnp.sum(hit, axis=1).astype(F32)
+    alone = here == jnp.sum(ids // per_group == group, axis=1).astype(F32)
+    first = count_earlier(jnp.where(alone, jnp.minimum(here, 1.0), here))
+    rank, seen = [], jnp.zeros((sources, tokens), F32)
+    for e in range(experts):
+        rank.append(seen)
+        seen = seen + hit[:, e].astype(F32)
+    unit = first[:, None] + jnp.where(alone[:, None], ALONE, jnp.stack(rank, axis=1)) + 1.0
+    code = jnp.sum(jnp.where(taken, unit[:, :, None, :], 0.0), axis=3)
+    lone = code > ALONE
+    return tok, place, weight, jnp.where(lone, code - ALONE, code) - 1.0, lone
+
+
+def longest_list(ids, per_group, experts, away):
+    devices = away.shape[1]
+    count = jnp.sum(ids[:, None] // experts == jnp.arange(devices)[None, :, None, None], axis=2)
+    half = per_group // experts
+    in_group = jnp.repeat(jnp.sum(count.reshape(ids.shape[0], devices // half, half, -1), axis=2), half, axis=1)
+    rows = jnp.where(count == in_group, jnp.minimum(count, 1), count)
+    return jnp.max(jnp.where(away, jnp.sum(rows, axis=2), 0))
 
 
 def count_earlier(marks):
@@ -346,7 +486,19 @@
         dy_pairs = [(dy_far, dy_far_c), (dy_far_x, dy_far_xc), (dy_loc, dy_near_c), (dy_near_x, dy_near_xc)]
 
         ids_rel, gates_rel = routing[:, :top_k].astype(jnp.int32), routing[:, top_k:]
-        tok_rel, place_rel, weight_rel = slot_tables(ids_rel, gates_rel, (grp * inner + ing) * experts, experts, grp, per_group, cap)
+        units = tokens * SENT_SHARE[0] // SENT_SHARE[1]
+        tok_rel, place_rel, weight_rel, unit_rel, lone_rel = slot_tables(ids_rel, gates_rel, (grp * inner + ing) * experts, experts, grp, per_group, cap)
+        far = devices // 2
+        source_ing = jnp.where(jnp.arange(devices) < far, 1 - ing, ing)
+        away = source_ing[:, None] != (jnp.arange(devices) % inner)[None, :]
+        over = longest_list(ids_rel, per_group, experts, away) > units
+        over_flag = over.astype(jnp.int32).reshape(1)
+        flat = [t[:far].reshape(far, 1, -1) for t in (unit_rel, place_rel, jnp.where(lone_rel, 1.0, weight_rel))]
+        sent_here = flat[0] == jnp.arange(units, dtype=F32)[None, :, None]
+        notes = jnp.stack([jnp.max(jnp.where(sent_here, flat[1], -1.0), axis=2), jnp.max(jnp.where(sent_here, flat[2], 0.0), axis=2)])
+        notes = hop_y(notes)
+        sent_place = notes[0].astype(jnp.int32).reshape(far, 1, units)
+        sent_weight = notes[1].reshape(far, 1, units)
         own_groups = ids_loc.T[None] // per_group == (grp ^ jnp.arange(groups))[:, None, None]
         own_member = jnp.any(own_groups, axis=1)
         q_cols = jnp.where(own_member, count_earlier(own_member), -1.0).astype(jnp.int32).T
@@ -356,8 +508,10 @@
         spare = ((0, 0), (0, 0), (0, pad - cap))
         q_rows = jnp.pad(place_rel, spare, constant_values=-1.0).astype(jnp.int32).reshape(devices, 1, experts * pad)
         g_rows = jnp.pad(weight_rel, spare).reshape(devices, 1, experts * pad)
-
-        xs, acts, ds, dh1s, dh3s, y_sums, dx_sums = ([None] * 4 for _ in range(7))
+        unit_rows = jnp.pad(unit_rel[:far], spare, constant_values=-1.0).astype(jnp.int32).reshape(far, 1, experts * pad)
+        form_rows = jnp.pad(jnp.where(lone_rel, weight_rel, 1.0)[:far], spare).reshape(far, 1, experts * pad)
+
+        xs, acts, ds, dh1s, dh3s, y_sums, dx_sums, y_sent, dx_sent = ([None] * 4 for _ in range(9))
         saved = {}
         last = None
         for step, c in KERNEL_ORDER:
@@ -365,6 +519,12 @@
             if step == 'n':
                 xs[c], acts[c], ds[c], dh1s[c], dh3s[c], *sums = near_pair(c, *x_pairs[c], *dy_pairs[c], tok_cols, g_cols, places, g_rows, w1, w3, w2, cap, pad, grp_cap)
                 y_sums[c], dx_sums[c] = sums[:PAIR], sums[PAIR:]
+            elif step == 'f' and c < 2:
+                xs[c], acts[c], *saved[c], y0, y1, r0, r1 = far_forward_pair(c, *x_pairs[c], tok_cols, places, g_rows, unit_rows, form_rows, over_flag, w1, w3, w2, cap, pad, grp_cap, units)
+                y_sums[c], y_sent[c] = (y0, y1), (r0, r1)
+            elif step == 'b' and c < 2:
+                ds[c], dh1s[c], dh3s[c], z0, z1, r0, r1 = far_backward_pair(c, *dy_pairs[c], tok_cols, g_cols, places, unit_rows, over_flag, w1, w3, w2, *saved[c], cap, pad, grp_cap, units)
+                dx_sums[c], dx_sent[c] = (z0, z1), (r0, r1)
             elif step == 'f':
                 xs[c], acts[c], *saved[c], y0, y1 = forward_pair(c, *x_pairs[c], tok_cols, places, g_rows, w1, w3, w2, cap, pad, grp_cap)
                 y_sums[c] = (y0, y1)
@@ -374,15 +534,23 @@
 
         grads = weight_grads(xs, acts, ds, dh1s, dh3s)
 
-        def combine(results):
+        def combine(results, sent, weighted):
             sums = []
-            for far, near in ((0, 2), (1, 3)):
-                for s in (0, 1):
-                    sums.append((results[near][s] + hop_y(results[far][s])).astype(BF))
+            for pair, near in ((0, 2), (1, 3)):
+                arrived = [hop_y(r) for r in sent[pair]]
+
+                def by_rows(ops):
+                    return list(merge_pair(pair, ops[0], ops[1], sent_place, sent_weight, weighted))
+
+                def by_sums(ops):
+                    return [(n + hop_y(f)).astype(BF) for n, f in zip(ops[0], ops[2])]
+
+                sums += lax.cond(over, by_sums, by_rows, (list(results[near]), arrived, list(results[pair])))
             return [sums[0]] + [hop_g(sums[k], k) for k in (1, 2, 3)]
 
-        y_out = collect(combine(y_sums), q_cols)
-        dx_out = collect(combine(dx_sums), q_cols)
+        y_parts = combine(y_sums, y_sent, True)
+        y_out = collect(y_parts, q_cols)
+        dx_out = collect(combine(dx_sums, dx_sent, False), q_cols)
         return y_out, dx_out, grads[0], grads[1], grads[2]
 
     return jax.shard_map(device_fn, mesh=mesh, in_specs=(tok_spec, tok_spec, tok_spec, tok_spec, weight_spec, weight_spec, weight_spec), out_specs=(tok_spec, tok_spec, grad_spec, grad_spec, grad_spec), check_vma=False)

time: 519 us -> 519 us (level)
  Pallas kernels: 241 us -> 271 us
  waiting for transfers between devices: 208 us -> 183 us
  other arithmetic: 26.2 us -> 15.1 us
  local copies, waits for them, and re-layouts: 7.37 us -> 14.6 us
    pallas_call x4 -> x8, Pallas kernels: 109 us -> 141 us  [the longest x2 62.2 us: far_forward_pair(): pl.pallas_call(functools.partial(far_fwd_kernel, cap, pad), grid=(experts...]
    ppermute x11 -> x12, waiting for transfers between devices: 190 us -> 162 us  [hop_y(): return lax.ppermute(a, 'ing', [(0, 1), (1, 0)])]
    convert_element_type x8 -> x1, other arithmetic: 15.9 us -> 0.01 us  [device_fn(): jnp.pad(unit_rel[:far], spare, constant_values=-1.0).astype(jnp.int32)]
    ppermute x11 -> x12, starting transfers between devices: 13.1 us -> 14.1 us  [hop_y(): return lax.ppermute(a, 'ing', [(0, 1), (1, 0)])]
  transfers between devices with their start and end apart: 31 -> 32, of which waited for: 8 -> 11; matrix products, arithmetic and copies ran while one was open for 6% -> 5% of each run, Pallas kernels for 46% -> 52%
where the time goes in v3:
time: 519 us; the launch traced here: 511 us
  Pallas kernels  271 us (52%)
  waiting for transfers between devices  183 us (35%)
  starting transfers between devices  24.5 us (5%)
  other arithmetic  15.1 us (3%)
  local copies, waits for them, and re-layouts  14.6 us (3%)
    ppermute x12, waiting for transfers between devices, hop_y(): return lax.ppermute(a, 'ing', [(0, 1), (1, 0)])  162 us
    pallas_call x2, Pallas kernels, near_pair(): pl.pallas_call(functools.partial(near_kernel, cap, pad), grid=(experts,),...  75.5 us
    pallas_call x2, Pallas kernels, far_forward_pair(): pl.pallas_call(functools.partial(far_fwd_kernel, cap, pad), grid=(experts...  62.2 us
    pallas_call x2, Pallas kernels, far_backward_pair(): pl.pallas_call(functools.partial(far_bwd_kernel, cap, pad), grid=(experts...  58.3 us
    pallas_call x1, Pallas kernels, weight_grads(): pl.pallas_call(functools.partial(dw_kernel, chunks), grid=(experts,), in_...  43.9 us
    ppermute x20, waiting for transfers between devices, hop_g(): return lax.ppermute(a, 'grp', [(g, g ^ bits) for g in range(groups)])  20.2 us
    pallas_call x4, Pallas kernels, merge_pair(): pl.pallas_call(functools.partial(merge_kernel, weighted), grid=(3,), in_s...  20.1 us
    ppermute x12, starting transfers between devices, hop_y(): return lax.ppermute(a, 'ing', [(0, 1), (1, 0)])  14.1 us
  transfers between devices with their start and end apart: 32, of which 11 were waited for; matrix products, arithmetic and copies ran while one was open for 5% of the time, Pallas kernels for 52%

profile of v3, /device:TPU:0, one launch (start us, length us, event | category | flops | bytes accessed | tf_op | source)
XLA Modules:
  0.0 510.9 jit_solution(8502123149373101194)
XLA Ops:
  2.1 3.4 collective-permute-start.8
  5.5 2.0 collective-permute-start.24
  7.7 1.2 collective-permute-done.9
  8.9 1.8 collective-permute-start.10
  10.7 3.8 collective-permute-done.10
  16.8 9.7 %select_reduce_fusion = (f32[8,8,72]{2,1,0:T(8,128)S(1)}, f32[8,8,72]{2,1,0:T(8,128)S(1)}, f32[8,8,72]{2,1,0:T(8,128)S(1)}, f32[8,8,72]{2,1,0:T(8,128)S(1)}) fusion(f32[8,8,512]{2,1,0:T(8,128)S(1)} %copy.58, f32[8,8,512]{2,1,0:T(8,128)S(1)} %slice.100, pred[8,8,512]{2,1,0:T(8,128)(4,1)S(1)} %compare_reduce_fusion, f32[8,512]{1,0:T(8,128)S(1)} %bitcast.41, ...), kind=kLoop, calls=%fused_computation.8 | loop fusion | flops 23574528 | bytes 518144 | tf_op jit(solution)/shard_map/reduce_sum | solution.py:423
  26.7 16.3 %collective-permute-done.13.xa_ref = bf16[512,1536]{1,0:T(8,128)(2,1)} collective-permute-done((bf16[512,1536]{1,0:T(8,128)(2,1)}, bf16[512,1536]{1,0:T(8,128)(2,1)}, u32[]{:S(2)}, u32[]{:S(2)}) %collective-permute-start.13) | collective-permute-done | bytes 1572896 | tf_op jit(solution)/shard_map/ppermute | solution.py:452
  43.6 1.1 select_reduce_fusion.5
  46.2 1.5 collective-permute-start.21
  47.7 2.1 reshape.248.gcol_ref
  53.2 2.1 convert_element_type.180.tok_ref
  55.3 20.3 %collective-permute-done.17 = f32[2,4,448]{2,1,0:T(4,128)S(1)} collective-permute-done((f32[2,4,448]{2,1,0:T(4,128)S(1)}, f32[2,4,448]{2,1,0:T(4,128)S(1)}, u32[]{:S(2)}, u32[]{:S(2)}) %collective-permute-start.17) | collective-permute-done | bytes 14368 | tf_op jit(solution)/shard_map/ppermute | solution.py:452
  75.6 1.5 collective-permute-start.25
  77.2 31.0 %far_fwd_pair.2 = (bf16[8,144,1536]{2,1,0:T(8,128)(2,1)}, bf16[8,144,512]{2,1,0:T(8,128)(2,1)}, f32[8,144,512]{2,1,0:T(8,128)}, f32[8,144,512]{2,1,0:T(8,128)}, ...) custom-call(bf16[512,1536]{1,0:T(8,128)(2,1)} %collective-permute-done.13.xa_r, ...), custom_call_target="tpu_custom_call" | custom-call | flops 14000000000 | bytes 50000000 | tf_op jit(solution)/shard_map/far_fwd_pair/pallas_call | solution.py:272
  109.0 1.2 collective-permute-start.16
  110.2 37.8 %near_pair.2 = (bf16[8,144,1536]{2,1,0:T(8,128)(2,1)}, bf16[8,144,512]{2,1,0:T(8,128)(2,1)}, bf16[8,144,1536]{2,1,0:T(8,128)(2,1)}, bf16[8,144,512]{2,1,0:T(8,12...) custom-call(bf16[512,1536]{1,0:T(8,128)(2,1)} %xa_ref.1, ...), custom_call_target="tpu_custom_call" | custom-call | flops 28000000000 | bytes 70000000 | tf_op jit(solution)/shard_map/near_pair/pallas_call | solution.py:326
  148.0 22.3 %collective-permute-done.16 = bf16[448,1536]{1,0:T(8,128)(2,1)} collective-permute-done((bf16[448,1536]{1,0:T(8,128)(2,1)}, bf16[448,1536]{1,0:T(8,128)(2,1)}, u32[]{:S(2)}, u32[]{:S(2)}) %collective-permute-start.16) | collective-permute-done | bytes 1376288 | tf_op jit(solution)/shard_map/ppermute | solution.py:452
  170.3 7.1 %conditional.4 = ((bf16[256,1536]{1,0:T(8,128)(2,1)}, bf16[256,1536]{1,0:T(8,128)(2,1)})) conditional(s32[]{:T(128)} %convert_element_type.160, (f32[256,1536]{1,0:T(8,128)}, f32[256,1536]{1,0:T(8,128)}, bf16[448,1536]{1,0:T(8,128)(2,1)}, bf16[448,1536]{1,0:T(8,128)(2,1)}, s32[4,1,448]{2,0,1:T(4,128)S(1)}, ...), branch_computations={%region_15.16_spmd, %region_16.17_spmd} | conditional | flops 2000000000 | bytes 26738820 | solution.py:548
  171.5 5.9 %merge_pair.4 = (bf16[256,1536]{1,0:T(8,128)(2,1)}, bf16[256,1536]{1,0:T(8,128)(2,1)}) custom-call(f32[256,1536]{1,0:T(8,128)} %get-tuple-element.80.n0_ref, f32[256,1536]{1,0:T(8,128)} %get-tuple-element.81.n1_ref, bf16[448,1536]{1,0:T(8,128)(2,1)} %get-tuple-element.82.r0_ref, bf16[448,1536]{1,0:T(8,128)(2,1)} %get-tuple-element.83.r1_ref, ...), custom_call_target="tpu_custom_call" | custom-call | flops 2000000000 | bytes 8000000 | tf_op jit(solution)/shard_map/cond/branch_0_fun/merge_pair/pallas_call | solution.py:308
  177.8 1.5 collective-permute-start.22
  179.4 31.2 %far_fwd_pair.3 = (bf16[8,144,1536]{2,1,0:T(8,128)(2,1)}, bf16[8,144,512]{2,1,0:T(8,128)(2,1)}, f32[8,144,512]{2,1,0:T(8,128)}, f32[8,144,512]{2,1,0:T(8,128)}, ...) custom-call(bf16[512,1536]{1,0:T(8,128)(2,1)} %collective-permute-done.21.xa_r, ...), custom_call_target="tpu_custom_call" | custom-call | flops 14000000000 | bytes 50000000 | tf_op jit(solution)/shard_map/far_fwd_pair/pallas_call | solution.py:272
  210.6 29.2 %far_bwd_pair.2 = (bf16[8,144,1536]{2,1,0:T(8,128)(2,1)}, bf16[8,144,512]{2,1,0:T(8,128)(2,1)}, bf16[8,144,512]{2,1,0:T(8,128)(2,1)}, f32[256,1536]{1,0:T(8,128)...) custom-call(bf16[512,1536]{1,0:T(8,128)(2,1)} %collective-permute-done.24.dya_ref, ...), custom_call_target="tpu_custom_call" | custom-call | flops 14000000000 | bytes 50000000 | tf_op jit(solution)/shard_map/far_bwd_pair/pallas_call | solution.py:291
  239.8 0.9 collective-permute-start.33
  240.7 1.2 collective-permute-start.34
  241.9 5.1 collective-permute-done.22.dya_ref
  247.3 1.0 fusion.1.refs_4_
  248.3 24.9 %collective-permute-done.33 = bf16[448,1536]{1,0:T(8,128)(2,1)} collective-permute-done((bf16[448,1536]{1,0:T(8,128)(2,1)}, bf16[448,1536]{1,0:T(8,128)(2,1)}, u32[]{:S(2)}, u32[]{:S(2)}) %collective-permute-start.33) | collective-permute-done | bytes 1376288 | tf_op jit(solution)/shard_map/ppermute | solution.py:452
  273.2 29.0 %collective-permute-done.34 = bf16[448,1536]{1,0:T(8,128)(2,1)} collective-permute-done((bf16[448,1536]{1,0:T(8,128)(2,1)}, bf16[448,1536]{1,0:T(8,128)(2,1)}, u32[]{:S(2)}, u32[]{:S(2)}) %collective-permute-start.34) | collective-permute-done | bytes 1376288 | tf_op jit(solution)/shard_map/ppermute | solution.py:452
  302.2 5.3 %conditional.6 = ((bf16[256,1536]{1,0:T(8,128)(2,1)}, bf16[256,1536]{1,0:T(8,128)(2,1)})) conditional(s32[]{:T(128)} %convert_element_type.160, (f32[256,1536]{1,0:T(8,128)S(1)}, f32[256,1536]{1,0:T(8,128)S(1)}, bf16[448,1536]{1,0:T(8,128)(2,1)}, bf16[448,1536]{1,0:T(8,128)(2,1)}, s32[4,1,448]{2,0,1:T(4,128)S(1)}, ...), branch_computations={%region_20.21_spmd, %region_21.22_spmd} | conditional | flops 2000000000 | bytes 20447336 | solution.py:548
  303.4 4.1 merge_pair.6
  308.4 1.2 collective-permute-start.30
  309.6 29.1 %far_bwd_pair.3 = (bf16[8,144,1536]{2,1,0:T(8,128)(2,1)}, bf16[8,144,512]{2,1,0:T(8,128)(2,1)}, bf16[8,144,512]{2,1,0:T(8,128)(2,1)}, f32[256,1536]{1,0:T(8,128)...) custom-call(bf16[512,1536]{1,0:T(8,128)(2,1)} %collective-permute-done.25.dya_ref, ...), custom_call_target="tpu_custom_call" | custom-call | flops 14000000000 | bytes 50000000 | tf_op jit(solution)/shard_map/far_bwd_pair/pallas_call | solution.py:291
  339.6 1.2 collective-permute-start.37
  340.8 37.7 %near_pair.3 = (bf16[8,144,1536]{2,1,0:T(8,128)(2,1)}, bf16[8,144,512]{2,1,0:T(8,128)(2,1)}, bf16[8,144,1536]{2,1,0:T(8,128)(2,1)}, bf16[8,144,512]{2,1,0:T(8,12...) custom-call(bf16[512,1536]{1,0:T(8,128)(2,1)} %collective-permute-do, ...), custom_call_target="tpu_custom_call" | custom-call | flops 28000000000 | bytes 70000000 | tf_op jit(solution)/shard_map/near_pair/pallas_call | solution.py:326
  378.5 21.4 %collective-permute-done.36 = bf16[448,1536]{1,0:T(8,128)(2,1)} collective-permute-done((bf16[448,1536]{1,0:T(8,128)(2,1)}, bf16[448,1536]{1,0:T(8,128)(2,1)}, u32[]{:S(2)}, u32[]{:S(2)}) %collective-permute-start.36) | collective-permute-done | bytes 1376288 | tf_op jit(solution)/shard_map/ppermute | solution.py:452
  399.9 28.1 %collective-permute-done.37 = bf16[448,1536]{1,0:T(8,128)(2,1)} collective-permute-done((bf16[448,1536]{1,0:T(8,128)(2,1)}, bf16[448,1536]{1,0:T(8,128)(2,1)}, u32[]{:S(2)}, u32[]{:S(2)}) %collective-permute-start.37) | collective-permute-done | bytes 1376288 | tf_op jit(solution)/shard_map/ppermute | solution.py:452
  428.1 6.1 %conditional.7 = ((bf16[256,1536]{1,0:T(8,128)(2,1)}, bf16[256,1536]{1,0:T(8,128)(2,1)})) conditional(s32[]{:T(128)} %convert_element_type.160, (f32[256,1536]{1,0:T(8,128)}, f32[256,1536]{1,0:T(8,128)}, bf16[448,1536]{1,0:T(8,128)(2,1)}, bf16[448,1536]{1,0:T(8,128)(2,1)}, s32[4,1,448]{2,0,1:T(4,128)S(1)}, ...), branch_computations={%region_22.23_spmd, %region_23.24_spmd} | conditional | flops 2000000000 | bytes 26738820 | solution.py:548
  429.3 4.9 merge_pair.7
  434.7 6.4 %conditional.5 = ((bf16[256,1536]{1,0:T(8,128)(2,1)}, bf16[256,1536]{1,0:T(8,128)(2,1)})) conditional(s32[]{:T(128)} %convert_element_type.160, (f32[256,1536]{1,0:T(8,128)S(1)}, f32[256,1536]{1,0:T(8,128)S(1)}, bf16[448,1536]{1,0:T(8,128)(2,1)}, bf16[448,1536]{1,0:T(8,128)(2,1)}, s32[4,1,448]{2,0,1:T(4,128)S(1)}, ...), branch_computations={%region_17.18_spmd, %region_18.19_spmd} | conditional | flops 2000000000 | bytes 20447336 | solution.py:548
  436.0 5.2 %merge_pair.5 = (bf16[256,1536]{1,0:T(8,128)(2,1)}, bf16[256,1536]{1,0:T(8,128)(2,1)}) custom-call(f32[256,1536]{1,0:T(8,128)S(1)} %get-tuple-element.90.n0_ref, f32[256,1536]{1,0:T(8,128)S(1)} %get-tuple-element.91.n1_ref, bf16[448,1536]{1,0:T(8,128)(2,1)} %get-tuple-element.92.r0_ref, bf16[448,1536]{1,0:T(8,128)(2,1)} %get-tuple-element.93.r1_ref, ...), custom_call_target="tpu_custom_call" | custom-call | flops 2000000000 | bytes 8000000 | tf_op jit(solution)/shard_map/cond/branch_0_fun/merge_pair/pallas_call | solution.py:308
  441.1 1.3 collective-permute-start.39
  443.0 1.2 collective-permute-start.32
  444.1 43.9 %weight_grads.1 = (f32[8,1536,512]{2,1,0:T(8,128)}, f32[8,1536,512]{2,1,0:T(8,128)}, f32[8,512,1536]{2,1,0:T(8,128)}) custom-call(bf16[8,144,1536]{2,1,0:T(8,128)(2,1)} %get-tuple-element.238.refs_0_, bf16[8,144,1536]{2,1,0:T(8,128)(2,1)} %get-tuple-element.239.refs_1_, bf16[8,144,1536]{2,1,0:T(8,128)(2,1)} %get-tuple-element.240.refs_2_, ...), custom_call_target="tpu_custom_call" | custom-call | flops 24999999488 | bytes 120000000 | tf_op jit(solution)/shard_map/weight_grads/pallas_call | solution.py:357
  488.1 0.9 copy-done.6
  489.0 5.4 %collect.3 = bf16[512,1536]{1,0:T(8,128)(2,1)} custom-call(bf16[256,1536]{1,0:T(8,128)(2,1)S(1)} %copy-done.8, bf16[256,1536]{1,0:T(8,128)(2,1)} %collective-permute-done.35.refs_1_, bf16[256,1536]{1,0:T(8,128)(2,1)} %collective-permute-done.38.refs_2_, bf16[256,1536]{1,0:T(8,128)(2,1)} %copy-done.6, s32[512,4]{1,0:T(8,128)} %fusion.1.refs_4_), custom_call_target="tpu_custom_call" | custom-call | flops 2000000000 | bytes 5000000 | tf_op jit(solution)/shard_map/collect/pallas_call | solution.py:385
  494.4 10.0 %collective-permute-done.32.refs_3_ = bf16[256,1536]{1,0:T(8,128)(2,1)S(1)} collective-permute-done((bf16[256,1536]{1,0:T(8,128)(2,1)}, bf16[256,1536]{1,0:T(8,128)(2,1)S(1)}, u32[]{:S(2)}, u32[]{:S(2)}) %collective-permute-start.32) | collective-permute-done | bytes 786464 | tf_op jit(solution)/shard_map/ppermute | solution.py:455
  504.4 0.9 copy-done.5
  505.4 5.3 %collect.2 = bf16[512,1536]{1,0:T(8,128)(2,1)} custom-call(bf16[256,1536]{1,0:T(8,128)(2,1)S(1)} %copy-done.7, bf16[256,1536]{1,0:T(8,128)(2,1)} %collective-permute-done.18.refs_1_, bf16[256,1536]{1,0:T(8,128)(2,1)} %copy-done.4, bf16[256,1536]{1,0:T(8,128)(2,1)} %copy-done.5, s32[512,4]{1,0:T(8,128)} %fusion.1.refs_4_), custom_call_target="tpu_custom_call" | custom-call | flops 2000000000 | bytes 5000000 | tf_op jit(solution)/shard_map/collect/pallas_call | solution.py:385
  (131 shorter events, 18.0 us)
Async XLA Ops:
  2.1 5.5 %collective-permute-start.8 = (f32[1,12,512]{2,1,0:T(8,128)S(1)}, f32[1,12,512]{2,1,0:T(8,128)S(1)}, u32[]{:S(2)}, u32[]{:S(2)}) collective-permute-start(f32[1,12,512]{2,1,0:T(8,128)S(1)} %maximum_bitcast_fusion), channel_id=1, source_target_pairs={{0,4},{4,0},{1,5},{5,1},{2,6},{6,2},{3,7},{7,3}} | collective-permute-start | bytes 73736 | tf_op jit(solution)/shard_map/ppermute | solution.py:452
  5.4 37.6 %collective-permute-start.13 = (bf16[512,1536]{1,0:T(8,128)(2,1)}, bf16[512,1536]{1,0:T(8,128)(2,1)}, u32[]{:S(2)}, u32[]{:S(2)}) collective-permute-start(bf16[512,1536]{1,0:T(8,128)(2,1)} %xa_ref.1), channel_id=1, source_target_pairs={{0,4},{4,0},{1,5},{5,1},{2,6},{6,2},{3,7},{7,3}} | collective-permute-start | bytes 4718600 | tf_op jit(solution)/shard_map/ppermute | solution.py:452
  5.5 70.1 %collective-permute-start.24 = (bf16[512,1536]{1,0:T(8,128)(2,1)}, bf16[512,1536]{1,0:T(8,128)(2,1)}, u32[]{:S(2)}, u32[]{:S(2)}) collective-permute-start(bf16[512,1536]{1,0:T(8,128)(2,1)} %dya_ref.1), channel_id=1, source_target_pairs={{0,4},{4,0},{1,5},{5,1},{2,6},{6,2},{3,7},{7,3}} | collective-permute-start | bytes 4718600 | tf_op jit(solution)/shard_map/ppermute | solution.py:452
  7.6 1.3 collective-permute-start.9
  8.9 5.6 %collective-permute-start.10 = (f32[4,12,512]{2,1,0:T(8,128)S(1)}, f32[4,12,512]{2,1,0:T(8,128)S(1)}, u32[]{:S(2)}, u32[]{:S(2)}) collective-permute-start(f32[4,12,512]{2,1,0:T(8,128)S(1)} %pad_maximum_fusion), channel_id=1, source_target_pairs={{0,2},{1,3},{2,0},{3,1},{4,6},{5,7},{6,4},{7,5}} | collective-permute-start | bytes 294920 | tf_op jit(solution)/shard_map/ppermute | solution.py:455
  10.7 37.0 %collective-permute-start.11 = (bf16[512,1536]{1,0:T(8,128)(2,1)}, bf16[512,1536]{1,0:T(8,128)(2,1)}, u32[]{:S(2)}, u32[]{:S(2)}) collective-permute-start(bf16[512,1536]{1,0:T(8,128)(2,1)} %xa_ref.1), channel_id=1, source_target_pairs={{0,1},{1,0},{2,3},{3,2},{4,5},{5,4},{6,7},{7,6}} | collective-permute-start | bytes 4718600 | tf_op jit(solution)/shard_map/ppermute | solution.py:455
  16.6 31.0 %copy-start.3 = (bf16[512,1536]{1,0:T(8,128)(2,1)S(1)}, bf16[512,1536]{1,0:T(8,128)(2,1)}, u32[]{:S(2)}) copy-start(bf16[512,1536]{1,0:T(8,128)(2,1)} %dya_ref.1) | copy-start | bytes 4718596
  43.0 34.1 %collective-permute-start.14 = (bf16[512,1536]{1,0:T(8,128)(2,1)}, bf16[512,1536]{1,0:T(8,128)(2,1)}, u32[]{:S(2)}, u32[]{:S(2)}) collective-permute-start(bf16[512,1536]{1,0:T(8,128)(2,1)} %collective-permute-done.13.xa_ref), channel_id=1, source_target_pairs={{0,1},{1,0},{2,3},{3,2},{4,5},{5,4},{6,7},{7,6}} | collective-permute-start | bytes 4718600 | tf_op jit(solution)/shard_map/ppermute | solution.py:455
  44.7 30.9 %collective-permute-start.17 = (f32[2,4,448]{2,1,0:T(4,128)S(1)}, f32[2,4,448]{2,1,0:T(4,128)S(1)}, u32[]{:S(2)}, u32[]{:S(2)}) collective-permute-start(f32[2,4,448]{2,1,0:T(4,128)S(1)} %pad_maximum_fusion.2), channel_id=1, source_target_pairs={{0,4},{4,0},{1,5},{5,1},{2,6},{6,2},{3,7},{7,3}} | collective-permute-start | bytes 43016 | tf_op jit(solution)/shard_map/ppermute | solution.py:452
  46.2 62.8 %collective-permute-start.21 = (bf16[512,1536]{1,0:T(8,128)(2,1)}, bf16[512,1536]{1,0:T(8,128)(2,1)}, u32[]{:S(2)}, u32[]{:S(2)}) collective-permute-start(bf16[512,1536]{1,0:T(8,128)(2,1)} %collective-permute-done.13.xa_ref), channel_id=1, source_target_pairs={{0,2},{1,3},{2,0},{3,1},{4,6},{5,7},{6,4},{7,5}} | collective-permute-start | bytes 4718600 | tf_op jit(solution)/shard_map/ppermute | solution.py:455
  47.7 62.5 %collective-permute-start.12 = (bf16[512,1536]{1,0:T(8,128)(2,1)S(1)}, bf16[512,1536]{1,0:T(8,128)(2,1)}, u32[]{:S(2)}, u32[]{:S(2)}) collective-permute-start(bf16[512,1536]{1,0:T(8,128)(2,1)S(1)} %copy-done.3), channel_id=1, source_target_pairs={{0,1},{1,0},{2,3},{3,2},{4,5},{5,4},{6,7},{7,6}} | collective-permute-start | bytes 4718600 | tf_op jit(solution)/shard_map/ppermute | solution.py:455
  75.6 135.0 %collective-permute-start.27 = (bf16[512,1536]{1,0:T(8,128)(2,1)}, bf16[512,1536]{1,0:T(8,128)(2,1)}, u32[]{:S(2)}, u32[]{:S(2)}) collective-permute-start(bf16[512,1536]{1,0:T(8,128)(2,1)} %collective-permute-done.24.dya_ref), channel_id=1, source_target_pairs={{0,1},{1,0},{2,3},{3,2},{4,5},{5,4},{6,7},{7,6}} | collective-permute-start | bytes 4718600 | tf_op jit(solution)/shard_map/ppermute | solution.py:455
  75.6 103.8 %collective-permute-start.25 = (bf16[512,1536]{1,0:T(8,128)(2,1)}, bf16[512,1536]{1,0:T(8,128)(2,1)}, u32[]{:S(2)}, u32[]{:S(2)}) collective-permute-start(bf16[512,1536]{1,0:T(8,128)(2,1)} %collective-permute-done.24.dya_ref), channel_id=1, source_target_pairs={{0,2},{1,3},{2,0},{3,1},{4,6},{5,7},{6,4},{7,5}} | collective-permute-start | bytes 4718600 | tf_op jit(solution)/shard_map/ppermute | solution.py:455
  108.2 39.8 %collective-permute-start.15 = (bf16[448,1536]{1,0:T(8,128)(2,1)}, bf16[448,1536]{1,0:T(8,128)(2,1)}, u32[]{:S(2)}, u32[]{:S(2)}) collective-permute-start(bf16[448,1536]{1,0:T(8,128)(2,1)} %get-tuple-element.199), channel_id=1, source_target_pairs={{0,4},{4,0},{1,5},{5,1},{2,6},{6,2},{3,7},{7,3}} | collective-permute-start | bytes 4128776 | tf_op jit(solution)/shard_map/ppermute | solution.py:452
  109.0 61.3 %collective-permute-start.16 = (bf16[448,1536]{1,0:T(8,128)(2,1)}, bf16[448,1536]{1,0:T(8,128)(2,1)}, u32[]{:S(2)}, u32[]{:S(2)}) collective-permute-start(bf16[448,1536]{1,0:T(8,128)(2,1)} %get-tuple-element.200), channel_id=1, source_target_pairs={{0,4},{4,0},{1,5},{5,1},{2,6},{6,2},{3,7},{7,3}} | collective-permute-start | bytes 4128776 | tf_op jit(solution)/shard_map/ppermute | solution.py:452
  110.2 69.2 %collective-permute-start.28 = (bf16[512,1536]{1,0:T(8,128)(2,1)}, bf16[512,1536]{1,0:T(8,128)(2,1)}, u32[]{:S(2)}, u32[]{:S(2)}) collective-permute-start(bf16[512,1536]{1,0:T(8,128)(2,1)} %collective-permute-done.21.xa_ref), channel_id=1, source_target_pairs={{0,1},{1,0},{2,3},{3,2},{4,5},{5,4},{6,7},{7,6}} | collective-permute-start | bytes 4718600 | tf_op jit(solution)/shard_map/ppermute | solution.py:455
  177.3 64.6 %collective-permute-start.19 = (bf16[512,1536]{1,0:T(8,128)(2,1)}, bf16[512,1536]{1,0:T(8,128)(2,1)}, u32[]{:S(2)}, u32[]{:S(2)}) collective-permute-start(bf16[512,1536]{1,0:T(8,128)(2,1)} %xa_ref.1), channel_id=1, source_target_pairs={{0,2},{1,3},{2,0},{3,1},{4,6},{5,7},{6,4},{7,5}} | collective-permute-start | bytes 4718600 | tf_op jit(solution)/shard_map/ppermute | solution.py:455
  177.8 69.1 %collective-permute-start.22 = (bf16[512,1536]{1,0:T(8,128)(2,1)}, bf16[512,1536]{1,0:T(8,128)(2,1)}, u32[]{:S(2)}, u32[]{:S(2)}) collective-permute-start(bf16[512,1536]{1,0:T(8,128)(2,1)} %dya_ref.1), channel_id=1, source_target_pairs={{0,2},{1,3},{2,0},{3,1},{4,6},{5,7},{6,4},{7,5}} | collective-permute-start | bytes 4718600 | tf_op jit(solution)/shard_map/ppermute | solution.py:455
  179.4 130.2 %collective-permute-start.26 = (bf16[512,1536]{1,0:T(8,128)(2,1)}, bf16[512,1536]{1,0:T(8,128)(2,1)}, u32[]{:S(2)}, u32[]{:S(2)}) collective-permute-start(bf16[512,1536]{1,0:T(8,128)(2,1)} %collective-permute-done.25.dya_ref), channel_id=1, source_target_pairs={{0,1},{1,0},{2,3},{3,2},{4,5},{5,4},{6,7},{7,6}} | collective-permute-start | bytes 4718600 | tf_op jit(solution)/shard_map/ppermute | solution.py:455
  210.6 31.3 %copy-start.2 = (s32[512,6]{0,1:T(8,128)S(1)}, s32[512,6]{0,1:T(8,128)}, u32[]{:S(2)}) copy-start(s32[512,6]{0,1:T(8,128)} %param.16) | copy-start | bytes 36868
  239.8 33.4 %collective-permute-start.33 = (bf16[448,1536]{1,0:T(8,128)(2,1)}, bf16[448,1536]{1,0:T(8,128)(2,1)}, u32[]{:S(2)}, u32[]{:S(2)}) collective-permute-start(bf16[448,1536]{1,0:T(8,128)(2,1)} %get-tuple-element.226), channel_id=1, source_target_pairs={{0,4},{4,0},{1,5},{5,1},{2,6},{6,2},{3,7},{7,3}} | collective-permute-start | bytes 4128776 | tf_op jit(solution)/shard_map/ppermute | solution.py:452
  240.7 61.5 %collective-permute-start.34 = (bf16[448,1536]{1,0:T(8,128)(2,1)}, bf16[448,1536]{1,0:T(8,128)(2,1)}, u32[]{:S(2)}, u32[]{:S(2)}) collective-permute-start(bf16[448,1536]{1,0:T(8,128)(2,1)} %get-tuple-element.227), channel_id=1, source_target_pairs={{0,4},{4,0},{1,5},{5,1},{2,6},{6,2},{3,7},{7,3}} | collective-permute-start | bytes 4128776 | tf_op jit(solution)/shard_map/ppermute | solution.py:452
  241.9 97.6 %collective-permute-start.20 = (bf16[512,1536]{1,0:T(8,128)(2,1)}, bf16[512,1536]{1,0:T(8,128)(2,1)}, u32[]{:S(2)}, u32[]{:S(2)}) collective-permute-start(bf16[512,1536]{1,0:T(8,128)(2,1)} %collective-permute-done.19.xa_ref), channel_id=1, source_target_pairs={{0,1},{1,0},{2,3},{3,2},{4,5},{5,4},{6,7},{7,6}} | collective-permute-start | bytes 4718600 | tf_op jit(solution)/shard_map/ppermute | solution.py:455
  247.0 93.8 %collective-permute-start.23 = (bf16[512,1536]{1,0:T(8,128)(2,1)}, bf16[512,1536]{1,0:T(8,128)(2,1)}, u32[]{:S(2)}, u32[]{:S(2)}) collective-permute-start(bf16[512,1536]{1,0:T(8,128)(2,1)} %collective-permute-done.22.dya_ref), channel_id=1, source_target_pairs={{0,1},{1,0},{2,3},{3,2},{4,5},{5,4},{6,7},{7,6}} | collective-permute-start | bytes 4718600 | tf_op jit(solution)/shard_map/ppermute | solution.py:455
  307.6 127.2 %collective-permute-start.29 = (bf16[448,1536]{1,0:T(8,128)(2,1)}, bf16[448,1536]{1,0:T(8,128)(2,1)}, u32[]{:S(2)}, u32[]{:S(2)}) collective-permute-start(bf16[448,1536]{1,0:T(8,128)(2,1)} %get-tuple-element.220), channel_id=1, source_target_pairs={{0,4},{4,0},{1,5},{5,1},{2,6},{6,2},{3,7},{7,3}} | collective-permute-start | bytes 4128776 | tf_op jit(solution)/shard_map/ppermute | solution.py:452
  308.4 126.3 %collective-permute-start.30 = (bf16[448,1536]{1,0:T(8,128)(2,1)}, bf16[448,1536]{1,0:T(8,128)(2,1)}, u32[]{:S(2)}, u32[]{:S(2)}) collective-permute-start(bf16[448,1536]{1,0:T(8,128)(2,1)} %get-tuple-element.221), channel_id=1, source_target_pairs={{0,4},{4,0},{1,5},{5,1},{2,6},{6,2},{3,7},{7,3}} | collective-permute-start | bytes 4128776 | tf_op jit(solution)/shard_map/ppermute | solution.py:452
  338.7 61.2 %collective-permute-start.36 = (bf16[448,1536]{1,0:T(8,128)(2,1)}, bf16[448,1536]{1,0:T(8,128)(2,1)}, u32[]{:S(2)}, u32[]{:S(2)}) collective-permute-start(bf16[448,1536]{1,0:T(8,128)(2,1)} %get-tuple-element.233), channel_id=1, source_target_pairs={{0,4},{4,0},{1,5},{5,1},{2,6},{6,2},{3,7},{7,3}} | collective-permute-start | bytes 4128776 | tf_op jit(solution)/shard_map/ppermute | solution.py:452
  339.6 88.5 %collective-permute-start.37 = (bf16[448,1536]{1,0:T(8,128)(2,1)}, bf16[448,1536]{1,0:T(8,128)(2,1)}, u32[]{:S(2)}, u32[]{:S(2)}) collective-permute-start(bf16[448,1536]{1,0:T(8,128)(2,1)} %get-tuple-element.234), channel_id=1, source_target_pairs={{0,4},{4,0},{1,5},{5,1},{2,6},{6,2},{3,7},{7,3}} | collective-permute-start | bytes 4128776 | tf_op jit(solution)/shard_map/ppermute | solution.py:452
  340.8 102.2 %collective-permute-start.35 = (bf16[256,1536]{1,0:T(8,128)(2,1)}, bf16[256,1536]{1,0:T(8,128)(2,1)}, u32[]{:S(2)}, u32[]{:S(2)}) collective-permute-start(bf16[256,1536]{1,0:T(8,128)(2,1)} %get-tuple-element.230), channel_id=1, source_target_pairs={{0,1},{1,0},{2,3},{3,2},{4,5},{5,4},{6,7},{7,6}} | collective-permute-start | bytes 2359304 | tf_op jit(solution)/shard_map/ppermute | solution.py:455
  434.2 60.2 %collective-permute-start.18 = (bf16[256,1536]{1,0:T(8,128)(2,1)}, bf16[256,1536]{1,0:T(8,128)(2,1)}, u32[]{:S(2)}, u32[]{:S(2)}) collective-permute-start(bf16[256,1536]{1,0:T(8,128)(2,1)} %get-tuple-element.203), channel_id=1, source_target_pairs={{0,1},{1,0},{2,3},{3,2},{4,5},{5,4},{6,7},{7,6}} | collective-permute-start | bytes 2359304 | tf_op jit(solution)/shard_map/ppermute | solution.py:455
  434.2 53.8 %collective-permute-start.38 = (bf16[256,1536]{1,0:T(8,128)(2,1)}, bf16[256,1536]{1,0:T(8,128)(2,1)}, u32[]{:S(2)}, u32[]{:S(2)}) collective-permute-start(bf16[256,1536]{1,0:T(8,128)(2,1)} %get-tuple-element.236), channel_id=1, source_target_pairs={{0,2},{1,3},{2,0},{3,1},{4,6},{5,7},{6,4},{7,5}} | collective-permute-start | bytes 2359304 | tf_op jit(solution)/shard_map/ppermute | solution.py:455
  441.1 46.9 %collective-permute-start.39 = (bf16[256,1536]{1,0:T(8,128)(2,1)}, bf16[256,1536]{1,0:T(8,128)(2,1)S(1)}, u32[]{:S(2)}, u32[]{:S(2)}) collective-permute-start(bf16[256,1536]{1,0:T(8,128)(2,1)} %get-tuple-element.237), channel_id=1, source_target_pairs={{0,3},{1,2},{2,1},{3,0},{4,7},{5,6},{6,5},{7,4}} | collective-permute-start | bytes 2359304 | tf_op jit(solution)/shard_map/ppermute | solution.py:455
  442.5 51.9 %collective-permute-start.31 = (bf16[256,1536]{1,0:T(8,128)(2,1)}, bf16[256,1536]{1,0:T(8,128)(2,1)S(1)}, u32[]{:S(2)}, u32[]{:S(2)}) collective-permute-start(bf16[256,1536]{1,0:T(8,128)(2,1)} %get-tuple-element.223), channel_id=1, source_target_pairs={{0,2},{1,3},{2,0},{3,1},{4,6},{5,7},{6,4},{7,5}} | collective-permute-start | bytes 2359304 | tf_op jit(solution)/shard_map/ppermute | solution.py:455
  443.0 61.5 %collective-permute-start.32 = (bf16[256,1536]{1,0:T(8,128)(2,1)}, bf16[256,1536]{1,0:T(8,128)(2,1)S(1)}, u32[]{:S(2)}, u32[]{:S(2)}) collective-permute-start(bf16[256,1536]{1,0:T(8,128)(2,1)} %get-tuple-element.224), channel_id=1, source_target_pairs={{0,3},{1,2},{2,1},{3,0},{4,7},{5,6},{6,5},{7,4}} | collective-permute-start | bytes 2359304 | tf_op jit(solution)/shard_map/ppermute | solution.py:455
  444.1 44.9 %copy-start.8 = (bf16[256,1536]{1,0:T(8,128)(2,1)S(1)}, bf16[256,1536]{1,0:T(8,128)(2,1)}, u32[]{:S(2)}) copy-start(bf16[256,1536]{1,0:T(8,128)(2,1)} %get-tuple-element.229.refs_0_) | copy-start | bytes 2359300
  488.1 0.9 copy-start.6
  489.0 16.3 %copy-start.7 = (bf16[256,1536]{1,0:T(8,128)(2,1)S(1)}, bf16[256,1536]{1,0:T(8,128)(2,1)}, u32[]{:S(2)}) copy-start(bf16[256,1536]{1,0:T(8,128)(2,1)} %get-tuple-element.202.refs_0_) | copy-start | bytes 2359300
  494.4 10.0 %copy-start.4 = (bf16[256,1536]{1,0:T(8,128)(2,1)}, bf16[256,1536]{1,0:T(8,128)(2,1)S(1)}, u32[]{:S(2)}) copy-start(bf16[256,1536]{1,0:T(8,128)(2,1)S(1)} %collective-permute-done.31.refs_2_) | copy-start | bytes 2359300
  504.4 0.9 copy-start.5

commit v4 on v3

--- a/solution.py
+++ b/solution.py
@@ -14,7 +14,7 @@
 SENT_SHARE = 7, 8
 PAIR = 2
 
-KERNEL_ORDER = (('f', 0), ('n', 2), ('f', 1), ('b', 0), ('b', 1), ('n', 3))
+KERNEL_ORDER = (('f', 0), ('b', 0), ('f', 1), ('b', 1), ('n', 2), ('n', 3))
 
 
 def dot(a, b):
@@ -474,13 +474,13 @@
         x_far = hop_y(x_loc)
         dy_far = hop_y(dy_loc)
         x_near_c = hop_g(after(pair_c, x_loc), 1)
-        x_near_x = hop_g(after(quad_x, x_loc), 2)
+        x_near_x = hop_g(x_loc, 2)
         dy_near_c = hop_g(after(x_near_c, dy_loc), 1)
         x_far_c, x_far_x = hop_g(x_far, 1), hop_g(x_far, 2)
         x_near_xc, x_far_xc = hop_g(x_near_x, 1), hop_g(x_far_x, 1)
         dy_far_c, dy_far_x = hop_g(dy_far, 1), hop_g(dy_far, 2)
         dy_far_xc = hop_g(dy_far_x, 1)
-        dy_near_x = hop_g(after(x_far_x, dy_loc), 2)
+        dy_near_x = hop_g(dy_loc, 2)
         dy_near_xc = hop_g(dy_near_x, 1)
         x_pairs = [(x_far, x_far_c), (x_far_x, x_far_xc), (x_loc, x_near_c), (x_near_x, x_near_xc)]
         dy_pairs = [(dy_far, dy_far_c), (dy_far_x, dy_far_xc), (dy_loc, dy_near_c), (dy_near_x, dy_near_xc)]

time: 519 us -> 555 us (1.069)
  waiting for transfers between devices: 183 us -> 216 us
    ppermute x20, waiting for transfers between devices: 20.2 us -> 73.1 us  [hop_g(): return lax.ppermute(a, 'grp', [(g, g ^ bits) for g in range(groups)])]
    ppermute x12, waiting for transfers between devices: 162 us -> 143 us  [hop_y(): return lax.ppermute(a, 'ing', [(0, 1), (1, 0)])]
  transfers between devices with their start and end apart: 32 -> 32, of which waited for: 11 -> 11; matrix products, arithmetic and copies ran while one was open for 5% -> 5% of each run, Pallas kernels for 52% -> 48%
where the time goes in v4:
time: 555 us; the launch traced here: 547 us
  Pallas kernels  270 us (49%)
  waiting for transfers between devices  216 us (39%)
  starting transfers between devices  27.4 us (5%)
  other arithmetic  15.1 us (3%)
  local copies, waits for them, and re-layouts  14.6 us (3%)
    ppermute x12, waiting for transfers between devices, hop_y(): return lax.ppermute(a, 'ing', [(0, 1), (1, 0)])  143 us
    pallas_call x2, Pallas kernels, near_pair(): pl.pallas_call(functools.partial(near_kernel, cap, pad), grid=(experts,),...  75.3 us
    ppermute x20, waiting for transfers between devices, hop_g(): return lax.ppermute(a, 'grp', [(g, g ^ bits) for g in range(groups)])  73.1 us
    pallas_call x2, Pallas kernels, far_forward_pair(): pl.pallas_call(functools.partial(far_fwd_kernel, cap, pad), grid=(experts...  62.2 us
    pallas_call x2, Pallas kernels, far_backward_pair(): pl.pallas_call(functools.partial(far_bwd_kernel, cap, pad), grid=(experts...  58.3 us
    pallas_call x1, Pallas kernels, weight_grads(): pl.pallas_call(functools.partial(dw_kernel, chunks), grid=(experts,), in_...  43.9 us
    pallas_call x4, Pallas kernels, merge_pair(): pl.pallas_call(functools.partial(merge_kernel, weighted), grid=(3,), in_s...  20.1 us
    ppermute x12, starting transfers between devices, hop_y(): return lax.ppermute(a, 'ing', [(0, 1), (1, 0)])  15.3 us
  transfers between devices with their start and end apart: 32, of which 11 were waited for; matrix products, arithmetic and copies ran while one was open for 5% of the time, Pallas kernels for 48%

profile of v4, /device:TPU:0, one launch (start us, length us, event | category | flops | bytes accessed | tf_op | source)
XLA Modules:
  0.0 547.4 jit_solution(10609256675899228804)
XLA Ops:
  0.6 3.4 collective-permute-start.16
  4.0 1.5 collective-permute-start.25
  7.5 1.5 collective-permute-start.13
  9.0 31.2 %collective-permute-done.8 = f32[1,12,512]{2,1,0:T(8,128)S(1)} collective-permute-done((f32[1,12,512]{2,1,0:T(8,128)S(1)}, f32[1,12,512]{2,1,0:T(8,128)S(1)}, u32[]{:S(2)}, u32[]{:S(2)}) %collective-permute-start.8) | collective-permute-done | bytes 24608 | tf_op jit(solution)/shard_map/ppermute | solution.py:452
  40.2 1.2 collective-permute-done.9
  41.4 2.0 collective-permute-start.10
  43.5 3.8 collective-permute-done.10
  47.3 0.7 constant_dynamic-update-slice_fusion.3
  49.6 9.7 %select_reduce_fusion = (f32[8,8,72]{2,1,0:T(8,128)S(1)}, f32[8,8,72]{2,1,0:T(8,128)S(1)}, f32[8,8,72]{2,1,0:T(8,128)S(1)}, f32[8,8,72]{2,1,0:T(8,128)S(1)}) fusion(f32[8,8,512]{2,1,0:T(8,128)S(1)} %copy.58, f32[8,8,512]{2,1,0:T(8,128)S(1)} %slice.100, pred[8,8,512]{2,1,0:T(8,128)(4,1)S(1)} %compare_reduce_fusion, f32[8,512]{1,0:T(8,128)S(1)} %bitcast.41, ...), kind=kLoop, calls=%fused_computation.8 | loop fusion | flops 23574528 | bytes 518144 | tf_op jit(solution)/shard_map/reduce_sum | solution.py:423
  59.6 1.1 select_reduce_fusion.5
  60.7 1.8 collective-permute-start.23
  62.5 10.8 %collective-permute-done.23 = f32[2,4,448]{2,1,0:T(4,128)S(1)} collective-permute-done((f32[2,4,448]{2,1,0:T(4,128)S(1)}, f32[2,4,448]{2,1,0:T(4,128)S(1)}, u32[]{:S(2)}, u32[]{:S(2)}) %collective-permute-start.23) | collective-permute-done | bytes 14368 | tf_op jit(solution)/shard_map/ppermute | solution.py:452
  73.4 1.7 collective-permute-start.27
  77.2 1.7 collective-permute-start.14
  78.9 2.1 reshape.248.gcol_ref
  84.4 2.1 convert_element_type.180.tok_ref
  86.5 24.2 %collective-permute-done.27.dya_ref = bf16[512,1536]{1,0:T(8,128)(2,1)} collective-permute-done((bf16[512,1536]{1,0:T(8,128)(2,1)S(1)}, bf16[512,1536]{1,0:T(8,128)(2,1)}, u32[]{:S(2)}, u32[]{:S(2)}) %collective-permute-start.27) | collective-permute-done | bytes 1572896 | tf_op jit(solution)/shard_map/ppermute | solution.py:455
  111.2 33.2 %collective-permute-done.17.xa_ref = bf16[512,1536]{1,0:T(8,128)(2,1)} collective-permute-done((bf16[512,1536]{1,0:T(8,128)(2,1)}, bf16[512,1536]{1,0:T(8,128)(2,1)}, u32[]{:S(2)}, u32[]{:S(2)}) %collective-permute-start.17) | collective-permute-done | bytes 1572896 | tf_op jit(solution)/shard_map/ppermute | solution.py:455
  144.4 31.0 %far_fwd_pair.2 = (bf16[8,144,1536]{2,1,0:T(8,128)(2,1)}, bf16[8,144,512]{2,1,0:T(8,128)(2,1)}, f32[8,144,512]{2,1,0:T(8,128)}, f32[8,144,512]{2,1,0:T(8,128)}, ...) custom-call(bf16[512,1536]{1,0:T(8,128)(2,1)} %collective-permute-done.16.xa_r, ...), custom_call_target="tpu_custom_call" | custom-call | flops 14000000000 | bytes 50000000 | tf_op jit(solution)/shard_map/far_fwd_pair/pallas_call | solution.py:272
  176.5 29.0 %far_bwd_pair.2 = (bf16[8,144,1536]{2,1,0:T(8,128)(2,1)}, bf16[8,144,512]{2,1,0:T(8,128)(2,1)}, bf16[8,144,512]{2,1,0:T(8,128)(2,1)}, f32[256,1536]{1,0:T(8,128)...) custom-call(bf16[512,1536]{1,0:T(8,128)(2,1)} %collective-permute-done.13.dya_ref, ...), custom_call_target="tpu_custom_call" | custom-call | flops 14000000000 | bytes 50000000 | tf_op jit(solution)/shard_map/far_bwd_pair/pallas_call | solution.py:291
  205.6 1.5 collective-permute-start.21
  207.1 31.2 %far_fwd_pair.3 = (bf16[8,144,1536]{2,1,0:T(8,128)(2,1)}, bf16[8,144,512]{2,1,0:T(8,128)(2,1)}, f32[8,144,512]{2,1,0:T(8,128)}, f32[8,144,512]{2,1,0:T(8,128)}, ...) custom-call(bf16[512,1536]{1,0:T(8,128)(2,1)} %collective-permute-done.17.xa_r, ...), custom_call_target="tpu_custom_call" | custom-call | flops 14000000000 | bytes 50000000 | tf_op jit(solution)/shard_map/far_fwd_pair/pallas_call | solution.py:272
  238.9 29.2 %far_bwd_pair.3 = (bf16[8,144,1536]{2,1,0:T(8,128)(2,1)}, bf16[8,144,512]{2,1,0:T(8,128)(2,1)}, bf16[8,144,512]{2,1,0:T(8,128)(2,1)}, f32[256,1536]{1,0:T(8,128)...) custom-call(bf16[512,1536]{1,0:T(8,128)(2,1)} %collective-permute-done.14.dya_ref, ...), custom_call_target="tpu_custom_call" | custom-call | flops 14000000000 | bytes 50000000 | tf_op jit(solution)/shard_map/far_bwd_pair/pallas_call | solution.py:291
  268.1 1.5 collective-permute-start.33
  269.6 37.5 %near_pair.2 = (bf16[8,144,1536]{2,1,0:T(8,128)(2,1)}, bf16[8,144,512]{2,1,0:T(8,128)(2,1)}, bf16[8,144,1536]{2,1,0:T(8,128)(2,1)}, bf16[8,144,512]{2,1,0:T(8,12...) custom-call(bf16[512,1536]{1,0:T(8,128)(2,1)} %xa_ref.1, ...), custom_call_target="tpu_custom_call" | custom-call | flops 28000000000 | bytes 70000000 | tf_op jit(solution)/shard_map/near_pair/pallas_call | solution.py:326
  307.2 7.1 %conditional.4 = ((bf16[256,1536]{1,0:T(8,128)(2,1)}, bf16[256,1536]{1,0:T(8,128)(2,1)})) conditional(s32[]{:T(128)} %convert_element_type.160, (f32[256,1536]{1,0:T(8,128)}, f32[256,1536]{1,0:T(8,128)}, bf16[448,1536]{1,0:T(8,128)(2,1)}, bf16[448,1536]{1,0:T(8,128)(2,1)}, s32[4,1,448]{2,0,1:T(4,128)S(1)}, ...), branch_computations={%region_15.16_spmd, %region_16.17_spmd} | conditional | flops 2000000000 | bytes 26738820 | solution.py:548
  308.4 5.9 %merge_pair.4 = (bf16[256,1536]{1,0:T(8,128)(2,1)}, bf16[256,1536]{1,0:T(8,128)(2,1)}) custom-call(f32[256,1536]{1,0:T(8,128)} %get-tuple-element.80.n0_ref, f32[256,1536]{1,0:T(8,128)} %get-tuple-element.81.n1_ref, bf16[448,1536]{1,0:T(8,128)(2,1)} %get-tuple-element.82.r0_ref, bf16[448,1536]{1,0:T(8,128)(2,1)} %get-tuple-element.83.r1_ref, ...), custom_call_target="tpu_custom_call" | custom-call | flops 2000000000 | bytes 8000000 | tf_op jit(solution)/shard_map/cond/branch_0_fun/merge_pair/pallas_call | solution.py:308
  315.2 1.0 fusion.1.refs_4_
  316.2 1.5 collective-permute-start.29
  317.6 30.0 %collective-permute-done.34 = bf16[448,1536]{1,0:T(8,128)(2,1)} collective-permute-done((bf16[448,1536]{1,0:T(8,128)(2,1)}, bf16[448,1536]{1,0:T(8,128)(2,1)}, u32[]{:S(2)}, u32[]{:S(2)}) %collective-permute-start.34) | collective-permute-done | bytes 1376288 | tf_op jit(solution)/shard_map/ppermute | solution.py:452
  347.6 5.3 conditional.6
  348.9 4.1 merge_pair.6
  353.5 1.5 collective-permute-start.36
  355.6 37.7 %near_pair.3 = (bf16[8,144,1536]{2,1,0:T(8,128)(2,1)}, bf16[8,144,512]{2,1,0:T(8,128)(2,1)}, bf16[8,144,1536]{2,1,0:T(8,128)(2,1)}, bf16[8,144,512]{2,1,0:T(8,12...) custom-call(bf16[512,1536]{1,0:T(8,128)(2,1)} %collective-permute-do, ...), custom_call_target="tpu_custom_call" | custom-call | flops 28000000000 | bytes 70000000 | tf_op jit(solution)/shard_map/near_pair/pallas_call | solution.py:326
  393.3 42.8 %collective-permute-done.36 = bf16[448,1536]{1,0:T(8,128)(2,1)} collective-permute-done((bf16[448,1536]{1,0:T(8,128)(2,1)}, bf16[448,1536]{1,0:T(8,128)(2,1)}, u32[]{:S(2)}, u32[]{:S(2)}) %collective-permute-start.36) | collective-permute-done | bytes 1376288 | tf_op jit(solution)/shard_map/ppermute | solution.py:452
  436.1 28.2 %collective-permute-done.37 = bf16[448,1536]{1,0:T(8,128)(2,1)} collective-permute-done((bf16[448,1536]{1,0:T(8,128)(2,1)}, bf16[448,1536]{1,0:T(8,128)(2,1)}, u32[]{:S(2)}, u32[]{:S(2)}) %collective-permute-start.37) | collective-permute-done | bytes 1376288 | tf_op jit(solution)/shard_map/ppermute | solution.py:452
  464.3 6.2 %conditional.7 = ((bf16[256,1536]{1,0:T(8,128)(2,1)}, bf16[256,1536]{1,0:T(8,128)(2,1)})) conditional(s32[]{:T(128)} %convert_element_type.160, (f32[256,1536]{1,0:T(8,128)}, f32[256,1536]{1,0:T(8,128)}, bf16[448,1536]{1,0:T(8,128)(2,1)}, bf16[448,1536]{1,0:T(8,128)(2,1)}, s32[4,1,448]{2,0,1:T(4,128)S(1)}, ...), branch_computations={%region_22.23_spmd, %region_23.24_spmd} | conditional | flops 2000000000 | bytes 26738820 | solution.py:548
  465.5 5.0 merge_pair.7
  470.5 1.5 collective-permute-start.38
  472.0 6.4 %conditional.5 = ((bf16[256,1536]{1,0:T(8,128)(2,1)}, bf16[256,1536]{1,0:T(8,128)(2,1)})) conditional(s32[]{:T(128)} %convert_element_type.160, (f32[256,1536]{1,0:T(8,128)S(1)}, f32[256,1536]{1,0:T(8,128)S(1)}, bf16[448,1536]{1,0:T(8,128)(2,1)}, bf16[448,1536]{1,0:T(8,128)(2,1)}, s32[4,1,448]{2,0,1:T(4,128)S(1)}, ...), branch_computations={%region_17.18_spmd, %region_18.19_spmd} | conditional | flops 2000000000 | bytes 20447336 | solution.py:548
  473.3 5.2 merge_pair.5
  478.8 1.5 collective-permute-start.31
  480.5 43.9 %weight_grads.1 = (f32[8,1536,512]{2,1,0:T(8,128)}, f32[8,1536,512]{2,1,0:T(8,128)}, f32[8,512,1536]{2,1,0:T(8,128)}) custom-call(bf16[8,144,1536]{2,1,0:T(8,128)(2,1)} %get-tuple-element.234.refs_0_, bf16[8,144,1536]{2,1,0:T(8,128)(2,1)} %get-tuple-element.235.refs_1_, bf16[8,144,1536]{2,1,0:T(8,128)(2,1)} %get-tuple-element.236.refs_2_, ...), custom_call_target="tpu_custom_call" | custom-call | flops 24999999488 | bytes 120000000 | tf_op jit(solution)/shard_map/weight_grads/pallas_call | solution.py:357
  524.4 0.9 copy-done.6
  525.3 5.4 collect.3
  530.7 10.0 %collective-permute-done.32.refs_3_ = bf16[256,1536]{1,0:T(8,128)(2,1)S(1)} collective-permute-done((bf16[256,1536]{1,0:T(8,128)(2,1)}, bf16[256,1536]{1,0:T(8,128)(2,1)S(1)}, u32[]{:S(2)}, u32[]{:S(2)}) %collective-permute-start.32) | collective-permute-done | bytes 786464 | tf_op jit(solution)/shard_map/ppermute | solution.py:455
  540.7 0.9 copy-done.5
  541.7 5.3 collect.2
  (131 shorter events, 18.2 us)
Async XLA Ops:
  0.6 74.4 %collective-permute-start.16 = (bf16[512,1536]{1,0:T(8,128)(2,1)}, bf16[512,1536]{1,0:T(8,128)(2,1)}, u32[]{:S(2)}, u32[]{:S(2)}) collective-permute-start(bf16[512,1536]{1,0:T(8,128)(2,1)} %xa_ref.1), channel_id=1, source_target_pairs={{0,4},{4,0},{1,5},{5,1},{2,6},{6,2},{3,7},{7,3}} | collective-permute-start | bytes 4718600 | tf_op jit(solution)/shard_map/ppermute | solution.py:452
  4.0 71.1 %collective-permute-start.25 = (bf16[512,1536]{1,0:T(8,128)(2,1)}, bf16[512,1536]{1,0:T(8,128)(2,1)}, u32[]{:S(2)}, u32[]{:S(2)}) collective-permute-start(bf16[512,1536]{1,0:T(8,128)(2,1)} %xa_ref.1), channel_id=1, source_target_pairs={{0,2},{1,3},{2,0},{3,1},{4,6},{5,7},{6,4},{7,5}} | collective-permute-start | bytes 4718600 | tf_op jit(solution)/shard_map/ppermute | solution.py:455
  6.9 33.2 %collective-permute-start.8 = (f32[1,12,512]{2,1,0:T(8,128)S(1)}, f32[1,12,512]{2,1,0:T(8,128)S(1)}, u32[]{:S(2)}, u32[]{:S(2)}) collective-permute-start(f32[1,12,512]{2,1,0:T(8,128)S(1)} %maximum_bitcast_fusion), channel_id=1, source_target_pairs={{0,4},{4,0},{1,5},{5,1},{2,6},{6,2},{3,7},{7,3}} | collective-permute-start | bytes 73736 | tf_op jit(solution)/shard_map/ppermute | solution.py:452
  7.5 69.5 %collective-permute-start.13 = (bf16[512,1536]{1,0:T(8,128)(2,1)}, bf16[512,1536]{1,0:T(8,128)(2,1)}, u32[]{:S(2)}, u32[]{:S(2)}) collective-permute-start(bf16[512,1536]{1,0:T(8,128)(2,1)} %dya_ref.1), channel_id=1, source_target_pairs={{0,4},{4,0},{1,5},{5,1},{2,6},{6,2},{3,7},{7,3}} | collective-permute-start | bytes 4718600 | tf_op jit(solution)/shard_map/ppermute | solution.py:452
  40.2 1.3 collective-permute-start.9
  41.4 5.8 %collective-permute-start.10 = (f32[4,12,512]{2,1,0:T(8,128)S(1)}, f32[4,12,512]{2,1,0:T(8,128)S(1)}, u32[]{:S(2)}, u32[]{:S(2)}) collective-permute-start(f32[4,12,512]{2,1,0:T(8,128)S(1)} %pad_maximum_fusion), channel_id=1, source_target_pairs={{0,2},{1,3},{2,0},{3,1},{4,6},{5,7},{6,4},{7,5}} | collective-permute-start | bytes 294920 | tf_op jit(solution)/shard_map/ppermute | solution.py:455
  43.5 33.7 %collective-permute-start.11 = (bf16[512,1536]{1,0:T(8,128)(2,1)}, bf16[512,1536]{1,0:T(8,128)(2,1)}, u32[]{:S(2)}, u32[]{:S(2)}) collective-permute-start(bf16[512,1536]{1,0:T(8,128)(2,1)} %xa_ref.1), channel_id=1, source_target_pairs={{0,1},{1,0},{2,3},{3,2},{4,5},{5,4},{6,7},{7,6}} | collective-permute-start | bytes 4718600 | tf_op jit(solution)/shard_map/ppermute | solution.py:455
  48.9 24.5 %copy-start.3 = (bf16[512,1536]{1,0:T(8,128)(2,1)S(1)}, bf16[512,1536]{1,0:T(8,128)(2,1)}, u32[]{:S(2)}) copy-start(bf16[512,1536]{1,0:T(8,128)(2,1)} %dya_ref.1) | copy-start | bytes 4718596
  60.7 12.6 %collective-permute-start.23 = (f32[2,4,448]{2,1,0:T(4,128)S(1)}, f32[2,4,448]{2,1,0:T(4,128)S(1)}, u32[]{:S(2)}, u32[]{:S(2)}) collective-permute-start(f32[2,4,448]{2,1,0:T(4,128)S(1)} %pad_maximum_fusion.2), channel_id=1, source_target_pairs={{0,4},{4,0},{1,5},{5,1},{2,6},{6,2},{3,7},{7,3}} | collective-permute-start | bytes 43016 | tf_op jit(solution)/shard_map/ppermute | solution.py:452
  73.4 37.4 %collective-permute-start.27 = (bf16[512,1536]{1,0:T(8,128)(2,1)S(1)}, bf16[512,1536]{1,0:T(8,128)(2,1)}, u32[]{:S(2)}, u32[]{:S(2)}) collective-permute-start(bf16[512,1536]{1,0:T(8,128)(2,1)S(1)} %copy-done.3), channel_id=1, source_target_pairs={{0,2},{1,3},{2,0},{3,1},{4,6},{5,7},{6,4},{7,5}} | collective-permute-start | bytes 4718600 | tf_op jit(solution)/shard_map/ppermute | solution.py:455
  75.1 35.7 %collective-permute-start.20 = (bf16[512,1536]{1,0:T(8,128)(2,1)}, bf16[512,1536]{1,0:T(8,128)(2,1)}, u32[]{:S(2)}, u32[]{:S(2)}) collective-permute-start(bf16[512,1536]{1,0:T(8,128)(2,1)} %collective-permute-done.16.xa_ref), channel_id=1, source_target_pairs={{0,1},{1,0},{2,3},{3,2},{4,5},{5,4},{6,7},{7,6}} | collective-permute-start | bytes 4718600 | tf_op jit(solution)/shard_map/ppermute | solution.py:455
  75.1 69.4 %collective-permute-start.17 = (bf16[512,1536]{1,0:T(8,128)(2,1)}, bf16[512,1536]{1,0:T(8,128)(2,1)}, u32[]{:S(2)}, u32[]{:S(2)}) collective-permute-start(bf16[512,1536]{1,0:T(8,128)(2,1)} %collective-permute-done.16.xa_ref), channel_id=1, source_target_pairs={{0,2},{1,3},{2,0},{3,1},{4,6},{5,7},{6,4},{7,5}} | collective-permute-start | bytes 4718600 | tf_op jit(solution)/shard_map/ppermute | solution.py:455
  76.9 98.5 %collective-permute-start.19 = (bf16[512,1536]{1,0:T(8,128)(2,1)}, bf16[512,1536]{1,0:T(8,128)(2,1)}, u32[]{:S(2)}, u32[]{:S(2)}) collective-permute-start(bf16[512,1536]{1,0:T(8,128)(2,1)} %collective-permute-done.13.dya_ref), channel_id=1, source_target_pairs={{0,1},{1,0},{2,3},{3,2},{4,5},{5,4},{6,7},{7,6}} | collective-permute-start | bytes 4718600 | tf_op jit(solution)/shard_map/ppermute | solution.py:455
  77.2 99.4 %collective-permute-start.14 = (bf16[512,1536]{1,0:T(8,128)(2,1)}, bf16[512,1536]{1,0:T(8,128)(2,1)}, u32[]{:S(2)}, u32[]{:S(2)}) collective-permute-start(bf16[512,1536]{1,0:T(8,128)(2,1)} %collective-permute-done.13.dya_ref), channel_id=1, source_target_pairs={{0,2},{1,3},{2,0},{3,1},{4,6},{5,7},{6,4},{7,5}} | collective-permute-start | bytes 4718600 | tf_op jit(solution)/shard_map/ppermute | solution.py:455
  110.7 244.2 %collective-permute-start.26 = (bf16[512,1536]{1,0:T(8,128)(2,1)}, bf16[512,1536]{1,0:T(8,128)(2,1)}, u32[]{:S(2)}, u32[]{:S(2)}) collective-permute-start(bf16[512,1536]{1,0:T(8,128)(2,1)} %collective-permute-done.25.xa_ref), channel_id=1, source_target_pairs={{0,1},{1,0},{2,3},{3,2},{4,5},{5,4},{6,7},{7,6}} | collective-permute-start | bytes 4718600 | tf_op jit(solution)/shard_map/ppermute | solution.py:455
  110.7 244.8 %collective-permute-start.28 = (bf16[512,1536]{1,0:T(8,128)(2,1)}, bf16[512,1536]{1,0:T(8,128)(2,1)}, u32[]{:S(2)}, u32[]{:S(2)}) collective-permute-start(bf16[512,1536]{1,0:T(8,128)(2,1)} %collective-permute-done.27.dya_ref), channel_id=1, source_target_pairs={{0,1},{1,0},{2,3},{3,2},{4,5},{5,4},{6,7},{7,6}} | collective-permute-start | bytes 4718600 | tf_op jit(solution)/shard_map/ppermute | solution.py:455
  144.4 61.2 %collective-permute-start.18 = (bf16[512,1536]{1,0:T(8,128)(2,1)}, bf16[512,1536]{1,0:T(8,128)(2,1)}, u32[]{:S(2)}, u32[]{:S(2)}) collective-permute-start(bf16[512,1536]{1,0:T(8,128)(2,1)} %collective-permute-done.17.xa_ref), channel_id=1, source_target_pairs={{0,1},{1,0},{2,3},{3,2},{4,5},{5,4},{6,7},{7,6}} | collective-permute-start | bytes 4718600 | tf_op jit(solution)/shard_map/ppermute | solution.py:455
  175.4 92.7 %collective-permute-start.12 = (bf16[512,1536]{1,0:T(8,128)(2,1)S(1)}, bf16[512,1536]{1,0:T(8,128)(2,1)}, u32[]{:S(2)}, u32[]{:S(2)}) collective-permute-start(bf16[512,1536]{1,0:T(8,128)(2,1)S(1)} %copy-done.3), channel_id=1, source_target_pairs={{0,1},{1,0},{2,3},{3,2},{4,5},{5,4},{6,7},{7,6}} | collective-permute-start | bytes 4718600 | tf_op jit(solution)/shard_map/ppermute | solution.py:455
  176.5 61.8 %collective-permute-start.15 = (bf16[512,1536]{1,0:T(8,128)(2,1)}, bf16[512,1536]{1,0:T(8,128)(2,1)}, u32[]{:S(2)}, u32[]{:S(2)}) collective-permute-start(bf16[512,1536]{1,0:T(8,128)(2,1)} %collective-permute-done.14.dya_ref), channel_id=1, source_target_pairs={{0,1},{1,0},{2,3},{3,2},{4,5},{5,4},{6,7},{7,6}} | collective-permute-start | bytes 4718600 | tf_op jit(solution)/shard_map/ppermute | solution.py:455
  205.6 101.6 %collective-permute-start.21 = (bf16[448,1536]{1,0:T(8,128)(2,1)}, bf16[448,1536]{1,0:T(8,128)(2,1)}, u32[]{:S(2)}, u32[]{:S(2)}) collective-permute-start(bf16[448,1536]{1,0:T(8,128)(2,1)} %get-tuple-element.207), channel_id=1, source_target_pairs={{0,4},{4,0},{1,5},{5,1},{2,6},{6,2},{3,7},{7,3}} | collective-permute-start | bytes 4128776 | tf_op jit(solution)/shard_map/ppermute | solution.py:452
  238.3 68.9 %collective-permute-start.22 = (bf16[448,1536]{1,0:T(8,128)(2,1)}, bf16[448,1536]{1,0:T(8,128)(2,1)}, u32[]{:S(2)}, u32[]{:S(2)}) collective-permute-start(bf16[448,1536]{1,0:T(8,128)(2,1)} %get-tuple-element.208), channel_id=1, source_target_pairs={{0,4},{4,0},{1,5},{5,1},{2,6},{6,2},{3,7},{7,3}} | collective-permute-start | bytes 4128776 | tf_op jit(solution)/shard_map/ppermute | solution.py:452
  268.1 49.5 %collective-permute-start.33 = (bf16[448,1536]{1,0:T(8,128)(2,1)}, bf16[448,1536]{1,0:T(8,128)(2,1)}, u32[]{:S(2)}, u32[]{:S(2)}) collective-permute-start(bf16[448,1536]{1,0:T(8,128)(2,1)} %get-tuple-element.222), channel_id=1, source_target_pairs={{0,4},{4,0},{1,5},{5,1},{2,6},{6,2},{3,7},{7,3}} | collective-permute-start | bytes 4128776 | tf_op jit(solution)/shard_map/ppermute | solution.py:452
  307.2 7.7 %copy-start.2 = (s32[512,6]{0,1:T(8,128)S(1)}, s32[512,6]{0,1:T(8,128)}, u32[]{:S(2)}) copy-start(s32[512,6]{0,1:T(8,128)} %param.16) | copy-start | bytes 36868
  314.3 33.4 %collective-permute-start.34 = (bf16[448,1536]{1,0:T(8,128)(2,1)}, bf16[448,1536]{1,0:T(8,128)(2,1)}, u32[]{:S(2)}, u32[]{:S(2)}) collective-permute-start(bf16[448,1536]{1,0:T(8,128)(2,1)} %get-tuple-element.223), channel_id=1, source_target_pairs={{0,4},{4,0},{1,5},{5,1},{2,6},{6,2},{3,7},{7,3}} | collective-permute-start | bytes 4128776 | tf_op jit(solution)/shard_map/ppermute | solution.py:452
  316.2 155.9 %collective-permute-start.29 = (bf16[448,1536]{1,0:T(8,128)(2,1)}, bf16[448,1536]{1,0:T(8,128)(2,1)}, u32[]{:S(2)}, u32[]{:S(2)}) collective-permute-start(bf16[448,1536]{1,0:T(8,128)(2,1)} %get-tuple-element.216), channel_id=1, source_target_pairs={{0,4},{4,0},{1,5},{5,1},{2,6},{6,2},{3,7},{7,3}} | collective-permute-start | bytes 4128776 | tf_op jit(solution)/shard_map/ppermute | solution.py:452
  352.9 119.1 %collective-permute-start.30 = (bf16[448,1536]{1,0:T(8,128)(2,1)}, bf16[448,1536]{1,0:T(8,128)(2,1)}, u32[]{:S(2)}, u32[]{:S(2)}) collective-permute-start(bf16[448,1536]{1,0:T(8,128)(2,1)} %get-tuple-element.217), channel_id=1, source_target_pairs={{0,4},{4,0},{1,5},{5,1},{2,6},{6,2},{3,7},{7,3}} | collective-permute-start | bytes 4128776 | tf_op jit(solution)/shard_map/ppermute | solution.py:452
  353.5 82.6 %collective-permute-start.36 = (bf16[448,1536]{1,0:T(8,128)(2,1)}, bf16[448,1536]{1,0:T(8,128)(2,1)}, u32[]{:S(2)}, u32[]{:S(2)}) collective-permute-start(bf16[448,1536]{1,0:T(8,128)(2,1)} %get-tuple-element.229), channel_id=1, source_target_pairs={{0,4},{4,0},{1,5},{5,1},{2,6},{6,2},{3,7},{7,3}} | collective-permute-start | bytes 4128776 | tf_op jit(solution)/shard_map/ppermute | solution.py:452
  355.0 109.3 %collective-permute-start.37 = (bf16[448,1536]{1,0:T(8,128)(2,1)}, bf16[448,1536]{1,0:T(8,128)(2,1)}, u32[]{:S(2)}, u32[]{:S(2)}) collective-permute-start(bf16[448,1536]{1,0:T(8,128)(2,1)} %get-tuple-element.230), channel_id=1, source_target_pairs={{0,4},{4,0},{1,5},{5,1},{2,6},{6,2},{3,7},{7,3}} | collective-permute-start | bytes 4128776 | tf_op jit(solution)/shard_map/ppermute | solution.py:452
  355.5 124.8 %collective-permute-start.35 = (bf16[256,1536]{1,0:T(8,128)(2,1)}, bf16[256,1536]{1,0:T(8,128)(2,1)}, u32[]{:S(2)}, u32[]{:S(2)}) collective-permute-start(bf16[256,1536]{1,0:T(8,128)(2,1)} %get-tuple-element.226), channel_id=1, source_target_pairs={{0,1},{1,0},{2,3},{3,2},{4,5},{5,4},{6,7},{7,6}} | collective-permute-start | bytes 2359304 | tf_op jit(solution)/shard_map/ppermute | solution.py:455
  470.5 60.2 %collective-permute-start.24 = (bf16[256,1536]{1,0:T(8,128)(2,1)}, bf16[256,1536]{1,0:T(8,128)(2,1)}, u32[]{:S(2)}, u32[]{:S(2)}) collective-permute-start(bf16[256,1536]{1,0:T(8,128)(2,1)} %get-tuple-element.211), channel_id=1, source_target_pairs={{0,1},{1,0},{2,3},{3,2},{4,5},{5,4},{6,7},{7,6}} | collective-permute-start | bytes 2359304 | tf_op jit(solution)/shard_map/ppermute | solution.py:455
  470.5 53.9 %collective-permute-start.38 = (bf16[256,1536]{1,0:T(8,128)(2,1)}, bf16[256,1536]{1,0:T(8,128)(2,1)}, u32[]{:S(2)}, u32[]{:S(2)}) collective-permute-start(bf16[256,1536]{1,0:T(8,128)(2,1)} %get-tuple-element.232), channel_id=1, source_target_pairs={{0,2},{1,3},{2,0},{3,1},{4,6},{5,7},{6,4},{7,5}} | collective-permute-start | bytes 2359304 | tf_op jit(solution)/shard_map/ppermute | solution.py:455
  478.5 45.9 %collective-permute-start.39 = (bf16[256,1536]{1,0:T(8,128)(2,1)}, bf16[256,1536]{1,0:T(8,128)(2,1)S(1)}, u32[]{:S(2)}, u32[]{:S(2)}) collective-permute-start(bf16[256,1536]{1,0:T(8,128)(2,1)} %get-tuple-element.233), channel_id=1, source_target_pairs={{0,3},{1,2},{2,1},{3,0},{4,7},{5,6},{6,5},{7,4}} | collective-permute-start | bytes 2359304 | tf_op jit(solution)/shard_map/ppermute | solution.py:455
  478.8 51.9 %collective-permute-start.31 = (bf16[256,1536]{1,0:T(8,128)(2,1)}, bf16[256,1536]{1,0:T(8,128)(2,1)S(1)}, u32[]{:S(2)}, u32[]{:S(2)}) collective-permute-start(bf16[256,1536]{1,0:T(8,128)(2,1)} %get-tuple-element.219), channel_id=1, source_target_pairs={{0,2},{1,3},{2,0},{3,1},{4,6},{5,7},{6,4},{7,5}} | collective-permute-start | bytes 2359304 | tf_op jit(solution)/shard_map/ppermute | solution.py:455
  480.3 60.4 %collective-permute-start.32 = (bf16[256,1536]{1,0:T(8,128)(2,1)}, bf16[256,1536]{1,0:T(8,128)(2,1)S(1)}, u32[]{:S(2)}, u32[]{:S(2)}) collective-permute-start(bf16[256,1536]{1,0:T(8,128)(2,1)} %get-tuple-element.220), channel_id=1, source_target_pairs={{0,3},{1,2},{2,1},{3,0},{4,7},{5,6},{6,5},{7,4}} | collective-permute-start | bytes 2359304 | tf_op jit(solution)/shard_map/ppermute | solution.py:455
  480.5 44.9 %copy-start.8 = (bf16[256,1536]{1,0:T(8,128)(2,1)S(1)}, bf16[256,1536]{1,0:T(8,128)(2,1)}, u32[]{:S(2)}) copy-start(bf16[256,1536]{1,0:T(8,128)(2,1)} %get-tuple-element.225.refs_0_) | copy-start | bytes 2359300
  524.4 0.9 copy-start.6
  525.3 16.3 %copy-start.7 = (bf16[256,1536]{1,0:T(8,128)(2,1)S(1)}, bf16[256,1536]{1,0:T(8,128)(2,1)}, u32[]{:S(2)}) copy-start(bf16[256,1536]{1,0:T(8,128)(2,1)} %get-tuple-element.210.refs_0_) | copy-start | bytes 2359300
  530.7 10.0 %copy-start.4 = (bf16[256,1536]{1,0:T(8,128)(2,1)}, bf16[256,1536]{1,0:T(8,128)(2,1)S(1)}, u32[]{:S(2)}) copy-start(bf16[256,1536]{1,0:T(8,128)(2,1)S(1)} %collective-permute-done.31.refs_2_) | copy-start | bytes 2359300
  540.7 0.9 copy-start.5

commit v5 on v4

--- a/solution.py
+++ b/solution.py
@@ -14,7 +14,7 @@
 SENT_SHARE = 7, 8
 PAIR = 2
 
-KERNEL_ORDER = (('f', 0), ('b', 0), ('f', 1), ('b', 1), ('n', 2), ('n', 3))
+KERNEL_ORDER = (('f', 0), ('b', 0), ('m', 1), ('n', 2), ('n', 3))
 
 
 def dot(a, b):
@@ -82,43 +82,6 @@
         p_ref[...] = weighted_rows(q_ref[s] == slots, None if g_ref is None else g_ref[s], rows_scr[s])
 
 
-def fwd_kernel(cap, pad, xa_ref, xb_ref, tok_ref, q_ref, g_ref, w1_ref, w3_ref, w2_ref, xg_ref, a_ref, u_ref, v_ref, p0_ref, p1_ref, xg_scr, o_scr):
-    e = pl.program_id(0)
-
-    @pl.when(e == 0)
-    def _():
-        spread_rows(xg_scr, tok_ref, (xa_ref, xb_ref), cap)
-
-    xg_ref[0] = xg_scr[e]
-    act, u_ref[0], v_ref[0] = forward_expert(xg_scr[e], w1_ref, w3_ref)
-    a_ref[0] = act
-    keep_rows(o_scr, dot(act, w2_ref[0]), e, cap, pad)
-
-    @pl.when(e == pl.num_programs(0) - 1)
-    def _():
-        group_sums((p0_ref, p1_ref), q_ref, o_scr, g_ref)
-
-
-def bwd_kernel(cap, pad, dya_ref, dyb_ref, tok_ref, gcol_ref, q_ref, w1_ref, w3_ref, w2_ref, u_ref, v_ref, d_ref, dh1_ref, dh3_ref, p0_ref, p1_ref, d_scr, r_scr):
-    e = pl.program_id(0)
-
-    @pl.when(e == 0)
-    def _():
-        spread_rows(d_scr, tok_ref, (dya_ref, dyb_ref), cap, gcol_ref)
-
-    d_ref[0] = d_scr[e]
-    da = dot_bt(d_scr[e], w2_ref[0])
-    dh1 = (da * u_ref[0]).astype(BF)
-    dh3 = (da * v_ref[0]).astype(BF)
-    dh1_ref[0] = dh1
-    dh3_ref[0] = dh3
-    keep_rows(r_scr, dot_bt(dh1, w1_ref[0]) + dot_bt(dh3, w3_ref[0]), e, cap, pad)
-
-    @pl.when(e == pl.num_programs(0) - 1)
-    def _():
-        group_sums((p0_ref, p1_ref), q_ref, r_scr)
-
-
 def unit_rows(u_refs, unit_ref, rows_scr, weight_ref=None):
     for s, u_ref in enumerate(u_refs):
         units = lax.broadcasted_iota(jnp.int32, (u_ref.shape[0], unit_ref.shape[2]), 0)
@@ -172,21 +135,15 @@
         group_sums((p0_ref, p1_ref), q_ref, r_scr)
 
 
-def merge_kernel(weighted, n0_ref, n1_ref, r0_ref, r1_ref, place_ref, weight_ref, p0_ref, p1_ref):
-    for s, (n_ref, r_ref, p_ref) in enumerate(((n0_ref, r0_ref, p0_ref), (n1_ref, r1_ref, p1_ref))):
-        places = lax.broadcasted_iota(jnp.int32, (n_ref.shape[0], r_ref.shape[0]), 0)
-        total = weighted_rows(place_ref[s] == places, weight_ref[s] if weighted else None, r_ref[...])
+def merge_kernel(weighted, count, *refs):
+    near, sent, places, weights, outs = (refs[k * count:(k + 1) * count] for k in range(5))
+    for n_ref, r_ref, place_ref, weight_ref, p_ref in zip(near, sent, places, weights, outs):
+        slots = lax.broadcasted_iota(jnp.int32, (n_ref.shape[0], r_ref.shape[0]), 0)
+        total = weighted_rows(place_ref[0] == slots, weight_ref[0] if weighted else None, r_ref[...])
         p_ref[...] = (n_ref[...] + total).astype(BF)
 
 
-def near_kernel(cap, pad, xa_ref, xb_ref, dya_ref, dyb_ref, tok_ref, gcol_ref, q_ref, g_ref, w1_ref, w3_ref, w2_ref, xg_ref, a_ref, d_ref, dh1_ref, dh3_ref, y0_ref, y1_ref, z0_ref, z1_ref, xg_scr, d_scr, o_scr, r_scr):
-    e = pl.program_id(0)
-
-    @pl.when(e == 0)
-    def _():
-        spread_rows(xg_scr, tok_ref, (xa_ref, xb_ref), cap)
-        spread_rows(d_scr, tok_ref, (dya_ref, dyb_ref), cap, gcol_ref)
-
+def both_ways(cap, pad, e, w1_ref, w3_ref, w2_ref, xg_ref, a_ref, d_ref, dh1_ref, dh3_ref, xg_scr, d_scr, o_scr, r_scr):
     xg_ref[0] = xg_scr[e]
     d_ref[0] = d_scr[e]
     act, u, v = forward_expert(xg_scr[e], w1_ref, w3_ref)
@@ -199,12 +156,45 @@
     dh3_ref[0] = dh3
     keep_rows(r_scr, dot_bt(dh1, w1_ref[0]) + dot_bt(dh3, w3_ref[0]), e, cap, pad)
 
+
+def near_kernel(cap, pad, xa_ref, xb_ref, dya_ref, dyb_ref, tok_ref, gcol_ref, q_ref, g_ref, w1_ref, w3_ref, w2_ref, xg_ref, a_ref, d_ref, dh1_ref, dh3_ref, y0_ref, y1_ref, z0_ref, z1_ref, xg_scr, d_scr, o_scr, r_scr):
+    e = pl.program_id(0)
+
+    @pl.when(e == 0)
+    def _():
+        spread_rows(xg_scr, tok_ref, (xa_ref, xb_ref), cap)
+        spread_rows(d_scr, tok_ref, (dya_ref, dyb_ref), cap, gcol_ref)
+
+    both_ways(cap, pad, e, w1_ref, w3_ref, w2_ref, xg_ref, a_ref, d_ref, dh1_ref, dh3_ref, xg_scr, d_scr, o_scr, r_scr)
+
     @pl.when(e == pl.num_programs(0) - 1)
     def _():
         group_sums((y0_ref, y1_ref), q_ref, o_scr, g_ref)
         group_sums((z0_ref, z1_ref), q_ref, r_scr)
 
 
+def far_both_kernel(cap, pad, xa_ref, xb_ref, dya_ref, dyb_ref, tok_ref, gcol_ref, q_ref, g_ref, unit_ref, form_ref, over_ref, w1_ref, w3_ref, w2_ref, xg_ref, a_ref, d_ref, dh1_ref, dh3_ref, y0_ref, y1_ref, z0_ref, z1_ref, ry0_ref, ry1_ref, rz0_ref, rz1_ref, xg_scr, d_scr, o_scr, r_scr):
+    e = pl.program_id(0)
+
+    @pl.when(e == 0)
+    def _():
+        spread_rows(xg_scr, tok_ref, (xa_ref, xb_ref), cap)
+        spread_rows(d_scr, tok_ref, (dya_ref, dyb_ref), cap, gcol_ref)
+
+    both_ways(cap, pad, e, w1_ref, w3_ref, w2_ref, xg_ref, a_ref, d_ref, dh1_ref, dh3_ref, xg_scr, d_scr, o_scr, r_scr)
+    done = e == pl.num_programs(0) - 1
+
+    @pl.when(done & (over_ref[0] == 0))
+    def _():
+        unit_rows((ry0_ref, ry1_ref), unit_ref, o_scr, form_ref)
+        unit_rows((rz0_ref, rz1_ref), unit_ref, r_scr)
+
+    @pl.when(done & (over_ref[0] != 0))
+    def _():
+        group_sums((y0_ref, y1_ref), q_ref, o_scr, g_ref)
+        group_sums((z0_ref, z1_ref), q_ref, r_scr)
+
+
 def whole(shape):
     return pl.BlockSpec(shape, lambda e: (0,) * len(shape))
 
@@ -223,40 +213,6 @@
 
 def params():
     return pltpu.CompilerParams(dimension_semantics=("arbitrary",), vmem_limit_bytes=60 * 1024 * 1024)
-
-
-def forward_pair(pair, xa, xb, tok_col, q_row, g_row, w1, w3, w2, cap, pad, grp_cap):
-    experts, hidden, ff = w1.shape
-    rows = PAIR * cap
-    outs = [((experts, rows, hidden), BF), ((experts, rows, ff), BF), ((experts, rows, ff), F32), ((experts, rows, ff), F32), ((grp_cap, hidden), F32), ((grp_cap, hidden), F32)]
-    return pl.pallas_call(
-        functools.partial(fwd_kernel, cap, pad),
-        grid=(experts,),
-        in_specs=[whole(xa.shape), whole(xb.shape), of_pair(pair, tok_col.shape), of_pair(pair, q_row.shape), of_pair(pair, g_row.shape), per_expert(w1.shape), per_expert(w3.shape), per_expert(w2.shape)],
-        out_specs=[per_expert(s) if len(s) == 3 else whole(s) for s, _ in outs],
-        out_shape=[jax.ShapeDtypeStruct(s, t) for s, t in outs],
-        scratch_shapes=[pltpu.VMEM((experts, rows, hidden), BF), pltpu.VMEM((PAIR, experts * pad, hidden), BF)],
-        compiler_params=params(),
-        cost_estimate=pl.CostEstimate(flops=14 * 10**9, bytes_accessed=50 * 10**6, transcendentals=0),
-        name="fwd_pair",
-    )(xa, xb, tok_col, q_row, g_row, w1, w3, w2)
-
-
-def backward_pair(pair, dya, dyb, tok_col, g_col, q_row, w1, w3, w2, u, v, cap, pad, grp_cap):
-    experts, hidden, ff = w1.shape
-    rows = PAIR * cap
-    outs = [((experts, rows, hidden), BF), ((experts, rows, ff), BF), ((experts, rows, ff), BF), ((grp_cap, hidden), F32), ((grp_cap, hidden), F32)]
-    return pl.pallas_call(
-        functools.partial(bwd_kernel, cap, pad),
-        grid=(experts,),
-        in_specs=[whole(dya.shape), whole(dyb.shape), of_pair(pair, tok_col.shape), of_pair(pair, g_col.shape), of_pair(pair, q_row.shape), per_expert(w1.shape), per_expert(w3.shape), per_expert(w2.shape), per_expert(u.shape), per_expert(v.shape)],
-        out_specs=[per_expert(s) if len(s) == 3 else whole(s) for s, _ in outs],
-        out_shape=[jax.ShapeDtypeStruct(s, t) for s, t in outs],
-        scratch_shapes=[pltpu.VMEM((experts, rows, hidden), BF), pltpu.VMEM((PAIR, experts * pad, hidden), BF)],
-        compiler_params=params(),
-        cost_estimate=pl.CostEstimate(flops=14 * 10**9, bytes_accessed=50 * 10**6, transcendentals=0),
-        name="bwd_pair",
-    )(dya, dyb, tok_col, g_col, q_row, w1, w3, w2, u, v)
 
 
 def flag():
@@ -301,20 +257,40 @@
     )(dya, dyb, *tables, over, w1, w3, w2, u, v)
 
 
-def merge_pair(pair, near, sent, place, weight, weighted):
+def far_both_pair(pair, xa, xb, dya, dyb, tok_col, g_col, q_row, g_row, unit_row, form_row, over, w1, w3, w2, cap, pad, grp_cap, units):
+    experts, hidden, ff = w1.shape
+    rows = PAIR * cap
+    wide, narrow, part, sent = ((experts, rows, hidden), BF), ((experts, rows, ff), BF), ((grp_cap, hidden), F32), ((units, hidden), BF)
+    outs = [wide, narrow, wide, narrow, narrow] + [part] * 4 + [sent] * 4
+    tables = [tok_col, g_col, q_row, g_row, unit_row, form_row]
+    return pl.pallas_call(
+        functools.partial(far_both_kernel, cap, pad),
+        grid=(experts,),
+        in_specs=[once(xa.shape)] * 4 + [of_pair(pair, t.shape) for t in tables] + [flag(), per_expert(w1.shape), per_expert(w3.shape), per_expert(w2.shape)],
+        out_specs=[per_expert(s) if len(s) == 3 else once(s) for s, _ in outs],
+        out_shape=[jax.ShapeDtypeStruct(s, t) for s, t in outs],
+        scratch_shapes=[pltpu.VMEM((experts, rows, hidden), BF)] * 2 + [pltpu.VMEM((PAIR, experts * pad, hidden), BF)] * 2,
+        compiler_params=params(),
+        cost_estimate=pl.CostEstimate(flops=28 * 10**9, bytes_accessed=70 * 10**6, transcendentals=0),
+        name="far_both_pair",
+    )(xa, xb, dya, dyb, *tables, over, w1, w3, w2)
+
+
+def merge_sources(sources, near, sent, place, weight, weighted):
     grp_cap, hidden = near[0].shape
-    units = sent[0].shape[0]
+    units, count = sent[0].shape[0], len(sources)
     block = hidden // 3
-    return pl.pallas_call(
-        functools.partial(merge_kernel, weighted),
+    notes = [pl.BlockSpec((1, 1, units), functools.partial(lambda k, n: (k, 0, 0), k)) for k in sources]
+    return pl.pallas_call(
+        functools.partial(merge_kernel, weighted, count),
         grid=(3,),
-        in_specs=[pl.BlockSpec((grp_cap, block), lambda n: (0, n))] * 2 + [pl.BlockSpec((units, block), lambda n: (0, n))] * 2 + [of_pair(pair, place.shape), of_pair(pair, weight.shape)],
-        out_specs=[pl.BlockSpec((grp_cap, block), lambda n: (0, n))] * 2,
-        out_shape=[jax.ShapeDtypeStruct((grp_cap, hidden), BF)] * 2,
-        compiler_params=params(),
-        cost_estimate=pl.CostEstimate(flops=2 * 10**9, bytes_accessed=8 * 10**6, transcendentals=0),
-        name="merge_pair",
-    )(*near, *sent, place, weight)
+        in_specs=[pl.BlockSpec((grp_cap, block), lambda n: (0, n))] * count + [pl.BlockSpec((units, block), lambda n: (0, n))] * count + notes * 2,
+        out_specs=[pl.BlockSpec((grp_cap, block), lambda n: (0, n))] * count,
+        out_shape=[jax.ShapeDtypeStruct((grp_cap, hidden), BF)] * count,
+        compiler_params=params(),
+        cost_estimate=pl.CostEstimate(flops=count * 10**9, bytes_accessed=count * 4 * 10**6, transcendentals=0),
+        name="merge_sources",
+    )(*near, *sent, *[place] * count, *[weight] * count)
 
 
 def near_pair(pair, xa, xb, dya, dyb, tok_col, g_col, q_row, g_row, w1, w3, w2, cap, pad, grp_cap):
@@ -519,38 +495,38 @@
             if step == 'n':
                 xs[c], acts[c], ds[c], dh1s[c], dh3s[c], *sums = near_pair(c, *x_pairs[c], *dy_pairs[c], tok_cols, g_cols, places, g_rows, w1, w3, w2, cap, pad, grp_cap)
                 y_sums[c], dx_sums[c] = sums[:PAIR], sums[PAIR:]
-            elif step == 'f' and c < 2:
+            elif step == 'm':
+                xs[c], acts[c], ds[c], dh1s[c], dh3s[c], *sums = far_both_pair(c, *x_pairs[c], *dy_pairs[c], tok_cols, g_cols, places, g_rows, unit_rows, form_rows, over_flag, w1, w3, w2, cap, pad, grp_cap, units)
+                y_sums[c], dx_sums[c], y_sent[c], dx_sent[c] = (sums[k:k + PAIR] for k in range(0, 4 * PAIR, PAIR))
+            elif step == 'f':
                 xs[c], acts[c], *saved[c], y0, y1, r0, r1 = far_forward_pair(c, *x_pairs[c], tok_cols, places, g_rows, unit_rows, form_rows, over_flag, w1, w3, w2, cap, pad, grp_cap, units)
                 y_sums[c], y_sent[c] = (y0, y1), (r0, r1)
-            elif step == 'b' and c < 2:
+            else:
                 ds[c], dh1s[c], dh3s[c], z0, z1, r0, r1 = far_backward_pair(c, *dy_pairs[c], tok_cols, g_cols, places, unit_rows, over_flag, w1, w3, w2, *saved[c], cap, pad, grp_cap, units)
                 dx_sums[c], dx_sent[c] = (z0, z1), (r0, r1)
-            elif step == 'f':
-                xs[c], acts[c], *saved[c], y0, y1 = forward_pair(c, *x_pairs[c], tok_cols, places, g_rows, w1, w3, w2, cap, pad, grp_cap)
-                y_sums[c] = (y0, y1)
-            else:
-                ds[c], dh1s[c], dh3s[c], *dx_sums[c] = backward_pair(c, *dy_pairs[c], tok_cols, g_cols, places, w1, w3, w2, *saved[c], cap, pad, grp_cap)
             last = (y_sums if step == 'f' else dx_sums)[c][0]
 
         grads = weight_grads(xs, acts, ds, dh1s, dh3s)
 
-        def combine(results, sent, weighted):
+        def combine(results, sent, weighted, split):
+            near = [*results[2], *results[3]]
+            full = [*results[0], *results[1]]
+            arrived = [hop_y(r) for r in (*sent[0], *sent[1])]
             sums = []
-            for pair, near in ((0, 2), (1, 3)):
-                arrived = [hop_y(r) for r in sent[pair]]
+            for sources in split:
 
                 def by_rows(ops):
-                    return list(merge_pair(pair, ops[0], ops[1], sent_place, sent_weight, weighted))
+                    return list(merge_sources(sources, ops[0], ops[1], sent_place, sent_weight, weighted))
 
                 def by_sums(ops):
                     return [(n + hop_y(f)).astype(BF) for n, f in zip(ops[0], ops[2])]
 
-                sums += lax.cond(over, by_sums, by_rows, (list(results[near]), arrived, list(results[pair])))
+                sums += lax.cond(over, by_sums, by_rows, tuple([rows[k] for k in sources] for rows in (near, arrived, full)))
             return [sums[0]] + [hop_g(sums[k], k) for k in (1, 2, 3)]
 
-        y_parts = combine(y_sums, y_sent, True)
+        y_parts = combine(y_sums, y_sent, True, ((0, 1), (2, 3)))
         y_out = collect(y_parts, q_cols)
-        dx_out = collect(combine(dx_sums, dx_sent, False), q_cols)
+        dx_out = collect(combine(dx_sums, dx_sent, False, ((0, 1), (2,), (3,))), q_cols)
         return y_out, dx_out, grads[0], grads[1], grads[2]
 
     return jax.shard_map(device_fn, mesh=mesh, in_specs=(tok_spec, tok_spec, tok_spec, tok_spec, weight_spec, weight_spec, weight_spec), out_specs=(tok_spec, tok_spec, grad_spec, grad_spec, grad_spec), check_vma=False)

time: 555 us -> 569 us (1.025)
  waiting for transfers between devices: 216 us -> 243 us
  Pallas kernels: 270 us -> 257 us
    pallas_call x4 -> x6, Pallas kernels: 20.1 us -> 66.6 us  [the longest x1 44.5 us: far_both_pair(): pl.pallas_call(functools.partial(far_both_kernel, cap, pad), grid=(expert...]
    ppermute x20, waiting for transfers between devices: 73.1 us -> 108 us  [hop_g(): return lax.ppermute(a, 'grp', [(g, g ^ bits) for g in range(groups)])]
    pallas_call x2 -> x1, Pallas kernels: 62.2 us -> 31 us  [far_forward_pair(): pl.pallas_call(functools.partial(far_fwd_kernel, cap, pad), grid=(experts...]
    pallas_call x2 -> x1, Pallas kernels: 58.3 us -> 29 us  [far_backward_pair(): pl.pallas_call(functools.partial(far_bwd_kernel, cap, pad), grid=(experts...]
    ppermute x12, waiting for transfers between devices: 143 us -> 135 us  [hop_y(): return lax.ppermute(a, 'ing', [(0, 1), (1, 0)])]
  transfers between devices with their start and end apart: 32 -> 32, of which waited for: 11 -> 11; matrix products, arithmetic and copies ran while one was open for 5% -> 5% of each run, Pallas kernels for 48% -> 45%
where the time goes in v5:
time: 569 us; the launch traced here: 561 us
  Pallas kernels  257 us (45%)
  waiting for transfers between devices  243 us (43%)
  starting transfers between devices  26.9 us (5%)
  local copies, waits for them, and re-layouts  15.8 us (3%)
  other arithmetic  15.1 us (3%)
    ppermute x12, waiting for transfers between devices, hop_y(): return lax.ppermute(a, 'ing', [(0, 1), (1, 0)])  135 us
    ppermute x20, waiting for transfers between devices, hop_g(): return lax.ppermute(a, 'grp', [(g, g ^ bits) for g in range(groups)])  108 us
    pallas_call x2, Pallas kernels, near_pair(): pl.pallas_call(functools.partial(near_kernel, cap, pad), grid=(experts,),...  75.4 us
    pallas_call x1, Pallas kernels, far_both_pair(): pl.pallas_call(functools.partial(far_both_kernel, cap, pad), grid=(expert...  44.5 us
    pallas_call x1, Pallas kernels, weight_grads(): pl.pallas_call(functools.partial(dw_kernel, chunks), grid=(experts,), in_...  43.9 us
    pallas_call x1, Pallas kernels, far_forward_pair(): pl.pallas_call(functools.partial(far_fwd_kernel, cap, pad), grid=(experts...  31 us
    pallas_call x1, Pallas kernels, far_backward_pair(): pl.pallas_call(functools.partial(far_bwd_kernel, cap, pad), grid=(experts...  29 us
    pallas_call x5, Pallas kernels, merge_sources(): pl.pallas_call(functools.partial(merge_kernel, weighted, count), grid=(3,...  22.2 us
  transfers between devices with their start and end apart: 32, of which 11 were waited for; matrix products, arithmetic and copies ran while one was open for 5% of the time, Pallas kernels for 45%

profile of v5, /device:TPU:0, one launch (start us, length us, event | category | flops | bytes accessed | tf_op | source)
XLA Modules:
  0.0 561.0 jit_solution(11378253162974566578)
XLA Ops:
  0.6 3.4 collective-permute-start.13
  4.0 1.5 collective-permute-start.25
  7.5 1.5 collective-permute-start.16
  9.0 31.2 %collective-permute-done.8 = f32[1,12,512]{2,1,0:T(8,128)S(1)} collective-permute-done((f32[1,12,512]{2,1,0:T(8,128)S(1)}, f32[1,12,512]{2,1,0:T(8,128)S(1)}, u32[]{:S(2)}, u32[]{:S(2)}) %collective-permute-start.8) | collective-permute-done | bytes 24608 | tf_op jit(solution)/shard_map/ppermute | solution.py:428
  40.2 1.2 collective-permute-done.9
  41.4 2.0 collective-permute-start.10
  43.5 3.8 collective-permute-done.10
  49.6 9.7 %select_reduce_fusion = (f32[8,8,72]{2,1,0:T(8,128)S(1)}, f32[8,8,72]{2,1,0:T(8,128)S(1)}, f32[8,8,72]{2,1,0:T(8,128)S(1)}, f32[8,8,72]{2,1,0:T(8,128)S(1)}) fusion(f32[8,8,512]{2,1,0:T(8,128)S(1)} %copy.58, f32[8,8,512]{2,1,0:T(8,128)S(1)} %slice.100, pred[8,8,512]{2,1,0:T(8,128)(4,1)S(1)} %compare_reduce_fusion, f32[8,512]{1,0:T(8,128)S(1)} %bitcast.41, ...), kind=kLoop, calls=%fused_computation.8 | loop fusion | flops 23574528 | bytes 518144 | tf_op jit(solution)/shard_map/reduce_sum | solution.py:399
  59.6 1.1 select_reduce_fusion.5
  60.7 1.8 collective-permute-start.23
  62.5 10.8 %collective-permute-done.23 = f32[2,4,448]{2,1,0:T(4,128)S(1)} collective-permute-done((f32[2,4,448]{2,1,0:T(4,128)S(1)}, f32[2,4,448]{2,1,0:T(4,128)S(1)}, u32[]{:S(2)}, u32[]{:S(2)}) %collective-permute-start.23) | collective-permute-done | bytes 14368 | tf_op jit(solution)/shard_map/ppermute | solution.py:428
  73.4 1.7 collective-permute-start.27
  75.4 1.7 collective-permute-start.17
  78.7 2.1 reshape.248.gcol_ref
  84.2 2.1 convert_element_type.181.tok_ref
  86.3 24.4 %collective-permute-done.27.dya_ref = bf16[512,1536]{1,0:T(8,128)(2,1)} collective-permute-done((bf16[512,1536]{1,0:T(8,128)(2,1)S(1)}, bf16[512,1536]{1,0:T(8,128)(2,1)}, u32[]{:S(2)}, u32[]{:S(2)}) %collective-permute-start.27) | collective-permute-done | bytes 1572896 | tf_op jit(solution)/shard_map/ppermute | solution.py:431
  111.2 33.2 %collective-permute-done.14.xa_ref = bf16[512,1536]{1,0:T(8,128)(2,1)} collective-permute-done((bf16[512,1536]{1,0:T(8,128)(2,1)}, bf16[512,1536]{1,0:T(8,128)(2,1)}, u32[]{:S(2)}, u32[]{:S(2)}) %collective-permute-start.14) | collective-permute-done | bytes 1572896 | tf_op jit(solution)/shard_map/ppermute | solution.py:431
  144.4 32.1 %collective-permute-done.17.dya_ref = bf16[512,1536]{1,0:T(8,128)(2,1)} collective-permute-done((bf16[512,1536]{1,0:T(8,128)(2,1)}, bf16[512,1536]{1,0:T(8,128)(2,1)}, u32[]{:S(2)}, u32[]{:S(2)}) %collective-permute-start.17) | collective-permute-done | bytes 1572896 | tf_op jit(solution)/shard_map/ppermute | solution.py:431
  176.5 31.0 %far_fwd_pair.1 = (bf16[8,144,1536]{2,1,0:T(8,128)(2,1)}, bf16[8,144,512]{2,1,0:T(8,128)(2,1)}, f32[8,144,512]{2,1,0:T(8,128)}, f32[8,144,512]{2,1,0:T(8,128)}, ...) custom-call(bf16[512,1536]{1,0:T(8,128)(2,1)} %collective-permute-done.13.xa_r, ...), custom_call_target="tpu_custom_call" | custom-call | flops 14000000000 | bytes 50000000 | tf_op jit(solution)/shard_map/far_fwd_pair/pallas_call | solution.py:228
  208.1 29.0 %far_bwd_pair.1 = (bf16[8,144,1536]{2,1,0:T(8,128)(2,1)}, bf16[8,144,512]{2,1,0:T(8,128)(2,1)}, bf16[8,144,512]{2,1,0:T(8,128)(2,1)}, f32[256,1536]{1,0:T(8,128)...) custom-call(bf16[512,1536]{1,0:T(8,128)(2,1)} %collective-permute-done.16.dya_ref, ...), custom_call_target="tpu_custom_call" | custom-call | flops 14000000000 | bytes 50000000 | tf_op jit(solution)/shard_map/far_bwd_pair/pallas_call | solution.py:247
  237.0 1.5 collective-permute-start.21
  239.1 44.5 %far_both_pair.1 = (bf16[8,144,1536]{2,1,0:T(8,128)(2,1)}, bf16[8,144,512]{2,1,0:T(8,128)(2,1)}, bf16[8,144,1536]{2,1,0:T(8,128)(2,1)}, bf16[8,144,512]{2,1,0:T(...) custom-call(bf16[512,1536]{1,0:T(8,128)(2,1)} %collective-permute-do, ...), custom_call_target="tpu_custom_call" | custom-call | flops 28000000000 | bytes 70000000 | tf_op jit(solution)/shard_map/far_both_pair/pallas_call | solution.py:266
  283.6 1.5 collective-permute-start.33
  285.1 37.5 %near_pair.2 = (bf16[8,144,1536]{2,1,0:T(8,128)(2,1)}, bf16[8,144,512]{2,1,0:T(8,128)(2,1)}, bf16[8,144,1536]{2,1,0:T(8,128)(2,1)}, bf16[8,144,512]{2,1,0:T(8,12...) custom-call(bf16[512,1536]{1,0:T(8,128)(2,1)} %xa_ref.1, ...), custom_call_target="tpu_custom_call" | custom-call | flops 28000000000 | bytes 70000000 | tf_op jit(solution)/shard_map/near_pair/pallas_call | solution.py:302
  322.7 7.1 %conditional.5 = ((bf16[256,1536]{1,0:T(8,128)(2,1)}, bf16[256,1536]{1,0:T(8,128)(2,1)})) conditional(s32[]{:T(128)} %convert_element_type.161, (f32[256,1536]{1,0:T(8,128)}, f32[256,1536]{1,0:T(8,128)}, bf16[448,1536]{1,0:T(8,128)(2,1)}, bf16[448,1536]{1,0:T(8,128)(2,1)}, s32[4,1,448]{2,0,1:T(4,128)S(1)}, ...), branch_computations={%region_15.16_spmd, %region_16.17_spmd} | conditional | flops 2000000000 | bytes 26738820 | solution.py:524
  323.9 5.9 %merge_sources.5 = (bf16[256,1536]{1,0:T(8,128)(2,1)}, bf16[256,1536]{1,0:T(8,128)(2,1)}) custom-call(f32[256,1536]{1,0:T(8,128)} %get-tuple-element.87.refs_0_, f32[256,1536]{1,0:T(8,128)} %get-tuple-element.88.refs_1_, bf16[448,1536]{1,0:T(8,128)(2,1)} %get-tuple-element.92.refs_2_, bf16[448,1536]{1,0:T(8,128)(2,1)} %get-tuple-element.93.refs_3_, ...), custom_call_target="tpu_custom_call" | custom-call | flops 2000000000 | bytes 8000000 | tf_op jit(solution)/shard_map/cond/branch_0_fun/merge_sources/pallas_call | solution.py:284
  330.6 1.0 fusion.1.refs_4_
  331.6 1.5 collective-permute-start.29
  333.1 30.0 %collective-permute-done.34 = bf16[448,1536]{1,0:T(8,128)(2,1)} collective-permute-done((bf16[448,1536]{1,0:T(8,128)(2,1)}, bf16[448,1536]{1,0:T(8,128)(2,1)}, u32[]{:S(2)}, u32[]{:S(2)}) %collective-permute-start.34) | collective-permute-done | bytes 1376288 | tf_op jit(solution)/shard_map/ppermute | solution.py:428
  363.1 5.3 conditional.7
  364.3 4.1 merge_sources.7
  369.0 1.5 collective-permute-start.36
  371.0 37.8 %near_pair.3 = (bf16[8,144,1536]{2,1,0:T(8,128)(2,1)}, bf16[8,144,512]{2,1,0:T(8,128)(2,1)}, bf16[8,144,1536]{2,1,0:T(8,128)(2,1)}, bf16[8,144,512]{2,1,0:T(8,12...) custom-call(bf16[512,1536]{1,0:T(8,128)(2,1)} %collective-permute-do, ...), custom_call_target="tpu_custom_call" | custom-call | flops 28000000000 | bytes 70000000 | tf_op jit(solution)/shard_map/near_pair/pallas_call | solution.py:302
  408.9 13.2 %collective-permute-done.30 = bf16[448,1536]{1,0:T(8,128)(2,1)} collective-permute-done((bf16[448,1536]{1,0:T(8,128)(2,1)}, bf16[448,1536]{1,0:T(8,128)(2,1)}, u32[]{:S(2)}, u32[]{:S(2)}) %collective-permute-start.30) | collective-permute-done | bytes 1376288 | tf_op jit(solution)/shard_map/ppermute | solution.py:428
  422.1 7.1 %conditional.6 = ((bf16[256,1536]{1,0:T(8,128)(2,1)}, bf16[256,1536]{1,0:T(8,128)(2,1)})) conditional(s32[]{:T(128)} %convert_element_type.161, (f32[256,1536]{1,0:T(8,128)}, f32[256,1536]{1,0:T(8,128)}, bf16[448,1536]{1,0:T(8,128)(2,1)}, bf16[448,1536]{1,0:T(8,128)(2,1)}, s32[4,1,448]{2,0,1:T(4,128)S(1)}, ...), branch_computations={%region_17.18_spmd, %region_18.19_spmd} | conditional | flops 2000000000 | bytes 26738820 | solution.py:524
  423.3 5.9 %merge_sources.6 = (bf16[256,1536]{1,0:T(8,128)(2,1)}, bf16[256,1536]{1,0:T(8,128)(2,1)}) custom-call(f32[256,1536]{1,0:T(8,128)} %get-tuple-element.100.refs_0_, f32[256,1536]{1,0:T(8,128)} %get-tuple-element.101.refs_1_, bf16[448,1536]{1,0:T(8,128)(2,1)} %get-tuple-element.102.refs_2_, bf16[448,1536]{1,0:T(8,128)(2,1)} %get-tuple-element.103.refs_3_, ...), custom_call_target="tpu_custom_call" | custom-call | flops 2000000000 | bytes 8000000 | tf_op jit(solution)/shard_map/cond/branch_0_fun/merge_sources/pallas_call | solution.py:284
  429.3 50.1 %collective-permute-done.38 = bf16[448,1536]{1,0:T(8,128)(2,1)} collective-permute-done((bf16[448,1536]{1,0:T(8,128)(2,1)}, bf16[448,1536]{1,0:T(8,128)(2,1)}, u32[]{:S(2)}, u32[]{:S(2)}) %collective-permute-start.38) | collective-permute-done | bytes 1376288 | tf_op jit(solution)/shard_map/ppermute | solution.py:428
  479.3 4.7 conditional.9
  480.5 3.5 merge_sources.9
  484.0 4.0 conditional.8
  485.3 2.8 merge_sources.8
  488.0 1.5 collective-permute-start.37
  490.1 1.2 collective-permute-start.32
  491.3 43.9 %weight_grads.1 = (f32[8,1536,512]{2,1,0:T(8,128)}, f32[8,1536,512]{2,1,0:T(8,128)}, f32[8,512,1536]{2,1,0:T(8,128)}) custom-call(bf16[8,144,1536]{2,1,0:T(8,128)(2,1)} %get-tuple-element.236.refs_0_, bf16[8,144,1536]{2,1,0:T(8,128)(2,1)} %get-tuple-element.237.refs_1_, bf16[8,144,1536]{2,1,0:T(8,128)(2,1)} %get-tuple-element.238.refs_2_, ...), custom_call_target="tpu_custom_call" | custom-call | flops 24999999488 | bytes 120000000 | tf_op jit(solution)/shard_map/weight_grads/pallas_call | solution.py:333
  536.0 5.6 collect.3
  541.6 13.0 %collective-permute-done.32.refs_3_ = bf16[256,1536]{1,0:T(8,128)(2,1)S(1)} collective-permute-done((bf16[256,1536]{1,0:T(8,128)(2,1)}, bf16[256,1536]{1,0:T(8,128)(2,1)S(1)}, u32[]{:S(2)}, u32[]{:S(2)}) %collective-permute-start.32) | collective-permute-done | bytes 786464 | tf_op jit(solution)/shard_map/ppermute | solution.py:431
  554.6 0.9 copy-done.6
  555.5 5.3 collect.2
  (132 shorter events, 20.1 us)
Async XLA Ops:
  0.6 74.4 %collective-permute-start.13 = (bf16[512,1536]{1,0:T(8,128)(2,1)}, bf16[512,1536]{1,0:T(8,128)(2,1)}, u32[]{:S(2)}, u32[]{:S(2)}) collective-permute-start(bf16[512,1536]{1,0:T(8,128)(2,1)} %xa_ref.1), channel_id=1, source_target_pairs={{0,4},{4,0},{1,5},{5,1},{2,6},{6,2},{3,7},{7,3}} | collective-permute-start | bytes 4718600 | tf_op jit(solution)/shard_map/ppermute | solution.py:428
  4.0 71.1 %collective-permute-start.25 = (bf16[512,1536]{1,0:T(8,128)(2,1)}, bf16[512,1536]{1,0:T(8,128)(2,1)}, u32[]{:S(2)}, u32[]{:S(2)}) collective-permute-start(bf16[512,1536]{1,0:T(8,128)(2,1)} %xa_ref.1), channel_id=1, source_target_pairs={{0,2},{1,3},{2,0},{3,1},{4,6},{5,7},{6,4},{7,5}} | collective-permute-start | bytes 4718600 | tf_op jit(solution)/shard_map/ppermute | solution.py:431
  6.9 33.2 %collective-permute-start.8 = (f32[1,12,512]{2,1,0:T(8,128)S(1)}, f32[1,12,512]{2,1,0:T(8,128)S(1)}, u32[]{:S(2)}, u32[]{:S(2)}) collective-permute-start(f32[1,12,512]{2,1,0:T(8,128)S(1)} %maximum_bitcast_fusion), channel_id=1, source_target_pairs={{0,4},{4,0},{1,5},{5,1},{2,6},{6,2},{3,7},{7,3}} | collective-permute-start | bytes 73736 | tf_op jit(solution)/shard_map/ppermute | solution.py:428
  7.5 68.0 %collective-permute-start.16 = (bf16[512,1536]{1,0:T(8,128)(2,1)}, bf16[512,1536]{1,0:T(8,128)(2,1)}, u32[]{:S(2)}, u32[]{:S(2)}) collective-permute-start(bf16[512,1536]{1,0:T(8,128)(2,1)} %dya_ref.1), channel_id=1, source_target_pairs={{0,4},{4,0},{1,5},{5,1},{2,6},{6,2},{3,7},{7,3}} | collective-permute-start | bytes 4718600 | tf_op jit(solution)/shard_map/ppermute | solution.py:428
  40.2 1.3 collective-permute-start.9
  41.4 5.8 %collective-permute-start.10 = (f32[4,12,512]{2,1,0:T(8,128)S(1)}, f32[4,12,512]{2,1,0:T(8,128)S(1)}, u32[]{:S(2)}, u32[]{:S(2)}) collective-permute-start(f32[4,12,512]{2,1,0:T(8,128)S(1)} %pad_maximum_fusion), channel_id=1, source_target_pairs={{0,2},{1,3},{2,0},{3,1},{4,6},{5,7},{6,4},{7,5}} | collective-permute-start | bytes 294920 | tf_op jit(solution)/shard_map/ppermute | solution.py:431
  43.5 35.2 %collective-permute-start.11 = (bf16[512,1536]{1,0:T(8,128)(2,1)}, bf16[512,1536]{1,0:T(8,128)(2,1)}, u32[]{:S(2)}, u32[]{:S(2)}) collective-permute-start(bf16[512,1536]{1,0:T(8,128)(2,1)} %xa_ref.1), channel_id=1, source_target_pairs={{0,1},{1,0},{2,3},{3,2},{4,5},{5,4},{6,7},{7,6}} | collective-permute-start | bytes 4718600 | tf_op jit(solution)/shard_map/ppermute | solution.py:431
  48.9 24.5 %copy-start.3 = (bf16[512,1536]{1,0:T(8,128)(2,1)S(1)}, bf16[512,1536]{1,0:T(8,128)(2,1)}, u32[]{:S(2)}) copy-start(bf16[512,1536]{1,0:T(8,128)(2,1)} %dya_ref.1) | copy-start | bytes 4718596
  60.7 12.6 %collective-permute-start.23 = (f32[2,4,448]{2,1,0:T(4,128)S(1)}, f32[2,4,448]{2,1,0:T(4,128)S(1)}, u32[]{:S(2)}, u32[]{:S(2)}) collective-permute-start(f32[2,4,448]{2,1,0:T(4,128)S(1)} %pad_maximum_fusion.2), channel_id=1, source_target_pairs={{0,4},{4,0},{1,5},{5,1},{2,6},{6,2},{3,7},{7,3}} | collective-permute-start | bytes 43016 | tf_op jit(solution)/shard_map/ppermute | solution.py:428
  73.4 37.4 %collective-permute-start.27 = (bf16[512,1536]{1,0:T(8,128)(2,1)S(1)}, bf16[512,1536]{1,0:T(8,128)(2,1)}, u32[]{:S(2)}, u32[]{:S(2)}) collective-permute-start(bf16[512,1536]{1,0:T(8,128)(2,1)S(1)} %copy-done.3), channel_id=1, source_target_pairs={{0,2},{1,3},{2,0},{3,1},{4,6},{5,7},{6,4},{7,5}} | collective-permute-start | bytes 4718600 | tf_op jit(solution)/shard_map/ppermute | solution.py:431
  75.1 35.7 %collective-permute-start.20 = (bf16[512,1536]{1,0:T(8,128)(2,1)}, bf16[512,1536]{1,0:T(8,128)(2,1)}, u32[]{:S(2)}, u32[]{:S(2)}) collective-permute-start(bf16[512,1536]{1,0:T(8,128)(2,1)} %collective-permute-done.13.xa_ref), channel_id=1, source_target_pairs={{0,1},{1,0},{2,3},{3,2},{4,5},{5,4},{6,7},{7,6}} | collective-permute-start | bytes 4718600 | tf_op jit(solution)/shard_map/ppermute | solution.py:431
  75.1 69.4 %collective-permute-start.14 = (bf16[512,1536]{1,0:T(8,128)(2,1)}, bf16[512,1536]{1,0:T(8,128)(2,1)}, u32[]{:S(2)}, u32[]{:S(2)}) collective-permute-start(bf16[512,1536]{1,0:T(8,128)(2,1)} %collective-permute-done.13.xa_ref), channel_id=1, source_target_pairs={{0,2},{1,3},{2,0},{3,1},{4,6},{5,7},{6,4},{7,5}} | collective-permute-start | bytes 4718600 | tf_op jit(solution)/shard_map/ppermute | solution.py:431
  75.4 101.1 %collective-permute-start.17 = (bf16[512,1536]{1,0:T(8,128)(2,1)}, bf16[512,1536]{1,0:T(8,128)(2,1)}, u32[]{:S(2)}, u32[]{:S(2)}) collective-permute-start(bf16[512,1536]{1,0:T(8,128)(2,1)} %collective-permute-done.16.dya_ref), channel_id=1, source_target_pairs={{0,2},{1,3},{2,0},{3,1},{4,6},{5,7},{6,4},{7,5}} | collective-permute-start | bytes 4718600 | tf_op jit(solution)/shard_map/ppermute | solution.py:431
  78.6 128.9 %collective-permute-start.19 = (bf16[512,1536]{1,0:T(8,128)(2,1)}, bf16[512,1536]{1,0:T(8,128)(2,1)}, u32[]{:S(2)}, u32[]{:S(2)}) collective-permute-start(bf16[512,1536]{1,0:T(8,128)(2,1)} %collective-permute-done.16.dya_ref), channel_id=1, source_target_pairs={{0,1},{1,0},{2,3},{3,2},{4,5},{5,4},{6,7},{7,6}} | collective-permute-start | bytes 4718600 | tf_op jit(solution)/shard_map/ppermute | solution.py:431
  110.7 259.8 %collective-permute-start.26 = (bf16[512,1536]{1,0:T(8,128)(2,1)}, bf16[512,1536]{1,0:T(8,128)(2,1)}, u32[]{:S(2)}, u32[]{:S(2)}) collective-permute-start(bf16[512,1536]{1,0:T(8,128)(2,1)} %collective-permute-done.25.xa_ref), channel_id=1, source_target_pairs={{0,1},{1,0},{2,3},{3,2},{4,5},{5,4},{6,7},{7,6}} | collective-permute-start | bytes 4718600 | tf_op jit(solution)/shard_map/ppermute | solution.py:431
  110.7 260.3 %collective-permute-start.28 = (bf16[512,1536]{1,0:T(8,128)(2,1)}, bf16[512,1536]{1,0:T(8,128)(2,1)}, u32[]{:S(2)}, u32[]{:S(2)}) collective-permute-start(bf16[512,1536]{1,0:T(8,128)(2,1)} %collective-permute-done.27.dya_ref), channel_id=1, source_target_pairs={{0,1},{1,0},{2,3},{3,2},{4,5},{5,4},{6,7},{7,6}} | collective-permute-start | bytes 4718600 | tf_op jit(solution)/shard_map/ppermute | solution.py:431
  144.4 92.6 %collective-permute-start.15 = (bf16[512,1536]{1,0:T(8,128)(2,1)}, bf16[512,1536]{1,0:T(8,128)(2,1)}, u32[]{:S(2)}, u32[]{:S(2)}) collective-permute-start(bf16[512,1536]{1,0:T(8,128)(2,1)} %collective-permute-done.14.xa_ref), channel_id=1, source_target_pairs={{0,1},{1,0},{2,3},{3,2},{4,5},{5,4},{6,7},{7,6}} | collective-permute-start | bytes 4718600 | tf_op jit(solution)/shard_map/ppermute | solution.py:431
  176.5 62.0 %collective-permute-start.18 = (bf16[512,1536]{1,0:T(8,128)(2,1)}, bf16[512,1536]{1,0:T(8,128)(2,1)}, u32[]{:S(2)}, u32[]{:S(2)}) collective-permute-start(bf16[512,1536]{1,0:T(8,128)(2,1)} %collective-permute-done.17.dya_ref), channel_id=1, source_target_pairs={{0,1},{1,0},{2,3},{3,2},{4,5},{5,4},{6,7},{7,6}} | collective-permute-start | bytes 4718600 | tf_op jit(solution)/shard_map/ppermute | solution.py:431
  207.6 76.0 %collective-permute-start.12 = (bf16[512,1536]{1,0:T(8,128)(2,1)S(1)}, bf16[512,1536]{1,0:T(8,128)(2,1)}, u32[]{:S(2)}, u32[]{:S(2)}) collective-permute-start(bf16[512,1536]{1,0:T(8,128)(2,1)S(1)} %copy-done.3), channel_id=1, source_target_pairs={{0,1},{1,0},{2,3},{3,2},{4,5},{5,4},{6,7},{7,6}} | collective-permute-start | bytes 4718600 | tf_op jit(solution)/shard_map/ppermute | solution.py:431
  237.0 85.6 %collective-permute-start.21 = (bf16[448,1536]{1,0:T(8,128)(2,1)}, bf16[448,1536]{1,0:T(8,128)(2,1)}, u32[]{:S(2)}, u32[]{:S(2)}) collective-permute-start(bf16[448,1536]{1,0:T(8,128)(2,1)} %get-tuple-element.210), channel_id=1, source_target_pairs={{0,4},{4,0},{1,5},{5,1},{2,6},{6,2},{3,7},{7,3}} | collective-permute-start | bytes 4128776 | tf_op jit(solution)/shard_map/ppermute | solution.py:428
  238.6 84.1 %collective-permute-start.22 = (bf16[448,1536]{1,0:T(8,128)(2,1)}, bf16[448,1536]{1,0:T(8,128)(2,1)}, u32[]{:S(2)}, u32[]{:S(2)}) collective-permute-start(bf16[448,1536]{1,0:T(8,128)(2,1)} %get-tuple-element.211), channel_id=1, source_target_pairs={{0,4},{4,0},{1,5},{5,1},{2,6},{6,2},{3,7},{7,3}} | collective-permute-start | bytes 4128776 | tf_op jit(solution)/shard_map/ppermute | solution.py:428
  283.6 49.5 %collective-permute-start.33 = (bf16[448,1536]{1,0:T(8,128)(2,1)}, bf16[448,1536]{1,0:T(8,128)(2,1)}, u32[]{:S(2)}, u32[]{:S(2)}) collective-permute-start(bf16[448,1536]{1,0:T(8,128)(2,1)} %get-tuple-element.226), channel_id=1, source_target_pairs={{0,4},{4,0},{1,5},{5,1},{2,6},{6,2},{3,7},{7,3}} | collective-permute-start | bytes 4128776 | tf_op jit(solution)/shard_map/ppermute | solution.py:428
  322.7 7.7 %copy-start.2 = (s32[512,6]{0,1:T(8,128)S(1)}, s32[512,6]{0,1:T(8,128)}, u32[]{:S(2)}) copy-start(s32[512,6]{0,1:T(8,128)} %param.18) | copy-start | bytes 36868
  329.8 33.4 %collective-permute-start.34 = (bf16[448,1536]{1,0:T(8,128)(2,1)}, bf16[448,1536]{1,0:T(8,128)(2,1)}, u32[]{:S(2)}, u32[]{:S(2)}) collective-permute-start(bf16[448,1536]{1,0:T(8,128)(2,1)} %get-tuple-element.227), channel_id=1, source_target_pairs={{0,4},{4,0},{1,5},{5,1},{2,6},{6,2},{3,7},{7,3}} | collective-permute-start | bytes 4128776 | tf_op jit(solution)/shard_map/ppermute | solution.py:428
  331.6 77.3 %collective-permute-start.29 = (bf16[448,1536]{1,0:T(8,128)(2,1)}, bf16[448,1536]{1,0:T(8,128)(2,1)}, u32[]{:S(2)}, u32[]{:S(2)}) collective-permute-start(bf16[448,1536]{1,0:T(8,128)(2,1)} %get-tuple-element.219), channel_id=1, source_target_pairs={{0,4},{4,0},{1,5},{5,1},{2,6},{6,2},{3,7},{7,3}} | collective-permute-start | bytes 4128776 | tf_op jit(solution)/shard_map/ppermute | solution.py:428
  368.5 53.6 %collective-permute-start.30 = (bf16[448,1536]{1,0:T(8,128)(2,1)}, bf16[448,1536]{1,0:T(8,128)(2,1)}, u32[]{:S(2)}, u32[]{:S(2)}) collective-permute-start(bf16[448,1536]{1,0:T(8,128)(2,1)} %get-tuple-element.220), channel_id=1, source_target_pairs={{0,4},{4,0},{1,5},{5,1},{2,6},{6,2},{3,7},{7,3}} | collective-permute-start | bytes 4128776 | tf_op jit(solution)/shard_map/ppermute | solution.py:428
  369.0 115.0 %collective-permute-start.36 = (bf16[448,1536]{1,0:T(8,128)(2,1)}, bf16[448,1536]{1,0:T(8,128)(2,1)}, u32[]{:S(2)}, u32[]{:S(2)}) collective-permute-start(bf16[448,1536]{1,0:T(8,128)(2,1)} %get-tuple-element.232), channel_id=1, source_target_pairs={{0,4},{4,0},{1,5},{5,1},{2,6},{6,2},{3,7},{7,3}} | collective-permute-start | bytes 4128776 | tf_op jit(solution)/shard_map/ppermute | solution.py:428
  370.5 108.8 %collective-permute-start.38 = (bf16[448,1536]{1,0:T(8,128)(2,1)}, bf16[448,1536]{1,0:T(8,128)(2,1)}, u32[]{:S(2)}, u32[]{:S(2)}) collective-permute-start(bf16[448,1536]{1,0:T(8,128)(2,1)} %get-tuple-element.234), channel_id=1, source_target_pairs={{0,4},{4,0},{1,5},{5,1},{2,6},{6,2},{3,7},{7,3}} | collective-permute-start | bytes 4128776 | tf_op jit(solution)/shard_map/ppermute | solution.py:428
  371.0 119.1 %collective-permute-start.35 = (bf16[256,1536]{1,0:T(8,128)(2,1)}, bf16[256,1536]{1,0:T(8,128)(2,1)}, u32[]{:S(2)}, u32[]{:S(2)}) collective-permute-start(bf16[256,1536]{1,0:T(8,128)(2,1)} %get-tuple-element.230), channel_id=1, source_target_pairs={{0,1},{1,0},{2,3},{3,2},{4,5},{5,4},{6,7},{7,6}} | collective-permute-start | bytes 2359304 | tf_op jit(solution)/shard_map/ppermute | solution.py:431
  429.2 112.4 %collective-permute-start.24 = (bf16[256,1536]{1,0:T(8,128)(2,1)}, bf16[256,1536]{1,0:T(8,128)(2,1)}, u32[]{:S(2)}, u32[]{:S(2)}) collective-permute-start(bf16[256,1536]{1,0:T(8,128)(2,1)} %get-tuple-element.214), channel_id=1, source_target_pairs={{0,1},{1,0},{2,3},{3,2},{4,5},{5,4},{6,7},{7,6}} | collective-permute-start | bytes 2359304 | tf_op jit(solution)/shard_map/ppermute | solution.py:431
  484.0 51.1 %collective-permute-start.39 = (bf16[256,1536]{1,0:T(8,128)(2,1)}, bf16[256,1536]{1,0:T(8,128)(2,1)S(1)}, u32[]{:S(2)}, u32[]{:S(2)}) collective-permute-start(bf16[256,1536]{1,0:T(8,128)(2,1)} %get-tuple-element.357), channel_id=1, source_target_pairs={{0,3},{1,2},{2,1},{3,0},{4,7},{5,6},{6,5},{7,4}} | collective-permute-start | bytes 2359304 | tf_op jit(solution)/shard_map/ppermute | solution.py:431
  488.0 47.1 %collective-permute-start.37 = (bf16[256,1536]{1,0:T(8,128)(2,1)S(1)}, bf16[256,1536]{1,0:T(8,128)(2,1)}, u32[]{:S(2)}, u32[]{:S(2)}) collective-permute-start(bf16[256,1536]{1,0:T(8,128)(2,1)S(1)} %get-tuple-element.356), channel_id=1, source_target_pairs={{0,2},{1,3},{2,0},{3,1},{4,6},{5,7},{6,4},{7,5}} | collective-permute-start | bytes 2359304 | tf_op jit(solution)/shard_map/ppermute | solution.py:431
  489.5 52.1 %collective-permute-start.31 = (bf16[256,1536]{1,0:T(8,128)(2,1)}, bf16[256,1536]{1,0:T(8,128)(2,1)S(1)}, u32[]{:S(2)}, u32[]{:S(2)}) collective-permute-start(bf16[256,1536]{1,0:T(8,128)(2,1)} %get-tuple-element.223), channel_id=1, source_target_pairs={{0,2},{1,3},{2,0},{3,1},{4,6},{5,7},{6,4},{7,5}} | collective-permute-start | bytes 2359304 | tf_op jit(solution)/shard_map/ppermute | solution.py:431
  490.1 64.5 %collective-permute-start.32 = (bf16[256,1536]{1,0:T(8,128)(2,1)}, bf16[256,1536]{1,0:T(8,128)(2,1)S(1)}, u32[]{:S(2)}, u32[]{:S(2)}) collective-permute-start(bf16[256,1536]{1,0:T(8,128)(2,1)} %get-tuple-element.224), channel_id=1, source_target_pairs={{0,3},{1,2},{2,1},{3,0},{4,7},{5,6},{6,5},{7,4}} | collective-permute-start | bytes 2359304 | tf_op jit(solution)/shard_map/ppermute | solution.py:431
  535.1 0.9 copy-start.4
  536.0 19.5 %copy-start.7 = (bf16[256,1536]{1,0:T(8,128)(2,1)S(1)}, bf16[256,1536]{1,0:T(8,128)(2,1)}, u32[]{:S(2)}) copy-start(bf16[256,1536]{1,0:T(8,128)(2,1)} %get-tuple-element.213.refs_0_) | copy-start | bytes 2359300
  541.6 13.0 %copy-start.5 = (bf16[256,1536]{1,0:T(8,128)(2,1)}, bf16[256,1536]{1,0:T(8,128)(2,1)S(1)}, u32[]{:S(2)}) copy-start(bf16[256,1536]{1,0:T(8,128)(2,1)S(1)} %collective-permute-done.31.refs_2_) | copy-start | bytes 2359300
  554.6 0.9 copy-start.6

commit v6 on v5

--- a/solution.py
+++ b/solution.py
@@ -11,7 +11,7 @@
 BF = jnp.bfloat16
 F32 = jnp.float32
 ALONE = 1024.0
-SENT_SHARE = 7, 8
+SENT_SHARE = 27, 32
 PAIR = 2
 
 KERNEL_ORDER = (('f', 0), ('b', 0), ('m', 1), ('n', 2), ('n', 3))
@@ -64,15 +64,22 @@
     return act, h3 * (sig * (1.0 + h1 * (1.0 - sig))), silu
 
 
+def mixers(hit, weight):
+    if weight is None:
+        return [jnp.where(hit, 1.0, 0.0).astype(BF)]
+    terms = []
+    for _ in range(3):
+        part = weight.astype(BF)
+        terms.append(jnp.where(hit, part.astype(F32), 0.0).astype(BF))
+        weight = weight - part.astype(F32)
+    return terms
+
+
 def weighted_rows(hit, weight, rows):
-    if weight is None:
-        return dot(jnp.where(hit, 1.0, 0.0).astype(BF), rows)
-    rest, total = weight, None
-    for _ in range(3):
-        part = rest.astype(BF)
-        term = dot(jnp.where(hit, part.astype(F32), 0.0).astype(BF), rows)
-        total = term if total is None else total + term
-        rest = rest - part.astype(F32)
+    total = None
+    for term in mixers(hit, weight):
+        product = dot(term, rows)
+        total = product if total is None else total + product
     return total
 
 
@@ -137,10 +144,20 @@
 
 def merge_kernel(weighted, count, *refs):
     near, sent, places, weights, outs = (refs[k * count:(k + 1) * count] for k in range(5))
-    for n_ref, r_ref, place_ref, weight_ref, p_ref in zip(near, sent, places, weights, outs):
-        slots = lax.broadcasted_iota(jnp.int32, (n_ref.shape[0], r_ref.shape[0]), 0)
-        total = weighted_rows(place_ref[0] == slots, weight_ref[0] if weighted else None, r_ref[...])
-        p_ref[...] = (n_ref[...] + total).astype(BF)
+    mix_ref = refs[5 * count]
+
+    @pl.when(pl.program_id(0) == 0)
+    def _():
+        for s, (place_ref, weight_ref) in enumerate(zip(places, weights)):
+            hit = place_ref[0] == lax.broadcasted_iota(jnp.int32, mix_ref.shape[2:], 0)
+            for k, term in enumerate(mixers(hit, weight_ref[0] if weighted else None)):
+                mix_ref[s, k] = term
+
+    for s, (n_ref, r_ref, p_ref) in enumerate(zip(near, sent, outs)):
+        total = n_ref[...]
+        for k in range(mix_ref.shape[1]):
+            total = total + dot(mix_ref[s, k], r_ref[...])
+        p_ref[...] = total.astype(BF)
 
 
 def both_ways(cap, pad, e, w1_ref, w3_ref, w2_ref, xg_ref, a_ref, d_ref, dh1_ref, dh3_ref, xg_scr, d_scr, o_scr, r_scr):
@@ -287,6 +304,7 @@
         in_specs=[pl.BlockSpec((grp_cap, block), lambda n: (0, n))] * count + [pl.BlockSpec((units, block), lambda n: (0, n))] * count + notes * 2,
         out_specs=[pl.BlockSpec((grp_cap, block), lambda n: (0, n))] * count,
         out_shape=[jax.ShapeDtypeStruct((grp_cap, hidden), BF)] * count,
+        scratch_shapes=[pltpu.VMEM((count, 3 if weighted else 1, grp_cap, units), BF)],
         compiler_params=params(),
         cost_estimate=pl.CostEstimate(flops=count * 10**9, bytes_accessed=count * 4 * 10**6, transcendentals=0),
         name="merge_sources",
@@ -524,9 +542,10 @@
                 sums += lax.cond(over, by_sums, by_rows, tuple([rows[k] for k in sources] for rows in (near, arrived, full)))
             return [sums[0]] + [hop_g(sums[k], k) for k in (1, 2, 3)]
 
-        y_parts = combine(y_sums, y_sent, True, ((0, 1), (2, 3)))
+        y_parts = combine(y_sums, y_sent, True, ((0, 1), (2,), (3,)))
         y_out = collect(y_parts, q_cols)
-        dx_out = collect(combine(dx_sums, dx_sent, False, ((0, 1), (2,), (3,))), q_cols)
+        dx_parts = combine(dx_sums, dx_sent, False, ((0, 1), (2, 3)))
+        dx_out = collect(dx_parts, q_cols)
         return y_out, dx_out, grads[0], grads[1], grads[2]
 
     return jax.shard_map(device_fn, mesh=mesh, in_specs=(tok_spec, tok_spec, tok_spec, tok_spec, weight_spec, weight_spec, weight_spec), out_specs=(tok_spec, tok_spec, grad_spec, grad_spec, grad_spec), check_vma=False)

time: 569 us -> 565 us (level)
  no operation moved by 1% of the time
where the time goes in v6:
time: 565 us; the launch traced here: 557 us
  Pallas kernels  257 us (45%)
  waiting for transfers between devices  239 us (42%)
  starting transfers between devices  27.5 us (5%)
  other arithmetic  15 us (3%)
  local copies, waits for them, and re-layouts  14.9 us (3%)
    ppermute x12, waiting for transfers between devices, hop_y(): return lax.ppermute(a, 'ing', [(0, 1), (1, 0)])  137 us
    ppermute x20, waiting for transfers between devices, hop_g(): return lax.ppermute(a, 'grp', [(g, g ^ bits) for g in range(groups)])  102 us
    pallas_call x2, Pallas kernels, near_pair(): pl.pallas_call(functools.partial(near_kernel, cap, pad), grid=(experts,),...  75.3 us
    pallas_call x1, Pallas kernels, far_both_pair(): pl.pallas_call(functools.partial(far_both_kernel, cap, pad), grid=(expert...  44.1 us
    pallas_call x1, Pallas kernels, weight_grads(): pl.pallas_call(functools.partial(dw_kernel, chunks), grid=(experts,), in_...  43.9 us
    pallas_call x1, Pallas kernels, far_forward_pair(): pl.pallas_call(functools.partial(far_fwd_kernel, cap, pad), grid=(experts...  30.7 us
    pallas_call x1, Pallas kernels, far_backward_pair(): pl.pallas_call(functools.partial(far_bwd_kernel, cap, pad), grid=(experts...  28.9 us
    pallas_call x5, Pallas kernels, merge_sources(): pl.pallas_call(functools.partial(merge_kernel, weighted, count), grid=(3,...  23.1 us
  transfers between devices with their start and end apart: 32, of which 11 were waited for; matrix products, arithmetic and copies ran while one was open for 5% of the time, Pallas kernels for 45%

profile of v6, /device:TPU:0, one launch (start us, length us, event | category | flops | bytes accessed | tf_op | source)
XLA Modules:
  0.0 557.3 jit_solution(11208013005836887918)
XLA Ops:
  0.6 3.4 collective-permute-start.13
  4.0 1.5 collective-permute-start.25
  7.5 1.5 collective-permute-start.16
  9.0 31.2 %collective-permute-done.8 = f32[1,12,512]{2,1,0:T(8,128)S(1)} collective-permute-done((f32[1,12,512]{2,1,0:T(8,128)S(1)}, f32[1,12,512]{2,1,0:T(8,128)S(1)}, u32[]{:S(2)}, u32[]{:S(2)}) %collective-permute-start.8) | collective-permute-done | bytes 24608 | tf_op jit(solution)/shard_map/ppermute | solution.py:446
  40.2 1.2 collective-permute-done.9
  41.4 2.0 collective-permute-start.10
  43.5 3.8 collective-permute-done.10
  49.6 9.7 %select_reduce_fusion = (f32[8,8,72]{2,1,0:T(8,128)S(1)}, f32[8,8,72]{2,1,0:T(8,128)S(1)}, f32[8,8,72]{2,1,0:T(8,128)S(1)}, f32[8,8,72]{2,1,0:T(8,128)S(1)}) fusion(f32[8,8,512]{2,1,0:T(8,128)S(1)} %copy.58, f32[8,8,512]{2,1,0:T(8,128)S(1)} %slice.100, pred[8,8,512]{2,1,0:T(8,128)(4,1)S(1)} %compare_reduce_fusion, f32[8,512]{1,0:T(8,128)S(1)} %bitcast.41, ...), kind=kLoop, calls=%fused_computation.8 | loop fusion | flops 23574528 | bytes 518144 | tf_op jit(solution)/shard_map/reduce_sum | solution.py:417
  59.6 1.1 select_reduce_fusion.5
  60.7 1.8 collective-permute-start.23
  62.5 10.9 %collective-permute-done.23 = f32[2,4,432]{2,1,0:T(4,128)S(1)} collective-permute-done((f32[2,4,432]{2,1,0:T(4,128)S(1)}, f32[2,4,432]{2,1,0:T(4,128)S(1)}, u32[]{:S(2)}, u32[]{:S(2)}) %collective-permute-start.23) | collective-permute-done | bytes 13856 | tf_op jit(solution)/shard_map/ppermute | solution.py:446
  73.4 1.7 collective-permute-start.27
  75.4 1.7 collective-permute-start.17
  78.7 2.1 reshape.248.gcol_ref
  84.2 2.1 convert_element_type.181.tok_ref
  86.3 24.4 %collective-permute-done.27.dya_ref = bf16[512,1536]{1,0:T(8,128)(2,1)} collective-permute-done((bf16[512,1536]{1,0:T(8,128)(2,1)S(1)}, bf16[512,1536]{1,0:T(8,128)(2,1)}, u32[]{:S(2)}, u32[]{:S(2)}) %collective-permute-start.27) | collective-permute-done | bytes 1572896 | tf_op jit(solution)/shard_map/ppermute | solution.py:449
  111.2 33.2 %collective-permute-done.14.xa_ref = bf16[512,1536]{1,0:T(8,128)(2,1)} collective-permute-done((bf16[512,1536]{1,0:T(8,128)(2,1)}, bf16[512,1536]{1,0:T(8,128)(2,1)}, u32[]{:S(2)}, u32[]{:S(2)}) %collective-permute-start.14) | collective-permute-done | bytes 1572896 | tf_op jit(solution)/shard_map/ppermute | solution.py:449
  144.4 32.1 %collective-permute-done.17.dya_ref = bf16[512,1536]{1,0:T(8,128)(2,1)} collective-permute-done((bf16[512,1536]{1,0:T(8,128)(2,1)}, bf16[512,1536]{1,0:T(8,128)(2,1)}, u32[]{:S(2)}, u32[]{:S(2)}) %collective-permute-start.17) | collective-permute-done | bytes 1572896 | tf_op jit(solution)/shard_map/ppermute | solution.py:449
  176.5 30.7 %far_fwd_pair.1 = (bf16[8,144,1536]{2,1,0:T(8,128)(2,1)}, bf16[8,144,512]{2,1,0:T(8,128)(2,1)}, f32[8,144,512]{2,1,0:T(8,128)}, f32[8,144,512]{2,1,0:T(8,128)}, ...) custom-call(bf16[512,1536]{1,0:T(8,128)(2,1)} %collective-permute-done.13.xa_r, ...), custom_call_target="tpu_custom_call" | custom-call | flops 14000000000 | bytes 50000000 | tf_op jit(solution)/shard_map/far_fwd_pair/pallas_call | solution.py:245
  207.8 28.9 %far_bwd_pair.1 = (bf16[8,144,1536]{2,1,0:T(8,128)(2,1)}, bf16[8,144,512]{2,1,0:T(8,128)(2,1)}, bf16[8,144,512]{2,1,0:T(8,128)(2,1)}, f32[256,1536]{1,0:T(8,128)...) custom-call(bf16[512,1536]{1,0:T(8,128)(2,1)} %collective-permute-done.16.dya_ref, ...), custom_call_target="tpu_custom_call" | custom-call | flops 14000000000 | bytes 50000000 | tf_op jit(solution)/shard_map/far_bwd_pair/pallas_call | solution.py:264
  236.7 1.5 collective-permute-start.21
  238.7 44.1 %far_both_pair.1 = (bf16[8,144,1536]{2,1,0:T(8,128)(2,1)}, bf16[8,144,512]{2,1,0:T(8,128)(2,1)}, bf16[8,144,1536]{2,1,0:T(8,128)(2,1)}, bf16[8,144,512]{2,1,0:T(...) custom-call(bf16[512,1536]{1,0:T(8,128)(2,1)} %collective-permute-do, ...), custom_call_target="tpu_custom_call" | custom-call | flops 28000000000 | bytes 70000000 | tf_op jit(solution)/shard_map/far_both_pair/pallas_call | solution.py:283
  282.9 1.5 collective-permute-start.33
  284.4 37.5 %near_pair.2 = (bf16[8,144,1536]{2,1,0:T(8,128)(2,1)}, bf16[8,144,512]{2,1,0:T(8,128)(2,1)}, bf16[8,144,1536]{2,1,0:T(8,128)(2,1)}, bf16[8,144,512]{2,1,0:T(8,12...) custom-call(bf16[512,1536]{1,0:T(8,128)(2,1)} %xa_ref.1, ...), custom_call_target="tpu_custom_call" | custom-call | flops 28000000000 | bytes 70000000 | tf_op jit(solution)/shard_map/near_pair/pallas_call | solution.py:320
  322.0 7.5 %conditional.5 = ((bf16[256,1536]{1,0:T(8,128)(2,1)}, bf16[256,1536]{1,0:T(8,128)(2,1)})) conditional(s32[]{:T(128)} %convert_element_type.161, (f32[256,1536]{1,0:T(8,128)}, f32[256,1536]{1,0:T(8,128)}, bf16[432,1536]{1,0:T(8,128)(2,1)}, bf16[432,1536]{1,0:T(8,128)(2,1)}, s32[4,1,432]{2,0,1:T(4,128)S(1)}, ...), branch_computations={%region_15.16_spmd, %region_16.17_spmd} | conditional | flops 2000000000 | bytes 26738820 | solution.py:542
  323.2 6.3 %merge_sources.5 = (bf16[256,1536]{1,0:T(8,128)(2,1)}, bf16[256,1536]{1,0:T(8,128)(2,1)}) custom-call(f32[256,1536]{1,0:T(8,128)} %get-tuple-element.86.refs_0_, f32[256,1536]{1,0:T(8,128)} %get-tuple-element.87.refs_1_, bf16[432,1536]{1,0:T(8,128)(2,1)} %get-tuple-element.92.refs_2_, bf16[432,1536]{1,0:T(8,128)(2,1)} %get-tuple-element.93.refs_3_, ...), custom_call_target="tpu_custom_call" | custom-call | flops 2000000000 | bytes 8000000 | tf_op jit(solution)/shard_map/cond/branch_0_fun/merge_sources/pallas_call | solution.py:301
  330.3 1.0 fusion.1.refs_4_
  331.3 1.5 collective-permute-start.29
  332.8 28.9 %collective-permute-done.34 = bf16[432,1536]{1,0:T(8,128)(2,1)} collective-permute-done((bf16[432,1536]{1,0:T(8,128)(2,1)}, bf16[432,1536]{1,0:T(8,128)(2,1)}, u32[]{:S(2)}, u32[]{:S(2)}) %collective-permute-start.34) | collective-permute-done | bytes 1327136 | tf_op jit(solution)/shard_map/ppermute | solution.py:446
  361.8 5.4 conditional.8
  363.0 4.2 merge_sources.8
  367.7 1.5 collective-permute-start.36
  369.7 37.7 %near_pair.3 = (bf16[8,144,1536]{2,1,0:T(8,128)(2,1)}, bf16[8,144,512]{2,1,0:T(8,128)(2,1)}, bf16[8,144,1536]{2,1,0:T(8,128)(2,1)}, bf16[8,144,512]{2,1,0:T(8,12...) custom-call(bf16[512,1536]{1,0:T(8,128)(2,1)} %collective-permute-do, ...), custom_call_target="tpu_custom_call" | custom-call | flops 28000000000 | bytes 70000000 | tf_op jit(solution)/shard_map/near_pair/pallas_call | solution.py:320
  407.5 39.6 %collective-permute-done.36 = bf16[432,1536]{1,0:T(8,128)(2,1)} collective-permute-done((bf16[432,1536]{1,0:T(8,128)(2,1)}, bf16[432,1536]{1,0:T(8,128)(2,1)}, u32[]{:S(2)}, u32[]{:S(2)}) %collective-permute-start.36) | collective-permute-done | bytes 1327136 | tf_op jit(solution)/shard_map/ppermute | solution.py:446
  447.1 26.6 %collective-permute-done.37 = bf16[432,1536]{1,0:T(8,128)(2,1)} collective-permute-done((bf16[432,1536]{1,0:T(8,128)(2,1)}, bf16[432,1536]{1,0:T(8,128)(2,1)}, u32[]{:S(2)}, u32[]{:S(2)}) %collective-permute-start.37) | collective-permute-done | bytes 1327136 | tf_op jit(solution)/shard_map/ppermute | solution.py:446
  473.7 6.2 %conditional.9 = ((bf16[256,1536]{1,0:T(8,128)(2,1)}, bf16[256,1536]{1,0:T(8,128)(2,1)})) conditional(s32[]{:T(128)} %convert_element_type.161, (f32[256,1536]{1,0:T(8,128)}, f32[256,1536]{1,0:T(8,128)}, bf16[432,1536]{1,0:T(8,128)(2,1)}, bf16[432,1536]{1,0:T(8,128)(2,1)}, s32[4,1,432]{2,0,1:T(4,128)S(1)}, ...), branch_computations={%region_24.25_spmd, %region_25.26_spmd} | conditional | flops 2000000000 | bytes 26738820 | solution.py:542
  474.9 5.0 merge_sources.9
  480.0 1.5 collective-permute-start.38
  481.5 5.4 conditional.6
  482.7 4.2 merge_sources.6
  487.2 4.7 conditional.7
  488.5 3.5 merge_sources.7
  491.9 1.4 collective-permute-start.32
  493.9 43.9 %weight_grads.1 = (f32[8,1536,512]{2,1,0:T(8,128)}, f32[8,1536,512]{2,1,0:T(8,128)}, f32[8,512,1536]{2,1,0:T(8,128)}) custom-call(bf16[8,144,1536]{2,1,0:T(8,128)(2,1)} %get-tuple-element.236.refs_0_, bf16[8,144,1536]{2,1,0:T(8,128)(2,1)} %get-tuple-element.237.refs_1_, bf16[8,144,1536]{2,1,0:T(8,128)(2,1)} %get-tuple-element.238.refs_2_, ...), custom_call_target="tpu_custom_call" | custom-call | flops 24999999488 | bytes 120000000 | tf_op jit(solution)/shard_map/weight_grads/pallas_call | solution.py:351
  537.8 5.5 collect.3
  543.4 7.3 %collective-permute-done.30.refs_2_ = bf16[256,1536]{1,0:T(8,128)(2,1)S(1)} collective-permute-done((bf16[256,1536]{1,0:T(8,128)(2,1)S(1)}, bf16[256,1536]{1,0:T(8,128)(2,1)S(1)}, u32[]{:S(2)}, u32[]{:S(2)}) %collective-permute-start.30) | collective-permute-done | bytes 786464 | tf_op jit(solution)/shard_map/ppermute | solution.py:449
  550.7 0.9 copy-done.6
  551.6 5.5 collect.2
  (130 shorter events, 19.6 us)
Async XLA Ops:
  0.6 74.4 %collective-permute-start.13 = (bf16[512,1536]{1,0:T(8,128)(2,1)}, bf16[512,1536]{1,0:T(8,128)(2,1)}, u32[]{:S(2)}, u32[]{:S(2)}) collective-permute-start(bf16[512,1536]{1,0:T(8,128)(2,1)} %xa_ref.1), channel_id=1, source_target_pairs={{0,4},{4,0},{1,5},{5,1},{2,6},{6,2},{3,7},{7,3}} | collective-permute-start | bytes 4718600 | tf_op jit(solution)/shard_map/ppermute | solution.py:446
  4.0 71.1 %collective-permute-start.25 = (bf16[512,1536]{1,0:T(8,128)(2,1)}, bf16[512,1536]{1,0:T(8,128)(2,1)}, u32[]{:S(2)}, u32[]{:S(2)}) collective-permute-start(bf16[512,1536]{1,0:T(8,128)(2,1)} %xa_ref.1), channel_id=1, source_target_pairs={{0,2},{1,3},{2,0},{3,1},{4,6},{5,7},{6,4},{7,5}} | collective-permute-start | bytes 4718600 | tf_op jit(solution)/shard_map/ppermute | solution.py:449
  6.9 33.2 %collective-permute-start.8 = (f32[1,12,512]{2,1,0:T(8,128)S(1)}, f32[1,12,512]{2,1,0:T(8,128)S(1)}, u32[]{:S(2)}, u32[]{:S(2)}) collective-permute-start(f32[1,12,512]{2,1,0:T(8,128)S(1)} %maximum_bitcast_fusion), channel_id=1, source_target_pairs={{0,4},{4,0},{1,5},{5,1},{2,6},{6,2},{3,7},{7,3}} | collective-permute-start | bytes 73736 | tf_op jit(solution)/shard_map/ppermute | solution.py:446
  7.5 68.0 %collective-permute-start.16 = (bf16[512,1536]{1,0:T(8,128)(2,1)}, bf16[512,1536]{1,0:T(8,128)(2,1)}, u32[]{:S(2)}, u32[]{:S(2)}) collective-permute-start(bf16[512,1536]{1,0:T(8,128)(2,1)} %dya_ref.1), channel_id=1, source_target_pairs={{0,4},{4,0},{1,5},{5,1},{2,6},{6,2},{3,7},{7,3}} | collective-permute-start | bytes 4718600 | tf_op jit(solution)/shard_map/ppermute | solution.py:446
  40.2 1.3 collective-permute-start.9
  41.4 5.8 %collective-permute-start.10 = (f32[4,12,512]{2,1,0:T(8,128)S(1)}, f32[4,12,512]{2,1,0:T(8,128)S(1)}, u32[]{:S(2)}, u32[]{:S(2)}) collective-permute-start(f32[4,12,512]{2,1,0:T(8,128)S(1)} %pad_maximum_fusion), channel_id=1, source_target_pairs={{0,2},{1,3},{2,0},{3,1},{4,6},{5,7},{6,4},{7,5}} | collective-permute-start | bytes 294920 | tf_op jit(solution)/shard_map/ppermute | solution.py:449
  43.5 35.2 %collective-permute-start.11 = (bf16[512,1536]{1,0:T(8,128)(2,1)}, bf16[512,1536]{1,0:T(8,128)(2,1)}, u32[]{:S(2)}, u32[]{:S(2)}) collective-permute-start(bf16[512,1536]{1,0:T(8,128)(2,1)} %xa_ref.1), channel_id=1, source_target_pairs={{0,1},{1,0},{2,3},{3,2},{4,5},{5,4},{6,7},{7,6}} | collective-permute-start | bytes 4718600 | tf_op jit(solution)/shard_map/ppermute | solution.py:449
  48.9 24.5 %copy-start.4 = (bf16[512,1536]{1,0:T(8,128)(2,1)S(1)}, bf16[512,1536]{1,0:T(8,128)(2,1)}, u32[]{:S(2)}) copy-start(bf16[512,1536]{1,0:T(8,128)(2,1)} %dya_ref.1) | copy-start | bytes 4718596
  60.7 12.7 %collective-permute-start.23 = (f32[2,4,432]{2,1,0:T(4,128)S(1)}, f32[2,4,432]{2,1,0:T(4,128)S(1)}, u32[]{:S(2)}, u32[]{:S(2)}) collective-permute-start(f32[2,4,432]{2,1,0:T(4,128)S(1)} %pad_maximum_fusion.2), channel_id=1, source_target_pairs={{0,4},{4,0},{1,5},{5,1},{2,6},{6,2},{3,7},{7,3}} | collective-permute-start | bytes 41480 | tf_op jit(solution)/shard_map/ppermute | solution.py:446
  73.4 37.4 %collective-permute-start.27 = (bf16[512,1536]{1,0:T(8,128)(2,1)S(1)}, bf16[512,1536]{1,0:T(8,128)(2,1)}, u32[]{:S(2)}, u32[]{:S(2)}) collective-permute-start(bf16[512,1536]{1,0:T(8,128)(2,1)S(1)} %copy-done.4), channel_id=1, source_target_pairs={{0,2},{1,3},{2,0},{3,1},{4,6},{5,7},{6,4},{7,5}} | collective-permute-start | bytes 4718600 | tf_op jit(solution)/shard_map/ppermute | solution.py:449
  75.1 35.7 %collective-permute-start.20 = (bf16[512,1536]{1,0:T(8,128)(2,1)}, bf16[512,1536]{1,0:T(8,128)(2,1)}, u32[]{:S(2)}, u32[]{:S(2)}) collective-permute-start(bf16[512,1536]{1,0:T(8,128)(2,1)} %collective-permute-done.13.xa_ref), channel_id=1, source_target_pairs={{0,1},{1,0},{2,3},{3,2},{4,5},{5,4},{6,7},{7,6}} | collective-permute-start | bytes 4718600 | tf_op jit(solution)/shard_map/ppermute | solution.py:449
  75.1 69.4 %collective-permute-start.14 = (bf16[512,1536]{1,0:T(8,128)(2,1)}, bf16[512,1536]{1,0:T(8,128)(2,1)}, u32[]{:S(2)}, u32[]{:S(2)}) collective-permute-start(bf16[512,1536]{1,0:T(8,128)(2,1)} %collective-permute-done.13.xa_ref), channel_id=1, source_target_pairs={{0,2},{1,3},{2,0},{3,1},{4,6},{5,7},{6,4},{7,5}} | collective-permute-start | bytes 4718600 | tf_op jit(solution)/shard_map/ppermute | solution.py:449
  75.4 101.1 %collective-permute-start.17 = (bf16[512,1536]{1,0:T(8,128)(2,1)}, bf16[512,1536]{1,0:T(8,128)(2,1)}, u32[]{:S(2)}, u32[]{:S(2)}) collective-permute-start(bf16[512,1536]{1,0:T(8,128)(2,1)} %collective-permute-done.16.dya_ref), channel_id=1, source_target_pairs={{0,2},{1,3},{2,0},{3,1},{4,6},{5,7},{6,4},{7,5}} | collective-permute-start | bytes 4718600 | tf_op jit(solution)/shard_map/ppermute | solution.py:449
  78.6 128.6 %collective-permute-start.19 = (bf16[512,1536]{1,0:T(8,128)(2,1)}, bf16[512,1536]{1,0:T(8,128)(2,1)}, u32[]{:S(2)}, u32[]{:S(2)}) collective-permute-start(bf16[512,1536]{1,0:T(8,128)(2,1)} %collective-permute-done.16.dya_ref), channel_id=1, source_target_pairs={{0,1},{1,0},{2,3},{3,2},{4,5},{5,4},{6,7},{7,6}} | collective-permute-start | bytes 4718600 | tf_op jit(solution)/shard_map/ppermute | solution.py:449
  110.7 258.4 %collective-permute-start.26 = (bf16[512,1536]{1,0:T(8,128)(2,1)}, bf16[512,1536]{1,0:T(8,128)(2,1)}, u32[]{:S(2)}, u32[]{:S(2)}) collective-permute-start(bf16[512,1536]{1,0:T(8,128)(2,1)} %collective-permute-done.25.xa_ref), channel_id=1, source_target_pairs={{0,1},{1,0},{2,3},{3,2},{4,5},{5,4},{6,7},{7,6}} | collective-permute-start | bytes 4718600 | tf_op jit(solution)/shard_map/ppermute | solution.py:449
  110.7 259.0 %collective-permute-start.28 = (bf16[512,1536]{1,0:T(8,128)(2,1)}, bf16[512,1536]{1,0:T(8,128)(2,1)}, u32[]{:S(2)}, u32[]{:S(2)}) collective-permute-start(bf16[512,1536]{1,0:T(8,128)(2,1)} %collective-permute-done.27.dya_ref), channel_id=1, source_target_pairs={{0,1},{1,0},{2,3},{3,2},{4,5},{5,4},{6,7},{7,6}} | collective-permute-start | bytes 4718600 | tf_op jit(solution)/shard_map/ppermute | solution.py:449
  144.4 92.2 %collective-permute-start.15 = (bf16[512,1536]{1,0:T(8,128)(2,1)}, bf16[512,1536]{1,0:T(8,128)(2,1)}, u32[]{:S(2)}, u32[]{:S(2)}) collective-permute-start(bf16[512,1536]{1,0:T(8,128)(2,1)} %collective-permute-done.14.xa_ref), channel_id=1, source_target_pairs={{0,1},{1,0},{2,3},{3,2},{4,5},{5,4},{6,7},{7,6}} | collective-permute-start | bytes 4718600 | tf_op jit(solution)/shard_map/ppermute | solution.py:449
  176.5 61.7 %collective-permute-start.18 = (bf16[512,1536]{1,0:T(8,128)(2,1)}, bf16[512,1536]{1,0:T(8,128)(2,1)}, u32[]{:S(2)}, u32[]{:S(2)}) collective-permute-start(bf16[512,1536]{1,0:T(8,128)(2,1)} %collective-permute-done.17.dya_ref), channel_id=1, source_target_pairs={{0,1},{1,0},{2,3},{3,2},{4,5},{5,4},{6,7},{7,6}} | collective-permute-start | bytes 4718600 | tf_op jit(solution)/shard_map/ppermute | solution.py:449
  207.3 75.6 %collective-permute-start.12 = (bf16[512,1536]{1,0:T(8,128)(2,1)S(1)}, bf16[512,1536]{1,0:T(8,128)(2,1)}, u32[]{:S(2)}, u32[]{:S(2)}) collective-permute-start(bf16[512,1536]{1,0:T(8,128)(2,1)S(1)} %copy-done.4), channel_id=1, source_target_pairs={{0,1},{1,0},{2,3},{3,2},{4,5},{5,4},{6,7},{7,6}} | collective-permute-start | bytes 4718600 | tf_op jit(solution)/shard_map/ppermute | solution.py:449
  236.7 85.2 %collective-permute-start.21 = (bf16[432,1536]{1,0:T(8,128)(2,1)}, bf16[432,1536]{1,0:T(8,128)(2,1)}, u32[]{:S(2)}, u32[]{:S(2)}) collective-permute-start(bf16[432,1536]{1,0:T(8,128)(2,1)} %get-tuple-element.210), channel_id=1, source_target_pairs={{0,4},{4,0},{1,5},{5,1},{2,6},{6,2},{3,7},{7,3}} | collective-permute-start | bytes 3981320 | tf_op jit(solution)/shard_map/ppermute | solution.py:446
  238.2 83.8 %collective-permute-start.22 = (bf16[432,1536]{1,0:T(8,128)(2,1)}, bf16[432,1536]{1,0:T(8,128)(2,1)}, u32[]{:S(2)}, u32[]{:S(2)}) collective-permute-start(bf16[432,1536]{1,0:T(8,128)(2,1)} %get-tuple-element.211), channel_id=1, source_target_pairs={{0,4},{4,0},{1,5},{5,1},{2,6},{6,2},{3,7},{7,3}} | collective-permute-start | bytes 3981320 | tf_op jit(solution)/shard_map/ppermute | solution.py:446
  282.9 49.9 %collective-permute-start.33 = (bf16[432,1536]{1,0:T(8,128)(2,1)}, bf16[432,1536]{1,0:T(8,128)(2,1)}, u32[]{:S(2)}, u32[]{:S(2)}) collective-permute-start(bf16[432,1536]{1,0:T(8,128)(2,1)} %get-tuple-element.224), channel_id=1, source_target_pairs={{0,4},{4,0},{1,5},{5,1},{2,6},{6,2},{3,7},{7,3}} | collective-permute-start | bytes 3981320 | tf_op jit(solution)/shard_map/ppermute | solution.py:446
  322.0 8.0 %copy-start.3 = (s32[512,6]{0,1:T(8,128)S(1)}, s32[512,6]{0,1:T(8,128)}, u32[]{:S(2)}) copy-start(s32[512,6]{0,1:T(8,128)} %param.18) | copy-start | bytes 36868
  329.4 32.3 %collective-permute-start.34 = (bf16[432,1536]{1,0:T(8,128)(2,1)}, bf16[432,1536]{1,0:T(8,128)(2,1)}, u32[]{:S(2)}, u32[]{:S(2)}) collective-permute-start(bf16[432,1536]{1,0:T(8,128)(2,1)} %get-tuple-element.225), channel_id=1, source_target_pairs={{0,4},{4,0},{1,5},{5,1},{2,6},{6,2},{3,7},{7,3}} | collective-permute-start | bytes 3981320 | tf_op jit(solution)/shard_map/ppermute | solution.py:446
  331.3 150.1 %collective-permute-start.29 = (bf16[432,1536]{1,0:T(8,128)(2,1)}, bf16[432,1536]{1,0:T(8,128)(2,1)}, u32[]{:S(2)}, u32[]{:S(2)}) collective-permute-start(bf16[432,1536]{1,0:T(8,128)(2,1)} %get-tuple-element.218), channel_id=1, source_target_pairs={{0,4},{4,0},{1,5},{5,1},{2,6},{6,2},{3,7},{7,3}} | collective-permute-start | bytes 3981320 | tf_op jit(solution)/shard_map/ppermute | solution.py:446
  367.1 120.1 %collective-permute-start.31 = (bf16[432,1536]{1,0:T(8,128)(2,1)}, bf16[432,1536]{1,0:T(8,128)(2,1)}, u32[]{:S(2)}, u32[]{:S(2)}) collective-permute-start(bf16[432,1536]{1,0:T(8,128)(2,1)} %get-tuple-element.221), channel_id=1, source_target_pairs={{0,4},{4,0},{1,5},{5,1},{2,6},{6,2},{3,7},{7,3}} | collective-permute-start | bytes 3981320 | tf_op jit(solution)/shard_map/ppermute | solution.py:446
  367.7 79.4 %collective-permute-start.36 = (bf16[432,1536]{1,0:T(8,128)(2,1)}, bf16[432,1536]{1,0:T(8,128)(2,1)}, u32[]{:S(2)}, u32[]{:S(2)}) collective-permute-start(bf16[432,1536]{1,0:T(8,128)(2,1)} %get-tuple-element.231), channel_id=1, source_target_pairs={{0,4},{4,0},{1,5},{5,1},{2,6},{6,2},{3,7},{7,3}} | collective-permute-start | bytes 3981320 | tf_op jit(solution)/shard_map/ppermute | solution.py:446
  369.2 104.5 %collective-permute-start.37 = (bf16[432,1536]{1,0:T(8,128)(2,1)}, bf16[432,1536]{1,0:T(8,128)(2,1)}, u32[]{:S(2)}, u32[]{:S(2)}) collective-permute-start(bf16[432,1536]{1,0:T(8,128)(2,1)} %get-tuple-element.232), channel_id=1, source_target_pairs={{0,4},{4,0},{1,5},{5,1},{2,6},{6,2},{3,7},{7,3}} | collective-permute-start | bytes 3981320 | tf_op jit(solution)/shard_map/ppermute | solution.py:446
  369.7 123.6 %collective-permute-start.35 = (bf16[256,1536]{1,0:T(8,128)(2,1)}, bf16[256,1536]{1,0:T(8,128)(2,1)}, u32[]{:S(2)}, u32[]{:S(2)}) collective-permute-start(bf16[256,1536]{1,0:T(8,128)(2,1)} %get-tuple-element.228), channel_id=1, source_target_pairs={{0,1},{1,0},{2,3},{3,2},{4,5},{5,4},{6,7},{7,6}} | collective-permute-start | bytes 2359304 | tf_op jit(solution)/shard_map/ppermute | solution.py:449
  480.0 63.4 %collective-permute-start.24 = (bf16[256,1536]{1,0:T(8,128)(2,1)}, bf16[256,1536]{1,0:T(8,128)(2,1)}, u32[]{:S(2)}, u32[]{:S(2)}) collective-permute-start(bf16[256,1536]{1,0:T(8,128)(2,1)} %get-tuple-element.214), channel_id=1, source_target_pairs={{0,1},{1,0},{2,3},{3,2},{4,5},{5,4},{6,7},{7,6}} | collective-permute-start | bytes 2359304 | tf_op jit(solution)/shard_map/ppermute | solution.py:449
  480.0 57.8 %collective-permute-start.38 = (bf16[256,1536]{1,0:T(8,128)(2,1)}, bf16[256,1536]{1,0:T(8,128)(2,1)}, u32[]{:S(2)}, u32[]{:S(2)}) collective-permute-start(bf16[256,1536]{1,0:T(8,128)(2,1)} %get-tuple-element.234), channel_id=1, source_target_pairs={{0,2},{1,3},{2,0},{3,1},{4,6},{5,7},{6,4},{7,5}} | collective-permute-start | bytes 2359304 | tf_op jit(solution)/shard_map/ppermute | solution.py:449
  486.9 50.9 %collective-permute-start.39 = (bf16[256,1536]{1,0:T(8,128)(2,1)}, bf16[256,1536]{1,0:T(8,128)(2,1)}, u32[]{:S(2)}, u32[]{:S(2)}) collective-permute-start(bf16[256,1536]{1,0:T(8,128)(2,1)} %get-tuple-element.235), channel_id=1, source_target_pairs={{0,3},{1,2},{2,1},{3,0},{4,7},{5,6},{6,5},{7,4}} | collective-permute-start | bytes 2359304 | tf_op jit(solution)/shard_map/ppermute | solution.py:449
  487.2 6.1 %copy-start.2 = (bf16[256,1536]{1,0:T(8,128)(2,1)S(1)}, bf16[256,1536]{1,0:T(8,128)(2,1)}, u32[]{:S(2)}) copy-start(bf16[256,1536]{1,0:T(8,128)(2,1)} %get-tuple-element.354) | copy-start | bytes 2359300
  491.9 51.4 %collective-permute-start.32 = (bf16[256,1536]{1,0:T(8,128)(2,1)S(1)}, bf16[256,1536]{1,0:T(8,128)(2,1)S(1)}, u32[]{:S(2)}, u32[]{:S(2)}) collective-permute-start(bf16[256,1536]{1,0:T(8,128)(2,1)S(1)} %get-tuple-element.355), channel_id=1, source_target_pairs={{0,3},{1,2},{2,1},{3,0},{4,7},{5,6},{6,5},{7,4}} | collective-permute-start | bytes 2359304 | tf_op jit(solution)/shard_map/ppermute | solution.py:449
  493.4 57.3 %collective-permute-start.30 = (bf16[256,1536]{1,0:T(8,128)(2,1)S(1)}, bf16[256,1536]{1,0:T(8,128)(2,1)S(1)}, u32[]{:S(2)}, u32[]{:S(2)}) collective-permute-start(bf16[256,1536]{1,0:T(8,128)(2,1)S(1)} %copy-done.2), channel_id=1, source_target_pairs={{0,2},{1,3},{2,0},{3,1},{4,6},{5,7},{6,4},{7,5}} | collective-permute-start | bytes 2359304 | tf_op jit(solution)/shard_map/ppermute | solution.py:449
  543.4 7.3 %copy-start.5 = (bf16[256,1536]{1,0:T(8,128)(2,1)}, bf16[256,1536]{1,0:T(8,128)(2,1)S(1)}, u32[]{:S(2)}) copy-start(bf16[256,1536]{1,0:T(8,128)(2,1)S(1)} %collective-permute-done.32.refs_3_) | copy-start | bytes 2359300
  550.7 0.9 copy-start.6

commit v7 on v6

--- a/solution.py
+++ b/solution.py
@@ -12,6 +12,7 @@
 F32 = jnp.float32
 ALONE = 1024.0
 SENT_SHARE = 27, 32
+STEP = 2
 PAIR = 2
 
 KERNEL_ORDER = (('f', 0), ('b', 0), ('m', 1), ('n', 2), ('n', 3))
@@ -55,9 +56,9 @@
     store_by_expert(dst_ref, picked, cap)
 
 
-def forward_expert(xg, w1_ref, w3_ref):
-    h1 = dot(xg, w1_ref[0])
-    h3 = dot(xg, w3_ref[0])
+def forward_expert(xg, w1, w3):
+    h1 = dot(xg, w1)
+    h3 = dot(xg, w3)
     sig = jax.nn.sigmoid(h1)
     silu = h1 * sig
     act = (silu * h3).astype(BF)
@@ -102,10 +103,11 @@
     def _():
         spread_rows(xg_scr, tok_ref, (xa_ref, xb_ref), cap)
 
-    xg_ref[0] = xg_scr[e]
-    act, u_ref[0], v_ref[0] = forward_expert(xg_scr[e], w1_ref, w3_ref)
-    a_ref[0] = act
-    keep_rows(o_scr, dot(act, w2_ref[0]), e, cap, pad)
+    for k in range(STEP):
+        xg_ref[k] = xg_scr[e * STEP + k]
+        act, u_ref[k], v_ref[k] = forward_expert(xg_scr[e * STEP + k], w1_ref[k], w3_ref[k])
+        a_ref[k] = act
+        keep_rows(o_scr, dot(act, w2_ref[k]), e * STEP + k, cap, pad)
     done = e == pl.num_programs(0) - 1
 
     @pl.when(done & (over_ref[0] == 0))
@@ -124,13 +126,14 @@
     def _():
         spread_rows(d_scr, tok_ref, (dya_ref, dyb_ref), cap, gcol_ref)
 
-    d_ref[0] = d_scr[e]
-    da = dot_bt(d_scr[e], w2_ref[0])
-    dh1 = (da * u_ref[0]).astype(BF)
-    dh3 = (da * v_ref[0]).astype(BF)
-    dh1_ref[0] = dh1
-    dh3_ref[0] = dh3
-    keep_rows(r_scr, dot_bt(dh1, w1_ref[0]) + dot_bt(dh3, w3_ref[0]), e, cap, pad)
+    for k in range(STEP):
+        d_ref[k] = d_scr[e * STEP + k]
+        da = dot_bt(d_scr[e * STEP + k], w2_ref[k])
+        dh1 = (da * u_ref[k]).astype(BF)
+        dh3 = (da * v_ref[k]).astype(BF)
+        dh1_ref[k] = dh1
+        dh3_ref[k] = dh3
+        keep_rows(r_scr, dot_bt(dh1, w1_ref[k]) + dot_bt(dh3, w3_ref[k]), e * STEP + k, cap, pad)
     done = e == pl.num_programs(0) - 1
 
     @pl.when(done & (over_ref[0] == 0))
@@ -160,18 +163,20 @@
         p_ref[...] = total.astype(BF)
 
 
-def both_ways(cap, pad, e, w1_ref, w3_ref, w2_ref, xg_ref, a_ref, d_ref, dh1_ref, dh3_ref, xg_scr, d_scr, o_scr, r_scr):
-    xg_ref[0] = xg_scr[e]
-    d_ref[0] = d_scr[e]
-    act, u, v = forward_expert(xg_scr[e], w1_ref, w3_ref)
-    a_ref[0] = act
-    keep_rows(o_scr, dot(act, w2_ref[0]), e, cap, pad)
-    da = dot_bt(d_scr[e], w2_ref[0])
-    dh1 = (da * u).astype(BF)
-    dh3 = (da * v).astype(BF)
-    dh1_ref[0] = dh1
-    dh3_ref[0] = dh3
-    keep_rows(r_scr, dot_bt(dh1, w1_ref[0]) + dot_bt(dh3, w3_ref[0]), e, cap, pad)
+def both_ways(cap, pad, step, w1_ref, w3_ref, w2_ref, xg_ref, a_ref, d_ref, dh1_ref, dh3_ref, xg_scr, d_scr, o_scr, r_scr):
+    for k in range(STEP):
+        e = step * STEP + k
+        xg_ref[k] = xg_scr[e]
+        d_ref[k] = d_scr[e]
+        act, u, v = forward_expert(xg_scr[e], w1_ref[k], w3_ref[k])
+        a_ref[k] = act
+        keep_rows(o_scr, dot(act, w2_ref[k]), e, cap, pad)
+        da = dot_bt(d_scr[e], w2_ref[k])
+        dh1 = (da * u).astype(BF)
+        dh3 = (da * v).astype(BF)
+        dh1_ref[k] = dh1
+        dh3_ref[k] = dh3
+        keep_rows(r_scr, dot_bt(dh1, w1_ref[k]) + dot_bt(dh3, w3_ref[k]), e, cap, pad)
 
 
 def near_kernel(cap, pad, xa_ref, xb_ref, dya_ref, dyb_ref, tok_ref, gcol_ref, q_ref, g_ref, w1_ref, w3_ref, w2_ref, xg_ref, a_ref, d_ref, dh1_ref, dh3_ref, y0_ref, y1_ref, z0_ref, z1_ref, xg_scr, d_scr, o_scr, r_scr):
@@ -216,6 +221,10 @@
     return pl.BlockSpec(shape, lambda e: (0,) * len(shape))
 
 
+def per_step(shape):
+    return pl.BlockSpec((STEP,) + shape[1:], lambda e: (e,) + (0,) * (len(shape) - 1))
+
+
 def per_expert(shape):
     return pl.BlockSpec((1,) + shape[1:], lambda e: (e,) + (0,) * (len(shape) - 1))
 
@@ -225,11 +234,11 @@
 
 
 def of_pair(pair, shape):
-    return pl.BlockSpec((PAIR,) + shape[1:], lambda e: (pair,) + (0,) * (len(shape) - 1))
-
-
-def params():
-    return pltpu.CompilerParams(dimension_semantics=("arbitrary",), vmem_limit_bytes=60 * 1024 * 1024)
+    return pl.BlockSpec((PAIR,) + shape[1:], lambda e: (pair,) + (0,) * (len(shape) - 1), pipeline_mode=pl.Buffered(1))
+
+
+def params(limit=60 * 1024 * 1024):
+    return pltpu.CompilerParams(dimension_semantics=("arbitrary",), vmem_limit_bytes=limit)
 
 
 def flag():
@@ -244,12 +253,12 @@
     tables = [tok_col, q_row, g_row, unit_row, form_row]
     return pl.pallas_call(
         functools.partial(far_fwd_kernel, cap, pad),
-        grid=(experts,),
-        in_specs=[whole(xa.shape), whole(xb.shape)] + [of_pair(pair, t.shape) for t in tables] + [flag(), per_expert(w1.shape), per_expert(w3.shape), per_expert(w2.shape)],
-        out_specs=[per_expert(s) if len(s) == 3 else whole(s) for s, _ in outs],
+        grid=(experts // STEP,),
+        in_specs=[once(xa.shape)] * 2 + [of_pair(pair, t.shape) for t in tables] + [flag(), per_step(w1.shape), per_step(w3.shape), per_step(w2.shape)],
+        out_specs=[per_step(s) if len(s) == 3 else once(s) for s, _ in outs],
         out_shape=[jax.ShapeDtypeStruct(s, t) for s, t in outs],
         scratch_shapes=[pltpu.VMEM((experts, rows, hidden), BF), pltpu.VMEM((PAIR, experts * pad, hidden), BF)],
-        compiler_params=params(),
+        compiler_params=params(67043328),
         cost_estimate=pl.CostEstimate(flops=14 * 10**9, bytes_accessed=50 * 10**6, transcendentals=0),
         name="far_fwd_pair",
     )(xa, xb, *tables, over, w1, w3, w2)
@@ -263,12 +272,12 @@
     tables = [tok_col, g_col, q_row, unit_row]
     return pl.pallas_call(
         functools.partial(far_bwd_kernel, cap, pad),
-        grid=(experts,),
-        in_specs=[whole(dya.shape), whole(dyb.shape)] + [of_pair(pair, t.shape) for t in tables] + [flag(), per_expert(w1.shape), per_expert(w3.shape), per_expert(w2.shape), per_expert(u.shape), per_expert(v.shape)],
-        out_specs=[per_expert(s) if len(s) == 3 else whole(s) for s, _ in outs],
+        grid=(experts // STEP,),
+        in_specs=[once(dya.shape)] * 2 + [of_pair(pair, t.shape) for t in tables] + [flag(), per_step(w1.shape), per_step(w3.shape), per_step(w2.shape), per_step(u.shape), per_step(v.shape)],
+        out_specs=[per_step(s) if len(s) == 3 else once(s) for s, _ in outs],
         out_shape=[jax.ShapeDtypeStruct(s, t) for s, t in outs],
         scratch_shapes=[pltpu.VMEM((experts, rows, hidden), BF), pltpu.VMEM((PAIR, experts * pad, hidden), BF)],
-        compiler_params=params(),
+        compiler_params=params(67043328),
         cost_estimate=pl.CostEstimate(flops=14 * 10**9, bytes_accessed=50 * 10**6, transcendentals=0),
         name="far_bwd_pair",
     )(dya, dyb, *tables, over, w1, w3, w2, u, v)
@@ -282,12 +291,12 @@
     tables = [tok_col, g_col, q_row, g_row, unit_row, form_row]
     return pl.pallas_call(
         functools.partial(far_both_kernel, cap, pad),
-        grid=(experts,),
-        in_specs=[once(xa.shape)] * 4 + [of_pair(pair, t.shape) for t in tables] + [flag(), per_expert(w1.shape), per_expert(w3.shape), per_expert(w2.shape)],
-        out_specs=[per_expert(s) if len(s) == 3 else once(s) for s, _ in outs],
+        grid=(experts // STEP,),
+        in_specs=[once(xa.shape)] * 4 + [of_pair(pair, t.shape) for t in tables] + [flag(), per_step(w1.shape), per_step(w3.shape), per_step(w2.shape)],
+        out_specs=[per_step(s) if len(s) == 3 else once(s) for s, _ in outs],
         out_shape=[jax.ShapeDtypeStruct(s, t) for s, t in outs],
         scratch_shapes=[pltpu.VMEM((experts, rows, hidden), BF)] * 2 + [pltpu.VMEM((PAIR, experts * pad, hidden), BF)] * 2,
-        compiler_params=params(),
+        compiler_params=params(67043328),
         cost_estimate=pl.CostEstimate(flops=28 * 10**9, bytes_accessed=70 * 10**6, transcendentals=0),
         name="far_both_pair",
     )(xa, xb, dya, dyb, *tables, over, w1, w3, w2)
@@ -319,12 +328,12 @@
     tables = [tok_col, g_col, q_row, g_row]
     return pl.pallas_call(
         functools.partial(near_kernel, cap, pad),
-        grid=(experts,),
-        in_specs=[once(xa.shape)] * 4 + [of_pair(pair, t.shape) for t in tables] + [per_expert(w1.shape), per_expert(w3.shape), per_expert(w2.shape)],
-        out_specs=[per_expert(s) if len(s) == 3 else whole(s) for s, _ in outs],
+        grid=(experts // STEP,),
+        in_specs=[once(xa.shape)] * 4 + [of_pair(pair, t.shape) for t in tables] + [per_step(w1.shape), per_step(w3.shape), per_step(w2.shape)],
+        out_specs=[per_step(s) if len(s) == 3 else once(s) for s, _ in outs],
         out_shape=[jax.ShapeDtypeStruct(s, t) for s, t in outs],
         scratch_shapes=[pltpu.VMEM((experts, rows, hidden), BF)] * 2 + [pltpu.VMEM((PAIR, experts * pad, hidden), BF)] * 2,
-        compiler_params=params(),
+        compiler_params=params(67043328),
         cost_estimate=pl.CostEstimate(flops=28 * 10**9, bytes_accessed=70 * 10**6, transcendentals=0),
         name="near_pair",
     )(xa, xb, dya, dyb, *tables, w1, w3, w2)

time: 565 us -> 570 us (level)
  local copies, waits for them, and re-layouts: 14.9 us -> 22.3 us
  waiting for transfers between devices: 239 us -> 232 us
    another operation x10, local copies, waits for them, and re-layouts: 6.06 us -> 13.5 us
  transfers between devices with their start and end apart: 32 -> 32, of which waited for: 11 -> 11; matrix products, arithmetic and copies ran while one was open for 5% -> 7% of each run, Pallas kernels for 45% -> 45%
where the time goes in v7:
time: 570 us; the launch traced here: 561 us
  Pallas kernels  259 us (45%)
  waiting for transfers between devices  232 us (41%)
  starting transfers between devices  27.9 us (5%)
  local copies, waits for them, and re-layouts  22.3 us (4%)
  other arithmetic  15.6 us (3%)
    ppermute x12, waiting for transfers between devices, hop_y(): return lax.ppermute(a, 'ing', [(0, 1), (1, 0)])  134 us
    ppermute x20, waiting for transfers between devices, hop_g(): return lax.ppermute(a, 'grp', [(g, g ^ bits) for g in range(groups)])  98.2 us
    pallas_call x2, Pallas kernels, near_pair(): pl.pallas_call(functools.partial(near_kernel, cap, pad), grid=(experts //...  78.8 us
    pallas_call x1, Pallas kernels, far_both_pair(): pl.pallas_call(functools.partial(far_both_kernel, cap, pad), grid=(expert...  44.9 us
    pallas_call x1, Pallas kernels, weight_grads(): pl.pallas_call(functools.partial(dw_kernel, chunks), grid=(experts,), in_...  43.7 us
    pallas_call x1, Pallas kernels, far_forward_pair(): pl.pallas_call(functools.partial(far_fwd_kernel, cap, pad), grid=(experts...  29.5 us
    pallas_call x1, Pallas kernels, far_backward_pair(): pl.pallas_call(functools.partial(far_bwd_kernel, cap, pad), grid=(experts...  28.6 us
    pallas_call x5, Pallas kernels, merge_sources(): pl.pallas_call(functools.partial(merge_kernel, weighted, count), grid=(3,...  22.8 us
  transfers between devices with their start and end apart: 32, of which 11 were waited for; matrix products, arithmetic and copies ran while one was open for 7% of the time, Pallas kernels for 45%

profile of v7, /device:TPU:0, one launch (start us, length us, event | category | flops | bytes accessed | tf_op | source)
XLA Modules:
  0.0 561.5 jit_solution(28204976245038668)
XLA Ops:
  0.6 3.4 collective-permute-start.13
  4.0 1.5 collective-permute-start.25
  7.5 1.5 collective-permute-start.16
  9.0 31.2 %collective-permute-done.8 = f32[1,12,512]{2,1,0:T(8,128)S(1)} collective-permute-done((f32[1,12,512]{2,1,0:T(8,128)S(1)}, f32[1,12,512]{2,1,0:T(8,128)S(1)}, u32[]{:S(2)}, u32[]{:S(2)}) %collective-permute-start.8) | collective-permute-done | bytes 24608 | tf_op jit(solution)/shard_map/ppermute | solution.py:455
  41.4 2.0 collective-permute-start.10
  43.5 3.8 collective-permute-done.10
  49.6 9.7 %select_reduce_fusion = (f32[8,8,72]{2,1,0:T(8,128)S(1)}, f32[8,8,72]{2,1,0:T(8,128)S(1)}, f32[8,8,72]{2,1,0:T(8,128)S(1)}, f32[8,8,72]{2,1,0:T(8,128)S(1)}) fusion(f32[8,8,512]{2,1,0:T(8,128)S(1)} %copy.58, f32[8,8,512]{2,1,0:T(8,128)S(1)} %slice.100, pred[8,8,512]{2,1,0:T(8,128)(4,1)S(1)} %compare_reduce_fusion, f32[8,512]{1,0:T(8,128)S(1)} %bitcast.41, ...), kind=kLoop, calls=%fused_computation.8 | loop fusion | flops 23574528 | bytes 518144 | tf_op jit(solution)/shard_map/reduce_sum | solution.py:426
  60.7 1.8 collective-permute-start.23
  62.5 10.9 %collective-permute-done.23 = f32[2,4,432]{2,1,0:T(4,128)S(1)} collective-permute-done((f32[2,4,432]{2,1,0:T(4,128)S(1)}, f32[2,4,432]{2,1,0:T(4,128)S(1)}, u32[]{:S(2)}, u32[]{:S(2)}) %collective-permute-start.23) | collective-permute-done | bytes 13856 | tf_op jit(solution)/shard_map/ppermute | solution.py:455
  73.4 1.7 collective-permute-start.27
  75.4 1.7 collective-permute-start.17
  78.7 2.1 reshape.248.gcol_ref
  84.2 2.1 convert_element_type.181.tok_ref
  86.9 23.8 %collective-permute-done.27.dya_ref = bf16[512,1536]{1,0:T(8,128)(2,1)} collective-permute-done((bf16[512,1536]{1,0:T(8,128)(2,1)S(1)}, bf16[512,1536]{1,0:T(8,128)(2,1)}, u32[]{:S(2)}, u32[]{:S(2)}) %collective-permute-start.27) | collective-permute-done | bytes 1572896 | tf_op jit(solution)/shard_map/ppermute | solution.py:458
  111.2 33.2 %collective-permute-done.14.xa_ref = bf16[512,1536]{1,0:T(8,128)(2,1)} collective-permute-done((bf16[512,1536]{1,0:T(8,128)(2,1)}, bf16[512,1536]{1,0:T(8,128)(2,1)}, u32[]{:S(2)}, u32[]{:S(2)}) %collective-permute-start.14) | collective-permute-done | bytes 1572896 | tf_op jit(solution)/shard_map/ppermute | solution.py:458
  144.4 32.1 %collective-permute-done.17.dya_ref = bf16[512,1536]{1,0:T(8,128)(2,1)} collective-permute-done((bf16[512,1536]{1,0:T(8,128)(2,1)}, bf16[512,1536]{1,0:T(8,128)(2,1)}, u32[]{:S(2)}, u32[]{:S(2)}) %collective-permute-start.17) | collective-permute-done | bytes 1572896 | tf_op jit(solution)/shard_map/ppermute | solution.py:458
  176.5 29.5 %far_fwd_pair.1 = (bf16[8,144,1536]{2,1,0:T(8,128)(2,1)}, bf16[8,144,512]{2,1,0:T(8,128)(2,1)}, f32[8,144,512]{2,1,0:T(8,128)}, f32[8,144,512]{2,1,0:T(8,128)}, ...) custom-call(bf16[512,1536]{1,0:T(8,128)(2,1)} %collective-permute-done.13.xa_r, ...), custom_call_target="tpu_custom_call" | custom-call | flops 14000000000 | bytes 50000000 | tf_op jit(solution)/shard_map/far_fwd_pair/pallas_call | solution.py:254
  206.6 28.6 %far_bwd_pair.1 = (bf16[8,144,1536]{2,1,0:T(8,128)(2,1)}, bf16[8,144,512]{2,1,0:T(8,128)(2,1)}, bf16[8,144,512]{2,1,0:T(8,128)(2,1)}, f32[256,1536]{1,0:T(8,128)...) custom-call(bf16[512,1536]{1,0:T(8,128)(2,1)} %collective-permute-done.16.dya_ref, ...), custom_call_target="tpu_custom_call" | custom-call | flops 14000000000 | bytes 50000000 | tf_op jit(solution)/shard_map/far_bwd_pair/pallas_call | solution.py:273
  235.2 1.5 collective-permute-start.21
  237.3 44.9 %far_both_pair.1 = (bf16[8,144,1536]{2,1,0:T(8,128)(2,1)}, bf16[8,144,512]{2,1,0:T(8,128)(2,1)}, bf16[8,144,1536]{2,1,0:T(8,128)(2,1)}, bf16[8,144,512]{2,1,0:T(...) custom-call(bf16[512,1536]{1,0:T(8,128)(2,1)} %collective-permute-do, ...), custom_call_target="tpu_custom_call" | custom-call | flops 28000000000 | bytes 70000000 | tf_op jit(solution)/shard_map/far_both_pair/pallas_call | solution.py:292
  282.2 1.5 collective-permute-start.33
  283.7 39.3 %near_pair.2 = (bf16[8,144,1536]{2,1,0:T(8,128)(2,1)}, bf16[8,144,512]{2,1,0:T(8,128)(2,1)}, bf16[8,144,1536]{2,1,0:T(8,128)(2,1)}, bf16[8,144,512]{2,1,0:T(8,12...) custom-call(bf16[512,1536]{1,0:T(8,128)(2,1)} %xa_ref.1, ...), custom_call_target="tpu_custom_call" | custom-call | flops 28000000000 | bytes 70000000 | tf_op jit(solution)/shard_map/near_pair/pallas_call | solution.py:329
  323.1 9.0 %conditional.5 = ((bf16[256,1536]{1,0:T(8,128)(2,1)}, bf16[256,1536]{1,0:T(8,128)(2,1)})) conditional(s32[]{:T(128)} %convert_element_type.161, (f32[256,1536]{1,0:T(8,128)}, f32[256,1536]{1,0:T(8,128)}, bf16[432,1536]{1,0:T(8,128)(2,1)}, bf16[432,1536]{1,0:T(8,128)(2,1)}, s32[4,1,432]{2,0,1:T(4,128)}, ...), branch_computations={%region_15.16_spmd, %region_16.17_spmd} | conditional | flops 2000000000 | bytes 26738820 | solution.py:551
  323.1 1.4 copy.67.refs_6_.refs_7_
  325.8 6.2 %merge_sources.5 = (bf16[256,1536]{1,0:T(8,128)(2,1)}, bf16[256,1536]{1,0:T(8,128)(2,1)}) custom-call(f32[256,1536]{1,0:T(8,128)} %get-tuple-element.86.refs_0_, f32[256,1536]{1,0:T(8,128)} %get-tuple-element.87.refs_1_, bf16[432,1536]{1,0:T(8,128)(2,1)} %get-tuple-element.92.refs_2_, bf16[432,1536]{1,0:T(8,128)(2,1)} %get-tuple-element.93.refs_3_, ...), custom_call_target="tpu_custom_call" | custom-call | flops 2000000000 | bytes 8000000 | tf_op jit(solution)/shard_map/cond/branch_0_fun/merge_sources/pallas_call | solution.py:310
  333.9 1.5 collective-permute-start.29
  335.4 28.9 %collective-permute-done.34 = bf16[432,1536]{1,0:T(8,128)(2,1)} collective-permute-done((bf16[432,1536]{1,0:T(8,128)(2,1)}, bf16[432,1536]{1,0:T(8,128)(2,1)}, u32[]{:S(2)}, u32[]{:S(2)}) %collective-permute-start.34) | collective-permute-done | bytes 1327136 | tf_op jit(solution)/shard_map/ppermute | solution.py:455
  364.3 7.0 %conditional.8 = ((bf16[256,1536]{1,0:T(8,128)(2,1)}, bf16[256,1536]{1,0:T(8,128)(2,1)})) conditional(s32[]{:T(128)} %convert_element_type.161, (f32[256,1536]{1,0:T(8,128)S(1)}, f32[256,1536]{1,0:T(8,128)S(1)}, bf16[432,1536]{1,0:T(8,128)(2,1)}, bf16[432,1536]{1,0:T(8,128)(2,1)}, s32[4,1,432]{2,0,1:T(4,128)}, ...), branch_computations={%region_22.23_spmd, %region_23.24_spmd} | conditional | flops 2000000000 | bytes 20447336 | solution.py:551
  367.0 4.2 merge_sources.8
  371.9 1.4 collective-permute-start.36
  374.0 39.5 %near_pair.3 = (bf16[8,144,1536]{2,1,0:T(8,128)(2,1)}, bf16[8,144,512]{2,1,0:T(8,128)(2,1)}, bf16[8,144,1536]{2,1,0:T(8,128)(2,1)}, bf16[8,144,512]{2,1,0:T(8,12...) custom-call(bf16[512,1536]{1,0:T(8,128)(2,1)} %collective-permute-do, ...), custom_call_target="tpu_custom_call" | custom-call | flops 28000000000 | bytes 70000000 | tf_op jit(solution)/shard_map/near_pair/pallas_call | solution.py:329
  413.4 36.2 %collective-permute-done.36 = bf16[432,1536]{1,0:T(8,128)(2,1)} collective-permute-done((bf16[432,1536]{1,0:T(8,128)(2,1)}, bf16[432,1536]{1,0:T(8,128)(2,1)}, u32[]{:S(2)}, u32[]{:S(2)}) %collective-permute-start.36) | collective-permute-done | bytes 1327136 | tf_op jit(solution)/shard_map/ppermute | solution.py:455
  449.7 26.7 %collective-permute-done.37 = bf16[432,1536]{1,0:T(8,128)(2,1)} collective-permute-done((bf16[432,1536]{1,0:T(8,128)(2,1)}, bf16[432,1536]{1,0:T(8,128)(2,1)}, u32[]{:S(2)}, u32[]{:S(2)}) %collective-permute-start.37) | collective-permute-done | bytes 1327136 | tf_op jit(solution)/shard_map/ppermute | solution.py:455
  476.3 7.5 %conditional.9 = ((bf16[256,1536]{1,0:T(8,128)(2,1)}, bf16[256,1536]{1,0:T(8,128)(2,1)S(1)})) conditional(s32[]{:T(128)} %convert_element_type.161, (f32[256,1536]{1,0:T(8,128)}, f32[256,1536]{1,0:T(8,128)}, bf16[432,1536]{1,0:T(8,128)(2,1)}, bf16[432,1536]{1,0:T(8,128)(2,1)}, s32[4,1,432]{2,0,1:T(4,128)}, ...), branch_computations={%region_24.25_spmd, %region_25.26_spmd} | conditional | flops 2000000000 | bytes 26738820 | solution.py:551
  476.3 1.4 copy.79.refs_6_.refs_7_
  479.1 4.8 merge_sources.9
  483.9 1.5 collective-permute-start.38
  485.4 6.9 %conditional.6 = (bf16[256,1536]{1,0:T(8,128)(2,1)}) conditional(s32[]{:T(128)} %convert_element_type.161, (f32[256,1536]{1,0:T(8,128)S(1)}, bf16[432,1536]{1,0:T(8,128)(2,1)}, s32[4,1,432]{2,0,1:T(4,128)}, f32[4,1,432]{2,0,1:T(4,128)}) %tuple.111, (f32[256,1536]{1,0:T(8,128)}, f32[256,1536]{1,0:T(8,128)S(1)}) %tuple.112), branch_computations={%region_17.18_spmd, %region_18.19_spmd} | conditional | flops 1000000000 | bytes 10223664 | solution.py:551
  485.4 1.4 copy.71.refs_3_
  488.2 4.2 merge_sources.6
  492.7 6.4 %conditional.7 = (bf16[256,1536]{1,0:T(8,128)(2,1)S(1)}) conditional(s32[]{:T(128)} %convert_element_type.161, (f32[256,1536]{1,0:T(8,128)S(1)}, bf16[432,1536]{1,0:T(8,128)(2,1)}, s32[4,1,432]{2,0,1:T(4,128)}, f32[4,1,432]{2,0,1:T(4,128)}) %tuple.109, (f32[256,1536]{1,0:T(8,128)}, f32[256,1536]{1,0:T(8,128)S(1)}) %tuple.110), branch_computations={%region_19.20_spmd, %region_20.21_spmd} | conditional | flops 1000000000 | bytes 10223664 | solution.py:551
  492.7 1.4 copy.73.refs_3_
  495.4 3.5 merge_sources.7
  499.1 1.4 collective-permute-start.32
  501.4 43.7 %weight_grads.1 = (f32[8,1536,512]{2,1,0:T(8,128)}, f32[8,1536,512]{2,1,0:T(8,128)}, f32[8,512,1536]{2,1,0:T(8,128)}) custom-call(bf16[8,144,1536]{2,1,0:T(8,128)(2,1)} %get-tuple-element.236.refs_0_, bf16[8,144,1536]{2,1,0:T(8,128)(2,1)} %get-tuple-element.237.refs_1_, bf16[8,144,1536]{2,1,0:T(8,128)(2,1)} %get-tuple-element.238.refs_2_, ...), custom_call_target="tpu_custom_call" | custom-call | flops 24999999488 | bytes 120000000 | tf_op jit(solution)/shard_map/weight_grads/pallas_call | solution.py:360
  545.1 5.5 collect.3
  550.6 4.0 collective-permute-done.30.refs_2_
  555.5 5.5 collect.2
  (140 shorter events, 26.6 us)
Async XLA Ops:
  0.6 74.4 %collective-permute-start.13 = (bf16[512,1536]{1,0:T(8,128)(2,1)}, bf16[512,1536]{1,0:T(8,128)(2,1)}, u32[]{:S(2)}, u32[]{:S(2)}) collective-permute-start(bf16[512,1536]{1,0:T(8,128)(2,1)} %xa_ref.1), channel_id=1, source_target_pairs={{0,4},{4,0},{1,5},{5,1},{2,6},{6,2},{3,7},{7,3}} | collective-permute-start | bytes 4718600 | tf_op jit(solution)/shard_map/ppermute | solution.py:455
  4.0 71.1 %collective-permute-start.25 = (bf16[512,1536]{1,0:T(8,128)(2,1)}, bf16[512,1536]{1,0:T(8,128)(2,1)}, u32[]{:S(2)}, u32[]{:S(2)}) collective-permute-start(bf16[512,1536]{1,0:T(8,128)(2,1)} %xa_ref.1), channel_id=1, source_target_pairs={{0,2},{1,3},{2,0},{3,1},{4,6},{5,7},{6,4},{7,5}} | collective-permute-start | bytes 4718600 | tf_op jit(solution)/shard_map/ppermute | solution.py:458
  6.9 33.2 %collective-permute-start.8 = (f32[1,12,512]{2,1,0:T(8,128)S(1)}, f32[1,12,512]{2,1,0:T(8,128)S(1)}, u32[]{:S(2)}, u32[]{:S(2)}) collective-permute-start(f32[1,12,512]{2,1,0:T(8,128)S(1)} %maximum_bitcast_fusion), channel_id=1, source_target_pairs={{0,4},{4,0},{1,5},{5,1},{2,6},{6,2},{3,7},{7,3}} | collective-permute-start | bytes 73736 | tf_op jit(solution)/shard_map/ppermute | solution.py:455
  7.5 68.0 %collective-permute-start.16 = (bf16[512,1536]{1,0:T(8,128)(2,1)}, bf16[512,1536]{1,0:T(8,128)(2,1)}, u32[]{:S(2)}, u32[]{:S(2)}) collective-permute-start(bf16[512,1536]{1,0:T(8,128)(2,1)} %dya_ref.1), channel_id=1, source_target_pairs={{0,4},{4,0},{1,5},{5,1},{2,6},{6,2},{3,7},{7,3}} | collective-permute-start | bytes 4718600 | tf_op jit(solution)/shard_map/ppermute | solution.py:455
  40.2 1.3 collective-permute-start.9
  41.4 5.8 %collective-permute-start.10 = (f32[4,12,512]{2,1,0:T(8,128)S(1)}, f32[4,12,512]{2,1,0:T(8,128)S(1)}, u32[]{:S(2)}, u32[]{:S(2)}) collective-permute-start(f32[4,12,512]{2,1,0:T(8,128)S(1)} %pad_maximum_fusion), channel_id=1, source_target_pairs={{0,2},{1,3},{2,0},{3,1},{4,6},{5,7},{6,4},{7,5}} | collective-permute-start | bytes 294920 | tf_op jit(solution)/shard_map/ppermute | solution.py:458
  43.5 35.2 %collective-permute-start.11 = (bf16[512,1536]{1,0:T(8,128)(2,1)}, bf16[512,1536]{1,0:T(8,128)(2,1)}, u32[]{:S(2)}, u32[]{:S(2)}) collective-permute-start(bf16[512,1536]{1,0:T(8,128)(2,1)} %xa_ref.1), channel_id=1, source_target_pairs={{0,1},{1,0},{2,3},{3,2},{4,5},{5,4},{6,7},{7,6}} | collective-permute-start | bytes 4718600 | tf_op jit(solution)/shard_map/ppermute | solution.py:458
  48.9 24.5 %copy-start.8 = (bf16[512,1536]{1,0:T(8,128)(2,1)S(1)}, bf16[512,1536]{1,0:T(8,128)(2,1)}, u32[]{:S(2)}) copy-start(bf16[512,1536]{1,0:T(8,128)(2,1)} %dya_ref.1) | copy-start | bytes 4718596
  60.7 12.7 %collective-permute-start.23 = (f32[2,4,432]{2,1,0:T(4,128)S(1)}, f32[2,4,432]{2,1,0:T(4,128)S(1)}, u32[]{:S(2)}, u32[]{:S(2)}) collective-permute-start(f32[2,4,432]{2,1,0:T(4,128)S(1)} %pad_maximum_fusion.2), channel_id=1, source_target_pairs={{0,4},{4,0},{1,5},{5,1},{2,6},{6,2},{3,7},{7,3}} | collective-permute-start | bytes 41480 | tf_op jit(solution)/shard_map/ppermute | solution.py:455
  73.4 37.4 %collective-permute-start.27 = (bf16[512,1536]{1,0:T(8,128)(2,1)S(1)}, bf16[512,1536]{1,0:T(8,128)(2,1)}, u32[]{:S(2)}, u32[]{:S(2)}) collective-permute-start(bf16[512,1536]{1,0:T(8,128)(2,1)S(1)} %copy-done.8), channel_id=1, source_target_pairs={{0,2},{1,3},{2,0},{3,1},{4,6},{5,7},{6,4},{7,5}} | collective-permute-start | bytes 4718600 | tf_op jit(solution)/shard_map/ppermute | solution.py:458
  75.1 35.7 %collective-permute-start.20 = (bf16[512,1536]{1,0:T(8,128)(2,1)}, bf16[512,1536]{1,0:T(8,128)(2,1)}, u32[]{:S(2)}, u32[]{:S(2)}) collective-permute-start(bf16[512,1536]{1,0:T(8,128)(2,1)} %collective-permute-done.13.xa_ref), channel_id=1, source_target_pairs={{0,1},{1,0},{2,3},{3,2},{4,5},{5,4},{6,7},{7,6}} | collective-permute-start | bytes 4718600 | tf_op jit(solution)/shard_map/ppermute | solution.py:458
  75.1 69.4 %collective-permute-start.14 = (bf16[512,1536]{1,0:T(8,128)(2,1)}, bf16[512,1536]{1,0:T(8,128)(2,1)}, u32[]{:S(2)}, u32[]{:S(2)}) collective-permute-start(bf16[512,1536]{1,0:T(8,128)(2,1)} %collective-permute-done.13.xa_ref), channel_id=1, source_target_pairs={{0,2},{1,3},{2,0},{3,1},{4,6},{5,7},{6,4},{7,5}} | collective-permute-start | bytes 4718600 | tf_op jit(solution)/shard_map/ppermute | solution.py:458
  75.4 101.1 %collective-permute-start.17 = (bf16[512,1536]{1,0:T(8,128)(2,1)}, bf16[512,1536]{1,0:T(8,128)(2,1)}, u32[]{:S(2)}, u32[]{:S(2)}) collective-permute-start(bf16[512,1536]{1,0:T(8,128)(2,1)} %collective-permute-done.16.dya_ref), channel_id=1, source_target_pairs={{0,2},{1,3},{2,0},{3,1},{4,6},{5,7},{6,4},{7,5}} | collective-permute-start | bytes 4718600 | tf_op jit(solution)/shard_map/ppermute | solution.py:458
  78.6 127.4 %collective-permute-start.19 = (bf16[512,1536]{1,0:T(8,128)(2,1)}, bf16[512,1536]{1,0:T(8,128)(2,1)}, u32[]{:S(2)}, u32[]{:S(2)}) collective-permute-start(bf16[512,1536]{1,0:T(8,128)(2,1)} %collective-permute-done.16.dya_ref), channel_id=1, source_target_pairs={{0,1},{1,0},{2,3},{3,2},{4,5},{5,4},{6,7},{7,6}} | collective-permute-start | bytes 4718600 | tf_op jit(solution)/shard_map/ppermute | solution.py:458
  110.7 262.6 %collective-permute-start.26 = (bf16[512,1536]{1,0:T(8,128)(2,1)}, bf16[512,1536]{1,0:T(8,128)(2,1)}, u32[]{:S(2)}, u32[]{:S(2)}) collective-permute-start(bf16[512,1536]{1,0:T(8,128)(2,1)} %collective-permute-done.25.xa_ref), channel_id=1, source_target_pairs={{0,1},{1,0},{2,3},{3,2},{4,5},{5,4},{6,7},{7,6}} | collective-permute-start | bytes 4718600 | tf_op jit(solution)/shard_map/ppermute | solution.py:458
  110.7 263.2 %collective-permute-start.28 = (bf16[512,1536]{1,0:T(8,128)(2,1)}, bf16[512,1536]{1,0:T(8,128)(2,1)}, u32[]{:S(2)}, u32[]{:S(2)}) collective-permute-start(bf16[512,1536]{1,0:T(8,128)(2,1)} %collective-permute-done.27.dya_ref), channel_id=1, source_target_pairs={{0,1},{1,0},{2,3},{3,2},{4,5},{5,4},{6,7},{7,6}} | collective-permute-start | bytes 4718600 | tf_op jit(solution)/shard_map/ppermute | solution.py:458
  144.4 90.8 %collective-permute-start.15 = (bf16[512,1536]{1,0:T(8,128)(2,1)}, bf16[512,1536]{1,0:T(8,128)(2,1)}, u32[]{:S(2)}, u32[]{:S(2)}) collective-permute-start(bf16[512,1536]{1,0:T(8,128)(2,1)} %collective-permute-done.14.xa_ref), channel_id=1, source_target_pairs={{0,1},{1,0},{2,3},{3,2},{4,5},{5,4},{6,7},{7,6}} | collective-permute-start | bytes 4718600 | tf_op jit(solution)/shard_map/ppermute | solution.py:458
  176.5 60.2 %collective-permute-start.18 = (bf16[512,1536]{1,0:T(8,128)(2,1)}, bf16[512,1536]{1,0:T(8,128)(2,1)}, u32[]{:S(2)}, u32[]{:S(2)}) collective-permute-start(bf16[512,1536]{1,0:T(8,128)(2,1)} %collective-permute-done.17.dya_ref), channel_id=1, source_target_pairs={{0,1},{1,0},{2,3},{3,2},{4,5},{5,4},{6,7},{7,6}} | collective-permute-start | bytes 4718600 | tf_op jit(solution)/shard_map/ppermute | solution.py:458
  206.1 76.1 %collective-permute-start.12 = (bf16[512,1536]{1,0:T(8,128)(2,1)}, bf16[512,1536]{1,0:T(8,128)(2,1)}, u32[]{:S(2)}, u32[]{:S(2)}) collective-permute-start(bf16[512,1536]{1,0:T(8,128)(2,1)} %dya_ref.1), channel_id=1, source_target_pairs={{0,1},{1,0},{2,3},{3,2},{4,5},{5,4},{6,7},{7,6}} | collective-permute-start | bytes 4718600 | tf_op jit(solution)/shard_map/ppermute | solution.py:458
  235.2 87.8 %collective-permute-start.21 = (bf16[432,1536]{1,0:T(8,128)(2,1)}, bf16[432,1536]{1,0:T(8,128)(2,1)}, u32[]{:S(2)}, u32[]{:S(2)}) collective-permute-start(bf16[432,1536]{1,0:T(8,128)(2,1)} %get-tuple-element.210), channel_id=1, source_target_pairs={{0,4},{4,0},{1,5},{5,1},{2,6},{6,2},{3,7},{7,3}} | collective-permute-start | bytes 3981320 | tf_op jit(solution)/shard_map/ppermute | solution.py:455
  236.7 86.3 %collective-permute-start.22 = (bf16[432,1536]{1,0:T(8,128)(2,1)}, bf16[432,1536]{1,0:T(8,128)(2,1)}, u32[]{:S(2)}, u32[]{:S(2)}) collective-permute-start(bf16[432,1536]{1,0:T(8,128)(2,1)} %get-tuple-element.211), channel_id=1, source_target_pairs={{0,4},{4,0},{1,5},{5,1},{2,6},{6,2},{3,7},{7,3}} | collective-permute-start | bytes 3981320 | tf_op jit(solution)/shard_map/ppermute | solution.py:455
  282.2 53.2 %collective-permute-start.33 = (bf16[432,1536]{1,0:T(8,128)(2,1)}, bf16[432,1536]{1,0:T(8,128)(2,1)}, u32[]{:S(2)}, u32[]{:S(2)}) collective-permute-start(bf16[432,1536]{1,0:T(8,128)(2,1)} %get-tuple-element.224), channel_id=1, source_target_pairs={{0,4},{4,0},{1,5},{5,1},{2,6},{6,2},{3,7},{7,3}} | collective-permute-start | bytes 3981320 | tf_op jit(solution)/shard_map/ppermute | solution.py:455
  323.0 9.6 %copy-start.7 = (s32[512,6]{0,1:T(8,128)S(1)}, s32[512,6]{0,1:T(8,128)}, u32[]{:S(2)}) copy-start(s32[512,6]{0,1:T(8,128)} %param.18) | copy-start | bytes 36868
  323.0 41.3 %copy-start.2 = (f32[256,1536]{1,0:T(8,128)S(1)}, f32[256,1536]{1,0:T(8,128)}, u32[]{:S(2)}) copy-start(f32[256,1536]{1,0:T(8,128)} %get-tuple-element.215) | copy-start | bytes 4718596
  323.0 41.3 %copy-start.3 = (f32[256,1536]{1,0:T(8,128)S(1)}, f32[256,1536]{1,0:T(8,128)}, u32[]{:S(2)}) copy-start(f32[256,1536]{1,0:T(8,128)} %get-tuple-element.223) | copy-start | bytes 4718596
  332.0 32.3 %collective-permute-start.34 = (bf16[432,1536]{1,0:T(8,128)(2,1)}, bf16[432,1536]{1,0:T(8,128)(2,1)}, u32[]{:S(2)}, u32[]{:S(2)}) collective-permute-start(bf16[432,1536]{1,0:T(8,128)(2,1)} %get-tuple-element.225), channel_id=1, source_target_pairs={{0,4},{4,0},{1,5},{5,1},{2,6},{6,2},{3,7},{7,3}} | collective-permute-start | bytes 3981320 | tf_op jit(solution)/shard_map/ppermute | solution.py:455
  333.9 151.5 %collective-permute-start.29 = (bf16[432,1536]{1,0:T(8,128)(2,1)}, bf16[432,1536]{1,0:T(8,128)(2,1)}, u32[]{:S(2)}, u32[]{:S(2)}) collective-permute-start(bf16[432,1536]{1,0:T(8,128)(2,1)} %get-tuple-element.218), channel_id=1, source_target_pairs={{0,4},{4,0},{1,5},{5,1},{2,6},{6,2},{3,7},{7,3}} | collective-permute-start | bytes 3981320 | tf_op jit(solution)/shard_map/ppermute | solution.py:455
  371.3 121.4 %collective-permute-start.31 = (bf16[432,1536]{1,0:T(8,128)(2,1)}, bf16[432,1536]{1,0:T(8,128)(2,1)}, u32[]{:S(2)}, u32[]{:S(2)}) collective-permute-start(bf16[432,1536]{1,0:T(8,128)(2,1)} %get-tuple-element.221), channel_id=1, source_target_pairs={{0,4},{4,0},{1,5},{5,1},{2,6},{6,2},{3,7},{7,3}} | collective-permute-start | bytes 3981320 | tf_op jit(solution)/shard_map/ppermute | solution.py:455
  371.9 77.7 %collective-permute-start.36 = (bf16[432,1536]{1,0:T(8,128)(2,1)}, bf16[432,1536]{1,0:T(8,128)(2,1)}, u32[]{:S(2)}, u32[]{:S(2)}) collective-permute-start(bf16[432,1536]{1,0:T(8,128)(2,1)} %get-tuple-element.231), channel_id=1, source_target_pairs={{0,4},{4,0},{1,5},{5,1},{2,6},{6,2},{3,7},{7,3}} | collective-permute-start | bytes 3981320 | tf_op jit(solution)/shard_map/ppermute | solution.py:455
  373.4 103.0 %collective-permute-start.37 = (bf16[432,1536]{1,0:T(8,128)(2,1)}, bf16[432,1536]{1,0:T(8,128)(2,1)}, u32[]{:S(2)}, u32[]{:S(2)}) collective-permute-start(bf16[432,1536]{1,0:T(8,128)(2,1)} %get-tuple-element.232), channel_id=1, source_target_pairs={{0,4},{4,0},{1,5},{5,1},{2,6},{6,2},{3,7},{7,3}} | collective-permute-start | bytes 3981320 | tf_op jit(solution)/shard_map/ppermute | solution.py:455
  373.9 126.6 %collective-permute-start.35 = (bf16[256,1536]{1,0:T(8,128)(2,1)}, bf16[256,1536]{1,0:T(8,128)(2,1)}, u32[]{:S(2)}, u32[]{:S(2)}) collective-permute-start(bf16[256,1536]{1,0:T(8,128)(2,1)} %get-tuple-element.228), channel_id=1, source_target_pairs={{0,1},{1,0},{2,3},{3,2},{4,5},{5,4},{6,7},{7,6}} | collective-permute-start | bytes 2359304 | tf_op jit(solution)/shard_map/ppermute | solution.py:458
  476.3 9.1 %copy-start.1 = (f32[256,1536]{1,0:T(8,128)S(1)}, f32[256,1536]{1,0:T(8,128)}, u32[]{:S(2)}) copy-start(f32[256,1536]{1,0:T(8,128)} %get-tuple-element.217) | copy-start | bytes 4718596
  483.9 1.5 copy-start.11
  483.9 66.7 %collective-permute-start.24 = (bf16[256,1536]{1,0:T(8,128)(2,1)}, bf16[256,1536]{1,0:T(8,128)(2,1)}, u32[]{:S(2)}, u32[]{:S(2)}) collective-permute-start(bf16[256,1536]{1,0:T(8,128)(2,1)} %get-tuple-element.214), channel_id=1, source_target_pairs={{0,1},{1,0},{2,3},{3,2},{4,5},{5,4},{6,7},{7,6}} | collective-permute-start | bytes 2359304 | tf_op jit(solution)/shard_map/ppermute | solution.py:458
  483.9 61.2 %collective-permute-start.38 = (bf16[256,1536]{1,0:T(8,128)(2,1)}, bf16[256,1536]{1,0:T(8,128)(2,1)}, u32[]{:S(2)}, u32[]{:S(2)}) collective-permute-start(bf16[256,1536]{1,0:T(8,128)(2,1)} %get-tuple-element.234), channel_id=1, source_target_pairs={{0,2},{1,3},{2,0},{3,1},{4,6},{5,7},{6,4},{7,5}} | collective-permute-start | bytes 2359304 | tf_op jit(solution)/shard_map/ppermute | solution.py:458
  485.4 7.3 %copy-start = (f32[256,1536]{1,0:T(8,128)S(1)}, f32[256,1536]{1,0:T(8,128)}, u32[]{:S(2)}) copy-start(f32[256,1536]{1,0:T(8,128)} %get-tuple-element.220) | copy-start | bytes 4718596
  492.4 52.7 %collective-permute-start.39 = (bf16[256,1536]{1,0:T(8,128)(2,1)}, bf16[256,1536]{1,0:T(8,128)(2,1)}, u32[]{:S(2)}, u32[]{:S(2)}) collective-permute-start(bf16[256,1536]{1,0:T(8,128)(2,1)} %copy-done.11), channel_id=1, source_target_pairs={{0,3},{1,2},{2,1},{3,0},{4,7},{5,6},{6,5},{7,4}} | collective-permute-start | bytes 2359304 | tf_op jit(solution)/shard_map/ppermute | solution.py:458
  492.7 7.9 %copy-start.6 = (bf16[256,1536]{1,0:T(8,128)(2,1)S(1)}, bf16[256,1536]{1,0:T(8,128)(2,1)}, u32[]{:S(2)}) copy-start(bf16[256,1536]{1,0:T(8,128)(2,1)} %get-tuple-element.354) | copy-start | bytes 2359300
  499.1 51.5 %collective-permute-start.32 = (bf16[256,1536]{1,0:T(8,128)(2,1)S(1)}, bf16[256,1536]{1,0:T(8,128)(2,1)S(1)}, u32[]{:S(2)}, u32[]{:S(2)}) collective-permute-start(bf16[256,1536]{1,0:T(8,128)(2,1)S(1)} %get-tuple-element.355), channel_id=1, source_target_pairs={{0,3},{1,2},{2,1},{3,0},{4,7},{5,6},{6,5},{7,4}} | collective-permute-start | bytes 2359304 | tf_op jit(solution)/shard_map/ppermute | solution.py:458
  500.6 54.0 %collective-permute-start.30 = (bf16[256,1536]{1,0:T(8,128)(2,1)S(1)}, bf16[256,1536]{1,0:T(8,128)(2,1)S(1)}, u32[]{:S(2)}, u32[]{:S(2)}) collective-permute-start(bf16[256,1536]{1,0:T(8,128)(2,1)S(1)} %copy-done.6), channel_id=1, source_target_pairs={{0,2},{1,3},{2,0},{3,1},{4,6},{5,7},{6,4},{7,5}} | collective-permute-start | bytes 2359304 | tf_op jit(solution)/shard_map/ppermute | solution.py:458
  550.6 4.0 copy-start.9
  554.6 0.9 copy-start.10

commit v8 on v6

--- a/solution.py
+++ b/solution.py
@@ -361,27 +361,32 @@
 
 
 def final_kernel(groups, *refs):
-    q_ref, out_ref = refs[groups], refs[groups + 1]
-    total = None
-    for h in range(groups):
-        lanes = lax.broadcasted_iota(jnp.int32, (out_ref.shape[0], refs[h].shape[0]), 1)
-        one_hot = jnp.where(q_ref[:, h:h + 1] == lanes, 1.0, 0.0).astype(BF)
-        term = dot(one_hot, refs[h][...])
-        total = term if total is None else total + term
+    q_ref, out_ref, pick_ref = refs[groups:]
+
+    @pl.when(pl.program_id(0) == 0)
+    def _():
+        lanes = lax.broadcasted_iota(jnp.int32, pick_ref.shape[1:], 1)
+        for h in range(groups):
+            pick_ref[h] = jnp.where(q_ref[:, h:h + 1] == lanes, 1.0, 0.0).astype(BF)
+
+    total = dot(pick_ref[0], refs[0][...])
+    for h in range(1, groups):
+        total = total + dot(pick_ref[h], refs[h][...])
     out_ref[...] = total.astype(BF)
 
 
 def collect(parts, q_cols):
     groups = len(parts)
     tokens = q_cols.shape[0]
-    hidden = parts[0].shape[1]
-    block = tokens // 4
+    grp_cap, hidden = parts[0].shape
+    block = hidden // 3
     return pl.pallas_call(
         functools.partial(final_kernel, groups),
-        grid=(4,),
-        in_specs=[whole(p.shape) for p in parts] + [pl.BlockSpec((block, groups), lambda e: (e, 0))],
-        out_specs=pl.BlockSpec((block, hidden), lambda e: (e, 0)),
+        grid=(3,),
+        in_specs=[pl.BlockSpec((grp_cap, block), lambda n: (0, n))] * groups + [whole(q_cols.shape)],
+        out_specs=pl.BlockSpec((tokens, block), lambda n: (0, n)),
         out_shape=jax.ShapeDtypeStruct((tokens, hidden), BF),
+        scratch_shapes=[pltpu.VMEM((groups, tokens, grp_cap), BF)],
         compiler_params=params(),
         cost_estimate=pl.CostEstimate(flops=2 * 10**9, bytes_accessed=5 * 10**6, transcendentals=0),
         name="collect",

time: 565 us -> 565 us (level)
  no operation moved by 1% of the time
where the time goes in v8:
time: 565 us; the launch traced here: 557 us
  Pallas kernels  257 us (45%)
  waiting for transfers between devices  240 us (42%)
  starting transfers between devices  27.5 us (5%)
  other arithmetic  15 us (3%)
  local copies, waits for them, and re-layouts  14.9 us (3%)
    ppermute x12, waiting for transfers between devices, hop_y(): return lax.ppermute(a, 'ing', [(0, 1), (1, 0)])  137 us
    ppermute x20, waiting for transfers between devices, hop_g(): return lax.ppermute(a, 'grp', [(g, g ^ bits) for g in range(groups)])  102 us
    pallas_call x2, Pallas kernels, near_pair(): pl.pallas_call(functools.partial(near_kernel, cap, pad), grid=(experts,),...  75.3 us
    pallas_call x1, Pallas kernels, far_both_pair(): pl.pallas_call(functools.partial(far_both_kernel, cap, pad), grid=(expert...  44.1 us
    pallas_call x1, Pallas kernels, weight_grads(): pl.pallas_call(functools.partial(dw_kernel, chunks), grid=(experts,), in_...  43.9 us
    pallas_call x1, Pallas kernels, far_forward_pair(): pl.pallas_call(functools.partial(far_fwd_kernel, cap, pad), grid=(experts...  30.7 us
    pallas_call x1, Pallas kernels, far_backward_pair(): pl.pallas_call(functools.partial(far_bwd_kernel, cap, pad), grid=(experts...  28.9 us
    pallas_call x5, Pallas kernels, merge_sources(): pl.pallas_call(functools.partial(merge_kernel, weighted, count), grid=(3,...  23.1 us
  transfers between devices with their start and end apart: 32, of which 11 were waited for; matrix products, arithmetic and copies ran while one was open for 5% of the time, Pallas kernels for 45%

profile of v8, /device:TPU:0, one launch (start us, length us, event | category | flops | bytes accessed | tf_op | source)
XLA Modules:
  0.0 557.1 jit_solution(18279217834597689640)
XLA Ops:
  0.6 3.4 collective-permute-start.13
  4.0 1.5 collective-permute-start.25
  7.5 1.5 collective-permute-start.16
  9.0 31.2 %collective-permute-done.8 = f32[1,12,512]{2,1,0:T(8,128)S(1)} collective-permute-done((f32[1,12,512]{2,1,0:T(8,128)S(1)}, f32[1,12,512]{2,1,0:T(8,128)S(1)}, u32[]{:S(2)}, u32[]{:S(2)}) %collective-permute-start.8) | collective-permute-done | bytes 24608 | tf_op jit(solution)/shard_map/ppermute | solution.py:451
  40.2 1.2 collective-permute-done.9
  41.4 2.0 collective-permute-start.10
  43.5 3.8 collective-permute-done.10
  49.6 9.7 %select_reduce_fusion = (f32[8,8,72]{2,1,0:T(8,128)S(1)}, f32[8,8,72]{2,1,0:T(8,128)S(1)}, f32[8,8,72]{2,1,0:T(8,128)S(1)}, f32[8,8,72]{2,1,0:T(8,128)S(1)}) fusion(f32[8,8,512]{2,1,0:T(8,128)S(1)} %copy.58, f32[8,8,512]{2,1,0:T(8,128)S(1)} %slice.100, pred[8,8,512]{2,1,0:T(8,128)(4,1)S(1)} %compare_reduce_fusion, f32[8,512]{1,0:T(8,128)S(1)} %bitcast.41, ...), kind=kLoop, calls=%fused_computation.8 | loop fusion | flops 23574528 | bytes 518144 | tf_op jit(solution)/shard_map/reduce_sum | solution.py:422
  59.6 1.1 select_reduce_fusion.5
  60.7 1.8 collective-permute-start.23
  62.5 10.9 %collective-permute-done.23 = f32[2,4,432]{2,1,0:T(4,128)S(1)} collective-permute-done((f32[2,4,432]{2,1,0:T(4,128)S(1)}, f32[2,4,432]{2,1,0:T(4,128)S(1)}, u32[]{:S(2)}, u32[]{:S(2)}) %collective-permute-start.23) | collective-permute-done | bytes 13856 | tf_op jit(solution)/shard_map/ppermute | solution.py:451
  73.4 1.7 collective-permute-start.27
  75.4 1.7 collective-permute-start.17
  78.7 2.1 reshape.248.gcol_ref
  84.2 2.1 convert_element_type.181.tok_ref
  86.3 24.4 %collective-permute-done.27.dya_ref = bf16[512,1536]{1,0:T(8,128)(2,1)} collective-permute-done((bf16[512,1536]{1,0:T(8,128)(2,1)S(1)}, bf16[512,1536]{1,0:T(8,128)(2,1)}, u32[]{:S(2)}, u32[]{:S(2)}) %collective-permute-start.27) | collective-permute-done | bytes 1572896 | tf_op jit(solution)/shard_map/ppermute | solution.py:454
  111.2 33.2 %collective-permute-done.14.xa_ref = bf16[512,1536]{1,0:T(8,128)(2,1)} collective-permute-done((bf16[512,1536]{1,0:T(8,128)(2,1)}, bf16[512,1536]{1,0:T(8,128)(2,1)}, u32[]{:S(2)}, u32[]{:S(2)}) %collective-permute-start.14) | collective-permute-done | bytes 1572896 | tf_op jit(solution)/shard_map/ppermute | solution.py:454
  144.4 32.1 %collective-permute-done.17.dya_ref = bf16[512,1536]{1,0:T(8,128)(2,1)} collective-permute-done((bf16[512,1536]{1,0:T(8,128)(2,1)}, bf16[512,1536]{1,0:T(8,128)(2,1)}, u32[]{:S(2)}, u32[]{:S(2)}) %collective-permute-start.17) | collective-permute-done | bytes 1572896 | tf_op jit(solution)/shard_map/ppermute | solution.py:454
  176.5 30.7 %far_fwd_pair.1 = (bf16[8,144,1536]{2,1,0:T(8,128)(2,1)}, bf16[8,144,512]{2,1,0:T(8,128)(2,1)}, f32[8,144,512]{2,1,0:T(8,128)}, f32[8,144,512]{2,1,0:T(8,128)}, ...) custom-call(bf16[512,1536]{1,0:T(8,128)(2,1)} %collective-permute-done.13.xa_r, ...), custom_call_target="tpu_custom_call" | custom-call | flops 14000000000 | bytes 50000000 | tf_op jit(solution)/shard_map/far_fwd_pair/pallas_call | solution.py:245
  207.8 28.9 %far_bwd_pair.1 = (bf16[8,144,1536]{2,1,0:T(8,128)(2,1)}, bf16[8,144,512]{2,1,0:T(8,128)(2,1)}, bf16[8,144,512]{2,1,0:T(8,128)(2,1)}, f32[256,1536]{1,0:T(8,128)...) custom-call(bf16[512,1536]{1,0:T(8,128)(2,1)} %collective-permute-done.16.dya_ref, ...), custom_call_target="tpu_custom_call" | custom-call | flops 14000000000 | bytes 50000000 | tf_op jit(solution)/shard_map/far_bwd_pair/pallas_call | solution.py:264
  236.7 1.5 collective-permute-start.21
  238.7 44.1 %far_both_pair.1 = (bf16[8,144,1536]{2,1,0:T(8,128)(2,1)}, bf16[8,144,512]{2,1,0:T(8,128)(2,1)}, bf16[8,144,1536]{2,1,0:T(8,128)(2,1)}, bf16[8,144,512]{2,1,0:T(...) custom-call(bf16[512,1536]{1,0:T(8,128)(2,1)} %collective-permute-do, ...), custom_call_target="tpu_custom_call" | custom-call | flops 28000000000 | bytes 70000000 | tf_op jit(solution)/shard_map/far_both_pair/pallas_call | solution.py:283
  282.9 1.5 collective-permute-start.33
  284.4 37.5 %near_pair.2 = (bf16[8,144,1536]{2,1,0:T(8,128)(2,1)}, bf16[8,144,512]{2,1,0:T(8,128)(2,1)}, bf16[8,144,1536]{2,1,0:T(8,128)(2,1)}, bf16[8,144,512]{2,1,0:T(8,12...) custom-call(bf16[512,1536]{1,0:T(8,128)(2,1)} %xa_ref.1, ...), custom_call_target="tpu_custom_call" | custom-call | flops 28000000000 | bytes 70000000 | tf_op jit(solution)/shard_map/near_pair/pallas_call | solution.py:320
  322.0 7.5 %conditional.5 = ((bf16[256,1536]{1,0:T(8,128)(2,1)}, bf16[256,1536]{1,0:T(8,128)(2,1)})) conditional(s32[]{:T(128)} %convert_element_type.161, (f32[256,1536]{1,0:T(8,128)}, f32[256,1536]{1,0:T(8,128)}, bf16[432,1536]{1,0:T(8,128)(2,1)}, bf16[432,1536]{1,0:T(8,128)(2,1)}, s32[4,1,432]{2,0,1:T(4,128)S(1)}, ...), branch_computations={%region_15.16_spmd, %region_16.17_spmd} | conditional | flops 2000000000 | bytes 26738820 | solution.py:547
  323.2 6.3 %merge_sources.5 = (bf16[256,1536]{1,0:T(8,128)(2,1)}, bf16[256,1536]{1,0:T(8,128)(2,1)}) custom-call(f32[256,1536]{1,0:T(8,128)} %get-tuple-element.86.refs_0_, f32[256,1536]{1,0:T(8,128)} %get-tuple-element.87.refs_1_, bf16[432,1536]{1,0:T(8,128)(2,1)} %get-tuple-element.92.refs_2_, bf16[432,1536]{1,0:T(8,128)(2,1)} %get-tuple-element.93.refs_3_, ...), custom_call_target="tpu_custom_call" | custom-call | flops 2000000000 | bytes 8000000 | tf_op jit(solution)/shard_map/cond/branch_0_fun/merge_sources/pallas_call | solution.py:301
  330.3 1.0 fusion.1.refs_4_
  331.3 1.5 collective-permute-start.29
  332.8 28.9 %collective-permute-done.34 = bf16[432,1536]{1,0:T(8,128)(2,1)} collective-permute-done((bf16[432,1536]{1,0:T(8,128)(2,1)}, bf16[432,1536]{1,0:T(8,128)(2,1)}, u32[]{:S(2)}, u32[]{:S(2)}) %collective-permute-start.34) | collective-permute-done | bytes 1327136 | tf_op jit(solution)/shard_map/ppermute | solution.py:451
  361.8 5.4 conditional.8
  363.0 4.2 merge_sources.8
  367.7 1.5 collective-permute-start.36
  369.7 37.7 %near_pair.3 = (bf16[8,144,1536]{2,1,0:T(8,128)(2,1)}, bf16[8,144,512]{2,1,0:T(8,128)(2,1)}, bf16[8,144,1536]{2,1,0:T(8,128)(2,1)}, bf16[8,144,512]{2,1,0:T(8,12...) custom-call(bf16[512,1536]{1,0:T(8,128)(2,1)} %collective-permute-do, ...), custom_call_target="tpu_custom_call" | custom-call | flops 28000000000 | bytes 70000000 | tf_op jit(solution)/shard_map/near_pair/pallas_call | solution.py:320
  407.5 39.6 %collective-permute-done.36 = bf16[432,1536]{1,0:T(8,128)(2,1)} collective-permute-done((bf16[432,1536]{1,0:T(8,128)(2,1)}, bf16[432,1536]{1,0:T(8,128)(2,1)}, u32[]{:S(2)}, u32[]{:S(2)}) %collective-permute-start.36) | collective-permute-done | bytes 1327136 | tf_op jit(solution)/shard_map/ppermute | solution.py:451
  447.1 26.6 %collective-permute-done.37 = bf16[432,1536]{1,0:T(8,128)(2,1)} collective-permute-done((bf16[432,1536]{1,0:T(8,128)(2,1)}, bf16[432,1536]{1,0:T(8,128)(2,1)}, u32[]{:S(2)}, u32[]{:S(2)}) %collective-permute-start.37) | collective-permute-done | bytes 1327136 | tf_op jit(solution)/shard_map/ppermute | solution.py:451
  473.7 6.2 %conditional.9 = ((bf16[256,1536]{1,0:T(8,128)(2,1)}, bf16[256,1536]{1,0:T(8,128)(2,1)})) conditional(s32[]{:T(128)} %convert_element_type.161, (f32[256,1536]{1,0:T(8,128)}, f32[256,1536]{1,0:T(8,128)}, bf16[432,1536]{1,0:T(8,128)(2,1)}, bf16[432,1536]{1,0:T(8,128)(2,1)}, s32[4,1,432]{2,0,1:T(4,128)S(1)}, ...), branch_computations={%region_24.25_spmd, %region_25.26_spmd} | conditional | flops 2000000000 | bytes 26738820 | solution.py:547
  474.9 5.0 merge_sources.9
  480.0 1.5 collective-permute-start.38
  481.5 5.4 conditional.6
  482.7 4.2 merge_sources.6
  487.2 4.7 conditional.7
  488.5 3.5 merge_sources.7
  491.9 1.4 collective-permute-start.32
  493.9 43.9 %weight_grads.1 = (f32[8,1536,512]{2,1,0:T(8,128)}, f32[8,1536,512]{2,1,0:T(8,128)}, f32[8,512,1536]{2,1,0:T(8,128)}) custom-call(bf16[8,144,1536]{2,1,0:T(8,128)(2,1)} %get-tuple-element.236.refs_0_, bf16[8,144,1536]{2,1,0:T(8,128)(2,1)} %get-tuple-element.237.refs_1_, bf16[8,144,1536]{2,1,0:T(8,128)(2,1)} %get-tuple-element.238.refs_2_, ...), custom_call_target="tpu_custom_call" | custom-call | flops 24999999488 | bytes 120000000 | tf_op jit(solution)/shard_map/weight_grads/pallas_call | solution.py:351
  537.8 5.3 collect.3
  543.2 7.5 %collective-permute-done.30.refs_2_ = bf16[256,1536]{1,0:T(8,128)(2,1)S(1)} collective-permute-done((bf16[256,1536]{1,0:T(8,128)(2,1)S(1)}, bf16[256,1536]{1,0:T(8,128)(2,1)S(1)}, u32[]{:S(2)}, u32[]{:S(2)}) %collective-permute-start.30) | collective-permute-done | bytes 786464 | tf_op jit(solution)/shard_map/ppermute | solution.py:454
  550.7 0.9 copy-done.6
  551.6 5.3 collect.2
  (130 shorter events, 19.6 us)
Async XLA Ops:
  0.6 74.4 %collective-permute-start.13 = (bf16[512,1536]{1,0:T(8,128)(2,1)}, bf16[512,1536]{1,0:T(8,128)(2,1)}, u32[]{:S(2)}, u32[]{:S(2)}) collective-permute-start(bf16[512,1536]{1,0:T(8,128)(2,1)} %xa_ref.1), channel_id=1, source_target_pairs={{0,4},{4,0},{1,5},{5,1},{2,6},{6,2},{3,7},{7,3}} | collective-permute-start | bytes 4718600 | tf_op jit(solution)/shard_map/ppermute | solution.py:451
  4.0 71.1 %collective-permute-start.25 = (bf16[512,1536]{1,0:T(8,128)(2,1)}, bf16[512,1536]{1,0:T(8,128)(2,1)}, u32[]{:S(2)}, u32[]{:S(2)}) collective-permute-start(bf16[512,1536]{1,0:T(8,128)(2,1)} %xa_ref.1), channel_id=1, source_target_pairs={{0,2},{1,3},{2,0},{3,1},{4,6},{5,7},{6,4},{7,5}} | collective-permute-start | bytes 4718600 | tf_op jit(solution)/shard_map/ppermute | solution.py:454
  6.9 33.2 %collective-permute-start.8 = (f32[1,12,512]{2,1,0:T(8,128)S(1)}, f32[1,12,512]{2,1,0:T(8,128)S(1)}, u32[]{:S(2)}, u32[]{:S(2)}) collective-permute-start(f32[1,12,512]{2,1,0:T(8,128)S(1)} %maximum_bitcast_fusion), channel_id=1, source_target_pairs={{0,4},{4,0},{1,5},{5,1},{2,6},{6,2},{3,7},{7,3}} | collective-permute-start | bytes 73736 | tf_op jit(solution)/shard_map/ppermute | solution.py:451
  7.5 68.0 %collective-permute-start.16 = (bf16[512,1536]{1,0:T(8,128)(2,1)}, bf16[512,1536]{1,0:T(8,128)(2,1)}, u32[]{:S(2)}, u32[]{:S(2)}) collective-permute-start(bf16[512,1536]{1,0:T(8,128)(2,1)} %dya_ref.1), channel_id=1, source_target_pairs={{0,4},{4,0},{1,5},{5,1},{2,6},{6,2},{3,7},{7,3}} | collective-permute-start | bytes 4718600 | tf_op jit(solution)/shard_map/ppermute | solution.py:451
  40.2 1.3 collective-permute-start.9
  41.4 5.8 %collective-permute-start.10 = (f32[4,12,512]{2,1,0:T(8,128)S(1)}, f32[4,12,512]{2,1,0:T(8,128)S(1)}, u32[]{:S(2)}, u32[]{:S(2)}) collective-permute-start(f32[4,12,512]{2,1,0:T(8,128)S(1)} %pad_maximum_fusion), channel_id=1, source_target_pairs={{0,2},{1,3},{2,0},{3,1},{4,6},{5,7},{6,4},{7,5}} | collective-permute-start | bytes 294920 | tf_op jit(solution)/shard_map/ppermute | solution.py:454
  43.5 35.2 %collective-permute-start.11 = (bf16[512,1536]{1,0:T(8,128)(2,1)}, bf16[512,1536]{1,0:T(8,128)(2,1)}, u32[]{:S(2)}, u32[]{:S(2)}) collective-permute-start(bf16[512,1536]{1,0:T(8,128)(2,1)} %xa_ref.1), channel_id=1, source_target_pairs={{0,1},{1,0},{2,3},{3,2},{4,5},{5,4},{6,7},{7,6}} | collective-permute-start | bytes 4718600 | tf_op jit(solution)/shard_map/ppermute | solution.py:454
  48.9 24.5 %copy-start.4 = (bf16[512,1536]{1,0:T(8,128)(2,1)S(1)}, bf16[512,1536]{1,0:T(8,128)(2,1)}, u32[]{:S(2)}) copy-start(bf16[512,1536]{1,0:T(8,128)(2,1)} %dya_ref.1) | copy-start | bytes 4718596
  60.7 12.7 %collective-permute-start.23 = (f32[2,4,432]{2,1,0:T(4,128)S(1)}, f32[2,4,432]{2,1,0:T(4,128)S(1)}, u32[]{:S(2)}, u32[]{:S(2)}) collective-permute-start(f32[2,4,432]{2,1,0:T(4,128)S(1)} %pad_maximum_fusion.2), channel_id=1, source_target_pairs={{0,4},{4,0},{1,5},{5,1},{2,6},{6,2},{3,7},{7,3}} | collective-permute-start | bytes 41480 | tf_op jit(solution)/shard_map/ppermute | solution.py:451
  73.4 37.4 %collective-permute-start.27 = (bf16[512,1536]{1,0:T(8,128)(2,1)S(1)}, bf16[512,1536]{1,0:T(8,128)(2,1)}, u32[]{:S(2)}, u32[]{:S(2)}) collective-permute-start(bf16[512,1536]{1,0:T(8,128)(2,1)S(1)} %copy-done.4), channel_id=1, source_target_pairs={{0,2},{1,3},{2,0},{3,1},{4,6},{5,7},{6,4},{7,5}} | collective-permute-start | bytes 4718600 | tf_op jit(solution)/shard_map/ppermute | solution.py:454
  75.1 35.7 %collective-permute-start.20 = (bf16[512,1536]{1,0:T(8,128)(2,1)}, bf16[512,1536]{1,0:T(8,128)(2,1)}, u32[]{:S(2)}, u32[]{:S(2)}) collective-permute-start(bf16[512,1536]{1,0:T(8,128)(2,1)} %collective-permute-done.13.xa_ref), channel_id=1, source_target_pairs={{0,1},{1,0},{2,3},{3,2},{4,5},{5,4},{6,7},{7,6}} | collective-permute-start | bytes 4718600 | tf_op jit(solution)/shard_map/ppermute | solution.py:454
  75.1 69.4 %collective-permute-start.14 = (bf16[512,1536]{1,0:T(8,128)(2,1)}, bf16[512,1536]{1,0:T(8,128)(2,1)}, u32[]{:S(2)}, u32[]{:S(2)}) collective-permute-start(bf16[512,1536]{1,0:T(8,128)(2,1)} %collective-permute-done.13.xa_ref), channel_id=1, source_target_pairs={{0,2},{1,3},{2,0},{3,1},{4,6},{5,7},{6,4},{7,5}} | collective-permute-start | bytes 4718600 | tf_op jit(solution)/shard_map/ppermute | solution.py:454
  75.4 101.1 %collective-permute-start.17 = (bf16[512,1536]{1,0:T(8,128)(2,1)}, bf16[512,1536]{1,0:T(8,128)(2,1)}, u32[]{:S(2)}, u32[]{:S(2)}) collective-permute-start(bf16[512,1536]{1,0:T(8,128)(2,1)} %collective-permute-done.16.dya_ref), channel_id=1, source_target_pairs={{0,2},{1,3},{2,0},{3,1},{4,6},{5,7},{6,4},{7,5}} | collective-permute-start | bytes 4718600 | tf_op jit(solution)/shard_map/ppermute | solution.py:454
  78.6 128.6 %collective-permute-start.19 = (bf16[512,1536]{1,0:T(8,128)(2,1)}, bf16[512,1536]{1,0:T(8,128)(2,1)}, u32[]{:S(2)}, u32[]{:S(2)}) collective-permute-start(bf16[512,1536]{1,0:T(8,128)(2,1)} %collective-permute-done.16.dya_ref), channel_id=1, source_target_pairs={{0,1},{1,0},{2,3},{3,2},{4,5},{5,4},{6,7},{7,6}} | collective-permute-start | bytes 4718600 | tf_op jit(solution)/shard_map/ppermute | solution.py:454
  110.7 258.4 %collective-permute-start.26 = (bf16[512,1536]{1,0:T(8,128)(2,1)}, bf16[512,1536]{1,0:T(8,128)(2,1)}, u32[]{:S(2)}, u32[]{:S(2)}) collective-permute-start(bf16[512,1536]{1,0:T(8,128)(2,1)} %collective-permute-done.25.xa_ref), channel_id=1, source_target_pairs={{0,1},{1,0},{2,3},{3,2},{4,5},{5,4},{6,7},{7,6}} | collective-permute-start | bytes 4718600 | tf_op jit(solution)/shard_map/ppermute | solution.py:454
  110.7 259.0 %collective-permute-start.28 = (bf16[512,1536]{1,0:T(8,128)(2,1)}, bf16[512,1536]{1,0:T(8,128)(2,1)}, u32[]{:S(2)}, u32[]{:S(2)}) collective-permute-start(bf16[512,1536]{1,0:T(8,128)(2,1)} %collective-permute-done.27.dya_ref), channel_id=1, source_target_pairs={{0,1},{1,0},{2,3},{3,2},{4,5},{5,4},{6,7},{7,6}} | collective-permute-start | bytes 4718600 | tf_op jit(solution)/shard_map/ppermute | solution.py:454
  144.4 92.2 %collective-permute-start.15 = (bf16[512,1536]{1,0:T(8,128)(2,1)}, bf16[512,1536]{1,0:T(8,128)(2,1)}, u32[]{:S(2)}, u32[]{:S(2)}) collective-permute-start(bf16[512,1536]{1,0:T(8,128)(2,1)} %collective-permute-done.14.xa_ref), channel_id=1, source_target_pairs={{0,1},{1,0},{2,3},{3,2},{4,5},{5,4},{6,7},{7,6}} | collective-permute-start | bytes 4718600 | tf_op jit(solution)/shard_map/ppermute | solution.py:454
  176.5 61.7 %collective-permute-start.18 = (bf16[512,1536]{1,0:T(8,128)(2,1)}, bf16[512,1536]{1,0:T(8,128)(2,1)}, u32[]{:S(2)}, u32[]{:S(2)}) collective-permute-start(bf16[512,1536]{1,0:T(8,128)(2,1)} %collective-permute-done.17.dya_ref), channel_id=1, source_target_pairs={{0,1},{1,0},{2,3},{3,2},{4,5},{5,4},{6,7},{7,6}} | collective-permute-start | bytes 4718600 | tf_op jit(solution)/shard_map/ppermute | solution.py:454
  207.3 75.6 %collective-permute-start.12 = (bf16[512,1536]{1,0:T(8,128)(2,1)S(1)}, bf16[512,1536]{1,0:T(8,128)(2,1)}, u32[]{:S(2)}, u32[]{:S(2)}) collective-permute-start(bf16[512,1536]{1,0:T(8,128)(2,1)S(1)} %copy-done.4), channel_id=1, source_target_pairs={{0,1},{1,0},{2,3},{3,2},{4,5},{5,4},{6,7},{7,6}} | collective-permute-start | bytes 4718600 | tf_op jit(solution)/shard_map/ppermute | solution.py:454
  236.7 85.2 %collective-permute-start.21 = (bf16[432,1536]{1,0:T(8,128)(2,1)}, bf16[432,1536]{1,0:T(8,128)(2,1)}, u32[]{:S(2)}, u32[]{:S(2)}) collective-permute-start(bf16[432,1536]{1,0:T(8,128)(2,1)} %get-tuple-element.210), channel_id=1, source_target_pairs={{0,4},{4,0},{1,5},{5,1},{2,6},{6,2},{3,7},{7,3}} | collective-permute-start | bytes 3981320 | tf_op jit(solution)/shard_map/ppermute | solution.py:451
  238.2 83.8 %collective-permute-start.22 = (bf16[432,1536]{1,0:T(8,128)(2,1)}, bf16[432,1536]{1,0:T(8,128)(2,1)}, u32[]{:S(2)}, u32[]{:S(2)}) collective-permute-start(bf16[432,1536]{1,0:T(8,128)(2,1)} %get-tuple-element.211), channel_id=1, source_target_pairs={{0,4},{4,0},{1,5},{5,1},{2,6},{6,2},{3,7},{7,3}} | collective-permute-start | bytes 3981320 | tf_op jit(solution)/shard_map/ppermute | solution.py:451
  282.9 49.9 %collective-permute-start.33 = (bf16[432,1536]{1,0:T(8,128)(2,1)}, bf16[432,1536]{1,0:T(8,128)(2,1)}, u32[]{:S(2)}, u32[]{:S(2)}) collective-permute-start(bf16[432,1536]{1,0:T(8,128)(2,1)} %get-tuple-element.224), channel_id=1, source_target_pairs={{0,4},{4,0},{1,5},{5,1},{2,6},{6,2},{3,7},{7,3}} | collective-permute-start | bytes 3981320 | tf_op jit(solution)/shard_map/ppermute | solution.py:451
  322.0 8.0 %copy-start.3 = (s32[512,6]{0,1:T(8,128)S(1)}, s32[512,6]{0,1:T(8,128)}, u32[]{:S(2)}) copy-start(s32[512,6]{0,1:T(8,128)} %param.18) | copy-start | bytes 36868
  329.4 32.3 %collective-permute-start.34 = (bf16[432,1536]{1,0:T(8,128)(2,1)}, bf16[432,1536]{1,0:T(8,128)(2,1)}, u32[]{:S(2)}, u32[]{:S(2)}) collective-permute-start(bf16[432,1536]{1,0:T(8,128)(2,1)} %get-tuple-element.225), channel_id=1, source_target_pairs={{0,4},{4,0},{1,5},{5,1},{2,6},{6,2},{3,7},{7,3}} | collective-permute-start | bytes 3981320 | tf_op jit(solution)/shard_map/ppermute | solution.py:451
  331.3 150.1 %collective-permute-start.29 = (bf16[432,1536]{1,0:T(8,128)(2,1)}, bf16[432,1536]{1,0:T(8,128)(2,1)}, u32[]{:S(2)}, u32[]{:S(2)}) collective-permute-start(bf16[432,1536]{1,0:T(8,128)(2,1)} %get-tuple-element.218), channel_id=1, source_target_pairs={{0,4},{4,0},{1,5},{5,1},{2,6},{6,2},{3,7},{7,3}} | collective-permute-start | bytes 3981320 | tf_op jit(solution)/shard_map/ppermute | solution.py:451
  367.1 120.1 %collective-permute-start.31 = (bf16[432,1536]{1,0:T(8,128)(2,1)}, bf16[432,1536]{1,0:T(8,128)(2,1)}, u32[]{:S(2)}, u32[]{:S(2)}) collective-permute-start(bf16[432,1536]{1,0:T(8,128)(2,1)} %get-tuple-element.221), channel_id=1, source_target_pairs={{0,4},{4,0},{1,5},{5,1},{2,6},{6,2},{3,7},{7,3}} | collective-permute-start | bytes 3981320 | tf_op jit(solution)/shard_map/ppermute | solution.py:451
  367.7 79.4 %collective-permute-start.36 = (bf16[432,1536]{1,0:T(8,128)(2,1)}, bf16[432,1536]{1,0:T(8,128)(2,1)}, u32[]{:S(2)}, u32[]{:S(2)}) collective-permute-start(bf16[432,1536]{1,0:T(8,128)(2,1)} %get-tuple-element.231), channel_id=1, source_target_pairs={{0,4},{4,0},{1,5},{5,1},{2,6},{6,2},{3,7},{7,3}} | collective-permute-start | bytes 3981320 | tf_op jit(solution)/shard_map/ppermute | solution.py:451
  369.2 104.5 %collective-permute-start.37 = (bf16[432,1536]{1,0:T(8,128)(2,1)}, bf16[432,1536]{1,0:T(8,128)(2,1)}, u32[]{:S(2)}, u32[]{:S(2)}) collective-permute-start(bf16[432,1536]{1,0:T(8,128)(2,1)} %get-tuple-element.232), channel_id=1, source_target_pairs={{0,4},{4,0},{1,5},{5,1},{2,6},{6,2},{3,7},{7,3}} | collective-permute-start | bytes 3981320 | tf_op jit(solution)/shard_map/ppermute | solution.py:451
  369.7 123.6 %collective-permute-start.35 = (bf16[256,1536]{1,0:T(8,128)(2,1)}, bf16[256,1536]{1,0:T(8,128)(2,1)}, u32[]{:S(2)}, u32[]{:S(2)}) collective-permute-start(bf16[256,1536]{1,0:T(8,128)(2,1)} %get-tuple-element.228), channel_id=1, source_target_pairs={{0,1},{1,0},{2,3},{3,2},{4,5},{5,4},{6,7},{7,6}} | collective-permute-start | bytes 2359304 | tf_op jit(solution)/shard_map/ppermute | solution.py:454
  480.0 63.2 %collective-permute-start.24 = (bf16[256,1536]{1,0:T(8,128)(2,1)}, bf16[256,1536]{1,0:T(8,128)(2,1)}, u32[]{:S(2)}, u32[]{:S(2)}) collective-permute-start(bf16[256,1536]{1,0:T(8,128)(2,1)} %get-tuple-element.214), channel_id=1, source_target_pairs={{0,1},{1,0},{2,3},{3,2},{4,5},{5,4},{6,7},{7,6}} | collective-permute-start | bytes 2359304 | tf_op jit(solution)/shard_map/ppermute | solution.py:454
  480.0 57.8 %collective-permute-start.38 = (bf16[256,1536]{1,0:T(8,128)(2,1)}, bf16[256,1536]{1,0:T(8,128)(2,1)}, u32[]{:S(2)}, u32[]{:S(2)}) collective-permute-start(bf16[256,1536]{1,0:T(8,128)(2,1)} %get-tuple-element.234), channel_id=1, source_target_pairs={{0,2},{1,3},{2,0},{3,1},{4,6},{5,7},{6,4},{7,5}} | collective-permute-start | bytes 2359304 | tf_op jit(solution)/shard_map/ppermute | solution.py:454
  486.9 50.9 %collective-permute-start.39 = (bf16[256,1536]{1,0:T(8,128)(2,1)}, bf16[256,1536]{1,0:T(8,128)(2,1)}, u32[]{:S(2)}, u32[]{:S(2)}) collective-permute-start(bf16[256,1536]{1,0:T(8,128)(2,1)} %get-tuple-element.235), channel_id=1, source_target_pairs={{0,3},{1,2},{2,1},{3,0},{4,7},{5,6},{6,5},{7,4}} | collective-permute-start | bytes 2359304 | tf_op jit(solution)/shard_map/ppermute | solution.py:454
  487.2 6.1 %copy-start.2 = (bf16[256,1536]{1,0:T(8,128)(2,1)S(1)}, bf16[256,1536]{1,0:T(8,128)(2,1)}, u32[]{:S(2)}) copy-start(bf16[256,1536]{1,0:T(8,128)(2,1)} %get-tuple-element.354) | copy-start | bytes 2359300
  491.9 51.2 %collective-permute-start.32 = (bf16[256,1536]{1,0:T(8,128)(2,1)S(1)}, bf16[256,1536]{1,0:T(8,128)(2,1)S(1)}, u32[]{:S(2)}, u32[]{:S(2)}) collective-permute-start(bf16[256,1536]{1,0:T(8,128)(2,1)S(1)} %get-tuple-element.355), channel_id=1, source_target_pairs={{0,3},{1,2},{2,1},{3,0},{4,7},{5,6},{6,5},{7,4}} | collective-permute-start | bytes 2359304 | tf_op jit(solution)/shard_map/ppermute | solution.py:454
  493.4 57.3 %collective-permute-start.30 = (bf16[256,1536]{1,0:T(8,128)(2,1)S(1)}, bf16[256,1536]{1,0:T(8,128)(2,1)S(1)}, u32[]{:S(2)}, u32[]{:S(2)}) collective-permute-start(bf16[256,1536]{1,0:T(8,128)(2,1)S(1)} %copy-done.2), channel_id=1, source_target_pairs={{0,2},{1,3},{2,0},{3,1},{4,6},{5,7},{6,4},{7,5}} | collective-permute-start | bytes 2359304 | tf_op jit(solution)/shard_map/ppermute | solution.py:454
  543.1 7.5 %copy-start.5 = (bf16[256,1536]{1,0:T(8,128)(2,1)}, bf16[256,1536]{1,0:T(8,128)(2,1)S(1)}, u32[]{:S(2)}) copy-start(bf16[256,1536]{1,0:T(8,128)(2,1)S(1)} %collective-permute-done.32.refs_3_) | copy-start | bytes 2359300
  550.7 0.9 copy-start.6
